TPU v7x, 32 devices: a whole 2x2x4 slice. The times are simulated.
32 devices in a mesh: dp: 4 (over y, x), ctx: 4 (over z), tensor: 2 (over core).
Axes of the slice: x: 2, y: 2, z: 4, core: 2. Of those that a mesh axis runs over, the one named last changes fastest.
Arguments:
- layer_input: bfloat16 [8192, 1536], P(('dp', 'ctx', 'tensor')), may hold values from -6 to 6
- teacher: bfloat16 [8192, 1536], P(('dp', 'ctx', 'tensor')), may hold values from -6 to 6
- cotangent: bfloat16 [8192, 1536], P(('dp', 'ctx', 'tensor')), may hold values from -6 to 6
- segment_ids: int32 [8192], P('dp'), may hold values from 0 to 8191, as said below
- positions: int32 [8192], P('dp'), may hold values from 0 to 2047, as said below
- valid_mask: int32 [8192], P('dp'), may hold values from 0 to 1
- gain_attn: bfloat16 [1536], replicated, may hold values from 0.5 to 1.5
- query_weight: bfloat16 [1536, 1536], P(('dp', 'ctx'), 'tensor'), may hold values from -0.15625 to 0.15625
- query_bias: bfloat16 [1536], replicated, may hold values from -3 to 3
- key_weight: bfloat16 [1536, 256], P(('dp', 'ctx'), 'tensor'), may hold values from -0.15625 to 0.15625
- key_bias: bfloat16 [256], replicated, may hold values from -3 to 3
- value_weight: bfloat16 [1536, 256], P(('dp', 'ctx'), 'tensor'), may hold values from -0.15625 to 0.15625
- value_bias: bfloat16 [256], replicated, may hold values from -3 to 3
- out_weight: bfloat16 [1536, 1536], P('tensor', ('dp', 'ctx')), may hold values from -1.25 to 1.25
- gain_mlp: bfloat16 [1536], replicated, may hold values from 0.5 to 1.5
- gate_weight: bfloat16 [1536, 8960], P(('dp', 'ctx'), 'tensor'), may hold values from -0.15625 to 0.15625
- up_weight: bfloat16 [1536, 8960], P(('dp', 'ctx'), 'tensor'), may hold values from -0.15625 to 0.15625
- down_weight: bfloat16 [8960, 1536], P('tensor', ('dp', 'ctx')), may hold values from -0.0625 to 0.0625
Outputs:
- layer_out: bfloat16 [8192, 1536], P(('dp', 'ctx', 'tensor'))
- loss: float32 [], replicated
- grad_input: float32 [8192, 1536], P(('dp', 'ctx', 'tensor'))
- grad_gain_attn: float32 [1536], replicated
- grad_query: float32 [1536, 1536], P(('dp', 'ctx'), 'tensor')
- grad_query_bias: float32 [1536], replicated
- grad_key: float32 [1536, 256], P(('dp', 'ctx'), 'tensor')
- grad_key_bias: float32 [256], replicated
- grad_value: float32 [1536, 256], P(('dp', 'ctx'), 'tensor')
- grad_value_bias: float32 [256], replicated
- grad_out: float32 [1536, 1536], P('tensor', ('dp', 'ctx'))
- grad_gain_mlp: float32 [1536], replicated
- grad_gate: float32 [1536, 8960], P(('dp', 'ctx'), 'tensor')
- grad_up: float32 [1536, 8960], P(('dp', 'ctx'), 'tensor')
- grad_down: float32 [8960, 1536], P('tensor', ('dp', 'ctx'))
Inputs may be any that keep to these rules, and one draw needn't show every extreme that they name: `segment_ids`: the index of the first token of the token's document; never falls along the tokens, every sequence of 2048 tokens begins a new document, and the last token alone forms a document. `positions`: 0 at a document's first token, rising by one token by token within the document; the first sequence is one document.
All inputs are finite; a program needn't handle non-finite values.
Results may differ from a plain program's by a relative error of at most 0.024.
Values may be sent and summed in bfloat16 or wider, within the bound.
A program may use at most 192 MiB of HBM per device.

v0:
```python
import math

import jax
import jax.numpy as jnp
from jax import lax
from jax.sharding import PartitionSpec as P

D = 1536
HEAD = 128


EPS = 1e-06
THETA = 10000.0
VERY_LOW = -1e30


def rope_tables(places):
    half_dim = HEAD // 2
    frequency = THETA ** (-(jnp.arange(half_dim, dtype=jnp.float32) * 2.0 / HEAD))
    angles = places.astype(jnp.float32)[:, None] * frequency[None, :]
    return (jnp.cos(angles), jnp.sin(angles))


def rotate(stacked, cosine, sine_table):
    half_dim = HEAD // 2
    first_half = stacked[..., :half_dim]
    second_half = stacked[..., half_dim:]
    cosine = cosine[:, None, :]
    sine_table = sine_table[:, None, :]
    return jnp.concatenate(
        [
            first_half * cosine - second_half * sine_table,
            second_half * cosine + first_half * sine_table,
        ],
        axis=-1,
    )


def matmul(first_op, second_op):
    return jnp.dot(first_op, second_op, preferred_element_type=jnp.float32)


def matmul_tn(first_op, second_op):
    return lax.dot_general(
        first_op, second_op, (((0,), (0,)), ((), ())), preferred_element_type=jnp.float32
    )


def matmul_nt(first_op, second_op):
    return lax.dot_general(
        first_op, second_op, (((1,), (1,)), ((), ())), preferred_element_type=jnp.float32
    )


def gather_weights(
    query_weight, key_weight, value_weight, out_weight, gate_weight, up_weight, down_weight
):
    return (
        lax.all_gather(query_weight, ("dp", "ctx"), axis=0, tiled=True),
        lax.all_gather(key_weight, ("dp", "ctx"), axis=0, tiled=True),
        lax.all_gather(value_weight, ("dp", "ctx"), axis=0, tiled=True),
        lax.all_gather(out_weight, ("dp", "ctx"), axis=1, tiled=True),
        lax.all_gather(gate_weight, ("dp", "ctx"), axis=0, tiled=True),
        lax.all_gather(up_weight, ("dp", "ctx"), axis=0, tiled=True),
        lax.all_gather(down_weight, ("dp", "ctx"), axis=1, tiled=True),
    )


def norm_back(grad_normed, normed, inverse, gain):
    scaled = grad_normed * gain
    return inverse * (scaled - normed * jnp.mean(scaled * normed, axis=1, keepdims=True))


def per_device(
    layer_input,
    teacher,
    cotangent,
    segment_ids,
    positions,
    valid_mask,
    gain_attn,
    query_weight,
    query_bias,
    key_weight,
    key_bias,
    value_weight,
    value_bias,
    out_weight,
    gain_mlp,
    gate_weight,
    up_weight,
    down_weight,
):
    tensor_rank = lax.axis_index("tensor")
    ctx_rank = lax.axis_index("ctx")
    own_rows = layer_input.shape[0]
    shard_rows = own_rows * lax.axis_size("tensor")
    seq_len = segment_ids.shape[0]
    q_width = query_weight.shape[1]
    kv_width = key_weight.shape[1]
    kv_local = kv_width // HEAD
    group_size = q_width // kv_width
    score_scale = 1.0 / math.sqrt(HEAD)
    key_rows = math.gcd(512, seq_len)
    block_count = seq_len // key_rows
    first_row = ctx_rank * shard_rows
    own_first = first_row + tensor_rank * own_rows
    full_query, full_key, full_value, full_out, full_gate, full_up, full_down = gather_weights(
        query_weight, key_weight, value_weight, out_weight, gate_weight, up_weight, down_weight
    )
    inputs = layer_input.astype(jnp.float32)
    gain_one = gain_attn.astype(jnp.float32)
    gain_two = gain_mlp.astype(jnp.float32)
    scale_attn = lax.rsqrt(jnp.mean(inputs * inputs, axis=1, keepdims=True) + EPS)
    normed_attn = inputs * scale_attn
    normed_rows = lax.all_gather(
        (normed_attn * gain_one).astype(jnp.bfloat16), "tensor", axis=0, tiled=True
    )
    bias_query = lax.dynamic_slice_in_dim(query_bias, tensor_rank * q_width, q_width).astype(
        jnp.float32
    )
    bias_key = lax.dynamic_slice_in_dim(key_bias, tensor_rank * kv_width, kv_width).astype(
        jnp.float32
    )
    bias_value = lax.dynamic_slice_in_dim(value_bias, tensor_rank * kv_width, kv_width).astype(
        jnp.float32
    )
    places = lax.dynamic_slice_in_dim(positions, first_row, shard_rows)
    cosine, sine_table = rope_tables(places)
    query_pre = matmul(normed_rows, full_query) + bias_query
    key_pre = matmul(normed_rows, full_key) + bias_key
    value_pre = matmul(normed_rows, full_value) + bias_value
    queries = (
        rotate(query_pre.reshape(shard_rows, q_width // HEAD, HEAD), cosine, sine_table)
        .astype(jnp.bfloat16)
        .reshape(shard_rows, kv_local, group_size, HEAD)
    )
    own_keys = (
        rotate(key_pre.reshape(shard_rows, kv_local, HEAD), cosine, sine_table)
        .astype(jnp.bfloat16)
        .reshape(shard_rows, kv_width)
    )
    all_keys, all_values = (
        lax.all_gather(own_keys, "ctx", axis=0, tiled=True),
        lax.all_gather(value_pre.astype(jnp.bfloat16), "ctx", axis=0, tiled=True),
    )
    query_index = first_row + jnp.arange(shard_rows, dtype=jnp.int32)
    query_seg = lax.dynamic_slice_in_dim(segment_ids, first_row, shard_rows)

    def block_scores(offset):
        key_block = lax.dynamic_slice_in_dim(all_keys, offset, key_rows).reshape(
            key_rows, kv_local, HEAD
        )
        value_block = lax.dynamic_slice_in_dim(all_values, offset, key_rows).reshape(
            key_rows, kv_local, HEAD
        )
        raw_scores = (
            jnp.einsum("icgd,jcd->cgij", queries, key_block, preferred_element_type=jnp.float32)
            * score_scale
        )
        key_index = offset + jnp.arange(key_rows, dtype=jnp.int32)
        key_seg = lax.dynamic_slice_in_dim(segment_ids, offset, key_rows)
        key_valid = lax.dynamic_slice_in_dim(valid_mask, offset, key_rows) > 0
        same_doc = query_seg[:, None] == key_seg[None, :]
        earlier = key_index[None, :] <= query_index[:, None]
        itself = key_index[None, :] == query_index[:, None]
        allowed = same_doc & earlier & (key_valid[None, :] | itself)
        return (jnp.where(allowed, raw_scores, -jnp.inf), key_block, value_block)

    def over_blocks(block_work, carried):

        def advance(block_index, current):
            offset = block_index * key_rows
            return block_work(offset, current)

        return lax.fori_loop(0, block_count, advance, carried)

    def row_stats(offset, current):
        running_max, running_sum = current
        scores, key_block, value_block = block_scores(offset)
        new_max = jnp.maximum(running_max, jnp.max(scores, axis=3))
        running_sum = running_sum * jnp.exp(running_max - new_max) + jnp.sum(
            jnp.exp(scores - new_max[..., None]), axis=3
        )
        return (new_max, running_sum)

    stat_shape = (kv_local, group_size, shard_rows)
    running_max, running_sum = over_blocks(
        row_stats, (jnp.full(stat_shape, VERY_LOW, jnp.float32), jnp.zeros(stat_shape, jnp.float32))
    )
    log_total = running_max + jnp.log(running_sum)

    def attend(offset, mixture):
        scores, key_block, value_block = block_scores(offset)
        attn_probs = jnp.exp(scores - log_total[..., None]).astype(jnp.bfloat16)
        return mixture + jnp.einsum(
            "cgij,jcd->icgd", attn_probs, value_block, preferred_element_type=jnp.float32
        )

    mixture = over_blocks(attend, jnp.zeros((shard_rows, kv_local, group_size, HEAD), jnp.float32))
    heads_out = mixture.reshape(shard_rows, q_width).astype(jnp.bfloat16)
    attention = lax.psum_scatter(
        matmul(heads_out, full_out), "tensor", scatter_dimension=0, tiled=True
    )
    residual_mid = inputs + attention
    scale_mlp = lax.rsqrt(jnp.mean(residual_mid * residual_mid, axis=1, keepdims=True) + EPS)
    normed_mlp = residual_mid * scale_mlp
    mlp_rows = lax.all_gather(
        (normed_mlp * gain_two).astype(jnp.bfloat16), "tensor", axis=0, tiled=True
    )
    gate_act = matmul(mlp_rows, full_gate)
    up_act = matmul(mlp_rows, full_up)
    sigmoid = jax.nn.sigmoid(gate_act)
    silu_gate = gate_act * sigmoid
    hidden = (silu_gate * up_act).astype(jnp.bfloat16)
    branch = lax.psum_scatter(
        matmul(hidden, full_down).astype(jnp.bfloat16), "tensor", scatter_dimension=0, tiled=True
    ).astype(jnp.float32)
    layer_result = residual_mid + branch
    valid_own = lax.dynamic_slice_in_dim(valid_mask, own_first, own_rows).astype(jnp.float32)
    difference = layer_result - teacher.astype(jnp.float32)
    squared_sum, valid_count = lax.psum(
        (jnp.sum(valid_own[:, None] * difference * difference), jnp.sum(valid_own)),
        ("dp", "ctx", "tensor"),
    )
    loss_value = squared_sum / (valid_count * D)
    grad_result = cotangent.astype(jnp.float32) + 2.0 * valid_own[:, None] * difference / (
        valid_count * D
    )
    grad_branch = lax.all_gather(grad_result.astype(jnp.bfloat16), "tensor", axis=0, tiled=True)
    grad_down = matmul_tn(hidden, grad_branch)
    grad_hidden = matmul_nt(grad_branch, full_down)
    grad_gate_act = (grad_hidden * up_act * sigmoid * (1.0 + gate_act * (1.0 - sigmoid))).astype(
        jnp.bfloat16
    )
    grad_up_act = (grad_hidden * silu_gate).astype(jnp.bfloat16)
    grad_gate = matmul_tn(mlp_rows, grad_gate_act)
    grad_up = matmul_tn(mlp_rows, grad_up_act)
    grad_mlp_rows = lax.psum_scatter(
        (matmul_nt(grad_gate_act, full_gate) + matmul_nt(grad_up_act, full_up)).astype(
            jnp.bfloat16
        ),
        "tensor",
        scatter_dimension=0,
        tiled=True,
    ).astype(jnp.float32)
    grad_gain_mlp = jnp.sum(grad_mlp_rows * normed_mlp, axis=0)
    grad_mid = grad_result + norm_back(grad_mlp_rows, normed_mlp, scale_mlp, gain_two)
    grad_attn_rows = lax.all_gather(grad_mid.astype(jnp.bfloat16), "tensor", axis=0, tiled=True)
    grad_out = matmul_tn(heads_out, grad_attn_rows)
    grad_heads = (
        matmul_nt(grad_attn_rows, full_out)
        .astype(jnp.bfloat16)
        .reshape(shard_rows, kv_local, group_size, HEAD)
    )

    def deltas(offset, running):
        scores, key_block, value_block = block_scores(offset)
        attn_probs = jnp.exp(scores - log_total[..., None])
        grad_probs = jnp.einsum(
            "icgd,jcd->cgij", grad_heads, value_block, preferred_element_type=jnp.float32
        )
        return running + jnp.sum(attn_probs * grad_probs, axis=3)

    delta = over_blocks(deltas, jnp.zeros(stat_shape, jnp.float32))

    def backward_block(offset, current):
        grad_queries, grad_keys, grad_values = current
        scores, key_block, value_block = block_scores(offset)
        attn_probs = jnp.exp(scores - log_total[..., None])
        grad_probs = jnp.einsum(
            "icgd,jcd->cgij", grad_heads, value_block, preferred_element_type=jnp.float32
        )
        grad_scores = (attn_probs * (grad_probs - delta[..., None])).astype(jnp.bfloat16)
        grad_queries = (
            grad_queries
            + jnp.einsum(
                "cgij,jcd->icgd", grad_scores, key_block, preferred_element_type=jnp.float32
            )
            * score_scale
        )
        key_piece = (
            jnp.einsum("cgij,icgd->jcd", grad_scores, queries, preferred_element_type=jnp.float32)
            * score_scale
        )
        value_piece = jnp.einsum(
            "cgij,icgd->jcd",
            attn_probs.astype(jnp.bfloat16),
            grad_heads,
            preferred_element_type=jnp.float32,
        )
        grad_keys = lax.dynamic_update_slice_in_dim(
            grad_keys,
            lax.dynamic_slice_in_dim(grad_keys, offset, key_rows)
            + key_piece.reshape(key_rows, kv_width),
            offset,
            0,
        )
        grad_values = lax.dynamic_update_slice_in_dim(
            grad_values,
            lax.dynamic_slice_in_dim(grad_values, offset, key_rows)
            + value_piece.reshape(key_rows, kv_width),
            offset,
            0,
        )
        return (grad_queries, grad_keys, grad_values)

    grad_queries, grad_keys, grad_values = over_blocks(
        backward_block,
        (
            jnp.zeros((shard_rows, kv_local, group_size, HEAD), jnp.float32),
            jnp.zeros((seq_len, kv_width), jnp.float32),
            jnp.zeros((seq_len, kv_width), jnp.float32),
        ),
    )
    grad_key_own, grad_value_own = (
        lax.psum_scatter(
            grad_keys.astype(jnp.bfloat16), "ctx", scatter_dimension=0, tiled=True
        ).astype(jnp.float32),
        lax.psum_scatter(
            grad_values.astype(jnp.bfloat16), "ctx", scatter_dimension=0, tiled=True
        ).astype(jnp.float32),
    )
    grad_query_pre = (
        rotate(grad_queries.reshape(shard_rows, q_width // HEAD, HEAD), cosine, -sine_table)
        .reshape(shard_rows, q_width)
        .astype(jnp.bfloat16)
    )
    grad_key_pre = (
        rotate(grad_key_own.reshape(shard_rows, kv_local, HEAD), cosine, -sine_table)
        .reshape(shard_rows, kv_width)
        .astype(jnp.bfloat16)
    )
    grad_value_pre = grad_value_own.astype(jnp.bfloat16)
    grad_query = matmul_tn(normed_rows, grad_query_pre)
    grad_key = matmul_tn(normed_rows, grad_key_pre)
    grad_value = matmul_tn(normed_rows, grad_value_pre)
    grad_normed = lax.psum_scatter(
        (
            matmul_nt(grad_query_pre, full_query)
            + matmul_nt(grad_key_pre, full_key)
            + matmul_nt(grad_value_pre, full_value)
        ).astype(jnp.bfloat16),
        "tensor",
        scatter_dimension=0,
        tiled=True,
    ).astype(jnp.float32)
    grad_gain_attn = jnp.sum(grad_normed * normed_attn, axis=0)
    grad_input = grad_mid + norm_back(grad_normed, normed_attn, scale_attn, gain_one)
    query_bias_grad = lax.dynamic_update_slice_in_dim(
        jnp.zeros((query_bias.shape[0],), jnp.float32),
        jnp.sum(grad_query_pre.astype(jnp.float32), axis=0),
        tensor_rank * q_width,
        0,
    )
    key_bias_grad = lax.dynamic_update_slice_in_dim(
        jnp.zeros((key_bias.shape[0],), jnp.float32),
        jnp.sum(grad_key_pre.astype(jnp.float32), axis=0),
        tensor_rank * kv_width,
        0,
    )
    value_bias_grad = lax.dynamic_update_slice_in_dim(
        jnp.zeros((value_bias.shape[0],), jnp.float32),
        jnp.sum(grad_value_pre.astype(jnp.float32), axis=0),
        tensor_rank * kv_width,
        0,
    )
    shard_query, shard_key, shard_value, shard_out, shard_gate, shard_up, shard_down = (
        lax.psum_scatter(grad_query, ("dp", "ctx"), scatter_dimension=0, tiled=True),
        lax.psum_scatter(grad_key, ("dp", "ctx"), scatter_dimension=0, tiled=True),
        lax.psum_scatter(grad_value, ("dp", "ctx"), scatter_dimension=0, tiled=True),
        lax.psum_scatter(grad_out, ("dp", "ctx"), scatter_dimension=1, tiled=True),
        lax.psum_scatter(grad_gate, ("dp", "ctx"), scatter_dimension=0, tiled=True),
        lax.psum_scatter(grad_up, ("dp", "ctx"), scatter_dimension=0, tiled=True),
        lax.psum_scatter(grad_down, ("dp", "ctx"), scatter_dimension=1, tiled=True),
    )
    summed_gain_attn, summed_query_bias, summed_key_bias, summed_value_bias, summed_gain_mlp = (
        lax.psum(
            (grad_gain_attn, query_bias_grad, key_bias_grad, value_bias_grad, grad_gain_mlp),
            ("dp", "ctx", "tensor"),
        )
    )
    return (
        layer_result.astype(jnp.bfloat16),
        loss_value,
        grad_input,
        summed_gain_attn,
        shard_query,
        summed_query_bias,
        shard_key,
        summed_key_bias,
        shard_value,
        summed_value_bias,
        shard_out,
        summed_gain_mlp,
        shard_gate,
        shard_up,
        shard_down,
    )


def solution(mesh):
    in_specs = (
        P(("dp", "ctx", "tensor"), None),
        P(("dp", "ctx", "tensor"), None),
        P(("dp", "ctx", "tensor"), None),
        P("dp"),
        P("dp"),
        P("dp"),
        P(),
        P(("dp", "ctx"), "tensor"),
        P(),
        P(("dp", "ctx"), "tensor"),
        P(),
        P(("dp", "ctx"), "tensor"),
        P(),
        P("tensor", ("dp", "ctx")),
        P(),
        P(("dp", "ctx"), "tensor"),
        P(("dp", "ctx"), "tensor"),
        P("tensor", ("dp", "ctx")),
    )
    out_specs = (
        P(("dp", "ctx", "tensor"), None),
        P(),
        P(("dp", "ctx", "tensor"), None),
        P(),
        P(("dp", "ctx"), "tensor"),
        P(),
        P(("dp", "ctx"), "tensor"),
        P(),
        P(("dp", "ctx"), "tensor"),
        P(),
        P("tensor", ("dp", "ctx")),
        P(),
        P(("dp", "ctx"), "tensor"),
        P(("dp", "ctx"), "tensor"),
        P("tensor", ("dp", "ctx")),
    )
    return jax.shard_map(
        per_device, mesh=mesh, in_specs=in_specs, out_specs=out_specs, check_vma=False
    )
```

profile of v0, /device:TPU:0, one launch (start us, length us, event | category | flops | bytes accessed | tf_op | source)
XLA Modules:
  0.0 2768.3 jit_solution(15806460646477085716)
XLA Ops:
  13.8 46.8 %all_gather.40 = bf16[1536,128]{1,0:T(8,128)(2,1)S(1)} all-gather(bf16[96,128]{1,0:T(8,128)(2,1)S(1)} %copy-done.44), channel_id=1, replica_groups=mesh['dp'=4,'ctx'=4,'tensor'=2] {'dp','ctx'}, dimensions={0}, use_global_device_ids=true | all-gather | bytes 417792 | tf_op jit(solution)/shard_map/all_gather | solution.py:61
  60.7 42.2 %all_gather.42 = bf16[1536,128]{1,0:T(8,128)(2,1)S(1)} all-gather(bf16[96,128]{1,0:T(8,128)(2,1)S(1)} %copy-done.45), channel_id=1, replica_groups=mesh['dp'=4,'ctx'=4,'tensor'=2] {'dp','ctx'}, dimensions={0}, use_global_device_ids=true | all-gather | bytes 417792 | tf_op jit(solution)/shard_map/all_gather | solution.py:60
  108.0 16.9 all_gather.41
  126.1 16.8 all_gather.43
  143.3 4.2 convolution_add_fusion.3
  150.3 36.7 %while.62 = (s32[]{:T(128)}, f32[1,6,512]{2,1,0:T(8,128)S(1)}, f32[1,6,512]{2,1,0:T(8,128)S(1)}, s32[512]{0:T(512)S(1)}, s32[2048]{0:T(1024)}, /*index=5*/s32[20...) while((s32[]{:T(128)}, f32[1,6,512]{2,1,0:T(8,128)S(1)}, ...), condition=%wide.region_4.5_spmd.clone, body=%wide.region_1.4_spmd.clone.sunk | while | flops 415252992 | bytes 14466258 | solution.py:176
  151.6 3.8 fusion.215
  155.3 4.1 exponential_reduce_fusion.2
  160.8 3.8 fusion.215
  164.5 4.1 exponential_reduce_fusion.2
  169.9 3.8 fusion.215
  173.7 4.1 exponential_reduce_fusion.2
  179.1 3.8 fusion.215
  182.9 4.1 exponential_reduce_fusion.2
  187.0 22.4 while.63
  188.3 3.3 bitcast_add_fusion.9
  192.9 4.7 bitcast_add_fusion.9
  198.8 4.7 bitcast_add_fusion.9
  204.8 4.7 bitcast_add_fusion.9
  211.7 5.0 fusion.138
  217.4 7.1 reduce-scatter.14.cloned.1.call-done
  229.6 8.9 all-gather.16.cloned.1.call-done
  238.5 166.4 %all-gather.18.cloned.1.call-done = bf16[1536,4480]{1,0:T(8,128)(2,1)} async-done(((bf16[96,4480]{1,0:T(8,128)(2,1)}), bf16[1536,4480]{1,0:T(8,128)(2,1)}) %all-gather.18.cloned.1.call-update) | async-done | bytes 13762576 | tf_op jit(solution)/shard_map/all_gather | solution.py:63
  404.9 13.2 fusion.139
  418.1 150.3 %all-gather.20.cloned.1.call-done = bf16[1536,4480]{1,0:T(8,128)(2,1)} async-done(((bf16[96,4480]{1,0:T(8,128)(2,1)}), bf16[1536,4480]{1,0:T(8,128)(2,1)}) %all-gather.20.cloned.1.call-update) | async-done | bytes 13762576 | tf_op jit(solution)/shard_map/all_gather | solution.py:64
  568.4 17.2 multiply_convert_fusion.2
  585.6 146.4 %all-gather.22.cloned.1.call-done = bf16[4480,1536]{0,1:T(8,128)(2,1)} async-done(((bf16[4480,96]{0,1:T(8,128)(2,1)}), bf16[4480,1536]{0,1:T(8,128)(2,1)}) %all-gather.22.cloned.1.call-update) | async-done | bytes 13762576 | tf_op jit(solution)/shard_map/all_gather | solution.py:65
  731.9 12.8 convolution_convert_fusion
  745.5 38.5 %psum.50 = f32[]{:T(128)} all-reduce(f32[]{:T(128)} %reduce_sum.130), channel_id=1, replica_groups=mesh['dp'=4,'ctx'=4,'tensor'=2] {'dp','ctx','tensor'}, use_global_device_ids=true, to_apply=%region_13.14 | all-reduce | flops 1 | bytes 8 | tf_op jit(solution)/shard_map/psum | solution.py:222
  787.8 10.4 all-gather.24.cloned.1.call-done
  798.2 18.0 multiply_convert_fusion
  816.2 11.8 fusion.140
  828.0 11.6 fusion.88
  839.6 10.3 reduce-scatter.18.cloned.1.call-done
  849.9 2.9 fusion.101
  855.6 11.0 all-gather.26.cloned.1.call-done
  866.6 4.4 convolution_convert_fusion.1
  875.8 18.2 while.64
  877.4 2.9 fusion.225
  896.1 85.8 %while.65 = (s32[]{:T(128)}, f32[512,1,6,128]{0,3,2,1:T(8,128)S(1)}, f32[2048,128]{0,1:T(8,128)}, f32[2048,128]{1,0:T(8,128)}, bf16[2048,128]{1,0:T(8,128)(2,1)S...) while((s32[]{:T(128)}, ...), condition=%wide.region_20.21_spmd.clone, body=%wide.region_19.20_spmd.clone.sunk | while | flops 2031945216 | bytes 68345184 | solution.py:176
  899.7 4.8 fusion.237
  912.2 5.4 fusion.239
  921.2 4.8 fusion.237
  933.6 5.4 fusion.239
  942.6 4.8 fusion.237
  955.1 5.4 fusion.239
  964.1 4.8 fusion.237
  976.5 5.4 fusion.239
  985.8 5.0 fusion.141
  990.8 16.5 reduce-scatter.20.cloned.1.call-done
  1012.2 18.0 reduce-scatter.22.cloned.1.call-done
  1038.2 3.6 fusion.142
  1043.5 3.6 fusion.144
  1048.4 14.8 fusion.145
  1063.6 14.7 fusion.146
  1079.7 14.7 fusion.147
  1097.8 39.3 %all-reduce = (f32[]{:T(128)}, f32[1536]{0:T(1024)}, f32[1536]{0:T(1024)}, f32[256]{0:T(256)}, f32[256]{0:T(256)}, /*index=5*/f32[1536]{0:T(1024)}) all-reduce(f32[]{:T(128)} %get-tuple-element.1009, f32[1536]{0:T(1024)S(1)} %get-tuple-element.1007, ...), channel_id=1, replica_groups=mesh['dp'=4,'ctx'=4,'tensor'=2] {'dp','ctx','tensor'}, use_global_device_ids=true, to_apply=%region_11.12 | all-reduce | flops 5121 | bytes 40968 | tf_op jit(solution)/shard_map/psum | solution.py:222
  1140.5 30.0 %reduce-scatter.28.cloned.1.call-done = f32[96,128]{1,0:T(8,128)} async-done(((f32[1536,128]{1,0:T(8,128)}), f32[96,128]{1,0:T(8,128)}) %reduce-scatter.28.cloned.1.call-update) | async-done | bytes 49168 | tf_op jit(solution)/shard_map/reduce_scatter | solution.py:370
  1170.5 128.0 %reduce-scatter.30.cloned.1.call-done = f32[96,128]{1,0:T(8,128)} async-done(((f32[1536,128]{1,0:T(8,128)}), f32[96,128]{1,0:T(8,128)}) %reduce-scatter.30.cloned.1.call-update) | async-done | bytes 49168 | tf_op jit(solution)/shard_map/reduce_scatter | solution.py:371
  1298.5 143.2 %reduce-scatter.26.cloned.1.call-done = f32[96,768]{1,0:T(8,128)} async-done(((f32[1536,768]{1,0:T(8,128)}), f32[96,768]{1,0:T(8,128)}) %reduce-scatter.26.cloned.1.call-update) | async-done | bytes 294928 | tf_op jit(solution)/shard_map/reduce_scatter | solution.py:369
  1441.7 142.9 %reduce-scatter.32.cloned.1.call-done = f32[768,96]{0,1:T(8,128)} async-done(((f32[768,1536]{0,1:T(8,128)}), f32[768,96]{0,1:T(8,128)}) %reduce-scatter.32.cloned.1.call-update) | async-done | bytes 294928 | tf_op jit(solution)/shard_map/reduce_scatter | solution.py:372
  1584.6 391.6 %reduce-scatter.34.cloned.1.call-done = f32[96,4480]{1,0:T(8,128)} async-done(((f32[1536,4480]{1,0:T(8,128)}), f32[96,4480]{1,0:T(8,128)}) %reduce-scatter.34.cloned.1.call-update) | async-done | bytes 1720336 | tf_op jit(solution)/shard_map/reduce_scatter | solution.py:373
  1976.1 391.9 %reduce-scatter.36.cloned.1.call-done = f32[96,4480]{1,0:T(8,128)} async-done(((f32[1536,4480]{1,0:T(8,128)}), f32[96,4480]{1,0:T(8,128)}) %reduce-scatter.36.cloned.1.call-update) | async-done | bytes 1720336 | tf_op jit(solution)/shard_map/reduce_scatter | solution.py:374
  2368.1 392.0 %reduce-scatter.38.cloned.1.call-done = f32[4480,96]{0,1:T(8,128)} async-done(((f32[4480,1536]{0,1:T(8,128)}), f32[4480,96]{0,1:T(8,128)}) %reduce-scatter.38.cloned.1.call-update) | async-done | bytes 1720336 | tf_op jit(solution)/shard_map/reduce_scatter | solution.py:375
  (371 shorter events, 134.5 us)
Async XLA Ops:
  7.2 98.7 %all-gather.10.cloned.1.call-start = ((), (), s32[]{:S(2)}) async-start(), calls=%async_computation.13 | async-start | bytes 2359296 | tf_op jit(solution)/shard_map/all_gather | solution.py:116
  7.9 5.9 copy-start.44
  9.3 51.4 %copy-start.45 = (bf16[96,128]{1,0:T(8,128)(2,1)S(1)}, bf16[96,128]{1,0:T(8,128)(2,1)}, u32[]{:S(2)}) copy-start(bf16[96,128]{1,0:T(8,128)(2,1)} %param.35) | copy-start | bytes 73732
  9.9 93.0 %copy-start.58 = (bf16[256]{0:T(256)(128)(2,1)S(1)}, bf16[256]{0:T(256)(128)(2,1)}, u32[]{:S(2)}) copy-start(bf16[256]{0:T(256)(128)(2,1)} %param.38) | copy-start | bytes 1540
  9.9 93.1 %copy-start.59 = (bf16[256]{0:T(256)(128)(2,1)S(1)}, bf16[256]{0:T(256)(128)(2,1)}, u32[]{:S(2)}) copy-start(bf16[256]{0:T(256)(128)(2,1)} %param.36) | copy-start | bytes 1540
  9.9 94.7 %copy-start.53 = (bf16[1536]{0:T(1024)(128)(2,1)S(1)}, bf16[1536]{0:T(1024)(128)(2,1)}, u32[]{:S(2)}) copy-start(bf16[1536]{0:T(1024)(128)(2,1)} %param.34) | copy-start | bytes 9220
  12.2 131.0 %all-gather.12.cloned.1.call-start = ((), (), s32[]{:S(2)}) async-start(), calls=%async_computation.14 | async-start | bytes 2506752 | tf_op jit(solution)/shard_map/all_gather | solution.py:59
  13.0 198.7 %all-gather.14.cloned.1.call-start = ((), (), s32[]{:S(2)}) async-start(), calls=%async_computation.15 | async-start | bytes 2506752 | tf_op jit(solution)/shard_map/all_gather | solution.py:62
  13.7 210.8 %reduce-scatter.14.cloned.1.call-start = ((), (), s32[]{:S(2)}) async-start(), calls=%async_computation.16 | async-start | bytes 4718592 | tf_op jit(solution)/shard_map/reduce_scatter | solution.py:202
  13.8 111.7 %copy-start.50 = (f32[64]{0:T(128)}, f32[64]{0:T(128)S(1)}, u32[]{:S(2)}) copy-start(f32[64]{0:T(128)S(1)} %negate_power_fusion) | copy-start | bytes 772
  60.7 64.2 %copy-start.14 = (bf16[1536,128]{1,0:T(8,128)(2,1)}, bf16[1536,128]{1,0:T(8,128)(2,1)S(1)}, u32[]{:S(2)}) copy-start(bf16[1536,128]{1,0:T(8,128)(2,1)S(1)} %all_gather.40) | copy-start | bytes 1179652
  102.9 22.6 copy-start.16
  104.6 21.0 copy-start.41
  105.9 43.5 %copy-start.22 = (f32[512,64]{0,1:T(8,128)}, f32[512,64]{0,1:T(8,128)S(1)}, u32[]{:S(2)}) copy-start(f32[512,64]{0,1:T(8,128)S(1)} %get-tuple-element.1135) | copy-start | bytes 393220
  105.9 19.0 copy-start.3
  209.4 7.2 copy-start
  209.4 7.2 copy-start.29
  209.4 7.2 copy-start.35
  209.5 7.2 copy-start.46
  211.6 5.0 copy-start.33
  216.7 7.8 copy-start.5
  216.7 21.8 all-gather.16.cloned.1.call-start
  227.3 177.6 %all-gather.18.cloned.1.call-start = ((), (), s32[]{:S(2)}) async-start(), calls=%async_computation.18 | async-start | bytes 14622720 | tf_op jit(solution)/shard_map/all_gather | solution.py:63
  227.9 340.5 %all-gather.20.cloned.1.call-start = ((), (), s32[]{:S(2)}) async-start(), calls=%async_computation.19 | async-start | bytes 14622720 | tf_op jit(solution)/shard_map/all_gather | solution.py:64
  228.6 503.3 %all-gather.22.cloned.1.call-start = ((), (), s32[]{:S(2)}) async-start(), calls=%async_computation.20 | async-start | bytes 14622720 | tf_op jit(solution)/shard_map/all_gather | solution.py:65
  229.4 555.4 %reduce-scatter.16.cloned.1.call-start = ((), (), s32[]{:S(2)}) async-start(), calls=%async_computation.21 | async-start | bytes 2359296 | tf_op jit(solution)/shard_map/reduce_scatter | solution.py:216
  238.5 329.9 %copy-start.54 = (bf16[512,1536]{1,0:T(8,128)(2,1)S(1)}, bf16[512,1536]{1,0:T(8,128)(2,1)}, u32[]{:S(2)}) copy-start(bf16[512,1536]{1,0:T(8,128)(2,1)} %all-gather.16.cloned.1.call-done) | copy-start | bytes 4718596
  744.7 40.0 %copy-start.9 = (bf16[256,1536]{1,0:T(8,128)(2,1)S(1)}, bf16[256,1536]{1,0:T(8,128)(2,1)}, u32[]{:S(2)}) copy-start(bf16[256,1536]{1,0:T(8,128)(2,1)} %param.27) | copy-start | bytes 2359300
  744.7 40.0 %copy-start.20 = (bf16[256,1536]{1,0:T(8,128)(2,1)S(1)}, bf16[256,1536]{1,0:T(8,128)(2,1)}, u32[]{:S(2)}) copy-start(bf16[256,1536]{1,0:T(8,128)(2,1)} %param.28) | copy-start | bytes 2359300
  744.8 53.4 %all-gather.24.cloned.1.call-start = ((), (), s32[]{:S(2)}) async-start(), calls=%async_computation.22 | async-start | bytes 2359296 | tf_op jit(solution)/shard_map/all_gather | solution.py:230
  787.3 62.6 %reduce-scatter.18.cloned.1.call-start = ((), (), s32[]{:S(2)}) async-start(), calls=%async_computation.23 | async-start | bytes 2359296 | tf_op jit(solution)/shard_map/reduce_scatter | solution.py:239
  816.2 11.8 copy-start.60
  839.5 10.4 copy-start.10
  839.6 27.1 all-gather.26.cloned.1.call-start
  855.4 151.9 %reduce-scatter.20.cloned.1.call-start = ((), (), s32[]{:S(2)}) async-start(), calls=%async_computation.25 | async-start | bytes 655360 | tf_op jit(solution)/shard_map/reduce_scatter | solution.py:317
  871.0 4.7 copy-start.1
  871.0 4.7 copy-start.8
  871.0 4.7 copy-start.30
  871.0 4.7 copy-start.37
  871.0 4.7 copy-start.47
  896.1 3.6 copy-start.32
  897.7 6.9 copy-start.11
  917.5 3.6 copy-start.32
  919.1 6.9 copy-start.11
  939.0 3.6 copy-start.32
  940.6 6.9 copy-start.11
  960.4 3.6 copy-start.32
  962.0 6.9 copy-start.11
  981.9 3.3 copy-start.36
  984.1 46.0 %reduce-scatter.22.cloned.1.call-start = ((), (), s32[]{:S(2)}) async-start(), calls=%async_computation.26 | async-start | bytes 655360 | tf_op jit(solution)/shard_map/reduce_scatter | solution.py:320
  985.7 5.2 copy-start.17
  985.7 110.2 %reduce-scatter.24.cloned.1.call-start = ((), (), s32[]{:S(2)}) async-start(), calls=%async_computation.27 | async-start | bytes 2359296 | tf_op jit(solution)/shard_map/reduce_scatter | solution.py:338
  985.7 22.5 copy-start.42
  985.8 22.5 copy-start.51
  1009.5 20.6 copy-start.15
  1032.8 3.9 copy-start.24
  1032.8 137.7 %reduce-scatter.28.cloned.1.call-start = ((), (), s32[]{:S(2)}) async-start(), calls=%async_computation.29 | async-start | bytes 835584 | tf_op jit(solution)/shard_map/reduce_scatter | solution.py:370
  1036.6 261.9 %reduce-scatter.30.cloned.1.call-start = ((), (), s32[]{:S(2)}) async-start(), calls=%async_computation.30 | async-start | bytes 835584 | tf_op jit(solution)/shard_map/reduce_scatter | solution.py:371
  1038.2 403.5 %reduce-scatter.26.cloned.1.call-start = ((), (), s32[]{:S(2)}) async-start(), calls=%async_computation.28 | async-start | bytes 5013504 | tf_op jit(solution)/shard_map/reduce_scatter | solution.py:369
  1041.8 542.7 %reduce-scatter.32.cloned.1.call-start = ((), (), s32[]{:S(2)}) async-start(), calls=%async_computation.31 | async-start | bytes 5013504 | tf_op jit(solution)/shard_map/reduce_scatter | solution.py:372
  1047.1 929.1 %reduce-scatter.34.cloned.1.call-start = ((), (), s32[]{:S(2)}) async-start(), calls=%async_computation.32 | async-start | bytes 29245440 | tf_op jit(solution)/shard_map/reduce_scatter | solution.py:373
  1063.3 1304.8 %reduce-scatter.36.cloned.1.call-start = ((), (), s32[]{:S(2)}) async-start(), calls=%async_computation.33 | async-start | bytes 29245440 | tf_op jit(solution)/shard_map/reduce_scatter | solution.py:374
  1078.3 1681.8 %reduce-scatter.38.cloned.1.call-start = ((), (), s32[]{:S(2)}) async-start(), calls=%async_computation.34 | async-start | bytes 29245440 | tf_op jit(solution)/shard_map/reduce_scatter | solution.py:375
  1094.4 43.3 %copy-start.12 = (f32[256,1536]{1,0:T(8,128)S(1)}, f32[256,1536]{1,0:T(8,128)}, u32[]{:S(2)}) copy-start(f32[256,1536]{1,0:T(8,128)} %get-tuple-element.1107) | copy-start | bytes 4718596
  (31 other events, 53.9 us)
Sparse Core Ops, SparseCore 0:
  12.3 12.5 all-gather.9
  27.7 65.1 all-gather.11
  95.6 62.5 all-gather.13
  216.9 7.5 reduce-scatter.13
  227.4 11.0 all-gather.15
  241.1 163.7 all-gather.17
  407.6 160.7 all-gather.19
  571.2 160.7 all-gather.21
  744.9 7.2 reduce-scatter.15
  787.4 10.6 all-gather.23
  839.7 10.2 reduce-scatter.17
  855.5 11.0 all-gather.25
  984.2 23.0 reduce-scatter.19
  1010.0 20.0 reduce-scatter.21
  1032.9 7.2 reduce-scatter.23
  1045.3 125.1 reduce-scatter.27
  1175.6 122.8 reduce-scatter.29
  1304.1 137.5 reduce-scatter.25
  1447.4 137.1 reduce-scatter.31
  1591.0 385.0 reduce-scatter.33
  1982.7 385.3 reduce-scatter.35
  2374.6 385.3 reduce-scatter.37
where the time goes:
time: 2770 us
  waiting for transfers between devices  2170 us (78%)
  matrix products  281 us (10%)
  blocking collectives  201 us (7%)
  other arithmetic  55.1 us (2%)
  local copies, waits for them, and re-layouts  42 us (2%)
    reduce_scatter x1, waiting for transfers between devices, per_device(): lax.psum_scatter(grad_down, ('dp', 'ctx'), scatter_dimension=1, tiled=True)  392 us
    reduce_scatter x1, waiting for transfers between devices, per_device(): lax.psum_scatter(grad_up, ('dp', 'ctx'), scatter_dimension=0, tiled=True)  392 us
    reduce_scatter x1, waiting for transfers between devices, per_device(): lax.psum_scatter(grad_gate, ('dp', 'ctx'), scatter_dimension=0, tiled=True)  392 us
    all_gather x1, waiting for transfers between devices, gather_weights(): lax.all_gather(gate_weight, ('dp', 'ctx'), axis=0, tiled=True)  166 us
    all_gather x1, waiting for transfers between devices, gather_weights(): lax.all_gather(up_weight, ('dp', 'ctx'), axis=0, tiled=True)  150 us
    all_gather x1, waiting for transfers between devices, gather_weights(): lax.all_gather(down_weight, ('dp', 'ctx'), axis=1, tiled=True)  146 us
    reduce_scatter x1, waiting for transfers between devices, per_device(): lax.psum_scatter(grad_query, ('dp', 'ctx'), scatter_dimension=0, tiled=True)  143 us
    reduce_scatter x1, waiting for transfers between devices, per_device(): lax.psum_scatter(grad_out, ('dp', 'ctx'), scatter_dimension=1, tiled=True)  143 us
  transfers between devices with their start and end apart: 22, of which 17 were waited for; matrix products, arithmetic and copies ran while one was open for 6% of the time, Pallas kernels for 0%

commit v1 on v0

v1 whole, which is shorter than its diff:
```python
import functools
import math

import jax
import jax.numpy as jnp
from jax import lax
from jax.experimental import pallas as pl
from jax.experimental.pallas import tpu as pltpu
from jax.sharding import PartitionSpec as P

D = 1536
HEAD = 128


EPS = 1e-06
THETA = 10000.0
VERY_LOW = -1e30


def rope_tables(places):
    half_dim = HEAD // 2
    frequency = THETA ** (-(jnp.arange(half_dim, dtype=jnp.float32) * 2.0 / HEAD))
    angles = places.astype(jnp.float32)[:, None] * frequency[None, :]
    return (jnp.cos(angles), jnp.sin(angles))


def rotate(stacked, cosine, sine_table):
    half_dim = HEAD // 2
    first_half = stacked[..., :half_dim]
    second_half = stacked[..., half_dim:]
    cosine = cosine[:, None, :]
    sine_table = sine_table[:, None, :]
    return jnp.concatenate(
        [
            first_half * cosine - second_half * sine_table,
            second_half * cosine + first_half * sine_table,
        ],
        axis=-1,
    )


def matmul(first_op, second_op):
    return jnp.dot(first_op, second_op, preferred_element_type=jnp.float32)


def matmul_tn(first_op, second_op):
    return lax.dot_general(
        first_op, second_op, (((0,), (0,)), ((), ())), preferred_element_type=jnp.float32
    )


def matmul_nt(first_op, second_op):
    return lax.dot_general(
        first_op, second_op, (((1,), (1,)), ((), ())), preferred_element_type=jnp.float32
    )


def norm_back(grad_normed, normed, inverse, gain):
    scaled = grad_normed * gain
    return inverse * (scaled - normed * jnp.mean(scaled * normed, axis=1, keepdims=True))


def exchange(blocks, axis):
    size = lax.axis_size(axis)
    rank = lax.axis_index(axis)
    received = [(rank, lax.dynamic_index_in_dim(blocks, rank, 0, keepdims=False))]
    for step in range(1, size):
        going = lax.dynamic_index_in_dim(blocks, (rank + step) % size, 0, keepdims=False)
        came = lax.ppermute(going, axis, [(i, (i + step) % size) for i in range(size)])
        received.append(((rank - step + size) % size, came))
    return received


def to_columns(shard, width):
    size = lax.axis_size("ctx")
    rows, columns = shard.shape
    padded = jnp.pad(shard, ((0, 0), (0, size * width - columns)))
    blocks = jnp.stack([padded[:, j * width : (j + 1) * width] for j in range(size)])
    gathered = jnp.zeros((size, rows, width), shard.dtype)
    for rank, block in exchange(blocks, "ctx"):
        gathered = lax.dynamic_update_index_in_dim(gathered, block, rank, 0)
    return lax.all_gather(gathered.reshape(size * rows, width), "dp", axis=0, tiled=True)


def to_rows(grad, columns):
    size = lax.axis_size("ctx")
    summed = lax.psum_scatter(grad, "dp", scatter_dimension=0, tiled=True)
    rows, width = summed.shape[0] // size, summed.shape[1]
    shard = jnp.zeros((rows, size * width), jnp.bfloat16)
    for rank, block in exchange(summed.reshape(size, rows, width), "ctx"):
        shard = lax.dynamic_update_slice_in_dim(shard, block, rank * width, 1)
    return shard[:, :columns].astype(jnp.float32)


def sum_everywhere(value):
    for axis in ("tensor", "ctx", "dp"):
        size = lax.axis_size(axis)
        if size & (size - 1):
            value = lax.psum(value, axis)
            continue
        step = 1
        while step < size:
            value = value + lax.ppermute(value, axis, [(i, i ^ step) for i in range(size)])
            step *= 2
    return value


def mask_into(bias_ref, first, seg_ref, place_ref):
    keys, rows = bias_ref.shape
    key_index = lax.broadcasted_iota(jnp.int32, (keys, rows), 0)
    row_index = lax.broadcasted_iota(jnp.int32, (keys, rows), 1) + first
    place = jnp.broadcast_to(place_ref[...], (keys, rows))
    start = jnp.broadcast_to(seg_ref[...], (keys, rows))
    allowed = ((place >= start) & (place <= row_index)) | (key_index == row_index)
    bias_ref[...] = jnp.where(allowed, 0.0, VERY_LOW)


def nn(first_op, second_op):
    return jnp.dot(first_op, second_op, preferred_element_type=jnp.float32)


def attend_kernel(scale, first_ref, seg_ref, place_ref, q_ref, k_ref, vt_ref, o_ref, lse_ref, bias_ref):
    @pl.when(pl.program_id(1) == 0)
    def _():
        mask_into(bias_ref, first_ref[0] + pl.program_id(0) * q_ref.shape[0], seg_ref, place_ref)

    scores = matmul_nt(k_ref[...], q_ref[...]) * scale + bias_ref[...]
    top = jnp.max(scores, axis=0, keepdims=True)
    powers = jnp.exp(scores - top)
    total = jnp.sum(powers, axis=0, keepdims=True)
    mixture = nn(vt_ref[...], powers.astype(jnp.bfloat16)) / total
    o_ref[...] = mixture.T.astype(jnp.bfloat16)
    lse_ref[0] = top + jnp.log(total)


def attend_back_kernel(
    scale, first_ref, seg_ref, place_ref, q_ref, do_ref, lse_ref, k_ref, v_ref, kt_ref,
    dq_ref, dkv_ref, bias_ref, dk_ref, dv_ref,
):
    block, head = pl.program_id(0), pl.program_id(1)

    @pl.when(head == 0)
    def _():
        mask_into(bias_ref, first_ref[0] + block * q_ref.shape[0], seg_ref, place_ref)

    @pl.when((head == 0) & (block == 0))
    def _():
        dk_ref[...] = jnp.zeros_like(dk_ref)
        dv_ref[...] = jnp.zeros_like(dv_ref)

    query, grad = q_ref[...], do_ref[...]
    scores = matmul_nt(k_ref[...], query) * scale + bias_ref[...]
    probs = jnp.exp(scores - lse_ref[0])
    grad_probs = matmul_nt(v_ref[...], grad)
    delta = jnp.sum(probs * grad_probs, axis=0, keepdims=True)
    grad_scores = (probs * (grad_probs - delta)).astype(jnp.bfloat16)
    dv_ref[...] += nn(probs.astype(jnp.bfloat16), grad)
    dk_ref[...] += nn(grad_scores, query)
    dq_ref[...] = (nn(kt_ref[...], grad_scores) * scale).T

    @pl.when((head == pl.num_programs(1) - 1) & (block == pl.num_programs(0) - 1))
    def _():
        dkv_ref[:, :HEAD] = (dk_ref[...] * scale).astype(jnp.bfloat16)
        dkv_ref[:, HEAD:] = dv_ref[...].astype(jnp.bfloat16)


def attention_calls(rows, keys, heads):
    block = math.gcd(256, rows)
    scale = 1.0 / math.sqrt(HEAD)
    smem = pl.BlockSpec(memory_space=pltpu.SMEM)
    seg = pl.BlockSpec((1, block), lambda i, h: (0, i))
    place = pl.BlockSpec((keys, 1), lambda i, h: (0, 0))
    head = pl.BlockSpec((block, HEAD), lambda i, h: (i, h))
    lse = pl.BlockSpec((1, 1, block), lambda i, h: (h, 0, i))
    tall = pl.BlockSpec((keys, HEAD), lambda i, h: (0, 0))
    wide = pl.BlockSpec((HEAD, keys), lambda i, h: (0, 0))
    params = pltpu.CompilerParams(vmem_limit_bytes=60000000)
    grid = (rows // block, heads)
    size = heads * rows * keys
    forward = pl.pallas_call(
        functools.partial(attend_kernel, scale),
        grid=grid,
        in_specs=[smem, seg, place, head, tall, wide],
        out_specs=[head, lse],
        out_shape=[
            jax.ShapeDtypeStruct((rows, heads * HEAD), jnp.bfloat16),
            jax.ShapeDtypeStruct((heads, 1, rows), jnp.float32),
        ],
        scratch_shapes=[pltpu.VMEM((keys, block), jnp.float32)],
        compiler_params=params,
        cost_estimate=pl.CostEstimate(flops=4 * size * HEAD, bytes_accessed=4 * rows * heads * HEAD, transcendentals=size),
        name="attend",
    )
    backward = pl.pallas_call(
        functools.partial(attend_back_kernel, scale),
        grid=grid,
        in_specs=[smem, seg, place, head, head, lse, tall, tall, wide],
        out_specs=[head, pl.BlockSpec((keys, 2 * HEAD), lambda i, h: (0, 0))],
        out_shape=[
            jax.ShapeDtypeStruct((rows, heads * HEAD), jnp.float32),
            jax.ShapeDtypeStruct((keys, 2 * HEAD), jnp.bfloat16),
        ],
        scratch_shapes=[
            pltpu.VMEM((keys, block), jnp.float32),
            pltpu.VMEM((keys, HEAD), jnp.float32),
            pltpu.VMEM((keys, HEAD), jnp.float32),
        ],
        compiler_params=params,
        cost_estimate=pl.CostEstimate(flops=10 * size * HEAD, bytes_accessed=8 * rows * heads * HEAD, transcendentals=size),
        name="attend_back",
    )
    return forward, backward


def per_device(
    layer_input,
    teacher,
    cotangent,
    segment_ids,
    positions,
    valid_mask,
    gain_attn,
    query_weight,
    query_bias,
    key_weight,
    key_bias,
    value_weight,
    value_bias,
    out_weight,
    gain_mlp,
    gate_weight,
    up_weight,
    down_weight,
):
    tensor_rank = lax.axis_index("tensor")
    ctx_rank = lax.axis_index("ctx")
    tensor_size, ctx_size = lax.axis_size("tensor"), lax.axis_size("ctx")
    own_rows = layer_input.shape[0]
    shard_rows = own_rows * tensor_size
    seq_len = segment_ids.shape[0]
    q_width = query_weight.shape[1]
    kv_width = key_weight.shape[1]
    kv_local = kv_width // HEAD
    group = q_width // kv_width
    hidden_width = gate_weight.shape[1]
    slice_width = -(-hidden_width // (128 * ctx_size)) * 128
    first_row = ctx_rank * shard_rows
    own_first = first_row + tensor_rank * own_rows

    inputs = layer_input.astype(jnp.float32)
    gain_one = gain_attn.astype(jnp.float32)
    gain_two = gain_mlp.astype(jnp.float32)
    scale_attn = lax.rsqrt(jnp.mean(inputs * inputs, axis=1, keepdims=True) + EPS)
    normed_attn = inputs * scale_attn
    normed_rows = lax.all_gather(
        (normed_attn * gain_one).astype(jnp.bfloat16), "tensor", axis=0, tiled=True
    )
    full_qkv = lax.all_gather(
        jnp.concatenate([query_weight, key_weight, value_weight], axis=1),
        ("dp", "ctx"),
        axis=0,
        tiled=True,
    )
    full_out = lax.all_gather(out_weight.T, ("dp", "ctx"), axis=0, tiled=True)
    full_gate = to_columns(gate_weight, slice_width)
    full_up = to_columns(up_weight, slice_width)
    full_down = to_columns(down_weight.T, slice_width)
    valid_count = jnp.sum(valid_mask.astype(jnp.float32))
    counts = [valid_count]
    dp_size = lax.axis_size("dp")
    for step in range(1, dp_size):
        counts.append(
            lax.ppermute(
                jnp.full((8, 128), valid_count), "dp", [(i, (i + step) % dp_size) for i in range(dp_size)]
            )[0, 0]
        )
    valid_count = sum(counts)

    bias = jnp.concatenate(
        [
            lax.dynamic_slice_in_dim(query_bias, tensor_rank * q_width, q_width),
            lax.dynamic_slice_in_dim(key_bias, tensor_rank * kv_width, kv_width),
            lax.dynamic_slice_in_dim(value_bias, tensor_rank * kv_width, kv_width),
        ]
    ).astype(jnp.float32)
    places = lax.dynamic_slice_in_dim(positions, first_row, shard_rows)
    cosine, sine_table = rope_tables(places)
    qkv_pre = matmul(normed_rows, full_qkv) + bias
    turned = q_width + kv_width
    rotated = (
        rotate(qkv_pre[:, :turned].reshape(shard_rows, turned // HEAD, HEAD), cosine, sine_table)
        .astype(jnp.bfloat16)
        .reshape(shard_rows, turned)
    )
    queries = rotated[:, :q_width]
    own_kv = jnp.concatenate([rotated[:, q_width:], qkv_pre[:, turned:].astype(jnp.bfloat16)], axis=1)
    all_kv = lax.all_gather(own_kv, "ctx", axis=0, tiled=True)

    key_index = jnp.arange(seq_len, dtype=jnp.int32)
    key_place = jnp.where(valid_mask > 0, key_index, -1)[:, None]
    seq_first = lax.axis_index("dp") * seq_len
    doc_start = (lax.dynamic_slice_in_dim(segment_ids, first_row, shard_rows) - seq_first)[None, :]
    first = jnp.reshape(first_row, (1,)).astype(jnp.int32)
    forward, backward = attention_calls(shard_rows, seq_len, group)
    kept = []
    for c in range(kv_local):
        key = all_kv[:, c * HEAD : (c + 1) * HEAD]
        value = all_kv[:, kv_width + c * HEAD : kv_width + (c + 1) * HEAD]
        query = queries[:, c * group * HEAD : (c + 1) * group * HEAD]
        kept.append((query, key, value) + tuple(forward(first, doc_start, key_place, query, key, value.T)))
    heads_out = jnp.concatenate([k[3] for k in kept], axis=1)
    attention = lax.psum_scatter(
        matmul_nt(heads_out, full_out), "tensor", scatter_dimension=0, tiled=True
    )
    residual_mid = inputs + attention
    scale_mlp = lax.rsqrt(jnp.mean(residual_mid * residual_mid, axis=1, keepdims=True) + EPS)
    normed_mlp = residual_mid * scale_mlp
    mlp_rows = lax.all_gather(
        (normed_mlp * gain_two).astype(jnp.bfloat16), ("ctx", "tensor"), axis=0, tiled=True
    )
    gate_act = matmul(mlp_rows, full_gate)
    up_act = matmul(mlp_rows, full_up)
    sigmoid = jax.nn.sigmoid(gate_act)
    silu_gate = gate_act * sigmoid
    hidden = (silu_gate * up_act).astype(jnp.bfloat16)
    branch = lax.psum_scatter(
        matmul_nt(hidden, full_down).astype(jnp.bfloat16), ("ctx", "tensor"), scatter_dimension=0, tiled=True
    ).astype(jnp.float32)
    layer_result = residual_mid + branch
    valid_own = lax.dynamic_slice_in_dim(valid_mask, own_first, own_rows).astype(jnp.float32)
    difference = layer_result - teacher.astype(jnp.float32)
    squared_sum = jnp.sum(valid_own[:, None] * difference * difference)
    grad_result = cotangent.astype(jnp.float32) + 2.0 * valid_own[:, None] * difference / (
        valid_count * D
    )
    grad_branch = lax.all_gather(grad_result.astype(jnp.bfloat16), ("ctx", "tensor"), axis=0, tiled=True)
    grad_hidden = matmul(grad_branch, full_down)
    grad_gate_act = (grad_hidden * up_act * sigmoid * (1.0 + gate_act * (1.0 - sigmoid))).astype(
        jnp.bfloat16
    )
    grad_up_act = (grad_hidden * silu_gate).astype(jnp.bfloat16)
    grad_mlp_rows = lax.psum_scatter(
        (matmul_nt(grad_gate_act, full_gate) + matmul_nt(grad_up_act, full_up)).astype(
            jnp.bfloat16
        ),
        ("ctx", "tensor"),
        scatter_dimension=0,
        tiled=True,
    ).astype(jnp.float32)
    shard_down = to_rows(matmul_tn(grad_branch, hidden).astype(jnp.bfloat16), hidden_width).T
    shard_gate = to_rows(matmul_tn(mlp_rows, grad_gate_act).astype(jnp.bfloat16), hidden_width)
    shard_up = to_rows(matmul_tn(mlp_rows, grad_up_act).astype(jnp.bfloat16), hidden_width)
    grad_gain_mlp = jnp.sum(grad_mlp_rows * normed_mlp, axis=0)
    grad_mid = grad_result + norm_back(grad_mlp_rows, normed_mlp, scale_mlp, gain_two)
    grad_attn_rows = lax.all_gather(grad_mid.astype(jnp.bfloat16), "tensor", axis=0, tiled=True)
    grad_heads = matmul(grad_attn_rows, full_out).astype(jnp.bfloat16)
    grad_out = matmul_tn(grad_attn_rows, heads_out).astype(jnp.bfloat16)

    def scatter(grad):
        grad = lax.psum_scatter(grad, "dp", scatter_dimension=0, tiled=True)
        return lax.psum_scatter(grad, "ctx", scatter_dimension=0, tiled=True).astype(jnp.float32)

    shard_out = scatter(grad_out).T
    query_grads, key_grads, value_grads = [], [], []
    for c in range(kv_local):
        query, key, value, _, log_total = kept[c]
        span = slice(c * group * HEAD, (c + 1) * group * HEAD)
        grad_query, grad_kv = backward(
            first, doc_start, key_place, query, grad_heads[:, span], log_total, key, value, key.T
        )
        query_grads.append(grad_query)
        key_grads.append(grad_kv[:, :HEAD])
        value_grads.append(grad_kv[:, HEAD:])
    grad_kv = grad_kv if kv_local == 1 else jnp.concatenate(key_grads + value_grads, axis=1)
    grad_kv = lax.psum_scatter(grad_kv, "ctx", scatter_dimension=0, tiled=True)
    back = jnp.concatenate(query_grads + [grad_kv[:, :kv_width].astype(jnp.float32)], axis=1)
    grad_pre = jnp.concatenate(
        [
            rotate(back.reshape(shard_rows, turned // HEAD, HEAD), cosine, -sine_table)
            .reshape(shard_rows, turned)
            .astype(jnp.bfloat16),
            grad_kv[:, kv_width:],
        ],
        axis=1,
    )
    shard_qkv = scatter(matmul_tn(normed_rows, grad_pre).astype(jnp.bfloat16))
    grad_normed = lax.psum_scatter(
        matmul_nt(grad_pre, full_qkv).astype(jnp.bfloat16), "tensor", scatter_dimension=0, tiled=True
    ).astype(jnp.float32)
    grad_gain_attn = jnp.sum(grad_normed * normed_attn, axis=0)
    grad_input = grad_mid + norm_back(grad_normed, normed_attn, scale_attn, gain_one)
    bias_sum = jnp.sum(grad_pre.astype(jnp.float32), axis=0)

    def spread(part, size):
        return lax.dynamic_update_slice_in_dim(
            jnp.zeros((size,), jnp.float32), part, tensor_rank * part.shape[0], 0
        )

    loss_part = jnp.zeros((128,), jnp.float32).at[0].set(squared_sum)
    parts = [
        grad_gain_attn,
        grad_gain_mlp,
        spread(bias_sum[:q_width], query_bias.shape[0]),
        spread(bias_sum[q_width:turned], key_bias.shape[0]),
        spread(bias_sum[turned:], value_bias.shape[0]),
        loss_part,
    ]
    sums = sum_everywhere(jnp.concatenate(parts).reshape(-1, 128)).reshape(-1)
    pieces, offset = [], 0
    for part in parts:
        pieces.append(sums[offset : offset + part.shape[0]])
        offset += part.shape[0]
    return (
        layer_result.astype(jnp.bfloat16),
        pieces[5][0] / (valid_count * D),
        grad_input,
        pieces[0],
        shard_qkv[:, :q_width],
        pieces[2],
        shard_qkv[:, q_width:turned],
        pieces[3],
        shard_qkv[:, turned:],
        pieces[4],
        shard_out,
        pieces[1],
        shard_gate,
        shard_up,
        shard_down,
    )


def solution(mesh):
    in_specs = (
        P(("dp", "ctx", "tensor"), None),
        P(("dp", "ctx", "tensor"), None),
        P(("dp", "ctx", "tensor"), None),
        P("dp"),
        P("dp"),
        P("dp"),
        P(),
        P(("dp", "ctx"), "tensor"),
        P(),
        P(("dp", "ctx"), "tensor"),
        P(),
        P(("dp", "ctx"), "tensor"),
        P(),
        P("tensor", ("dp", "ctx")),
        P(),
        P(("dp", "ctx"), "tensor"),
        P(("dp", "ctx"), "tensor"),
        P("tensor", ("dp", "ctx")),
    )
    out_specs = (
        P(("dp", "ctx", "tensor"), None),
        P(),
        P(("dp", "ctx", "tensor"), None),
        P(),
        P(("dp", "ctx"), "tensor"),
        P(),
        P(("dp", "ctx"), "tensor"),
        P(),
        P(("dp", "ctx"), "tensor"),
        P(),
        P("tensor", ("dp", "ctx")),
        P(),
        P(("dp", "ctx"), "tensor"),
        P(("dp", "ctx"), "tensor"),
        P("tensor", ("dp", "ctx")),
    )
    return jax.shard_map(
        per_device, mesh=mesh, in_specs=in_specs, out_specs=out_specs, check_vma=False
    )
```

time: 2770 us -> 1090 us (0.39)
  waiting for transfers between devices: 2170 us -> 731 us
  blocking collectives: 201 us -> 0 us
  matrix products: 281 us -> 152 us
  starting transfers between devices: 2.15 us -> 51.8 us
  Pallas kernels: 0 us -> 45.5 us
    reduce_scatter x12 -> x11, waiting for transfers between devices: 1660 us -> 263 us  [the longest x3 102 us: to_rows(): summed = lax.psum_scatter(grad, 'dp', scatter_dimension=0, tiled=True)]
    all_gather x7 -> x8, waiting for transfers between devices: 482 us -> 335 us  [the longest x1 72.5 us: per_device(): lax.all_gather(jnp.concatenate([query_weight, key_weight, value_weight],...]
    all_gather x4 -> x0, blocking collectives: 123 us -> none  [the longest x1 46.8 us: gather_weights(): lax.all_gather(value_weight, ('dp', 'ctx'), axis=0, tiled=True)]
    dot_general x36 -> x0, matrix products: 115 us -> none  [the longest x12 22.8 us: block_scores(): jnp.einsum('icgd,jcd->cgij', queries, key_block, preferred_element_type=j...]
    psum x2 -> x0, blocking collectives: 77.9 us -> none  [per_device(): lax.psum((jnp.sum(valid_own[:, None] * difference * difference), jnp.sum(...]
    reduce_scatter x1, waiting for transfers between devices: 10.3 us -> 68.3 us  [per_device(): lax.psum_scatter((matmul_nt(grad_gate_act, full_gate) + matmul_nt(grad_up...]
    ppermute x0 -> x26, starting transfers between devices: none -> 49.6 us  [the longest x18 37.2 us: exchange(): lax.ppermute(going, axis, [(i, (i + step) % size) for i in range(size)])]
    ppermute x0 -> x26, waiting for transfers between devices: none -> 48.5 us  [the longest x18 42.6 us: exchange(): lax.ppermute(going, axis, [(i, (i + step) % size) for i in range(size)])]
  transfers between devices with their start and end apart: 22 -> 48, of which waited for: 17 -> 32; matrix products, arithmetic and copies ran while one was open for 6% -> 12% of each run, Pallas kernels for 0% -> 2%
where the time goes in v1:
time: 1090 us; the launch traced here: 1080 us
  waiting for transfers between devices  731 us (67%)
  matrix products  152 us (14%)
  starting transfers between devices  51.8 us (5%)
  Pallas kernels  45.5 us (4%)
  local copies, waits for them, and re-layouts  42.5 us (4%)
  other arithmetic  36.3 us (3%)
  between operations  21.1 us (2%)
    reduce_scatter x3, waiting for transfers between devices, to_rows(): summed = lax.psum_scatter(grad, 'dp', scatter_dimension=0, tiled=True)  102 us
    all_gather x1, waiting for transfers between devices, per_device(): lax.all_gather(jnp.concatenate([query_weight, key_weight, value_weight],...  72.5 us
    all_gather x3, waiting for transfers between devices, to_columns(): lax.all_gather(gathered.reshape(size * rows, width), 'dp', axis=0, tiled=...  68.9 us
    reduce_scatter x1, waiting for transfers between devices, per_device(): lax.psum_scatter((matmul_nt(grad_gate_act, full_gate) + matmul_nt(grad_up...  68.3 us
    all_gather x1, waiting for transfers between devices, per_device(): lax.all_gather((normed_mlp * gain_two).astype(jnp.bfloat16), ('ctx', 'ten...  66.7 us
    all_gather x1, waiting for transfers between devices, per_device(): lax.all_gather(grad_result.astype(jnp.bfloat16), ('ctx', 'tensor'), axis=...  62.7 us
    reduce_scatter x1, waiting for transfers between devices, per_device(): lax.psum_scatter(matmul_nt(hidden, full_down).astype(jnp.bfloat16), ('ctx...  59.7 us
    dot_general x5, matrix products, matmul(): return jnp.dot(first_op, second_op, preferred_element_type=jnp.float32)  57.8 us
  transfers between devices with their start and end apart: 48, of which 32 were waited for; matrix products, arithmetic and copies ran while one was open for 12% of the time, Pallas kernels for 2%

profile of v1, /device:TPU:0, one launch (start us, length us, event | category | flops | bytes accessed | tf_op | source)
XLA Modules:
  0.0 1080.0 jit_solution(10864074643717930286)
XLA Ops:
  10.8 2.3 fusion.14
  16.2 9.6 all-gather.11.cloned.1.call-done
  25.8 72.5 %all-gather.13.cloned.1.call-done = bf16[1536,1024]{1,0:T(8,128)(2,1)} async-done(((bf16[96,1024]{1,0:T(8,128)(2,1)}), bf16[1536,1024]{1,0:T(8,128)(2,1)}) %all-gather.13.cloned.1.call-update) | async-done | bytes 3145744 | tf_op jit(solution)/shard_map/all_gather | solution.py:258
  98.3 4.2 convolution_add_fusion
  108.4 22.1 %all-gather.15.cloned.1.call-done = bf16[2048,256]{0,1:T(8,128)(2,1)} async-done(((bf16[512,256]{0,1:T(8,128)(2,1)}), bf16[2048,256]{0,1:T(8,128)(2,1)}) %all-gather.15.cloned.1.call-update) | async-done | bytes 1048592 | tf_op jit(solution)/shard_map/all_gather | solution.py:297
  130.5 2.5 slice_bitcast_fusion.15
  134.0 19.0 %attend.1 = (bf16[512,768]{1,0:T(8,128)(2,1)}, f32[6,1,512]{2,1,0:T(1,128)}) custom-call(s32[1]{0:T(128)} %bitcast.first_ref, s32[1,512]{1,0:T(1,128)} %bitcast.174, s32[2048,1]{1,0:T(8,128)} %copy.43.place_ref, bf16[512,768]{1,0:T(8,128)(2,1)} %copy.44.q_ref, bf16[2048,128]{1,0:T(8,128)(2,1)} %copy.45.k_ref, bf16[128,2048]{1,0:T(8,128)(2,1)} %get-tuple-element.54.vt_ref), custom_call_target="tpu_custom_call" | custom-call | flops 3221225472 | bytes 1572864 | tf_op jit(solution)/shard_map/attend/pallas_call | solution.py:310
  153.1 41.8 %all-gather.17.cloned.1.call-done = bf16[1536,768]{1,0:T(8,128)(2,1)} async-done(((bf16[96,768]{1,0:T(8,128)(2,1)}), bf16[1536,768]{1,0:T(8,128)(2,1)}) %all-gather.17.cloned.1.call-update) | async-done | bytes 2359312 | tf_op jit(solution)/shard_map/all_gather | solution.py:264
  194.8 5.0 fusion.30
  203.7 2.4 collective-permute-start.2
  206.1 5.6 collective-permute-done
  211.7 7.3 collective-permute-done.1
  223.4 5.2 collective-permute-start.3
  231.1 3.4 collective-permute-done.3
  234.5 8.0 collective-permute-done.4
  244.5 5.1 collective-permute-start.6
  249.5 3.4 collective-permute-start.7
  252.9 5.8 collective-permute-done.6
  258.8 8.2 collective-permute-done.7
  269.3 66.7 %all-gather.19.cloned.1.call-done = bf16[2048,1536]{1,0:T(8,128)(2,1)} async-done(((bf16[256,1536]{1,0:T(8,128)(2,1)}), bf16[2048,1536]{1,0:T(8,128)(2,1)}) %all-gather.19.cloned.1.call-update) | async-done | bytes 6291472 | tf_op jit(solution)/shard_map/all_gather | solution.py:318
  336.0 13.6 %fusion.31 = f32[2048,1152]{1,0:T(8,128)} fusion(bf16[2048,1536]{1,0:T(8,128)(2,1)} %all-gather.19.cloned.1.call-done, bf16[1536,1152]{1,0:T(8,128)(2,1)} %all-gather.21.cloned.1.call-done), kind=kOutput, calls=%fused_computation.161 | convolution fusion | flops 7247757312 | bytes 19267584 | tf_op jit(solution)/shard_map/dot_general | solution.py:43
  349.6 34.3 %all-gather.23.cloned.1.call-done = bf16[1536,1152]{1,0:T(8,128)(2,1)} async-done(((bf16[384,1152]{1,0:T(8,128)(2,1)}), bf16[1536,1152]{1,0:T(8,128)(2,1)}) %all-gather.23.cloned.1.call-update) | async-done | bytes 3538960 | tf_op jit(solution)/shard_map/all_gather | solution.py:82
  383.9 15.9 %multiply_convert_fusion.2 = (bf16[2048,1152]{1,0:T(8,128)(2,1)}, f32[2048,1152]{1,0:T(8,128)}) fusion(f32[2048,1152]{1,0:T(8,128)} %fusion.31, bf16[2048,1536]{1,0:T(8,128)(2,1)} %all-gather.19.cloned.1.call-done, bf16[1536,1152]{1,0:T(8,128)(2,1)} %all-gather.23.cloned.1.call-done), kind=kOutput, calls=%fused_computation.3 | convolution fusion | flops 7261913088 | bytes 33423360 | tf_op jit(solution)/shard_map/dot_general | solution.py:43
  399.8 33.6 %all-gather.25.cloned.1.call-done = bf16[1536,1152]{1,0:T(8,128)(2,1)} async-done(((bf16[384,1152]{1,0:T(8,128)(2,1)}), bf16[1536,1152]{1,0:T(8,128)(2,1)}) %all-gather.25.cloned.1.call-update) | async-done | bytes 3538960 | tf_op jit(solution)/shard_map/all_gather | solution.py:82
  433.4 13.2 %convolution_convert_fusion.3 = bf16[2048,1536]{1,0:T(8,128)(2,1)} fusion(bf16[2048,1152]{1,0:T(8,128)(2,1)} %get-tuple-element.102, bf16[1536,1152]{1,0:T(8,128)(2,1)} %all-gather.25.cloned.1.call-done), kind=kOutput, calls=%fused_computation.9 | convolution fusion | flops 7250903040 | bytes 14548992 | tf_op jit(solution)/shard_map/dot_general | solution.py:53
  450.0 2.4 collective-permute-start.11
  456.6 59.7 %reduce-scatter.15.cloned.1.call-done = bf16[256,1536]{1,0:T(8,128)(2,1)} async-done(((bf16[2048,1536]{1,0:T(8,128)(2,1)}), bf16[256,1536]{1,0:T(8,128)(2,1)}) %reduce-scatter.15.cloned.1.call-update) | async-done | bytes 786448 | tf_op jit(solution)/shard_map/reduce_scatter | solution.py:326
  516.4 2.5 fusion.26
  519.4 62.7 %all-gather.27.cloned.1.call-done = bf16[2048,1536]{1,0:T(8,128)(2,1)} async-done(((bf16[256,1536]{1,0:T(8,128)(2,1)}), bf16[2048,1536]{1,0:T(8,128)(2,1)}) %all-gather.27.cloned.1.call-update) | async-done | bytes 6291472 | tf_op jit(solution)/shard_map/all_gather | solution.py:336
  582.1 19.7 %multiply_convert_fusion.1 = (bf16[2048,1152]{1,0:T(8,128)(2,1)}, bf16[2048,1152]{1,0:T(8,128)(2,1)}) fusion(f32[2048,1152]{1,0:T(8,128)} %fusion.31, f32[2048,1152]{1,0:T(8,128)} %get-tuple-element.103, bf16[2048,1536]{1,0:T(8,128)(2,1)} %all-gather.27.cloned.1.call-done, bf16[1536,1152]{1,0:T(8,128)(2,1)} %all-gather.25.cloned.1.call-done), kind=kOutput, calls=%fused_computation.2 | convolution fusion | flops 7278428160 | bytes 38141952 | tf_op jit(solution)/shard_map/dot_general | solution.py:43
  601.7 13.1 %fusion.32 = f32[2048,1536]{1,0:T(8,128)} fusion(bf16[2048,1152]{1,0:T(8,128)(2,1)} %get-tuple-element.47, bf16[1536,1152]{1,0:T(8,128)(2,1)S(1)} %copy-done.30), kind=kOutput, calls=%fused_computation.162 | convolution fusion | flops 7247757312 | bytes 20840448 | tf_op jit(solution)/shard_map/dot_general | solution.py:53
  614.8 13.9 %add_convert_fusion = bf16[2048,1536]{1,0:T(8,128)(2,1)} fusion(f32[2048,1536]{1,0:T(8,128)} %fusion.32, bf16[2048,1152]{1,0:T(8,128)(2,1)} %get-tuple-element.46, bf16[1536,1152]{1,0:T(8,128)(2,1)S(1)} %copy-done.29), kind=kOutput, calls=%fused_computation | convolution fusion | flops 7254048768 | bytes 27131904 | tf_op jit(solution)/shard_map/dot_general | solution.py:53
  628.8 68.3 %reduce-scatter.17.cloned.1.call-done = bf16[256,1536]{1,0:T(8,128)(2,1)} async-done(((bf16[2048,1536]{1,0:T(8,128)(2,1)}), bf16[256,1536]{1,0:T(8,128)(2,1)}) %reduce-scatter.17.cloned.1.call-update) | async-done | bytes 786448 | tf_op jit(solution)/shard_map/reduce_scatter | solution.py:342
  697.1 2.9 fusion.13
  700.1 2.5 fusion.27
  702.8 2.1 copy.49.v_ref
  704.9 6.2 all-gather.29.cloned.1.call-done
  711.1 4.4 convolution_convert_fusion.7.do_ref
  715.5 26.4 %attend_back.1 = (f32[512,768]{1,0:T(8,128)}, bf16[2048,256]{1,0:T(8,128)(2,1)}) custom-call(s32[1]{0:T(128)} %bitcast.first_ref, s32[1,512]{1,0:T(1,128)} %bitcast.175, s32[2048,1]{1,0:T(8,128)} %copy.43.place_ref, bf16[512,768]{1,0:T(8,128)(2,1)} %copy.44.q_ref, bf16[512,768]{1,0:T(8,128)(2,1)} %convolution_convert_fusion.7.do_ref, ...), custom_call_target="tpu_custom_call" | custom-call | flops 8053063680 | bytes 3145728 | tf_op jit(solution)/shard_map/attend_back/pallas_call | solution.py:368
  742.0 13.1 %convolution_convert_fusion = bf16[1536,1152]{1,0:T(8,128)(2,1)} fusion(bf16[2048,1536]{1,0:T(8,128)(2,1)} %all-gather.27.cloned.1.call-done, bf16[2048,1152]{1,0:T(8,128)(2,1)} %get-tuple-element.102), kind=kOutput, calls=%fused_computation.6 | convolution fusion | flops 7249526784 | bytes 14548992 | tf_op jit(solution)/shard_map/dot_general | solution.py:47
  755.5 13.2 %convolution_convert_fusion.1 = bf16[1536,1152]{1,0:T(8,128)(2,1)} fusion(bf16[2048,1536]{1,0:T(8,128)(2,1)} %all-gather.19.cloned.1.call-done, bf16[2048,1152]{1,0:T(8,128)(2,1)} %get-tuple-element.47), kind=kOutput, calls=%fused_computation.7 | convolution fusion | flops 7249526784 | bytes 14548992 | tf_op jit(solution)/shard_map/dot_general | solution.py:47
  768.7 13.3 %convolution_convert_fusion.2 = bf16[1536,1152]{1,0:T(8,128)(2,1)} fusion(bf16[2048,1536]{1,0:T(8,128)(2,1)} %all-gather.19.cloned.1.call-done, bf16[2048,1152]{1,0:T(8,128)(2,1)} %get-tuple-element.46), kind=kOutput, calls=%fused_computation.8 | convolution fusion | flops 7249526784 | bytes 14548992 | tf_op jit(solution)/shard_map/dot_general | solution.py:47
  783.6 2.8 convolution_convert_fusion.5
  792.8 3.0 convolution_convert_fusion.6
  795.9 3.5 convolution_convert_fusion.4
  799.5 19.9 %reduce-scatter.35.cloned.1.call-done = bf16[384,1152]{1,0:T(8,128)(2,1)} async-done(((bf16[1536,1152]{1,0:T(8,128)(2,1)}), bf16[384,1152]{1,0:T(8,128)(2,1)}) %reduce-scatter.35.cloned.1.call-update) | async-done | bytes 884752 | tf_op jit(solution)/shard_map/reduce_scatter | solution.py:87
  819.4 2.0 dynamic-slice_bitcast_fusion
  822.8 2.4 collective-permute-start.24
  826.7 43.0 %reduce-scatter.33.cloned.1.call-done = bf16[384,1152]{1,0:T(8,128)(2,1)} async-done(((bf16[1536,1152]{1,0:T(8,128)(2,1)}), bf16[384,1152]{1,0:T(8,128)(2,1)}) %reduce-scatter.33.cloned.1.call-update) | async-done | bytes 884752 | tf_op jit(solution)/shard_map/reduce_scatter | solution.py:87
  869.6 2.0 dynamic-slice_bitcast_fusion.3
  873.1 2.4 collective-permute-start.21
  880.8 39.0 %reduce-scatter.31.cloned.1.call-done = bf16[384,1152]{1,0:T(8,128)(2,1)} async-done(((bf16[1536,1152]{1,0:T(8,128)(2,1)}), bf16[384,1152]{1,0:T(8,128)(2,1)}) %reduce-scatter.31.cloned.1.call-update) | async-done | bytes 884752 | tf_op jit(solution)/shard_map/reduce_scatter | solution.py:87
  922.8 3.4 collective-permute-start.22
  929.4 2.7 collective-permute-start.19
  934.3 3.7 collective-permute-done.17
  938.0 2.5 convert_bitcast_fusion
  940.5 2.5 slice_convert_fusion
  943.6 16.7 %reduce-scatter.27.cloned.1.call-done = bf16[384,768]{1,0:T(8,128)(2,1)} async-done(((bf16[1536,768]{1,0:T(8,128)(2,1)}), bf16[384,768]{1,0:T(8,128)(2,1)}) %reduce-scatter.27.cloned.1.call-update) | async-done | bytes 589840 | tf_op jit(solution)/shard_map/reduce_scatter | solution.py:360
  960.3 11.7 %reduce-scatter.21.cloned.1.call-done = bf16[256,1536]{1,0:T(8,128)(2,1)} async-done(((bf16[512,1536]{1,0:T(8,128)(2,1)}), bf16[256,1536]{1,0:T(8,128)(2,1)}) %reduce-scatter.21.cloned.1.call-update) | async-done | bytes 786448 | tf_op jit(solution)/shard_map/reduce_scatter | solution.py:387
  979.6 2.8 collective-permute-start.14
  982.4 37.8 %reduce-scatter.23.cloned.1.call-done = bf16[384,1024]{1,0:T(8,128)(2,1)} async-done(((bf16[1536,1024]{1,0:T(8,128)(2,1)}), bf16[384,1024]{1,0:T(8,128)(2,1)}) %reduce-scatter.23.cloned.1.call-update) | async-done | bytes 786448 | tf_op jit(solution)/shard_map/reduce_scatter | solution.py:360
  1023.1 2.4 collective-permute-done.15
  1031.6 12.9 %reduce-scatter.29.cloned.1.call-done = bf16[96,768]{1,0:T(8,128)(2,1)} async-done(((bf16[384,768]{1,0:T(8,128)(2,1)}), bf16[96,768]{1,0:T(8,128)(2,1)}) %reduce-scatter.29.cloned.1.call-update) | async-done | bytes 147472 | tf_op jit(solution)/shard_map/reduce_scatter | solution.py:361
  1046.2 22.1 %reduce-scatter.25.cloned.1.call-done = bf16[96,1024]{1,0:T(8,128)(2,1)} async-done(((bf16[384,1024]{1,0:T(8,128)(2,1)}), bf16[96,1024]{1,0:T(8,128)(2,1)}) %reduce-scatter.25.cloned.1.call-update) | async-done | bytes 196624 | tf_op jit(solution)/shard_map/reduce_scatter | solution.py:361
  (261 shorter events, 80.9 us)
Async XLA Ops:
  8.1 6.0 copy-start.35
  8.1 6.1 copy-start.28
  8.1 17.7 %all-gather.11.cloned.1.call-start = ((), (), s32[]{:S(2)}) async-start(), calls=%async_computation.12 | async-start | bytes 2359296 | tf_op jit(solution)/shard_map/all_gather | solution.py:255
  13.1 85.2 %all-gather.13.cloned.1.call-start = ((), (), s32[]{:S(2)}) async-start(), calls=%async_computation.13 | async-start | bytes 3342336 | tf_op jit(solution)/shard_map/all_gather | solution.py:258
  13.9 116.6 %all-gather.15.cloned.1.call-start = ((), (), s32[]{:S(2)}) async-start(), calls=%async_computation.14 | async-start | bytes 1310720 | tf_op jit(solution)/shard_map/all_gather | solution.py:297
  16.2 86.5 %copy-start.16 = (f32[512,64]{0,1:T(8,128)}, f32[512,64]{0,1:T(8,128)S(1)}, u32[]{:S(2)}) copy-start(f32[512,64]{0,1:T(8,128)S(1)} %get-tuple-element.101) | copy-start | bytes 393220
  103.9 91.0 %all-gather.17.cloned.1.call-start = ((), (), s32[]{:S(2)}) async-start(), calls=%async_computation.15 | async-start | bytes 2506752 | tf_op jit(solution)/shard_map/all_gather | solution.py:264
  104.4 115.7 %reduce-scatter.13.cloned.1.call-start = ((), (), s32[]{:S(2)}) async-start(), calls=%async_computation.16 | async-start | bytes 4718592 | tf_op jit(solution)/shard_map/reduce_scatter | solution.py:312
  199.8 69.4 %all-gather.21.cloned.1.call-start = ((), (), s32[]{:S(2)}) async-start(), calls=%async_computation.18 | async-start | bytes 4423680 | tf_op jit(solution)/shard_map/all_gather | solution.py:82
  201.3 18.8 %copy-start.27 = (bf16[1536]{0:T(1024)(128)(2,1)S(1)}, bf16[1536]{0:T(1024)(128)(2,1)}, u32[]{:S(2)}) copy-start(bf16[1536]{0:T(1024)(128)(2,1)} %param.34) | copy-start | bytes 9220
  201.3 18.8 %copy-start = (bf16[256,1536]{1,0:T(8,128)(2,1)S(1)}, bf16[256,1536]{1,0:T(8,128)(2,1)}, u32[]{:S(2)}) copy-start(bf16[256,1536]{1,0:T(8,128)(2,1)} %param.20) | copy-start | bytes 2359300
  201.4 10.3 collective-permute-start
  202.9 16.1 %collective-permute-start.1 = (bf16[96,1152]{1,0:T(8,128)(2,1)S(1)}, bf16[96,1152]{1,0:T(8,128)(2,1)S(1)}, u32[]{:S(2)}, u32[]{:S(2)}) collective-permute-start(bf16[96,1152]{1,0:T(8,128)(2,1)S(1)} %get-tuple-element.71), channel_id=1, source_target_pairs={{0,4},{2,6},{4,0},{6,2},{1,5},{3,7},{5,1},{7,3},{8,12},{10,14},{12... | collective-permute-start | bytes 663560 | tf_op jit(solution)/shard_map/ppermute | solution.py:69
  203.7 15.3 %collective-permute-start.2 = (bf16[96,1152]{1,0:T(8,128)(2,1)S(1)}, bf16[96,1152]{1,0:T(8,128)(2,1)S(1)}, u32[]{:S(2)}, u32[]{:S(2)}) collective-permute-start(bf16[96,1152]{1,0:T(8,128)(2,1)S(1)} %get-tuple-element.70), channel_id=1, source_target_pairs={{0,6},{2,0},{4,2},{6,4},{1,7},{3,1},{5,3},{7,5},{8,14},{10,8},{12,... | collective-permute-start | bytes 663560 | tf_op jit(solution)/shard_map/ppermute | solution.py:69
  220.0 115.9 %all-gather.19.cloned.1.call-start = ((), (), s32[]{:S(2)}) async-start(), calls=%async_computation.17 | async-start | bytes 7077888 | tf_op jit(solution)/shard_map/all_gather | solution.py:318
  222.9 161.0 %all-gather.23.cloned.1.call-start = ((), (), s32[]{:S(2)}) async-start(), calls=%async_computation.19 | async-start | bytes 4423680 | tf_op jit(solution)/shard_map/all_gather | solution.py:82
  223.3 20.7 %copy-start.14 = (bf16[4480,96]{0,1:T(8,128)(2,1)S(1)}, bf16[4480,96]{0,1:T(8,128)(2,1)}, u32[]{:S(2)}) copy-start(bf16[4480,96]{0,1:T(8,128)(2,1)} %param.37) | copy-start | bytes 2580484
  223.4 11.0 %collective-permute-start.3 = (bf16[96,1152]{1,0:T(8,128)(2,1)S(1)}, bf16[96,1152]{1,0:T(8,128)(2,1)S(1)}, u32[]{:S(2)}, u32[]{:S(2)}) collective-permute-start(bf16[96,1152]{1,0:T(8,128)(2,1)S(1)} %get-tuple-element.76), channel_id=1, source_target_pairs={{0,2},{2,4},{4,6},{6,0},{1,3},{3,5},{5,7},{7,1},{8,10},{10,12},{12... | collective-permute-start | bytes 663560 | tf_op jit(solution)/shard_map/ppermute | solution.py:69
  228.6 13.8 %collective-permute-start.4 = (bf16[96,1152]{1,0:T(8,128)(2,1)S(1)}, bf16[96,1152]{1,0:T(8,128)(2,1)S(1)}, u32[]{:S(2)}, u32[]{:S(2)}) collective-permute-start(bf16[96,1152]{1,0:T(8,128)(2,1)S(1)} %get-tuple-element.75), channel_id=1, source_target_pairs={{0,4},{2,6},{4,0},{6,2},{1,5},{3,7},{5,1},{7,3},{8,12},{10,14},{12... | collective-permute-start | bytes 663560 | tf_op jit(solution)/shard_map/ppermute | solution.py:69
  229.5 13.5 %collective-permute-start.5 = (bf16[96,1152]{1,0:T(8,128)(2,1)S(1)}, bf16[96,1152]{1,0:T(8,128)(2,1)S(1)}, u32[]{:S(2)}, u32[]{:S(2)}) collective-permute-start(bf16[96,1152]{1,0:T(8,128)(2,1)S(1)} %get-tuple-element.74), channel_id=1, source_target_pairs={{0,6},{2,0},{4,2},{6,4},{1,7},{3,1},{5,3},{7,5},{8,14},{10,8},{12,... | collective-permute-start | bytes 663560 | tf_op jit(solution)/shard_map/ppermute | solution.py:69
  244.0 189.4 %all-gather.25.cloned.1.call-start = ((), (), s32[]{:S(2)}) async-start(), calls=%async_computation.20 | async-start | bytes 4423680 | tf_op jit(solution)/shard_map/all_gather | solution.py:82
  244.5 14.3 %collective-permute-start.6 = (bf16[96,1152]{1,0:T(8,128)(2,1)S(1)}, bf16[96,1152]{1,0:T(8,128)(2,1)S(1)}, u32[]{:S(2)}, u32[]{:S(2)}) collective-permute-start(bf16[96,1152]{1,0:T(8,128)(2,1)S(1)} %get-tuple-element.68), channel_id=1, source_target_pairs={{0,2},{2,4},{4,6},{6,0},{1,3},{3,5},{5,7},{7,1},{8,10},{10,12},{12... | collective-permute-start | bytes 663560 | tf_op jit(solution)/shard_map/ppermute | solution.py:69
  249.5 17.5 %collective-permute-start.7 = (bf16[96,1152]{1,0:T(8,128)(2,1)S(1)}, bf16[96,1152]{1,0:T(8,128)(2,1)S(1)}, u32[]{:S(2)}, u32[]{:S(2)}) collective-permute-start(bf16[96,1152]{1,0:T(8,128)(2,1)S(1)} %get-tuple-element.67), channel_id=1, source_target_pairs={{0,4},{2,6},{4,0},{6,2},{1,5},{3,7},{5,1},{7,3},{8,12},{10,14},{12... | collective-permute-start | bytes 663560 | tf_op jit(solution)/shard_map/ppermute | solution.py:69
  252.9 14.1 %collective-permute-start.8 = (bf16[96,1152]{1,0:T(8,128)(2,1)S(1)}, bf16[96,1152]{1,0:T(8,128)(2,1)S(1)}, u32[]{:S(2)}, u32[]{:S(2)}) collective-permute-start(bf16[96,1152]{1,0:T(8,128)(2,1)S(1)} %get-tuple-element.66), channel_id=1, source_target_pairs={{0,6},{2,0},{4,2},{6,4},{1,7},{3,1},{5,3},{7,5},{8,14},{10,8},{12,... | collective-permute-start | bytes 663560 | tf_op jit(solution)/shard_map/ppermute | solution.py:69
  268.0 248.4 %reduce-scatter.15.cloned.1.call-start = ((), (), s32[]{:S(2)}) async-start(), calls=%async_computation.21 | async-start | bytes 7077888 | tf_op jit(solution)/shard_map/reduce_scatter | solution.py:326
  446.6 69.8 %copy-start.2 = (bf16[256,1536]{1,0:T(8,128)(2,1)S(1)}, bf16[256,1536]{1,0:T(8,128)(2,1)}, u32[]{:S(2)}) copy-start(bf16[256,1536]{1,0:T(8,128)(2,1)} %param.21) | copy-start | bytes 2359300
  446.6 69.8 %copy-start.10 = (bf16[256,1536]{1,0:T(8,128)(2,1)S(1)}, bf16[256,1536]{1,0:T(8,128)(2,1)}, u32[]{:S(2)}) copy-start(bf16[256,1536]{1,0:T(8,128)(2,1)} %param.22) | copy-start | bytes 2359300
  446.6 135.4 %all-gather.27.cloned.1.call-start = ((), (), s32[]{:S(2)}) async-start(), calls=%async_computation.22 | async-start | bytes 7077888 | tf_op jit(solution)/shard_map/all_gather | solution.py:336
  447.9 4.6 collective-permute-start.9
  449.4 4.8 collective-permute-start.10
  450.0 5.5 collective-permute-start.11
  518.9 178.2 %reduce-scatter.17.cloned.1.call-start = ((), (), s32[]{:S(2)}) async-start(), calls=%async_computation.23 | async-start | bytes 7077888 | tf_op jit(solution)/shard_map/reduce_scatter | solution.py:342
  582.1 19.7 %copy-start.30 = (bf16[1536,1152]{1,0:T(8,128)(2,1)S(1)}, bf16[1536,1152]{1,0:T(8,128)(2,1)}, u32[]{:S(2)}) copy-start(bf16[1536,1152]{1,0:T(8,128)(2,1)} %all-gather.23.cloned.1.call-done) | copy-start | bytes 10616836
  601.7 13.1 %copy-start.29 = (bf16[1536,1152]{1,0:T(8,128)(2,1)S(1)}, bf16[1536,1152]{1,0:T(8,128)(2,1)}, u32[]{:S(2)}) copy-start(bf16[1536,1152]{1,0:T(8,128)(2,1)} %all-gather.21.cloned.1.call-done) | copy-start | bytes 10616836
  628.8 68.4 %copy-start.3 = (bf16[256,1536]{1,0:T(8,128)(2,1)S(1)}, bf16[256,1536]{1,0:T(8,128)(2,1)}, u32[]{:S(2)}) copy-start(bf16[256,1536]{1,0:T(8,128)(2,1)} %reduce-scatter.15.cloned.1.call-done) | copy-start | bytes 2359300
  628.8 82.3 %all-gather.29.cloned.1.call-start = ((), (), s32[]{:S(2)}) async-start(), calls=%async_computation.24 | async-start | bytes 2359296 | tf_op jit(solution)/shard_map/all_gather | solution.py:355
  702.6 84.1 %reduce-scatter.19.cloned.1.call-start = ((), (), s32[]{:S(2)}) async-start(), calls=%async_computation.25 | async-start | bytes 1310720 | tf_op jit(solution)/shard_map/reduce_scatter | solution.py:375
  742.0 77.4 %reduce-scatter.35.cloned.1.call-start = ((), (), s32[]{:S(2)}) async-start(), calls=%async_computation.33 | async-start | bytes 4423680 | tf_op jit(solution)/shard_map/reduce_scatter | solution.py:87
  755.2 114.4 %reduce-scatter.33.cloned.1.call-start = ((), (), s32[]{:S(2)}) async-start(), calls=%async_computation.32 | async-start | bytes 4423680 | tf_op jit(solution)/shard_map/reduce_scatter | solution.py:87
  768.6 151.2 %reduce-scatter.31.cloned.1.call-start = ((), (), s32[]{:S(2)}) async-start(), calls=%async_computation.31 | async-start | bytes 4423680 | tf_op jit(solution)/shard_map/reduce_scatter | solution.py:87
  782.0 178.3 %reduce-scatter.27.cloned.1.call-start = ((), (), s32[]{:S(2)}) async-start(), calls=%async_computation.29 | async-start | bytes 2949120 | tf_op jit(solution)/shard_map/reduce_scatter | solution.py:360
  786.4 185.6 %reduce-scatter.21.cloned.1.call-start = ((), (), s32[]{:S(2)}) async-start(), calls=%async_computation.26 | async-start | bytes 2359296 | tf_op jit(solution)/shard_map/reduce_scatter | solution.py:387
  795.9 224.4 %reduce-scatter.23.cloned.1.call-start = ((), (), s32[]{:S(2)}) async-start(), calls=%async_computation.27 | async-start | bytes 3932160 | tf_op jit(solution)/shard_map/reduce_scatter | solution.py:360
  799.4 245.1 %reduce-scatter.29.cloned.1.call-start = ((), (), s32[]{:S(2)}) async-start(), calls=%async_computation.30 | async-start | bytes 737280 | tf_op jit(solution)/shard_map/reduce_scatter | solution.py:361
  821.3 101.5 %collective-permute-start.23 = (bf16[96,1152]{1,0:T(8,128)(2,1)}, bf16[96,1152]{1,0:T(8,128)(2,1)S(1)}, u32[]{:S(2)}, u32[]{:S(2)}) collective-permute-start(bf16[96,1152]{1,0:T(8,128)(2,1)} %get-tuple-element.59), channel_id=1, source_target_pairs={{0,2},{2,4},{4,6},{6,0},{1,3},{3,5},{5,7},{7,1},{8,10},{10,12},{12... | collective-permute-start | bytes 663560 | tf_op jit(solution)/shard_map/ppermute | solution.py:69
  822.8 104.8 %collective-permute-start.24 = (bf16[96,1152]{1,0:T(8,128)(2,1)S(1)}, bf16[96,1152]{1,0:T(8,128)(2,1)S(1)}, u32[]{:S(2)}, u32[]{:S(2)}) collective-permute-start(bf16[96,1152]{1,0:T(8,128)(2,1)S(1)} %get-tuple-element.58), channel_id=1, source_target_pairs={{0,4},{2,6},{4,0},{6,2},{1,5},{3,7},{5,1},{7,3},{8,12},{10,14},{12... | collective-permute-start | bytes 663560 | tf_op jit(solution)/shard_map/ppermute | solution.py:69
  825.2 107.6 %collective-permute-start.25 = (bf16[96,1152]{1,0:T(8,128)(2,1)}, bf16[96,1152]{1,0:T(8,128)(2,1)S(1)}, u32[]{:S(2)}, u32[]{:S(2)}) collective-permute-start(bf16[96,1152]{1,0:T(8,128)(2,1)} %get-tuple-element.57), channel_id=1, source_target_pairs={{0,6},{2,0},{4,2},{6,4},{1,7},{3,1},{5,3},{7,5},{8,14},{10,8},{12,... | collective-permute-start | bytes 663560 | tf_op jit(solution)/shard_map/ppermute | solution.py:69
  871.6 55.2 %collective-permute-start.20 = (bf16[96,1152]{1,0:T(8,128)(2,1)}, bf16[96,1152]{1,0:T(8,128)(2,1)S(1)}, u32[]{:S(2)}, u32[]{:S(2)}) collective-permute-start(bf16[96,1152]{1,0:T(8,128)(2,1)} %get-tuple-element.62), channel_id=1, source_target_pairs={{0,2},{2,4},{4,6},{6,0},{1,3},{3,5},{5,7},{7,1},{8,10},{10,12},{12... | collective-permute-start | bytes 663560 | tf_op jit(solution)/shard_map/ppermute | solution.py:69
  873.1 56.3 %collective-permute-start.21 = (bf16[96,1152]{1,0:T(8,128)(2,1)}, bf16[96,1152]{1,0:T(8,128)(2,1)S(1)}, u32[]{:S(2)}, u32[]{:S(2)}) collective-permute-start(bf16[96,1152]{1,0:T(8,128)(2,1)} %get-tuple-element.61), channel_id=1, source_target_pairs={{0,4},{2,6},{4,0},{6,2},{1,5},{3,7},{5,1},{7,3},{8,12},{10,14},{12... | collective-permute-start | bytes 663560 | tf_op jit(solution)/shard_map/ppermute | solution.py:69
  922.8 10.8 collective-permute-start.22
  926.9 11.1 %collective-permute-start.17 = (bf16[96,1152]{1,0:T(8,128)(2,1)S(1)}, bf16[96,1152]{1,0:T(8,128)(2,1)S(1)}, u32[]{:S(2)}, u32[]{:S(2)}) collective-permute-start(bf16[96,1152]{1,0:T(8,128)(2,1)S(1)} %get-tuple-element.65), channel_id=1, source_target_pairs={{0,2},{2,4},{4,6},{6,0},{1,3},{3,5},{5,7},{7,1},{8,10},{10,12},{12... | collective-permute-start | bytes 663560 | tf_op jit(solution)/shard_map/ppermute | solution.py:69
  927.6 47.3 %collective-permute-start.18 = (bf16[96,1152]{1,0:T(8,128)(2,1)}, bf16[96,1152]{1,0:T(8,128)(2,1)S(1)}, u32[]{:S(2)}, u32[]{:S(2)}) collective-permute-start(bf16[96,1152]{1,0:T(8,128)(2,1)} %get-tuple-element.64), channel_id=1, source_target_pairs={{0,4},{2,6},{4,0},{6,2},{1,5},{3,7},{5,1},{7,3},{8,12},{10,14},{12... | collective-permute-start | bytes 663560 | tf_op jit(solution)/shard_map/ppermute | solution.py:69
  929.4 48.2 %collective-permute-start.19 = (bf16[96,1152]{1,0:T(8,128)(2,1)}, bf16[96,1152]{1,0:T(8,128)(2,1)S(1)}, u32[]{:S(2)}, u32[]{:S(2)}) collective-permute-start(bf16[96,1152]{1,0:T(8,128)(2,1)} %get-tuple-element.63), channel_id=1, source_target_pairs={{0,6},{2,0},{4,2},{6,4},{1,7},{3,1},{5,3},{7,5},{8,14},{10,8},{12,... | collective-permute-start | bytes 663560 | tf_op jit(solution)/shard_map/ppermute | solution.py:69
  940.5 31.5 %copy-start.1 = (bf16[256,1536]{1,0:T(8,128)(2,1)S(1)}, bf16[256,1536]{1,0:T(8,128)(2,1)}, u32[]{:S(2)}) copy-start(bf16[256,1536]{1,0:T(8,128)(2,1)} %param.20) | copy-start | bytes 2359300
  940.5 31.5 %copy-start.21 = (f32[1536]{0:T(1024)S(1)}, f32[1536]{0:T(1024)}, u32[]{:S(2)}) copy-start(f32[1536]{0:T(1024)} %copy-done.20) | copy-start | bytes 18436
  940.5 31.5 %copy-start.26 = (f32[256]{0:T(256)S(1)}, f32[256]{0:T(256)}, u32[]{:S(2)}) copy-start(f32[256]{0:T(256)} %copy-done.25) | copy-start | bytes 3076
  960.3 108.0 %reduce-scatter.25.cloned.1.call-start = ((), (), s32[]{:S(2)}) async-start(), calls=%async_computation.28 | async-start | bytes 983040 | tf_op jit(solution)/shard_map/reduce_scatter | solution.py:361
  974.5 1.3 collective-permute-start.12
  974.9 52.0 %copy-start.4 = (f32[256,1536]{1,0:T(8,128)S(1)}, f32[256,1536]{1,0:T(8,128)}, u32[]{:S(2)}) copy-start(f32[256,1536]{1,0:T(8,128)} %get-tuple-element.41) | copy-start | bytes 4718596
  975.8 3.8 collective-permute-start.13
  979.6 41.9 %collective-permute-start.14 = (f32[41,128]{1,0:T(8,128)S(1)}, f32[41,128]{1,0:T(8,128)S(1)}, u32[]{:S(2)}, u32[]{:S(2)}) collective-permute-start(f32[41,128]{1,0:T(8,128)S(1)} %fusion.61), channel_id=1, source_target_pairs={{0,4},{2,6},{4,0},{6,2},{1,5},{3,7},{5,1},{7,3},{8,12},{10,14},{12... | collective-permute-start | bytes 62984 | tf_op jit(solution)/shard_map/ppermute | solution.py:103
  1020.2 6.7 copy-start.8
  1021.6 3.9 collective-permute-start.15
  1025.5 3.8 collective-permute-start.16
  (21 other events, 50.0 us)
Sparse Core Ops, SparseCore 0:
  13.2 12.5 all-gather.10
  29.2 69.0 all-gather.12
  104.0 26.5 all-gather.14
  133.2 61.6 all-gather.16
  200.0 9.5 reduce-scatter.12
  702.7 8.3 all-gather.28
  742.1 28.4 reduce-scatter.18
  773.7 45.6 reduce-scatter.34
  822.5 47.1 reduce-scatter.32
  872.6 47.1 reduce-scatter.30
  922.9 37.3 reduce-scatter.26
  962.9 9.0 reduce-scatter.20
  975.0 45.1 reduce-scatter.22
  1022.3 22.1 reduce-scatter.28
  1046.7 21.5 reduce-scatter.24
Sparse Core Ops, SparseCore 1:
  220.1 49.1 all-gather.20
  271.4 64.5 all-gather.18
  338.3 45.6 all-gather.22
  386.4 47.0 all-gather.24
  446.7 69.6 reduce-scatter.14
  519.0 63.0 all-gather.26
  628.9 68.2 reduce-scatter.16

commit v2 on v1

--- a/solution.py
+++ b/solution.py
@@ -71,17 +71,6 @@
     return received
 
 
-def to_columns(shard, width):
-    size = lax.axis_size("ctx")
-    rows, columns = shard.shape
-    padded = jnp.pad(shard, ((0, 0), (0, size * width - columns)))
-    blocks = jnp.stack([padded[:, j * width : (j + 1) * width] for j in range(size)])
-    gathered = jnp.zeros((size, rows, width), shard.dtype)
-    for rank, block in exchange(blocks, "ctx"):
-        gathered = lax.dynamic_update_index_in_dim(gathered, block, rank, 0)
-    return lax.all_gather(gathered.reshape(size * rows, width), "dp", axis=0, tiled=True)
-
-
 def to_rows(grad, columns):
     size = lax.axis_size("ctx")
     summed = lax.psum_scatter(grad, "dp", scatter_dimension=0, tiled=True)
@@ -103,6 +92,405 @@
             value = value + lax.ppermute(value, axis, [(i, i ^ step) for i in range(size)])
             step *= 2
     return value
+
+
+MESH = pl.DeviceIdType.MESH
+ANY = pl.BlockSpec(memory_space=pl.ANY)
+IN_VMEM = pl.BlockSpec(memory_space=pltpu.VMEM)
+
+
+def remote(source, target, send_sem, recv_sem, device):
+    return pltpu.make_async_remote_copy(
+        src_ref=source,
+        dst_ref=target,
+        send_sem=send_sem,
+        recv_sem=recv_sem,
+        device_id=device,
+        device_id_type=MESH,
+    )
+
+
+def greet(barrier, device):
+    pl.semaphore_signal(barrier, inc=1, device_id=device, device_id_type=MESH)
+
+
+def greet_chain(size, paired):
+    place = lax.axis_index("ctx")
+    barrier = pltpu.get_barrier_semaphore()
+    if size > 1:
+        pl.when(place < size - 1)(lambda: greet(barrier, {"ctx": place + 1}))
+        pl.when(place > 0)(lambda: greet(barrier, {"ctx": place - 1}))
+    if paired:
+        greet(barrier, {"tensor": 1 - lax.axis_index("tensor")})
+    if size == 1:
+        pl.semaphore_wait(barrier, 1)
+        return
+    ends = (place == 0) | (place == size - 1)
+    pl.when(ends)(lambda: pl.semaphore_wait(barrier, 1 + paired))
+    pl.when(jnp.logical_not(ends))(lambda: pl.semaphore_wait(barrier, 2 + paired))
+
+
+def gather_kernel(size, paired, pieces, x_ref, o_ref, local_sem, up_send, up_recv, down_send, down_recv, mate_send, mate_recv):
+    place = lax.axis_index("ctx") if size > 1 else 0
+    core = lax.axis_index("tensor")
+    rows = x_ref.shape[0]
+    part = rows // pieces
+    greet_chain(size, paired)
+
+    def block(rank, which, p):
+        index = rank * 2 + which if paired else rank
+        return o_ref.at[pl.ds(pl.multiple_of(index * rows + p * part, part), part)]
+
+    def source(rank, k, p):
+        return x_ref.at[pl.ds(p * part, part)] if k == 0 else block(rank, core, p)
+
+    def going_up(k, p):
+        return remote(
+            source(place - k, k, p), block(place - k, core, p), up_send.at[k, p], up_recv.at[k, p], {"ctx": place + 1}
+        )
+
+    def going_down(k, p):
+        return remote(
+            source(place + k, k, p), block(place + k, core, p), down_send.at[k, p], down_recv.at[k, p], {"ctx": place - 1}
+        )
+
+    def to_mate(rank, k, p):
+        return remote(
+            source(rank, k, p), block(rank, core, p), mate_send.at[k, p], mate_recv.at[rank, p], {"tensor": 1 - core}
+        )
+
+    def from_mate(rank, p):
+        there = block(rank, 1 - core, p)
+        return remote(there, there, mate_send.at[0, p], mate_recv.at[rank, p], {"tensor": 1 - core})
+
+    own = pltpu.make_async_copy(x_ref, o_ref.at[pl.ds(pl.multiple_of((place * 2 + core if paired else place) * rows, rows), rows)], local_sem)
+    for p in range(pieces):
+        if size > 1:
+            pl.when(place < size - 1)(lambda p=p: going_up(0, p).start())
+            pl.when(place > 0)(lambda p=p: going_down(0, p).start())
+    for p in range(pieces):
+        if paired:
+            to_mate(place, 0, p).start()
+    own.start()
+    for k in range(size - 1):
+        for p in range(pieces):
+
+            @pl.when(place - 1 - k >= 0)
+            def _(k=k, p=p):
+                there = block(place - 1 - k, core, p)
+                remote(there, there, up_send.at[k, p], up_recv.at[k, p], {"ctx": place - 1}).wait_recv()
+                if k + 1 < size - 1:
+                    pl.when(place < size - 1)(lambda: going_up(k + 1, p).start())
+                if paired:
+                    to_mate(place - 1 - k, 1 + k, p).start()
+
+            @pl.when(place + 1 + k <= size - 1)
+            def _(k=k, p=p):
+                there = block(place + 1 + k, core, p)
+                remote(there, there, down_send.at[k, p], down_recv.at[k, p], {"ctx": place + 1}).wait_recv()
+                if k + 1 < size - 1:
+                    pl.when(place > 0)(lambda: going_down(k + 1, p).start())
+                if paired:
+                    to_mate(place + 1 + k, size + k, p).start()
+
+    own.wait()
+    for p in range(pieces):
+        if paired:
+            for rank in range(size):
+                from_mate(rank, p).wait_recv()
+            to_mate(place, 0, p).wait_send()
+        for k in range(size - 1):
+            pl.when((place < size - 1) & (place - k >= 0))(lambda k=k, p=p: going_up(k, p).wait_send())
+            pl.when((place > 0) & (place + k <= size - 1))(lambda k=k, p=p: going_down(k, p).wait_send())
+            if paired:
+                pl.when(place - 1 - k >= 0)(lambda k=k, p=p: to_mate(place - 1 - k, 1 + k, p).wait_send())
+                pl.when(place + 1 + k <= size - 1)(lambda k=k, p=p: to_mate(place + 1 + k, size + k, p).wait_send())
+
+
+def pieces_of(rows, columns):
+    return math.gcd(4, rows // 64) if rows * columns >= 1 << 18 else 1
+
+
+def gather(x, size, paired, ident):
+    copies = size * 2 if paired else size
+    wide = max(size, 2)
+    pieces = pieces_of(*x.shape)
+    dma = pltpu.SemaphoreType.DMA
+    return pl.pallas_call(
+        functools.partial(gather_kernel, size, paired, pieces),
+        in_specs=[IN_VMEM],
+        out_specs=ANY,
+        out_shape=jax.ShapeDtypeStruct((copies * x.shape[0], x.shape[1]), x.dtype),
+        scratch_shapes=[dma] + [dma((wide, pieces))] * 4 + [dma((2 * wide, pieces)), dma((wide, pieces))],
+        compiler_params=pltpu.CompilerParams(collective_id=ident, has_side_effects=True),
+        cost_estimate=pl.CostEstimate(flops=0, bytes_accessed=30 * copies * x.size, transcendentals=0),
+        name="gather",
+    )(x)
+
+
+def add_blocks(target, parts):
+    rows = target.shape[0]
+    step = math.gcd(rows, 32)
+
+    def some(i, carry):
+        span = pl.ds(pl.multiple_of(i * step, step), step)
+        total = parts[0][span].astype(jnp.float32)
+        for part in parts[1:]:
+            total += part[span].astype(jnp.float32)
+        target[span] = total.astype(target.dtype)
+        return carry
+
+    lax.fori_loop(0, rows // step, some, 0)
+
+
+def scatter_kernel(
+    size, paired, pieces, x_ref, o_ref, mine, mate, above, below, own_sem, mate_send, mate_recv, up_send, up_recv, down_send, down_recv
+):
+    place = lax.axis_index("ctx") if size > 1 else 0
+    core = lax.axis_index("tensor")
+    rows = o_ref.shape[0]
+    part = rows // pieces
+    order = sorted(range(size), key=lambda d: min(d, size - 1 - d))
+    every = [(d, p) for d in order for p in range(pieces)]
+
+    def block(rank, which, p):
+        index = rank * 2 + which if paired else rank
+        return x_ref.at[pl.ds(pl.multiple_of(index * rows + p * part, part), part)]
+
+    def at(ref, d, p):
+        return ref.at[d, pl.ds(p * part, part)]
+
+    def load(d, p):
+        return pltpu.make_async_copy(block(d, core, p), at(mine, d, p), own_sem.at[d, p])
+
+    def to_mate(d, p):
+        return remote(
+            block(d, 1 - core, p), at(mate, d, p), mate_send.at[d, p], mate_recv.at[d, p], {"tensor": 1 - core}
+        )
+
+    def going_up(d, p):
+        return remote(at(mine, d, p), at(below, d, p), up_send.at[d, p], up_recv.at[d, p], {"ctx": place + 1})
+
+    def going_down(d, p):
+        return remote(at(mine, d, p), at(above, d, p), down_send.at[d, p], down_recv.at[d, p], {"ctx": place - 1})
+
+    for d, p in every:
+        load(d, p).start()
+    greet_chain(size, paired)
+    if paired:
+        for d, p in every:
+            to_mate(d, p).start()
+
+    def here(d, p):
+        load(d, p).wait()
+        if paired:
+            to_mate(d, p).wait_recv()
+            return [at(mine, d, p), at(mate, d, p)]
+        return [at(mine, d, p)]
+
+    for k in range(size - 1):
+        for p in range(pieces):
+
+            @pl.when(place < size - 1 - k)
+            def _(d=size - 1 - k, p=p):
+                parts = here(d, p)
+
+                @pl.when(place > 0)
+                def _():
+                    going_up(d, p).wait_recv()
+                    add_blocks(at(mine, d, p), parts + [at(below, d, p)])
+
+                if paired:
+                    pl.when(place == 0)(lambda: add_blocks(at(mine, d, p), parts))
+                going_up(d, p).start()
+
+            @pl.when(place > k)
+            def _(d=k, p=p):
+                parts = here(d, p)
+
+                @pl.when(place < size - 1)
+                def _():
+                    going_down(d, p).wait_recv()
+                    add_blocks(at(mine, d, p), parts + [at(above, d, p)])
+
+                if paired:
+                    pl.when(place == size - 1)(lambda: add_blocks(at(mine, d, p), parts))
+                going_down(d, p).start()
+
+    for d in range(size):
+
+        @pl.when(place == d)
+        def _(d=d):
+            for p in range(pieces):
+                parts = here(d, p)
+                if d > 0:
+                    going_up(d, p).wait_recv()
+                    parts = parts + [at(below, d, p)]
+                if d < size - 1:
+                    going_down(d, p).wait_recv()
+                    parts = parts + [at(above, d, p)]
+                add_blocks(o_ref.at[pl.ds(p * part, part)], parts)
+
+    for d, p in every:
+        if d > 0:
+            pl.when(place < d)(lambda d=d, p=p: going_up(d, p).wait_send())
+        if d < size - 1:
+            pl.when(place > d)(lambda d=d, p=p: going_down(d, p).wait_send())
+        if paired:
+            to_mate(d, p).wait_send()
+
+
+def scatter(x, size, paired, ident):
+    copies = size * 2 if paired else size
+    rows = x.shape[0] // copies
+    pieces = pieces_of(rows, x.shape[1])
+    dma = pltpu.SemaphoreType.DMA
+    slots = pltpu.VMEM((size, rows, x.shape[1]), x.dtype)
+    one = pltpu.VMEM((1, 32, 128), x.dtype)
+    chain = slots if size > 1 else one
+    return pl.pallas_call(
+        functools.partial(scatter_kernel, size, paired, pieces),
+        in_specs=[ANY],
+        out_specs=IN_VMEM,
+        out_shape=jax.ShapeDtypeStruct((rows, x.shape[1]), jnp.float32),
+        scratch_shapes=[slots, slots if paired else one, chain, chain] + [dma((size, pieces))] * 7,
+        compiler_params=pltpu.CompilerParams(collective_id=ident, has_side_effects=True, vmem_limit_bytes=60000000),
+        cost_estimate=pl.CostEstimate(flops=0, bytes_accessed=30 * x.size, transcendentals=0),
+        name="scatter",
+    )(x)
+
+
+def front_kernel(
+    size, groups, a_ref, b_ref, g_ref, u_ref, d_ref, fa_ref, fb_ref, og_ref, ou_ref, od_ref,
+    local_sem, up_send, up_recv, down_send, down_recv, far_send, far_recv, swap_send, swap_recv,
+):
+    place, group = lax.axis_index("ctx"), lax.axis_index("dp")
+    rows, width = a_ref.shape[0], og_ref.shape[1]
+    wholes, owns = (fa_ref, fb_ref), (a_ref, b_ref)
+    parts, slices = (g_ref, u_ref, d_ref), (og_ref, ou_ref, od_ref)
+    barrier = pltpu.get_barrier_semaphore()
+    for step in range(1, size):
+        greet(barrier, {"ctx": lax.rem(place + step, size)})
+    for step in range(1, groups):
+        greet(barrier, {"dp": lax.rem(group + step, groups)})
+    pl.semaphore_wait(barrier, size + groups - 2)
+
+    def chunk(which, in_group, rank):
+        return wholes[which].at[pl.ds(pl.multiple_of((in_group * size + rank) * rows, rows), rows)]
+
+    def source(which, rank, k):
+        return owns[which] if k == 0 else chunk(which, group, rank)
+
+    def going_up(which, k):
+        return remote(
+            source(which, place - k, k), chunk(which, group, place - k),
+            up_send.at[which, k], up_recv.at[which, k], {"ctx": place + 1},
+        )
+
+    def going_down(which, k):
+        return remote(
+            source(which, place + k, k), chunk(which, group, place + k),
+            down_send.at[which, k], down_recv.at[which, k], {"ctx": place - 1},
+        )
+
+    def across(which, rank, step, k):
+        return remote(
+            source(which, rank, k), chunk(which, group, rank),
+            far_send.at[which, rank, step], far_recv.at[which, rank, step], {"dp": lax.rem(group + step, groups)},
+        )
+
+    def from_across(which, rank, step):
+        there = chunk(which, lax.rem(group - step + groups, groups), rank)
+        return remote(there, there, far_send.at[which, rank, step], far_recv.at[which, rank, step], {"dp": lax.rem(group + step, groups)})
+
+    def columns(which, rank):
+        return parts[which].at[:, pl.ds(pl.multiple_of(rank * width, 128), width)]
+
+    def swap(which, step):
+        return remote(
+            columns(which, lax.rem(place + step, size)),
+            slices[which].at[pl.ds(pl.multiple_of(place * rows, rows), rows)],
+            swap_send.at[which, step], swap_recv.at[which, step], {"ctx": lax.rem(place + step, size)},
+        )
+
+    def swapped(which, step):
+        there = slices[which].at[pl.ds(pl.multiple_of(lax.rem(place - step + size, size) * rows, rows), rows)]
+        return remote(there, there, swap_send.at[which, step], swap_recv.at[which, step], {"ctx": lax.rem(place + step, size)})
+
+    locals_ = [pltpu.make_async_copy(owns[w], chunk(w, group, place), local_sem.at[w]) for w in range(2)]
+    locals_ += [
+        pltpu.make_async_copy(
+            columns(w, place), slices[w].at[pl.ds(pl.multiple_of(place * rows, rows), rows)], local_sem.at[2 + w]
+        )
+        for w in range(3)
+    ]
+    for w in range(2):
+        pl.when(place < size - 1)(lambda w=w: going_up(w, 0).start())
+        pl.when(place > 0)(lambda w=w: going_down(w, 0).start())
+        for step in range(1, groups):
+            across(w, place, step, 0).start()
+    for copy in locals_:
+        copy.start()
+    for k in range(size - 1):
+        for w in range(2):
+
+            @pl.when(place - 1 - k >= 0)
+            def _(k=k, w=w):
+                there = chunk(w, group, place - 1 - k)
+                remote(there, there, up_send.at[w, k], up_recv.at[w, k], {"ctx": place - 1}).wait_recv()
+                if k + 1 < size - 1:
+                    pl.when(place < size - 1)(lambda: going_up(w, k + 1).start())
+                for step in range(1, groups):
+                    across(w, place - 1 - k, step, 1).start()
+
+            @pl.when(place + 1 + k <= size - 1)
+            def _(k=k, w=w):
+                there = chunk(w, group, place + 1 + k)
+                remote(there, there, down_send.at[w, k], down_recv.at[w, k], {"ctx": place + 1}).wait_recv()
+                if k + 1 < size - 1:
+                    pl.when(place > 0)(lambda: going_down(w, k + 1).start())
+                for step in range(1, groups):
+                    across(w, place + 1 + k, step, 1).start()
+
+    for w in range(3):
+        for step in range(1, size):
+            swap(w, step).start()
+    for rank in range(size):
+        for w in range(2):
+            for step in range(1, groups):
+                from_across(w, rank, step).wait_recv()
+    for w in range(3):
+        for step in range(1, size):
+            swapped(w, step).wait_recv()
+    for copy in locals_:
+        copy.wait()
+    for w in range(2):
+        for k in range(size - 1):
+            pl.when((place < size - 1) & (place - k >= 0))(lambda k=k, w=w: going_up(w, k).wait_send())
+            pl.when((place > 0) & (place + k <= size - 1))(lambda k=k, w=w: going_down(w, k).wait_send())
+        for rank in range(size):
+            for step in range(1, groups):
+                across(w, rank, step, 1).wait_send()
+    for w in range(3):
+        for step in range(1, size):
+            swap(w, step).wait_send()
+
+
+def front(a, b, parts, width, ident):
+    size, groups = lax.axis_size("ctx"), lax.axis_size("dp")
+    rows = a.shape[0]
+    dma = pltpu.SemaphoreType.DMA
+    slices = jax.ShapeDtypeStruct((size * rows, width), a.dtype)
+    return pl.pallas_call(
+        functools.partial(front_kernel, size, groups),
+        in_specs=[IN_VMEM] * 5,
+        out_specs=[ANY] * 5,
+        out_shape=[jax.ShapeDtypeStruct((groups * size * rows, x.shape[1]), x.dtype) for x in (a, b)] + [slices] * 3,
+        scratch_shapes=[dma((5,))] + [dma((2, size))] * 4 + [dma((2, size, groups))] * 2 + [dma((3, size))] * 2,
+        compiler_params=pltpu.CompilerParams(collective_id=ident, has_side_effects=True),
+        cost_estimate=pl.CostEstimate(flops=0, bytes_accessed=200000000, transcendentals=0),
+        name="front",
+    )(a, b, *parts)
 
 
 def mask_into(bias_ref, first, seg_ref, place_ref):
@@ -252,19 +640,16 @@
     gain_two = gain_mlp.astype(jnp.float32)
     scale_attn = lax.rsqrt(jnp.mean(inputs * inputs, axis=1, keepdims=True) + EPS)
     normed_attn = inputs * scale_attn
-    normed_rows = lax.all_gather(
-        (normed_attn * gain_one).astype(jnp.bfloat16), "tensor", axis=0, tiled=True
-    )
-    full_qkv = lax.all_gather(
+    extra = ((0, 0), (0, ctx_size * slice_width - hidden_width))
+    full_qkv, full_out, *slices = front(
         jnp.concatenate([query_weight, key_weight, value_weight], axis=1),
-        ("dp", "ctx"),
-        axis=0,
-        tiled=True,
-    )
-    full_out = lax.all_gather(out_weight.T, ("dp", "ctx"), axis=0, tiled=True)
-    full_gate = to_columns(gate_weight, slice_width)
-    full_up = to_columns(up_weight, slice_width)
-    full_down = to_columns(down_weight.T, slice_width)
+        out_weight.T,
+        [jnp.pad(w, extra) for w in (gate_weight, up_weight, down_weight.T)],
+        slice_width,
+        1,
+    )
+    full_gate, full_up, full_down = [lax.all_gather(w, "dp", axis=0, tiled=True) for w in slices]
+    normed_rows = gather((normed_attn * gain_one).astype(jnp.bfloat16), 1, True, 2)
     valid_count = jnp.sum(valid_mask.astype(jnp.float32))
     counts = [valid_count]
     dp_size = lax.axis_size("dp")
@@ -294,7 +679,7 @@
     )
     queries = rotated[:, :q_width]
     own_kv = jnp.concatenate([rotated[:, q_width:], qkv_pre[:, turned:].astype(jnp.bfloat16)], axis=1)
-    all_kv = lax.all_gather(own_kv, "ctx", axis=0, tiled=True)
+    all_kv = gather(own_kv, ctx_size, False, 3)
 
     key_index = jnp.arange(seq_len, dtype=jnp.int32)
     key_place = jnp.where(valid_mask > 0, key_index, -1)[:, None]
@@ -309,23 +694,17 @@
         query = queries[:, c * group * HEAD : (c + 1) * group * HEAD]
         kept.append((query, key, value) + tuple(forward(first, doc_start, key_place, query, key, value.T)))
     heads_out = jnp.concatenate([k[3] for k in kept], axis=1)
-    attention = lax.psum_scatter(
-        matmul_nt(heads_out, full_out), "tensor", scatter_dimension=0, tiled=True
-    )
+    attention = scatter(matmul_nt(heads_out, full_out), 1, True, 4)
     residual_mid = inputs + attention
     scale_mlp = lax.rsqrt(jnp.mean(residual_mid * residual_mid, axis=1, keepdims=True) + EPS)
     normed_mlp = residual_mid * scale_mlp
-    mlp_rows = lax.all_gather(
-        (normed_mlp * gain_two).astype(jnp.bfloat16), ("ctx", "tensor"), axis=0, tiled=True
-    )
+    mlp_rows = gather((normed_mlp * gain_two).astype(jnp.bfloat16), ctx_size, True, 5)
     gate_act = matmul(mlp_rows, full_gate)
     up_act = matmul(mlp_rows, full_up)
     sigmoid = jax.nn.sigmoid(gate_act)
     silu_gate = gate_act * sigmoid
     hidden = (silu_gate * up_act).astype(jnp.bfloat16)
-    branch = lax.psum_scatter(
-        matmul_nt(hidden, full_down).astype(jnp.bfloat16), ("ctx", "tensor"), scatter_dimension=0, tiled=True
-    ).astype(jnp.float32)
+    branch = scatter(matmul_nt(hidden, full_down).astype(jnp.bfloat16), ctx_size, True, 6)
     layer_result = residual_mid + branch
     valid_own = lax.dynamic_slice_in_dim(valid_mask, own_first, own_rows).astype(jnp.float32)
     difference = layer_result - teacher.astype(jnp.float32)
@@ -333,7 +712,7 @@
     grad_result = cotangent.astype(jnp.float32) + 2.0 * valid_own[:, None] * difference / (
         valid_count * D
     )
-    grad_branch = lax.all_gather(grad_result.astype(jnp.bfloat16), ("ctx", "tensor"), axis=0, tiled=True)
+    grad_branch = gather(grad_result.astype(jnp.bfloat16), ctx_size, True, 5)
     grad_hidden = matmul(grad_branch, full_down)
     grad_gate_act = (grad_hidden * up_act * sigmoid * (1.0 + gate_act * (1.0 - sigmoid))).astype(
         jnp.bfloat16
@@ -352,15 +731,15 @@
     shard_up = to_rows(matmul_tn(mlp_rows, grad_up_act).astype(jnp.bfloat16), hidden_width)
     grad_gain_mlp = jnp.sum(grad_mlp_rows * normed_mlp, axis=0)
     grad_mid = grad_result + norm_back(grad_mlp_rows, normed_mlp, scale_mlp, gain_two)
-    grad_attn_rows = lax.all_gather(grad_mid.astype(jnp.bfloat16), "tensor", axis=0, tiled=True)
+    grad_attn_rows = gather(grad_mid.astype(jnp.bfloat16), 1, True, 2)
     grad_heads = matmul(grad_attn_rows, full_out).astype(jnp.bfloat16)
     grad_out = matmul_tn(grad_attn_rows, heads_out).astype(jnp.bfloat16)
 
-    def scatter(grad):
+    def to_owner(grad):
         grad = lax.psum_scatter(grad, "dp", scatter_dimension=0, tiled=True)
         return lax.psum_scatter(grad, "ctx", scatter_dimension=0, tiled=True).astype(jnp.float32)
 
-    shard_out = scatter(grad_out).T
+    shard_out = to_owner(grad_out).T
     query_grads, key_grads, value_grads = [], [], []
     for c in range(kv_local):
         query, key, value, _, log_total = kept[c]
@@ -372,21 +751,19 @@
         key_grads.append(grad_kv[:, :HEAD])
         value_grads.append(grad_kv[:, HEAD:])
     grad_kv = grad_kv if kv_local == 1 else jnp.concatenate(key_grads + value_grads, axis=1)
-    grad_kv = lax.psum_scatter(grad_kv, "ctx", scatter_dimension=0, tiled=True)
-    back = jnp.concatenate(query_grads + [grad_kv[:, :kv_width].astype(jnp.float32)], axis=1)
+    grad_kv = scatter(grad_kv, ctx_size, False, 7)
+    back = jnp.concatenate(query_grads + [grad_kv[:, :kv_width]], axis=1)
     grad_pre = jnp.concatenate(
         [
             rotate(back.reshape(shard_rows, turned // HEAD, HEAD), cosine, -sine_table)
             .reshape(shard_rows, turned)
             .astype(jnp.bfloat16),
-            grad_kv[:, kv_width:],
+            grad_kv[:, kv_width:].astype(jnp.bfloat16),
         ],
         axis=1,
     )
-    shard_qkv = scatter(matmul_tn(normed_rows, grad_pre).astype(jnp.bfloat16))
-    grad_normed = lax.psum_scatter(
-        matmul_nt(grad_pre, full_qkv).astype(jnp.bfloat16), "tensor", scatter_dimension=0, tiled=True
-    ).astype(jnp.float32)
+    shard_qkv = to_owner(matmul_tn(normed_rows, grad_pre).astype(jnp.bfloat16))
+    grad_normed = scatter(matmul_nt(grad_pre, full_qkv), 1, True, 4)
     grad_gain_attn = jnp.sum(grad_normed * normed_attn, axis=0)
     grad_input = grad_mid + norm_back(grad_normed, normed_attn, scale_attn, gain_one)
     bias_sum = jnp.sum(grad_pre.astype(jnp.float32), axis=0)

time: 1090 us -> 831 us (0.76)
  waiting for transfers between devices: 731 us -> 152 us
  Pallas kernels: 45.5 us -> 379 us
  starting transfers between devices: 51.8 us -> 37.7 us
    all_gather x10 -> x3, waiting for transfers between devices: 350 us -> 0.02 us  [per_device(): lax.all_gather(w, 'dp', axis=0, tiled=True)]
    pallas_call x0 -> x10, Pallas kernels: none -> 333 us  [the longest x5 155 us: gather(): pl.pallas_call(functools.partial(gather_kernel, size, paired, pieces), in...]
    reduce_scatter x8 -> x4, waiting for transfers between devices: 161 us -> 44.5 us  [the longest x2 35 us: to_owner(): lax.psum_scatter(grad, 'ctx', scatter_dimension=0, tiled=True)]
    ppermute x18 -> x9, waiting for transfers between devices: 42.6 us -> 0.03 us  [exchange(): lax.ppermute(going, axis, [(i, (i + step) % size) for i in range(size)])]
    reduce_scatter x1, waiting for transfers between devices: 68.3 us -> 27.5 us  [per_device(): lax.psum_scatter((matmul_nt(grad_gate_act, full_gate) + matmul_nt(grad_up...]
    reduce_scatter x3, waiting for transfers between devices: 102 us -> 72.2 us  [to_rows(): summed = lax.psum_scatter(grad, 'dp', scatter_dimension=0, tiled=True)]
    ppermute x18 -> x9, starting transfers between devices: 37.2 us -> 27.9 us  [exchange(): lax.ppermute(going, axis, [(i, (i + step) % size) for i in range(size)])]
  transfers between devices with their start and end apart: 48 -> 28, of which waited for: 32 -> 10; matrix products, arithmetic and copies ran while one was open for 12% -> 20% of each run, Pallas kernels for 2% -> 21%
where the time goes in v2:
time: 831 us; the launch traced here: 822 us
  Pallas kernels  379 us (46%)
  waiting for transfers between devices  152 us (18%)
  matrix products  151 us (18%)
  local copies, waits for them, and re-layouts  49.2 us (6%)
  starting transfers between devices  37.7 us (5%)
  other arithmetic  33.9 us (4%)
  between operations  19.5 us (2%)
    pallas_call x5, Pallas kernels, gather(): pl.pallas_call(functools.partial(gather_kernel, size, paired, pieces), in...  155 us
    pallas_call x4, Pallas kernels, scatter(): pl.pallas_call(functools.partial(scatter_kernel, size, paired, pieces), i...  98.4 us
    pallas_call x1, Pallas kernels, front(): pl.pallas_call(functools.partial(front_kernel, size, groups), in_specs=[I...  79.8 us
    reduce_scatter x3, waiting for transfers between devices, to_rows(): summed = lax.psum_scatter(grad, 'dp', scatter_dimension=0, tiled=True)  72.2 us
    dot_general x5, matrix products, matmul(): return jnp.dot(first_op, second_op, preferred_element_type=jnp.float32)  57.1 us
    dot_general x5, matrix products, matmul_tn(): lax.dot_general(first_op, second_op, (((0,), (0,)), ((), ())), preferred_...  47.5 us
    dot_general x5, matrix products, matmul_nt(): lax.dot_general(first_op, second_op, (((1,), (1,)), ((), ())), preferred_...  46.5 us
    reduce_scatter x2, waiting for transfers between devices, to_owner(): lax.psum_scatter(grad, 'ctx', scatter_dimension=0, tiled=True)  35 us
  transfers between devices with their start and end apart: 28, of which 10 were waited for; matrix products, arithmetic and copies ran while one was open for 20% of the time, Pallas kernels for 21%

profile of v2, /device:TPU:0, one launch (start us, length us, event | category | flops | bytes accessed | tf_op | source)
XLA Modules:
  0.0 822.2 jit_solution(8544658615656082730)
XLA Ops:
  7.2 2.2 pad.13.g_ref
  12.2 79.8 %front.1 = (bf16[1536,1024]{1,0:T(8,128)(2,1)}, bf16[1536,768]{1,0:T(8,128)(2,1)}, bf16[384,1152]{1,0:T(8,128)(2,1)}, bf16[384,1152]{1,0:T(8,128)(2,1)}, bf16[384,1152]{1,0:T(8,128)(2,1)}) custom-call(bf16[96,1024]{1,0:T(8,128)(2,1)} %pad_maximum_fusion.7.a_ref, bf16[96,768]{1,0:T(8,128)(2,1)} %bitcast.105, bf16[96,4608]{1,0:T(8,128)(2,1)} %pad.13.g_ref, ...), custom_call_target="tpu_custom_call" | custom-call | bytes 200000000 | tf_op jit(solution)/shard_map/front/pallas_call | solution.py:484
  94.1 2.9 collective-permute-start
  102.5 4.2 gather.5
  106.8 4.2 convolution_add_fusion
  112.4 2.8 copy.37
  117.8 1.8 subtract_convert_fusion.1
  120.6 25.6 %gather.6 = bf16[2048,256]{1,0:T(8,128)(2,1)} custom-call(bf16[512,256]{1,0:T(8,128)(2,1)} %pad_maximum_fusion.6.x_ref), custom_call_target="tpu_custom_call" | custom-call | bytes 15728640 | tf_op jit(solution)/shard_map/gather/pallas_call | solution.py:219
  146.3 2.4 fusion.26
  152.2 19.3 %attend.1 = (bf16[512,768]{1,0:T(8,128)(2,1)}, f32[6,1,512]{2,1,0:T(1,128)}) custom-call(s32[1]{0:T(128)} %bitcast.first_ref, s32[1,512]{1,0:T(1,128)} %bitcast.108, s32[2048,1]{1,0:T(8,128)} %copy.41.place_ref, bf16[512,768]{1,0:T(8,128)(2,1)} %copy.48.q_ref, bf16[2048,128]{1,0:T(8,128)(2,1)} %get-tuple-element.65.k_ref, bf16[128,2048]{1,0:T(8,128)(2,1)} %copy.43.vt_ref), custom_call_target="tpu_custom_call" | custom-call | flops 3221225472 | bytes 1572864 | tf_op jit(solution)/shard_map/attend/pallas_call | solution.py:695
  171.5 4.2 fusion.28.x_ref
  175.7 5.1 scatter.11
  180.8 1.7 multiply_reduce_fusion
  184.3 57.1 %gather.7 = bf16[2048,1536]{1,0:T(8,128)(2,1)} custom-call(bf16[256,1536]{1,0:T(8,128)(2,1)} %multiply_convert_fusion.3.x_ref), custom_call_target="tpu_custom_call" | custom-call | bytes 94371840 | tf_op jit(solution)/shard_map/gather/pallas_call | solution.py:219
  245.6 13.6 %fusion.29 = f32[2048,1152]{1,0:T(8,128)} fusion(bf16[2048,1536]{1,0:T(8,128)(2,1)} %gather.7, bf16[1536,1152]{1,0:T(8,128)(2,1)} %all-gather.4.cloned.1.call-done), kind=kOutput, calls=%fused_computation.120 | convolution fusion | flops 7247757312 | bytes 19267584 | tf_op jit(solution)/shard_map/dot_general | solution.py:43
  259.2 15.7 %multiply_convert_fusion.2 = (bf16[2048,1152]{1,0:T(8,128)(2,1)}, f32[2048,1152]{1,0:T(8,128)}) fusion(f32[2048,1152]{1,0:T(8,128)} %fusion.29, bf16[2048,1536]{1,0:T(8,128)(2,1)} %gather.7, bf16[1536,1152]{1,0:T(8,128)(2,1)} %all-gather.6.cloned.1.call-done), kind=kOutput, calls=%fused_computation.3 | convolution fusion | flops 7261913088 | bytes 33423360 | tf_op jit(solution)/shard_map/dot_general | solution.py:43
  275.0 13.2 %convolution_convert_fusion.3.x_ref = bf16[2048,1536]{1,0:T(8,128)(2,1)} fusion(bf16[2048,1152]{1,0:T(8,128)(2,1)} %get-tuple-element.85, bf16[1536,1152]{1,0:T(8,128)(2,1)} %all-gather.8.cloned.1.call-done), kind=kOutput, calls=%fused_computation.9 | convolution fusion | flops 7250903040 | bytes 14548992 | tf_op jit(solution)/shard_map/dot_general | solution.py:53
  288.1 58.7 %scatter.12 = f32[256,1536]{1,0:T(8,128)} custom-call(bf16[2048,1536]{1,0:T(8,128)(2,1)} %convolution_convert_fusion.3.x_ref), custom_call_target="tpu_custom_call" | custom-call | bytes 94371840 | tf_op jit(solution)/shard_map/scatter/pallas_call | solution.py:351
  346.9 3.0 fusion.23.x_ref
  349.8 63.5 %gather.8 = bf16[2048,1536]{1,0:T(8,128)(2,1)} custom-call(bf16[256,1536]{1,0:T(8,128)(2,1)} %fusion.23.x_ref), custom_call_target="tpu_custom_call" | custom-call | bytes 94371840 | tf_op jit(solution)/shard_map/gather/pallas_call | solution.py:219
  413.4 19.7 %multiply_convert_fusion = (bf16[2048,1152]{1,0:T(8,128)(2,1)}, bf16[2048,1152]{1,0:T(8,128)(2,1)}) fusion(f32[2048,1152]{1,0:T(8,128)} %fusion.29, f32[2048,1152]{1,0:T(8,128)} %get-tuple-element.86, bf16[2048,1536]{1,0:T(8,128)(2,1)} %gather.8, bf16[1536,1152]{1,0:T(8,128)(2,1)} %all-gather.8.cloned.1.call-done), kind=kOutput, calls=%fused_computation.1 | convolution fusion | flops 7278428160 | bytes 38141952 | tf_op jit(solution)/shard_map/dot_general | solution.py:43
  433.0 13.1 %fusion.30 = f32[2048,1536]{1,0:T(8,128)} fusion(bf16[2048,1152]{1,0:T(8,128)(2,1)} %get-tuple-element.57, bf16[1536,1152]{1,0:T(8,128)(2,1)S(1)} %copy-done.36), kind=kOutput, calls=%fused_computation.121 | convolution fusion | flops 7247757312 | bytes 20840448 | tf_op jit(solution)/shard_map/dot_general | solution.py:53
  446.1 12.6 %add_convert_fusion = bf16[2048,1536]{1,0:T(8,128)(2,1)} fusion(f32[2048,1536]{1,0:T(8,128)} %fusion.30, bf16[2048,1152]{1,0:T(8,128)(2,1)S(1)} %copy-done.43, bf16[1536,1152]{1,0:T(8,128)(2,1)S(1)} %copy-done.37), kind=kOutput, calls=%fused_computation | convolution fusion | flops 7254048768 | bytes 27131904 | tf_op jit(solution)/shard_map/dot_general | solution.py:53
  458.9 13.1 %convolution_convert_fusion = bf16[1536,1152]{1,0:T(8,128)(2,1)} fusion(bf16[2048,1536]{1,0:T(8,128)(2,1)} %gather.8, bf16[2048,1152]{1,0:T(8,128)(2,1)} %get-tuple-element.85), kind=kOutput, calls=%fused_computation.6 | convolution fusion | flops 7249526784 | bytes 14548992 | tf_op jit(solution)/shard_map/dot_general | solution.py:47
  472.1 13.2 %convolution_convert_fusion.1 = bf16[1536,1152]{1,0:T(8,128)(2,1)} fusion(bf16[2048,1536]{1,0:T(8,128)(2,1)} %gather.7, bf16[2048,1152]{1,0:T(8,128)(2,1)} %get-tuple-element.56), kind=kOutput, calls=%fused_computation.7 | convolution fusion | flops 7249526784 | bytes 14548992 | tf_op jit(solution)/shard_map/dot_general | solution.py:47
  485.6 13.4 %convolution_convert_fusion.2 = bf16[1536,1152]{1,0:T(8,128)(2,1)} fusion(bf16[2048,1536]{1,0:T(8,128)(2,1)} %gather.7, bf16[2048,1152]{1,0:T(8,128)(2,1)} %get-tuple-element.57), kind=kOutput, calls=%fused_computation.8 | convolution fusion | flops 7249526784 | bytes 14548992 | tf_op jit(solution)/shard_map/dot_general | solution.py:47
  499.1 27.5 %reduce-scatter.9.cloned.1.call-done = bf16[256,1536]{1,0:T(8,128)(2,1)} async-done(((bf16[2048,1536]{1,0:T(8,128)(2,1)}), bf16[256,1536]{1,0:T(8,128)(2,1)}) %reduce-scatter.9.cloned.1.call-update) | async-done | bytes 786448 | tf_op jit(solution)/shard_map/reduce_scatter | solution.py:721
  526.6 3.2 fusion.10
  529.9 2.5 fusion.24
  532.3 4.1 gather.9
  536.5 4.2 convolution_convert_fusion.5
  542.8 32.4 %reduce-scatter.23.cloned.1.call-done = bf16[384,1152]{1,0:T(8,128)(2,1)} async-done(((bf16[1536,1152]{1,0:T(8,128)(2,1)}), bf16[384,1152]{1,0:T(8,128)(2,1)}) %reduce-scatter.23.cloned.1.call-update) | async-done | bytes 884752 | tf_op jit(solution)/shard_map/reduce_scatter | solution.py:76
  575.2 2.0 dynamic-slice_bitcast_fusion
  578.7 2.4 collective-permute-start.15
  581.1 1.6 collective-permute-start.16
  583.7 1.7 bitcast_dynamic-update-slice_fusion
  585.4 39.8 %reduce-scatter.21.cloned.1.call-done = bf16[384,1152]{1,0:T(8,128)(2,1)} async-done(((bf16[1536,1152]{1,0:T(8,128)(2,1)}), bf16[384,1152]{1,0:T(8,128)(2,1)}) %reduce-scatter.21.cloned.1.call-update) | async-done | bytes 884752 | tf_op jit(solution)/shard_map/reduce_scatter | solution.py:76
  625.3 2.1 dynamic-slice_bitcast_fusion.3
  627.3 4.0 convolution_convert_fusion.6.do_ref
  631.3 26.5 %attend_back.1 = (f32[512,768]{1,0:T(8,128)}, bf16[2048,256]{1,0:T(8,128)(2,1)}) custom-call(s32[1]{0:T(128)} %bitcast.first_ref, s32[1,512]{1,0:T(1,128)} %bitcast.109, s32[2048,1]{1,0:T(8,128)} %copy.41.place_ref, bf16[512,768]{1,0:T(8,128)(2,1)} %copy.48.q_ref, bf16[512,768]{1,0:T(8,128)(2,1)} %convolution_convert_fusion.6.do_ref, ...), custom_call_target="tpu_custom_call" | custom-call | flops 8053063680 | bytes 3145728 | tf_op jit(solution)/shard_map/attend_back/pallas_call | solution.py:747
  657.8 29.5 %scatter.13 = f32[512,256]{1,0:T(8,128)} custom-call(bf16[2048,256]{1,0:T(8,128)(2,1)} %get-tuple-element.44.x_ref), custom_call_target="tpu_custom_call" | custom-call | bytes 15728640 | tf_op jit(solution)/shard_map/scatter/pallas_call | solution.py:351
  689.4 1.8 copy.46
  691.3 2.0 subtract_convert_fusion
  693.4 3.5 convolution_convert_fusion.4
  697.9 1.6 bitcast_dynamic-update-slice_fusion.1
  701.2 2.0 dynamic-slice_bitcast_fusion.6
  704.2 3.0 collective-permute-start.13
  707.2 1.7 constant_dynamic-update-slice_fusion
  708.9 2.9 collective-permute-start.8
  712.5 6.9 collective-permute-start.9
  719.4 1.7 constant_dynamic-update-slice_fusion.8
  721.1 8.0 collective-permute-start.10
  731.3 2.6 convert_bitcast_fusion
  733.9 2.5 slice_convert_fusion
  736.3 3.6 fusion.19.x_ref
  739.9 5.1 scatter.14
  745.3 2.0 fusion.13
  750.6 2.8 collective-permute-done.4
  753.5 9.5 %reduce-scatter.11.cloned.1.call-done = bf16[384,1024]{1,0:T(8,128)(2,1)} async-done(((bf16[1536,1024]{1,0:T(8,128)(2,1)}), bf16[384,1024]{1,0:T(8,128)(2,1)}) %reduce-scatter.11.cloned.1.call-update) | async-done | bytes 786448 | tf_op jit(solution)/shard_map/reduce_scatter | solution.py:739
  765.8 2.4 collective-permute-done.6
  774.4 12.9 %reduce-scatter.17.cloned.1.call-done = bf16[96,768]{1,0:T(8,128)(2,1)} async-done(((bf16[384,768]{1,0:T(8,128)(2,1)}), bf16[96,768]{1,0:T(8,128)(2,1)}) %reduce-scatter.17.cloned.1.call-update) | async-done | bytes 147472 | tf_op jit(solution)/shard_map/reduce_scatter | solution.py:740
  787.3 1.6 convert_bitcast_fusion.1
  788.9 22.1 %reduce-scatter.13.cloned.1.call-done = bf16[96,1024]{1,0:T(8,128)(2,1)} async-done(((bf16[384,1024]{1,0:T(8,128)(2,1)}), bf16[96,1024]{1,0:T(8,128)(2,1)}) %reduce-scatter.13.cloned.1.call-update) | async-done | bytes 196624 | tf_op jit(solution)/shard_map/reduce_scatter | solution.py:740
  811.1 1.6 slice.166
  (218 shorter events, 49.4 us)
Async XLA Ops:
  7.2 2.3 copy-start.16
  7.2 3.3 copy-start.17
  7.2 238.4 %all-gather.4.cloned.1.call-start = ((), (), s32[]{:S(2)}) async-start(), calls=%async_computation.8 | async-start | bytes 4423680 | tf_op jit(solution)/shard_map/all_gather | solution.py:651
  9.5 2.0 copy-start.26
  9.5 2.0 copy-start.27
  12.2 80.7 %copy-start.25 = (s32[2048]{0:T(1024)S(1)}, s32[2048]{0:T(1024)}, u32[]{:S(2)}) copy-start(s32[2048]{0:T(1024)} %param.25) | copy-start | bytes 24580
  92.0 8.1 copy-start.40
  92.0 8.1 copy-start.41
  92.0 8.2 copy-start.33
  92.0 8.2 copy-start.1
  92.1 167.2 %all-gather.6.cloned.1.call-start = ((), (), s32[]{:S(2)}) async-start(), calls=%async_computation.9 | async-start | bytes 4423680 | tf_op jit(solution)/shard_map/all_gather | solution.py:651
  92.8 182.1 %all-gather.8.cloned.1.call-start = ((), (), s32[]{:S(2)}) async-start(), calls=%async_computation.10 | async-start | bytes 4423680 | tf_op jit(solution)/shard_map/all_gather | solution.py:651
  94.1 147.3 %collective-permute-start = (f32[8,128]{1,0:T(8,128)S(1)}, f32[8,128]{1,0:T(8,128)S(1)}, u32[]{:S(2)}, u32[]{:S(2)}) collective-permute-start(f32[8,128]{1,0:T(8,128)S(1)} %broadcast_in_dim.15), channel_id=1, source_target_pairs={{0,8},{8,16},{16,24},{24,0},{1,9},{9,17},{17,25},{25,1},{2,10},{10... | collective-permute-start | bytes 12296 | tf_op jit(solution)/shard_map/ppermute | solution.py:658
  97.0 146.2 %collective-permute-start.1 = (f32[8,128]{1,0:T(8,128)S(1)}, f32[8,128]{1,0:T(8,128)S(1)}, u32[]{:S(2)}, u32[]{:S(2)}) collective-permute-start(f32[8,128]{1,0:T(8,128)S(1)} %broadcast_in_dim.15), channel_id=1, source_target_pairs={{0,16},{8,24},{16,0},{24,8},{1,17},{9,25},{17,1},{25,9},{2,18},{10... | collective-permute-start | bytes 12296 | tf_op jit(solution)/shard_map/ppermute | solution.py:658
  98.5 145.9 %collective-permute-start.2 = (f32[8,128]{1,0:T(8,128)S(1)}, f32[8,128]{1,0:T(8,128)S(1)}, u32[]{:S(2)}, u32[]{:S(2)}) collective-permute-start(f32[8,128]{1,0:T(8,128)S(1)} %broadcast_in_dim.15), channel_id=1, source_target_pairs={{0,24},{8,0},{16,8},{24,16},{1,25},{9,1},{17,9},{25,17},{2,26},{10... | collective-permute-start | bytes 12296 | tf_op jit(solution)/shard_map/ppermute | solution.py:658
  100.0 426.6 %reduce-scatter.9.cloned.1.call-start = ((), (), s32[]{:S(2)}) async-start(), calls=%async_computation.11 | async-start | bytes 7077888 | tf_op jit(solution)/shard_map/reduce_scatter | solution.py:721
  100.5 6.2 copy-start.35
  152.2 19.3 %copy-start.39 = (bf16[1536,768]{1,0:T(8,128)(2,1)S(1)}, bf16[1536,768]{1,0:T(8,128)(2,1)}, u32[]{:S(2)}) copy-start(bf16[1536,768]{1,0:T(8,128)(2,1)} %get-tuple-element.38) | copy-start | bytes 7077892
  182.5 58.9 %copy-start.28 = (f32[256]{0:T(256)}, f32[256]{0:T(256)S(1)}, u32[]{:S(2)}) copy-start(f32[256]{0:T(256)S(1)} %add_rsqrt_fusion) | copy-start | bytes 3076
  182.5 58.9 %copy-start.23 = (f32[1536]{0:T(1024)}, f32[1536]{0:T(1024)S(1)}, u32[]{:S(2)}) copy-start(f32[1536]{0:T(1024)S(1)} %convert_element_type.117) | copy-start | bytes 18436
  288.1 58.7 %copy-start.4 = (bf16[256,1536]{1,0:T(8,128)(2,1)S(1)}, bf16[256,1536]{1,0:T(8,128)(2,1)}, u32[]{:S(2)}) copy-start(bf16[256,1536]{1,0:T(8,128)(2,1)} %param.21) | copy-start | bytes 2359300
  288.1 58.7 %copy-start.7 = (bf16[256,1536]{1,0:T(8,128)(2,1)S(1)}, bf16[256,1536]{1,0:T(8,128)(2,1)}, u32[]{:S(2)}) copy-start(bf16[256,1536]{1,0:T(8,128)(2,1)} %param.22) | copy-start | bytes 2359300
  413.3 19.7 %copy-start.36 = (bf16[1536,1152]{1,0:T(8,128)(2,1)S(1)}, bf16[1536,1152]{1,0:T(8,128)(2,1)}, u32[]{:S(2)}) copy-start(bf16[1536,1152]{1,0:T(8,128)(2,1)} %all-gather.4.cloned.1.call-done) | copy-start | bytes 10616836
  433.0 13.1 %copy-start.37 = (bf16[1536,1152]{1,0:T(8,128)(2,1)S(1)}, bf16[1536,1152]{1,0:T(8,128)(2,1)}, u32[]{:S(2)}) copy-start(bf16[1536,1152]{1,0:T(8,128)(2,1)} %all-gather.6.cloned.1.call-done) | copy-start | bytes 10616836
  433.0 13.1 %copy-start.43 = (bf16[2048,1152]{1,0:T(8,128)(2,1)S(1)}, bf16[2048,1152]{1,0:T(8,128)(2,1)}, u32[]{:S(2)}) copy-start(bf16[2048,1152]{1,0:T(8,128)(2,1)} %get-tuple-element.56) | copy-start | bytes 14155780
  458.7 116.5 %reduce-scatter.23.cloned.1.call-start = ((), (), s32[]{:S(2)}) async-start(), calls=%async_computation.18 | async-start | bytes 4423680 | tf_op jit(solution)/shard_map/reduce_scatter | solution.py:76
  472.0 153.2 %reduce-scatter.21.cloned.1.call-start = ((), (), s32[]{:S(2)}) async-start(), calls=%async_computation.17 | async-start | bytes 4423680 | tf_op jit(solution)/shard_map/reduce_scatter | solution.py:76
  485.3 215.9 %reduce-scatter.19.cloned.1.call-start = ((), (), s32[]{:S(2)}) async-start(), calls=%async_computation.16 | async-start | bytes 4423680 | tf_op jit(solution)/shard_map/reduce_scatter | solution.py:76
  499.0 27.6 %copy-start = (f32[256,1536]{1,0:T(8,128)S(1)}, f32[256,1536]{1,0:T(8,128)}, u32[]{:S(2)}) copy-start(f32[256,1536]{1,0:T(8,128)} %scatter.12) | copy-start | bytes 4718596
  499.0 27.6 %copy-start.24 = (f32[1536]{0:T(1024)S(1)}, f32[1536]{0:T(1024)}, u32[]{:S(2)}) copy-start(f32[1536]{0:T(1024)} %copy-done.23) | copy-start | bytes 18436
  499.0 27.6 %copy-start.29 = (f32[256]{0:T(256)S(1)}, f32[256]{0:T(256)}, u32[]{:S(2)}) copy-start(f32[256]{0:T(256)} %copy-done.28) | copy-start | bytes 3076
  499.0 27.6 %copy-start.32 = (f32[256]{0:T(256)S(1)}, f32[256]{0:T(256)}, u32[]{:S(2)}) copy-start(f32[256]{0:T(256)} %get-tuple-element.53) | copy-start | bytes 3076
  499.0 248.6 %reduce-scatter.15.cloned.1.call-start = ((), (), s32[]{:S(2)}) async-start(), calls=%async_computation.14 | async-start | bytes 2949120 | tf_op jit(solution)/shard_map/reduce_scatter | solution.py:739
  526.6 3.3 copy-start.5
  526.6 3.3 copy-start.8
  526.6 3.2 copy-start.9
  532.3 4.1 copy-start.42
  540.7 222.2 %reduce-scatter.11.cloned.1.call-start = ((), (), s32[]{:S(2)}) async-start(), calls=%async_computation.12 | async-start | bytes 3932160 | tf_op jit(solution)/shard_map/reduce_scatter | solution.py:739
  542.8 84.5 %copy-start.13 = (bf16[512,1536]{1,0:T(8,128)(2,1)S(1)}, bf16[512,1536]{1,0:T(8,128)(2,1)}, u32[]{:S(2)}) copy-start(bf16[512,1536]{1,0:T(8,128)(2,1)} %gather.9) | copy-start | bytes 4718596
  577.2 127.0 %collective-permute-start.14 = (bf16[96,1152]{1,0:T(8,128)(2,1)}, bf16[96,1152]{1,0:T(8,128)(2,1)}, u32[]{:S(2)}, u32[]{:S(2)}) collective-permute-start(bf16[96,1152]{1,0:T(8,128)(2,1)} %get-tuple-element.68), channel_id=1, source_target_pairs={{0,2},{2,4},{4,6},{6,0},{1,3},{3,5},{5,7},{7,1},{8,10},{10,12},{12... | collective-permute-start | bytes 663560 | tf_op jit(solution)/shard_map/ppermute | solution.py:69
  578.7 133.8 %collective-permute-start.15 = (bf16[96,1152]{1,0:T(8,128)(2,1)}, bf16[96,1152]{1,0:T(8,128)(2,1)}, u32[]{:S(2)}, u32[]{:S(2)}) collective-permute-start(bf16[96,1152]{1,0:T(8,128)(2,1)} %get-tuple-element.67), channel_id=1, source_target_pairs={{0,4},{2,6},{4,0},{6,2},{1,5},{3,7},{5,1},{7,3},{8,12},{10,14},{12... | collective-permute-start | bytes 663560 | tf_op jit(solution)/shard_map/ppermute | solution.py:69
  581.1 148.7 %collective-permute-start.16 = (bf16[96,1152]{1,0:T(8,128)(2,1)}, bf16[96,1152]{1,0:T(8,128)(2,1)S(1)}, u32[]{:S(2)}, u32[]{:S(2)}) collective-permute-start(bf16[96,1152]{1,0:T(8,128)(2,1)} %get-tuple-element.66), channel_id=1, source_target_pairs={{0,6},{2,0},{4,2},{6,4},{1,7},{3,1},{5,3},{7,5},{8,14},{10,8},{12,... | collective-permute-start | bytes 663560 | tf_op jit(solution)/shard_map/ppermute | solution.py:69
  657.8 31.5 %copy-start.11 = (f32[512,768]{1,0:T(8,128)S(1)}, f32[512,768]{1,0:T(8,128)}, u32[]{:S(2)}) copy-start(f32[512,768]{1,0:T(8,128)} %get-tuple-element.43) | copy-start | bytes 4718596
  691.3 2.1 copy-start.12
  696.9 7.3 copy-start.19
  696.9 90.4 %reduce-scatter.17.cloned.1.call-start = ((), (), s32[]{:S(2)}) async-start(), calls=%async_computation.15 | async-start | bytes 737280 | tf_op jit(solution)/shard_map/reduce_scatter | solution.py:740
  699.6 9.3 %collective-permute-start.11 = (bf16[96,1152]{1,0:T(8,128)(2,1)}, bf16[96,1152]{1,0:T(8,128)(2,1)S(1)}, u32[]{:S(2)}, u32[]{:S(2)}) collective-permute-start(bf16[96,1152]{1,0:T(8,128)(2,1)} %get-tuple-element.71), channel_id=1, source_target_pairs={{0,2},{2,4},{4,6},{6,0},{1,3},{3,5},{5,7},{7,1},{8,10},{10,12},{12... | collective-permute-start | bytes 663560 | tf_op jit(solution)/shard_map/ppermute | solution.py:69
  699.6 21.5 %collective-permute-start.12 = (bf16[96,1152]{1,0:T(8,128)(2,1)}, bf16[96,1152]{1,0:T(8,128)(2,1)S(1)}, u32[]{:S(2)}, u32[]{:S(2)}) collective-permute-start(bf16[96,1152]{1,0:T(8,128)(2,1)} %get-tuple-element.70), channel_id=1, source_target_pairs={{0,4},{2,6},{4,0},{6,2},{1,5},{3,7},{5,1},{7,3},{8,12},{10,14},{12... | collective-permute-start | bytes 663560 | tf_op jit(solution)/shard_map/ppermute | solution.py:69
  704.2 26.3 %collective-permute-start.13 = (bf16[96,1152]{1,0:T(8,128)(2,1)S(1)}, bf16[96,1152]{1,0:T(8,128)(2,1)S(1)}, u32[]{:S(2)}, u32[]{:S(2)}) collective-permute-start(bf16[96,1152]{1,0:T(8,128)(2,1)S(1)} %copy-done.19), channel_id=1, source_target_pairs={{0,6},{2,0},{4,2},{6,4},{1,7},{3,1},{5,3},{7,5},{8,14},{10,8},{12,... | collective-permute-start | bytes 663560 | tf_op jit(solution)/shard_map/ppermute | solution.py:69
  708.9 22.3 %collective-permute-start.8 = (bf16[96,1152]{1,0:T(8,128)(2,1)S(1)}, bf16[96,1152]{1,0:T(8,128)(2,1)S(1)}, u32[]{:S(2)}, u32[]{:S(2)}) collective-permute-start(bf16[96,1152]{1,0:T(8,128)(2,1)S(1)} %get-tuple-element.74), channel_id=1, source_target_pairs={{0,2},{2,4},{4,6},{6,0},{1,3},{3,5},{5,7},{7,1},{8,10},{10,12},{12... | collective-permute-start | bytes 663560 | tf_op jit(solution)/shard_map/ppermute | solution.py:69
  712.5 36.0 %collective-permute-start.9 = (bf16[96,1152]{1,0:T(8,128)(2,1)}, bf16[96,1152]{1,0:T(8,128)(2,1)S(1)}, u32[]{:S(2)}, u32[]{:S(2)}) collective-permute-start(bf16[96,1152]{1,0:T(8,128)(2,1)} %get-tuple-element.73), channel_id=1, source_target_pairs={{0,4},{2,6},{4,0},{6,2},{1,5},{3,7},{5,1},{7,3},{8,12},{10,14},{12... | collective-permute-start | bytes 663560 | tf_op jit(solution)/shard_map/ppermute | solution.py:69
  721.1 28.6 %collective-permute-start.10 = (bf16[96,1152]{1,0:T(8,128)(2,1)}, bf16[96,1152]{1,0:T(8,128)(2,1)}, u32[]{:S(2)}, u32[]{:S(2)}) collective-permute-start(bf16[96,1152]{1,0:T(8,128)(2,1)} %get-tuple-element.72), channel_id=1, source_target_pairs={{0,6},{2,0},{4,2},{6,4},{1,7},{3,1},{5,3},{7,5},{8,14},{10,8},{12,... | collective-permute-start | bytes 663560 | tf_op jit(solution)/shard_map/ppermute | solution.py:69
  731.2 5.1 copy-start.38
  739.9 5.4 copy-start.2
  739.9 5.4 copy-start.22
  739.9 5.4 copy-start.31
  747.7 63.4 %reduce-scatter.13.cloned.1.call-start = ((), (), s32[]{:S(2)}) async-start(), calls=%async_computation.13 | async-start | bytes 983040 | tf_op jit(solution)/shard_map/reduce_scatter | solution.py:740
  748.4 1.3 collective-permute-start.3
  748.5 21.1 %copy-start.3 = (f32[256,1536]{1,0:T(8,128)S(1)}, f32[256,1536]{1,0:T(8,128)}, u32[]{:S(2)}) copy-start(f32[256,1536]{1,0:T(8,128)} %scatter.14) | copy-start | bytes 4718596
  749.7 3.8 collective-permute-start.4
  753.5 10.8 %collective-permute-start.5 = (f32[41,128]{1,0:T(8,128)S(1)}, f32[41,128]{1,0:T(8,128)S(1)}, u32[]{:S(2)}, u32[]{:S(2)}) collective-permute-start(f32[41,128]{1,0:T(8,128)S(1)} %fusion.59), channel_id=1, source_target_pairs={{0,4},{2,6},{4,0},{6,2},{1,5},{3,7},{5,1},{7,3},{8,12},{10,14},{12... | collective-permute-start | bytes 62984 | tf_op jit(solution)/shard_map/ppermute | solution.py:92
  763.0 6.7 copy-start.6
  764.3 3.9 collective-permute-start.6
  768.2 3.8 collective-permute-start.7
  (8 other events, 11.5 us)
Sparse Core Ops, SparseCore 0:
  92.2 50.4 all-gather.3
  144.6 47.1 all-gather.5
  193.7 47.1 all-gather.7
  458.8 67.7 reduce-scatter.8
  529.5 45.6 reduce-scatter.22
  578.1 47.1 reduce-scatter.20
  628.4 47.1 reduce-scatter.18
  678.6 37.3 reduce-scatter.14
  719.0 43.8 reduce-scatter.10
  765.1 22.1 reduce-scatter.16
  789.6 21.4 reduce-scatter.12

commit v3 on v2

--- a/solution.py
+++ b/solution.py
@@ -7,6 +7,7 @@
 from jax.experimental import pallas as pl
 from jax.experimental.pallas import tpu as pltpu
 from jax.sharding import PartitionSpec as P
+
 
 D = 1536
 HEAD = 128
@@ -71,14 +72,14 @@
     return received
 
 
-def to_rows(grad, columns):
+def to_rows(summed, columns):
     size = lax.axis_size("ctx")
-    summed = lax.psum_scatter(grad, "dp", scatter_dimension=0, tiled=True)
-    rows, width = summed.shape[0] // size, summed.shape[1]
-    shard = jnp.zeros((rows, size * width), jnp.bfloat16)
-    for rank, block in exchange(summed.reshape(size, rows, width), "ctx"):
-        shard = lax.dynamic_update_slice_in_dim(shard, block, rank * width, 1)
-    return shard[:, :columns].astype(jnp.float32)
+    rows, width = summed[0].shape[0] // size, summed[0].shape[1]
+    blocks = jnp.stack([s.reshape(size, rows, width) for s in summed], axis=1)
+    shards = jnp.zeros((len(summed), rows, size * width), jnp.bfloat16)
+    for rank, block in exchange(blocks, "ctx"):
+        shards = lax.dynamic_update_slice_in_dim(shards, block, rank * width, 2)
+    return [s[:, :columns].astype(jnp.float32) for s in shards]
 
 
 def sum_everywhere(value):
@@ -491,6 +492,81 @@
         cost_estimate=pl.CostEstimate(flops=0, bytes_accessed=200000000, transcendentals=0),
         name="front",
     )(a, b, *parts)
+
+
+def back_kernel(size, groups, x_ref, o_ref, mine, far, near, own_sem, far_send, far_recv, near_send, near_recv):
+    place, group = lax.axis_index("ctx"), lax.axis_index("dp")
+    rows = o_ref.shape[0]
+    barrier = pltpu.get_barrier_semaphore()
+
+    def rank_at(k):
+        return lax.rem(place + 1 + k, size)
+
+    def block(in_group, rank):
+        return x_ref.at[pl.ds(pl.multiple_of((in_group * size + rank) * rows, rows), rows)]
+
+    def load(k):
+        return pltpu.make_async_copy(block(group, rank_at(k)), mine.at[k], own_sem.at[k])
+
+    def across(k, step):
+        to = lax.rem(group + step, groups)
+        return remote(block(to, rank_at(k)), far.at[k, step], far_send.at[k, step], far_recv.at[k, step], {"dp": to})
+
+    def along(k):
+        return remote(mine.at[k], near.at[k], near_send.at[k], near_recv.at[k], {"ctx": rank_at(k)})
+
+    for k in range(size):
+        load(k).start()
+    for step in range(1, size):
+        greet(barrier, {"ctx": lax.rem(place + step, size)})
+    for step in range(1, groups):
+        greet(barrier, {"dp": lax.rem(group + step, groups)})
+    pl.semaphore_wait(barrier, size + groups - 2)
+    for k in range(size):
+        for step in range(1, groups):
+            across(k, step).start()
+    for k in range(size):
+        load(k).wait()
+        for step in range(1, groups):
+            across(k, step).wait_recv()
+        parts = [mine.at[k]] + [far.at[k, step] for step in range(1, groups)]
+        if k < size - 1:
+            add_blocks(mine.at[k], parts)
+            along(k).start()
+    for k in range(size - 1):
+        along(k).wait_recv()
+        parts.append(near.at[k])
+    add_blocks(o_ref, parts)
+    for k in range(size):
+        for step in range(1, groups):
+            across(k, step).wait_send()
+        if k < size - 1:
+            along(k).wait_send()
+
+
+def back(x, ident):
+    size, groups = lax.axis_size("ctx"), lax.axis_size("dp")
+    rows, columns = x.shape[0] // (size * groups), x.shape[1]
+    dma = pltpu.SemaphoreType.DMA
+    return pl.pallas_call(
+        functools.partial(back_kernel, size, groups),
+        in_specs=[ANY],
+        out_specs=IN_VMEM,
+        out_shape=jax.ShapeDtypeStruct((rows, columns), jnp.float32),
+        scratch_shapes=[
+            pltpu.VMEM((size, rows, columns), x.dtype),
+            pltpu.VMEM((size, groups, rows, columns), x.dtype),
+            pltpu.VMEM((size, rows, columns), x.dtype),
+            dma((size,)),
+            dma((size, groups)),
+            dma((size, groups)),
+            dma((size,)),
+            dma((size,)),
+        ],
+        compiler_params=pltpu.CompilerParams(collective_id=ident, has_side_effects=True, vmem_limit_bytes=60000000),
+        cost_estimate=pl.CostEstimate(flops=0, bytes_accessed=100 * x.size, transcendentals=0),
+        name="back",
+    )(x)
 
 
 def mask_into(bias_ref, first, seg_ref, place_ref):
@@ -718,28 +794,20 @@
         jnp.bfloat16
     )
     grad_up_act = (grad_hidden * silu_gate).astype(jnp.bfloat16)
-    grad_mlp_rows = lax.psum_scatter(
-        (matmul_nt(grad_gate_act, full_gate) + matmul_nt(grad_up_act, full_up)).astype(
-            jnp.bfloat16
-        ),
-        ("ctx", "tensor"),
-        scatter_dimension=0,
-        tiled=True,
-    ).astype(jnp.float32)
-    shard_down = to_rows(matmul_tn(grad_branch, hidden).astype(jnp.bfloat16), hidden_width).T
-    shard_gate = to_rows(matmul_tn(mlp_rows, grad_gate_act).astype(jnp.bfloat16), hidden_width)
-    shard_up = to_rows(matmul_tn(mlp_rows, grad_up_act).astype(jnp.bfloat16), hidden_width)
+    summed = []
+    for left, right in ((grad_branch, hidden), (mlp_rows, grad_gate_act), (mlp_rows, grad_up_act)):
+        grad = matmul_tn(left, right).astype(jnp.bfloat16)
+        grad_gate_act, grad_up_act, grad = lax.optimization_barrier((grad_gate_act, grad_up_act, grad))
+        summed.append(lax.psum_scatter(grad, "dp", scatter_dimension=0, tiled=True))
+    grad_mlp_rows = (matmul_nt(grad_gate_act, full_gate) + matmul_nt(grad_up_act, full_up)).astype(jnp.bfloat16)
+    grad_mlp_rows = scatter(grad_mlp_rows, ctx_size, True, 6)
     grad_gain_mlp = jnp.sum(grad_mlp_rows * normed_mlp, axis=0)
     grad_mid = grad_result + norm_back(grad_mlp_rows, normed_mlp, scale_mlp, gain_two)
     grad_attn_rows = gather(grad_mid.astype(jnp.bfloat16), 1, True, 2)
     grad_heads = matmul(grad_attn_rows, full_out).astype(jnp.bfloat16)
     grad_out = matmul_tn(grad_attn_rows, heads_out).astype(jnp.bfloat16)
 
-    def to_owner(grad):
-        grad = lax.psum_scatter(grad, "dp", scatter_dimension=0, tiled=True)
-        return lax.psum_scatter(grad, "ctx", scatter_dimension=0, tiled=True).astype(jnp.float32)
-
-    shard_out = to_owner(grad_out).T
+    grad_out = lax.psum_scatter(grad_out, "dp", scatter_dimension=0, tiled=True)
     query_grads, key_grads, value_grads = [], [], []
     for c in range(kv_local):
         query, key, value, _, log_total = kept[c]
@@ -751,18 +819,23 @@
         key_grads.append(grad_kv[:, :HEAD])
         value_grads.append(grad_kv[:, HEAD:])
     grad_kv = grad_kv if kv_local == 1 else jnp.concatenate(key_grads + value_grads, axis=1)
+    grad_kv, *summed = lax.optimization_barrier((grad_kv, *summed))
+    shard_down, shard_gate, shard_up = to_rows(summed, hidden_width)
+    shard_down = shard_down.T
     grad_kv = scatter(grad_kv, ctx_size, False, 7)
-    back = jnp.concatenate(query_grads + [grad_kv[:, :kv_width]], axis=1)
+    grad_turned = jnp.concatenate(query_grads + [grad_kv[:, :kv_width]], axis=1)
     grad_pre = jnp.concatenate(
         [
-            rotate(back.reshape(shard_rows, turned // HEAD, HEAD), cosine, -sine_table)
+            rotate(grad_turned.reshape(shard_rows, turned // HEAD, HEAD), cosine, -sine_table)
             .reshape(shard_rows, turned)
             .astype(jnp.bfloat16),
             grad_kv[:, kv_width:].astype(jnp.bfloat16),
         ],
         axis=1,
     )
-    shard_qkv = to_owner(matmul_tn(normed_rows, grad_pre).astype(jnp.bfloat16))
+    grad_pre, grad_out = lax.optimization_barrier((grad_pre, grad_out))
+    shard_out = lax.psum_scatter(grad_out, "ctx", scatter_dimension=0, tiled=True).astype(jnp.float32).T
+    shard_qkv = back(matmul_tn(normed_rows, grad_pre).astype(jnp.bfloat16), 8)
     grad_normed = scatter(matmul_nt(grad_pre, full_qkv), 1, True, 4)
     grad_gain_attn = jnp.sum(grad_normed * normed_attn, axis=0)
     grad_input = grad_mid + norm_back(grad_normed, normed_attn, scale_attn, gain_one)
@@ -844,6 +917,5 @@
         P(("dp", "ctx"), "tensor"),
         P("tensor", ("dp", "ctx")),
     )
-    return jax.shard_map(
-        per_device, mesh=mesh, in_specs=in_specs, out_specs=out_specs, check_vma=False
-    )
+
+    return jax.shard_map(per_device, mesh=mesh, in_specs=in_specs, out_specs=out_specs, check_vma=False)

time: 831 us -> 823 us (level)
  the two profiles are of different devices: /device:TPU:0 before, /device:TPU:25 now
where the time goes in v3:
time: 823 us; the launch traced here: 814 us
  Pallas kernels  460 us (56%)
  matrix products  154 us (19%)
  waiting for transfers between devices  98.2 us (12%)
  local copies, waits for them, and re-layouts  38 us (5%)
  other arithmetic  32.9 us (4%)
  between operations  19.8 us (2%)
  starting transfers between devices  10.2 us (1%)
    pallas_call x5, Pallas kernels, gather(): pl.pallas_call(functools.partial(gather_kernel, size, paired, pieces), in...  164 us
    pallas_call x5, Pallas kernels, scatter(): pl.pallas_call(functools.partial(scatter_kernel, size, paired, pieces), i...  140 us
    pallas_call x1, Pallas kernels, front(): pl.pallas_call(functools.partial(front_kernel, size, groups), in_specs=[I...  72.9 us
    dot_general x5, matrix products, matmul(): return jnp.dot(first_op, second_op, preferred_element_type=jnp.float32)  56.3 us
    dot_general x5, matrix products, matmul_nt(): lax.dot_general(first_op, second_op, (((1,), (1,)), ((), ())), preferred_...  51.8 us
    dot_general x5, matrix products, matmul_tn(): lax.dot_general(first_op, second_op, (((0,), (0,)), ((), ())), preferred_...  46.4 us
    ppermute x3, waiting for transfers between devices, exchange(): lax.ppermute(going, axis, [(i, (i + step) % size) for i in range(size)])  41.7 us
    pallas_call x1, Pallas kernels, back(): pl.pallas_call(functools.partial(back_kernel, size, groups), in_specs=[AN...  37.1 us
  transfers between devices with their start and end apart: 19, of which 5 were waited for; matrix products, arithmetic and copies ran while one was open for 16% of the time, Pallas kernels for 32%

profile of v3, /device:TPU:25, one launch (start us, length us, event | category | flops | bytes accessed | tf_op | source)
XLA Modules:
  0.0 814.0 jit_solution(1612834485784725977)
XLA Ops:
  7.3 2.2 pad.13.g_ref
  9.5 2.1 pad.14.u_ref
  13.3 72.9 %front.1 = (bf16[1536,1024]{1,0:T(8,128)(2,1)}, bf16[1536,768]{1,0:T(8,128)(2,1)}, bf16[384,1152]{1,0:T(8,128)(2,1)}, bf16[384,1152]{1,0:T(8,128)(2,1)}, bf16[384,1152]{1,0:T(8,128)(2,1)}) custom-call(bf16[96,1024]{1,0:T(8,128)(2,1)} %pad_maximum_fusion.6.a_ref, bf16[96,768]{1,0:T(8,128)(2,1)} %bitcast.92, bf16[96,4608]{1,0:T(8,128)(2,1)} %pad.13.g_ref, ...), custom_call_target="tpu_custom_call" | custom-call | bytes 200000000 | tf_op jit(solution)/shard_map/front/pallas_call | solution.py:485
  89.0 1.2 collective-permute-start.1
  90.1 1.2 collective-permute-start.2
  93.4 13.6 %gather.5 = bf16[512,1536]{1,0:T(8,128)(2,1)} custom-call(bf16[256,1536]{1,0:T(8,128)(2,1)} %fusion.5.x_ref), custom_call_target="tpu_custom_call" | custom-call | bytes 23592960 | tf_op jit(solution)/shard_map/gather/pallas_call | solution.py:220
  107.1 4.2 convolution_add_fusion
  111.4 1.8 copy.37
  113.2 1.4 dynamic-slice_convert_fusion
  114.5 1.2 fusion.13
  115.7 1.8 subtract_convert_fusion.1
  118.6 19.2 %gather.6 = bf16[2048,256]{1,0:T(8,128)(2,1)} custom-call(bf16[512,256]{1,0:T(8,128)(2,1)} %pad_maximum_fusion.5.x_ref), custom_call_target="tpu_custom_call" | custom-call | bytes 15728640 | tf_op jit(solution)/shard_map/gather/pallas_call | solution.py:220
  137.8 2.4 fusion.16
  142.4 1.3 copy.41.place_ref
  143.7 19.2 %attend.1 = (bf16[512,768]{1,0:T(8,128)(2,1)}, f32[6,1,512]{2,1,0:T(1,128)}) custom-call(s32[1]{0:T(128)} %bitcast.first_ref, s32[1,512]{1,0:T(1,128)} %bitcast.95, s32[2048,1]{1,0:T(8,128)} %copy.41.place_ref, bf16[512,768]{1,0:T(8,128)(2,1)} %copy.48.q_ref, bf16[2048,128]{1,0:T(8,128)(2,1)} %get-tuple-element.101.k_ref, bf16[128,2048]{1,0:T(8,128)(2,1)} %copy.43.vt_ref), custom_call_target="tpu_custom_call" | custom-call | flops 3221225472 | bytes 1572864 | tf_op jit(solution)/shard_map/attend/pallas_call | solution.py:771
  162.9 4.3 fusion.18.x_ref
  167.2 7.0 scatter.12
  174.2 1.7 multiply_reduce_fusion.2
  177.7 57.8 %gather.7 = bf16[2048,1536]{1,0:T(8,128)(2,1)} custom-call(bf16[256,1536]{1,0:T(8,128)(2,1)} %multiply_convert_fusion.3.x_ref), custom_call_target="tpu_custom_call" | custom-call | bytes 94371840 | tf_op jit(solution)/shard_map/gather/pallas_call | solution.py:220
  239.7 13.6 %fusion.19 = f32[2048,1152]{1,0:T(8,128)} fusion(bf16[2048,1536]{1,0:T(8,128)(2,1)} %gather.7, bf16[1536,1152]{1,0:T(8,128)(2,1)} %all-gather.4.cloned.1.call-done), kind=kOutput, calls=%fused_computation.102 | convolution fusion | flops 7247757312 | bytes 19267584 | tf_op jit(solution)/shard_map/dot_general | solution.py:44
  253.3 15.8 %multiply_convert_fusion.2 = (bf16[2048,1152]{1,0:T(8,128)(2,1)}, f32[2048,1152]{1,0:T(8,128)}) fusion(f32[2048,1152]{1,0:T(8,128)} %fusion.19, bf16[2048,1536]{1,0:T(8,128)(2,1)} %gather.7, bf16[1536,1152]{1,0:T(8,128)(2,1)} %all-gather.6.cloned.1.call-done), kind=kOutput, calls=%fused_computation.3 | convolution fusion | flops 7261913088 | bytes 33423360 | tf_op jit(solution)/shard_map/dot_general | solution.py:44
  269.1 13.3 %convolution_convert_fusion.3.x_ref = bf16[2048,1536]{1,0:T(8,128)(2,1)} fusion(bf16[2048,1152]{1,0:T(8,128)(2,1)} %get-tuple-element.112, bf16[1536,1152]{1,0:T(8,128)(2,1)} %all-gather.8.cloned.1.call-done), kind=kOutput, calls=%fused_computation.9 | convolution fusion | flops 7250903040 | bytes 14548992 | tf_op jit(solution)/shard_map/dot_general | solution.py:54
  282.4 54.7 %scatter.13 = f32[256,1536]{1,0:T(8,128)} custom-call(bf16[2048,1536]{1,0:T(8,128)(2,1)} %convolution_convert_fusion.3.x_ref), custom_call_target="tpu_custom_call" | custom-call | bytes 94371840 | tf_op jit(solution)/shard_map/scatter/pallas_call | solution.py:352
  337.1 2.8 fusion.14.x_ref
  339.9 69.0 %gather.8 = bf16[2048,1536]{1,0:T(8,128)(2,1)} custom-call(bf16[256,1536]{1,0:T(8,128)(2,1)} %fusion.14.x_ref), custom_call_target="tpu_custom_call" | custom-call | bytes 94371840 | tf_op jit(solution)/shard_map/gather/pallas_call | solution.py:220
  409.0 13.2 %convolution_convert_fusion.2 = bf16[1536,1152]{1,0:T(8,128)(2,1)} fusion(bf16[2048,1536]{1,0:T(8,128)(2,1)} %gather.8, bf16[2048,1152]{1,0:T(8,128)(2,1)} %get-tuple-element.112), kind=kOutput, calls=%fused_computation.8 | convolution fusion | flops 7249526784 | bytes 14548992 | tf_op jit(solution)/shard_map/dot_general | solution.py:48
  422.1 18.8 %multiply_convert_fusion = (bf16[2048,1152]{1,0:T(8,128)(2,1)S(1)}, bf16[2048,1152]{1,0:T(8,128)(2,1)}) fusion(f32[2048,1152]{1,0:T(8,128)} %fusion.19, f32[2048,1152]{1,0:T(8,128)} %get-tuple-element.113, bf16[2048,1536]{1,0:T(8,128)(2,1)} %gather.8, bf16[1536,1152]{1,0:T(8,128)(2,1)} %all-gather.8.cloned.1.call-done), kind=kOutput, calls=%fused_computation.1 | convolution fusion | flops 7278428160 | bytes 38141952 | tf_op jit(solution)/shard_map/dot_general | solution.py:44
  440.9 2.3 copy-done.40
  443.2 12.0 %convolution_convert_fusion = bf16[1536,1152]{1,0:T(8,128)(2,1)} fusion(bf16[2048,1536]{1,0:T(8,128)(2,1)} %gather.7, bf16[2048,1152]{1,0:T(8,128)(2,1)S(1)} %get-tuple-element.62), kind=kOutput, calls=%fused_computation.6 | convolution fusion | flops 7249526784 | bytes 14548992 | tf_op jit(solution)/shard_map/dot_general | solution.py:48
  455.2 13.2 %convolution_convert_fusion.1 = bf16[1536,1152]{1,0:T(8,128)(2,1)} fusion(bf16[2048,1536]{1,0:T(8,128)(2,1)} %gather.7, bf16[2048,1152]{1,0:T(8,128)(2,1)} %get-tuple-element.61), kind=kOutput, calls=%fused_computation.7 | convolution fusion | flops 7249526784 | bytes 14548992 | tf_op jit(solution)/shard_map/dot_general | solution.py:48
  469.6 14.6 %fusion.20 = f32[2048,1536]{1,0:T(8,128)} fusion(bf16[2048,1152]{1,0:T(8,128)(2,1)} %get-tuple-element.61, bf16[1536,1152]{1,0:T(8,128)(2,1)} %all-gather.4.cloned.1.call-done), kind=kOutput, calls=%fused_computation.103 | convolution fusion | flops 7247757312 | bytes 20840448 | tf_op jit(solution)/shard_map/dot_general | solution.py:54
  484.2 14.2 %add_convert_fusion.x_ref = bf16[2048,1536]{1,0:T(8,128)(2,1)} fusion(f32[2048,1536]{1,0:T(8,128)} %fusion.20, bf16[2048,1152]{1,0:T(8,128)(2,1)} %copy-done.40, bf16[1536,1152]{1,0:T(8,128)(2,1)S(1)} %copy-done.36), kind=kOutput, calls=%fused_computation | convolution fusion | flops 7254048768 | bytes 27131904 | tf_op jit(solution)/shard_map/dot_general | solution.py:54
  498.4 54.6 %scatter.14 = f32[256,1536]{1,0:T(8,128)} custom-call(bf16[2048,1536]{1,0:T(8,128)(2,1)} %add_convert_fusion.x_ref), custom_call_target="tpu_custom_call" | custom-call | bytes 94371840 | tf_op jit(solution)/shard_map/scatter/pallas_call | solution.py:352
  553.0 3.2 multiply_reduce_fusion
  556.2 2.5 fusion.15
  558.7 4.5 gather.9
  563.3 4.5 convolution_convert_fusion.5
  569.9 3.9 convolution_convert_fusion.6.do_ref
  573.8 26.9 %attend_back.1 = (f32[512,768]{1,0:T(8,128)}, bf16[2048,256]{1,0:T(8,128)(2,1)}) custom-call(s32[1]{0:T(128)} %bitcast.first_ref, s32[1,512]{1,0:T(1,128)} %bitcast.96, s32[2048,1]{1,0:T(8,128)} %copy.41.place_ref, bf16[512,768]{1,0:T(8,128)(2,1)} %copy.48.q_ref, bf16[512,768]{1,0:T(8,128)(2,1)} %convolution_convert_fusion.6.do_ref, ...), custom_call_target="tpu_custom_call" | custom-call | flops 8053063680 | bytes 3145728 | tf_op jit(solution)/shard_map/attend_back/pallas_call | solution.py:815
  600.8 13.6 %reduce-scatter.6.cloned.1.call-done = bf16[384,1152]{1,0:T(8,128)(2,1)} async-done(((bf16[1536,1152]{1,0:T(8,128)(2,1)}), bf16[384,1152]{1,0:T(8,128)(2,1)}) %reduce-scatter.6.cloned.1.call-update) | async-done | bytes 884752 | tf_op jit(solution)/shard_map/reduce_scatter | solution.py:801
  614.4 18.4 %scatter.15 = f32[512,256]{1,0:T(8,128)} custom-call(bf16[2048,256]{1,0:T(8,128)(2,1)} %get-tuple-element.69.x_ref), custom_call_target="tpu_custom_call" | custom-call | bytes 15728640 | tf_op jit(solution)/shard_map/scatter/pallas_call | solution.py:352
  634.9 1.7 copy.46
  636.7 1.8 subtract_convert_fusion
  638.6 16.2 %reduce-scatter.12.cloned.1.call-done = bf16[384,768]{1,0:T(8,128)(2,1)} async-done(((bf16[1536,768]{1,0:T(8,128)(2,1)}), bf16[384,768]{1,0:T(8,128)(2,1)}) %reduce-scatter.12.cloned.1.call-update) | async-done | bytes 589840 | tf_op jit(solution)/shard_map/reduce_scatter | solution.py:810
  654.8 5.5 fusion.21.x_ref
  660.3 3.5 convolution_convert_fusion.4.x_ref
  664.1 5.6 scatter.16
  669.7 1.9 fusion.7
  673.5 1.5 copy-done.5
  675.0 1.2 dynamic-slice_bitcast_fusion
  676.5 1.3 collective-permute-start.4
  677.8 24.3 %collective-permute-done.4 = f32[41,128]{1,0:T(8,128)S(1)} collective-permute-done((f32[41,128]{1,0:T(8,128)S(1)}, f32[41,128]{1,0:T(8,128)S(1)}, u32[]{:S(2)}, u32[]{:S(2)}) %collective-permute-start.4) | collective-permute-done | bytes 21024 | tf_op jit(solution)/shard_map/ppermute | solution.py:93
  702.1 3.0 fusion.10
  705.7 1.2 collective-permute-start.6
  708.3 37.1 %back.1 = f32[96,1024]{1,0:T(8,128)} custom-call(bf16[1536,1024]{1,0:T(8,128)(2,1)} %convolution_convert_fusion.4.x_ref), custom_call_target="tpu_custom_call" | custom-call | bytes 157286400 | tf_op jit(solution)/shard_map/back/pallas_call | solution.py:551
  745.4 2.4 collective-permute-start.7
  747.8 1.5 fusion.17
  749.3 1.7 slice.141
  751.0 1.2 collective-permute-start.9
  755.7 41.7 %collective-permute-done.9 = bf16[3,96,1152]{2,1,0:T(8,128)(2,1)} collective-permute-done((bf16[3,96,1152]{2,1,0:T(8,128)(2,1)}, bf16[3,96,1152]{2,1,0:T(8,128)(2,1)}, u32[]{:S(2)}, u32[]{:S(2)}) %collective-permute-start.9) | collective-permute-done | bytes 663584 | tf_op jit(solution)/shard_map/ppermute | solution.py:70
  800.0 1.3 convert_bitcast_fusion
  801.3 1.3 slice_convert_fusion
  802.6 1.3 slice_convert_fusion.1
  803.9 1.6 convert_bitcast_fusion.1
  (184 shorter events, 28.6 us)
Async XLA Ops:
  7.2 4.4 copy-start.17
  7.2 5.4 copy-start.19
  7.2 5.4 copy-start.27
  7.2 5.4 copy-start.26
  7.2 232.5 %all-gather.4.cloned.1.call-start = ((), (), s32[]{:S(2)}) async-start(), calls=%async_computation.5 | async-start | bytes 4423680 | tf_op jit(solution)/shard_map/all_gather | solution.py:727
  12.6 74.4 %copy-start.25 = (s32[2048]{0:T(1024)S(1)}, s32[2048]{0:T(1024)}, u32[]{:S(2)}) copy-start(s32[2048]{0:T(1024)} %param.25) | copy-start | bytes 24580
  13.3 78.2 %copy-start.38 = (bf16[256]{0:T(256)(128)(2,1)S(1)}, bf16[256]{0:T(256)(128)(2,1)}, u32[]{:S(2)}) copy-start(bf16[256]{0:T(256)(128)(2,1)} %param.30) | copy-start | bytes 1540
  13.3 78.3 %copy-start.39 = (bf16[256]{0:T(256)(128)(2,1)S(1)}, bf16[256]{0:T(256)(128)(2,1)}, u32[]{:S(2)}) copy-start(bf16[256]{0:T(256)(128)(2,1)} %param.32) | copy-start | bytes 1540
  13.3 78.3 %copy-start.33 = (bf16[1536]{0:T(1024)(128)(2,1)S(1)}, bf16[1536]{0:T(1024)(128)(2,1)}, u32[]{:S(2)}) copy-start(bf16[1536]{0:T(1024)(128)(2,1)} %param.26) | copy-start | bytes 9220
  13.3 78.3 %copy-start.1 = (bf16[256,1536]{1,0:T(8,128)(2,1)S(1)}, bf16[256,1536]{1,0:T(8,128)(2,1)}, u32[]{:S(2)}) copy-start(bf16[256,1536]{1,0:T(8,128)(2,1)} %param.20) | copy-start | bytes 2359300
  86.2 167.1 %all-gather.6.cloned.1.call-start = ((), (), s32[]{:S(2)}) async-start(), calls=%async_computation.6 | async-start | bytes 4423680 | tf_op jit(solution)/shard_map/all_gather | solution.py:727
  87.0 182.1 %all-gather.8.cloned.1.call-start = ((), (), s32[]{:S(2)}) async-start(), calls=%async_computation.7 | async-start | bytes 4423680 | tf_op jit(solution)/shard_map/all_gather | solution.py:727
  88.3 147.2 %collective-permute-start = (f32[8,128]{1,0:T(8,128)S(1)}, f32[8,128]{1,0:T(8,128)S(1)}, u32[]{:S(2)}, u32[]{:S(2)}) collective-permute-start(f32[8,128]{1,0:T(8,128)S(1)} %broadcast_in_dim.17), channel_id=1, source_target_pairs={{0,8},{8,16},{16,24},{24,0},{1,9},{9,17},{17,25},{25,1},{2,10},{10... | collective-permute-start | bytes 12296 | tf_op jit(solution)/shard_map/ppermute | solution.py:734
  89.0 148.4 %collective-permute-start.1 = (f32[8,128]{1,0:T(8,128)S(1)}, f32[8,128]{1,0:T(8,128)S(1)}, u32[]{:S(2)}, u32[]{:S(2)}) collective-permute-start(f32[8,128]{1,0:T(8,128)S(1)} %broadcast_in_dim.17), channel_id=1, source_target_pairs={{0,16},{8,24},{16,0},{24,8},{1,17},{9,25},{17,1},{25,9},{2,18},{10... | collective-permute-start | bytes 12296 | tf_op jit(solution)/shard_map/ppermute | solution.py:734
  90.1 148.4 %collective-permute-start.2 = (f32[8,128]{1,0:T(8,128)S(1)}, f32[8,128]{1,0:T(8,128)S(1)}, u32[]{:S(2)}, u32[]{:S(2)}) collective-permute-start(f32[8,128]{1,0:T(8,128)S(1)} %broadcast_in_dim.17), channel_id=1, source_target_pairs={{0,24},{8,0},{16,8},{24,16},{1,25},{9,1},{17,9},{25,17},{2,26},{10... | collective-permute-start | bytes 12296 | tf_op jit(solution)/shard_map/ppermute | solution.py:734
  91.4 15.6 %copy-start.35 = (bf16[1536]{0:T(1024)(128)(2,1)S(1)}, bf16[1536]{0:T(1024)(128)(2,1)}, u32[]{:S(2)}) copy-start(bf16[1536]{0:T(1024)(128)(2,1)} %param.28) | copy-start | bytes 9220
  91.4 509.4 %reduce-scatter.10.cloned.1.call-start = ((), (), s32[]{:S(2)}) async-start(), calls=%async_computation.10 | async-start | bytes 4423680 | tf_op jit(solution)/shard_map/reduce_scatter | solution.py:801
  91.6 0.6 copy-start.20
  92.2 14.8 %copy-start.30 = (f32[256]{0:T(256)}, f32[256]{0:T(256)S(1)}, u32[]{:S(2)}) copy-start(f32[256]{0:T(256)S(1)} %add_rsqrt_fusion.1) | copy-start | bytes 3076
  115.7 1.8 copy-start.12
  143.7 19.2 %copy-start.37 = (bf16[1536,768]{1,0:T(8,128)(2,1)S(1)}, bf16[1536,768]{1,0:T(8,128)(2,1)}, u32[]{:S(2)}) copy-start(bf16[1536,768]{1,0:T(8,128)(2,1)} %get-tuple-element.53) | copy-start | bytes 7077892
  174.2 1.7 copy-start.34
  175.9 59.5 %copy-start.28 = (f32[256]{0:T(256)}, f32[256]{0:T(256)S(1)}, u32[]{:S(2)}) copy-start(f32[256]{0:T(256)S(1)} %add_rsqrt_fusion) | copy-start | bytes 3076
  176.0 59.5 %copy-start.22 = (f32[1536]{0:T(1024)}, f32[1536]{0:T(1024)S(1)}, u32[]{:S(2)}) copy-start(f32[1536]{0:T(1024)S(1)} %convert_element_type.111) | copy-start | bytes 18436
  282.4 54.7 %copy-start.6 = (bf16[256,1536]{1,0:T(8,128)(2,1)S(1)}, bf16[256,1536]{1,0:T(8,128)(2,1)}, u32[]{:S(2)}) copy-start(bf16[256,1536]{1,0:T(8,128)(2,1)} %param.21) | copy-start | bytes 2359300
  282.4 54.7 %copy-start.7 = (bf16[256,1536]{1,0:T(8,128)(2,1)S(1)}, bf16[256,1536]{1,0:T(8,128)(2,1)}, u32[]{:S(2)}) copy-start(bf16[256,1536]{1,0:T(8,128)(2,1)} %param.22) | copy-start | bytes 2359300
  440.9 2.3 copy-start.40
  468.4 132.4 %reduce-scatter.8.cloned.1.call-start = ((), (), s32[]{:S(2)}) async-start(), calls=%async_computation.9 | async-start | bytes 4423680 | tf_op jit(solution)/shard_map/reduce_scatter | solution.py:801
  468.9 145.4 %reduce-scatter.6.cloned.1.call-start = ((), (), s32[]{:S(2)}) async-start(), calls=%async_computation.8 | async-start | bytes 4423680 | tf_op jit(solution)/shard_map/reduce_scatter | solution.py:801
  469.5 185.3 %reduce-scatter.12.cloned.1.call-start = ((), (), s32[]{:S(2)}) async-start(), calls=%async_computation.11 | async-start | bytes 2949120 | tf_op jit(solution)/shard_map/reduce_scatter | solution.py:810
  469.6 14.6 %copy-start.36 = (bf16[1536,1152]{1,0:T(8,128)(2,1)S(1)}, bf16[1536,1152]{1,0:T(8,128)(2,1)}, u32[]{:S(2)}) copy-start(bf16[1536,1152]{1,0:T(8,128)(2,1)} %all-gather.6.cloned.1.call-done) | copy-start | bytes 10616836
  498.3 54.6 %copy-start = (f32[256,1536]{1,0:T(8,128)S(1)}, f32[256,1536]{1,0:T(8,128)}, u32[]{:S(2)}) copy-start(f32[256,1536]{1,0:T(8,128)} %scatter.13) | copy-start | bytes 4718596
  498.4 54.7 %copy-start.23 = (f32[1536]{0:T(1024)S(1)}, f32[1536]{0:T(1024)}, u32[]{:S(2)}) copy-start(f32[1536]{0:T(1024)} %copy-done.22) | copy-start | bytes 18436
  498.4 54.7 %copy-start.29 = (f32[256]{0:T(256)S(1)}, f32[256]{0:T(256)}, u32[]{:S(2)}) copy-start(f32[256]{0:T(256)} %copy-done.28) | copy-start | bytes 3076
  498.4 54.7 %copy-start.32 = (f32[256]{0:T(256)S(1)}, f32[256]{0:T(256)}, u32[]{:S(2)}) copy-start(f32[256]{0:T(256)} %get-tuple-element.83) | copy-start | bytes 3076
  553.0 3.2 copy-start.4
  567.8 1.0 copy-start.8
  567.8 2.1 copy-start.11
  567.8 236.1 %reduce-scatter.14.cloned.1.call-start = ((), (), s32[]{:S(2)}) async-start(), calls=%async_computation.12 | async-start | bytes 737280 | tf_op jit(solution)/shard_map/reduce_scatter | solution.py:837
  600.7 33.9 %copy-start.9 = (f32[512,768]{1,0:T(8,128)S(1)}, f32[512,768]{1,0:T(8,128)}, u32[]{:S(2)}) copy-start(f32[512,768]{1,0:T(8,128)} %get-tuple-element.64) | copy-start | bytes 4718596
  634.8 1.9 copy-start.13
  634.8 1.9 copy-start.18
  654.8 5.5 copy-start.10
  663.8 5.9 copy-start.2
  663.8 5.9 copy-start.21
  663.8 5.9 copy-start.31
  664.1 7.9 copy-start.24
  664.1 9.1 %copy-start.14 = (bf16[384,1152]{1,0:T(8,128)(2,1)S(1)}, bf16[384,1152]{1,0:T(8,128)(2,1)}, u32[]{:S(2)}) copy-start(bf16[384,1152]{1,0:T(8,128)(2,1)} %reduce-scatter.10.cloned.1.call-done) | copy-start | bytes 2654212
  664.1 9.1 %copy-start.15 = (bf16[384,1152]{1,0:T(8,128)(2,1)S(1)}, bf16[384,1152]{1,0:T(8,128)(2,1)}, u32[]{:S(2)}) copy-start(bf16[384,1152]{1,0:T(8,128)(2,1)} %reduce-scatter.8.cloned.1.call-done) | copy-start | bytes 2654212
  664.1 9.1 %copy-start.16 = (bf16[384,1152]{1,0:T(8,128)(2,1)S(1)}, bf16[384,1152]{1,0:T(8,128)(2,1)}, u32[]{:S(2)}) copy-start(bf16[384,1152]{1,0:T(8,128)(2,1)} %reduce-scatter.6.cloned.1.call-done) | copy-start | bytes 2654212
  672.7 3.8 collective-permute-start.3
  673.5 1.5 copy-start.5
  675.0 27.1 %copy-start.3 = (f32[256,1536]{1,0:T(8,128)S(1)}, f32[256,1536]{1,0:T(8,128)}, u32[]{:S(2)}) copy-start(f32[256,1536]{1,0:T(8,128)} %scatter.16) | copy-start | bytes 4718596
  676.2 78.3 %collective-permute-start.8 = (bf16[3,96,1152]{2,1,0:T(8,128)(2,1)}, bf16[3,96,1152]{2,1,0:T(8,128)(2,1)}, u32[]{:S(2)}, u32[]{:S(2)}) collective-permute-start(bf16[3,96,1152]{2,1,0:T(8,128)(2,1)} %get-tuple-element.94), channel_id=1, source_target_pairs={{0,2},{2,4},{4,6},{6,0},{1,3},{3,5},{5,7},{7,1},{8,10},{10,12},{12... | collective-permute-start | bytes 1990664 | tf_op jit(solution)/shard_map/ppermute | solution.py:70
  676.5 25.7 %collective-permute-start.4 = (f32[41,128]{1,0:T(8,128)S(1)}, f32[41,128]{1,0:T(8,128)S(1)}, u32[]{:S(2)}, u32[]{:S(2)}) collective-permute-start(f32[41,128]{1,0:T(8,128)S(1)} %bitcast_add_fusion), channel_id=1, source_target_pairs={{0,2},{2,0},{4,6},{6,4},{1,3},{3,1},{5,7},{7,5},{8,10},{10,8},{12,... | collective-permute-start | bytes 62984 | tf_op jit(solution)/shard_map/ppermute | solution.py:93
  702.1 3.6 collective-permute-start.5
  705.7 39.7 %collective-permute-start.6 = (f32[41,128]{1,0:T(8,128)S(1)}, f32[41,128]{1,0:T(8,128)S(1)}, u32[]{:S(2)}, u32[]{:S(2)}) collective-permute-start(f32[41,128]{1,0:T(8,128)S(1)} %add.200), channel_id=1, source_target_pairs={{0,8},{8,0},{16,24},{24,16},{1,9},{9,1},{17,25},{25,17},{2,10},{10... | collective-permute-start | bytes 62984 | tf_op jit(solution)/shard_map/ppermute | solution.py:93
  745.4 6.7 collective-permute-start.7
  751.0 46.5 %collective-permute-start.9 = (bf16[3,96,1152]{2,1,0:T(8,128)(2,1)}, bf16[3,96,1152]{2,1,0:T(8,128)(2,1)}, u32[]{:S(2)}, u32[]{:S(2)}) collective-permute-start(bf16[3,96,1152]{2,1,0:T(8,128)(2,1)} %get-tuple-element.93), channel_id=1, source_target_pairs={{0,4},{2,6},{4,0},{6,2},{1,5},{3,7},{5,1},{7,3},{8,12},{10,14},{12... | collective-permute-start | bytes 1990664 | tf_op jit(solution)/shard_map/ppermute | solution.py:70
  752.2 46.4 %collective-permute-start.10 = (bf16[3,96,1152]{2,1,0:T(8,128)(2,1)S(1)}, bf16[3,96,1152]{2,1,0:T(8,128)(2,1)}, u32[]{:S(2)}, u32[]{:S(2)}) collective-permute-start(bf16[3,96,1152]{2,1,0:T(8,128)(2,1)S(1)} %get-tuple-element.92), channel_id=1, source_target_pairs={{0,6},{2,0},{4,2},{6,4},{1,7},{3,1},{5,3},{7,5},{8,14},{10,8},{12,... | collective-permute-start | bytes 1990664 | tf_op jit(solution)/shard_map/ppermute | solution.py:70
Sparse Core Ops, SparseCore 0:
  86.3 55.6 all-gather.3
  143.8 47.2 all-gather.5
  193.0 47.1 all-gather.7
  468.5 45.5 reduce-scatter.9
  517.0 47.1 reduce-scatter.7
  567.2 47.1 reduce-scatter.5
  617.4 37.3 reduce-scatter.11
  677.9 26.4 reduce-scatter.13

commit v4 on v3

--- a/solution.py
+++ b/solution.py
@@ -82,17 +82,8 @@
     return [s[:, :columns].astype(jnp.float32) for s in shards]
 
 
-def sum_everywhere(value):
-    for axis in ("tensor", "ctx", "dp"):
-        size = lax.axis_size(axis)
-        if size & (size - 1):
-            value = lax.psum(value, axis)
-            continue
-        step = 1
-        while step < size:
-            value = value + lax.ppermute(value, axis, [(i, i ^ step) for i in range(size)])
-            step *= 2
-    return value
+def nn(first_op, second_op):
+    return jnp.dot(first_op, second_op, preferred_element_type=jnp.float32)
 
 
 MESH = pl.DeviceIdType.MESH
@@ -494,8 +485,12 @@
     )(a, b, *parts)
 
 
-def back_kernel(size, groups, x_ref, o_ref, mine, far, near, own_sem, far_send, far_recv, near_send, near_recv):
+def back_kernel(
+    size, groups, x_ref, s_ref, o_ref, t_ref, mine, far, near, pair, crowd, row,
+    own_sem, far_send, far_recv, near_send, near_recv, pair_sems, crowd_send, crowd_recv, row_send, row_recv,
+):
     place, group = lax.axis_index("ctx"), lax.axis_index("dp")
+    core = lax.axis_index("tensor")
     rows = o_ref.shape[0]
     barrier = pltpu.get_barrier_semaphore()
 
@@ -514,6 +509,19 @@
 
     def along(k):
         return remote(mine.at[k], near.at[k], near_send.at[k], near_recv.at[k], {"ctx": rank_at(k)})
+
+    to_mate = remote(s_ref, pair, pair_sems.at[0], pair_sems.at[1], {"tensor": 1 - core})
+
+    def to_crowd(step):
+        return remote(
+            crowd.at[group], crowd.at[group], crowd_send.at[step], crowd_recv.at[step],
+            {"dp": lax.rem(group + step, groups)},
+        )
+
+    def to_row(step):
+        return remote(
+            row.at[place], row.at[place], row_send.at[step], row_recv.at[step], {"ctx": lax.rem(place + step, size)}
+        )
 
     for k in range(size):
         load(k).start()
@@ -521,10 +529,24 @@
         greet(barrier, {"ctx": lax.rem(place + step, size)})
     for step in range(1, groups):
         greet(barrier, {"dp": lax.rem(group + step, groups)})
-    pl.semaphore_wait(barrier, size + groups - 2)
+    greet(barrier, {"tensor": 1 - core})
+    pl.semaphore_wait(barrier, size + groups - 1)
+    to_mate.start()
+    to_mate.wait_recv()
+    crowd[group] = s_ref[...] + pair[...]
+    for step in range(1, groups):
+        to_crowd(step).start()
     for k in range(size):
         for step in range(1, groups):
             across(k, step).start()
+    for step in range(1, groups):
+        to_crowd(step).wait_recv()
+    total = crowd[0]
+    for g in range(1, groups):
+        total += crowd[g]
+    row[place] = total
+    for step in range(1, size):
+        to_row(step).start()
     for k in range(size):
         load(k).wait()
         for step in range(1, groups):
@@ -537,6 +559,17 @@
         along(k).wait_recv()
         parts.append(near.at[k])
     add_blocks(o_ref, parts)
+    for step in range(1, size):
+        to_row(step).wait_recv()
+    total = row[0]
+    for c in range(1, size):
+        total += row[c]
+    t_ref[...] = total
+    to_mate.wait_send()
+    for step in range(1, groups):
+        to_crowd(step).wait_send()
+    for step in range(1, size):
+        to_row(step).wait_send()
     for k in range(size):
         for step in range(1, groups):
             across(k, step).wait_send()
@@ -544,29 +577,232 @@
             along(k).wait_send()
 
 
-def back(x, ident):
+def back(x, small, ident):
     size, groups = lax.axis_size("ctx"), lax.axis_size("dp")
     rows, columns = x.shape[0] // (size * groups), x.shape[1]
     dma = pltpu.SemaphoreType.DMA
     return pl.pallas_call(
         functools.partial(back_kernel, size, groups),
-        in_specs=[ANY],
-        out_specs=IN_VMEM,
-        out_shape=jax.ShapeDtypeStruct((rows, columns), jnp.float32),
+        in_specs=[ANY, IN_VMEM],
+        out_specs=[IN_VMEM, IN_VMEM],
+        out_shape=[
+            jax.ShapeDtypeStruct((rows, columns), jnp.float32),
+            jax.ShapeDtypeStruct(small.shape, jnp.float32),
+        ],
         scratch_shapes=[
             pltpu.VMEM((size, rows, columns), x.dtype),
             pltpu.VMEM((size, groups, rows, columns), x.dtype),
             pltpu.VMEM((size, rows, columns), x.dtype),
+            pltpu.VMEM(small.shape, jnp.float32),
+            pltpu.VMEM((groups,) + small.shape, jnp.float32),
+            pltpu.VMEM((size,) + small.shape, jnp.float32),
             dma((size,)),
             dma((size, groups)),
             dma((size, groups)),
+            dma((size,)),
+            dma((size,)),
+            dma((2,)),
+            dma((groups,)),
+            dma((groups,)),
             dma((size,)),
             dma((size,)),
         ],
         compiler_params=pltpu.CompilerParams(collective_id=ident, has_side_effects=True, vmem_limit_bytes=60000000),
         cost_estimate=pl.CostEstimate(flops=0, bytes_accessed=100 * x.size, transcendentals=0),
         name="back",
-    )(x)
+    )(x, small)
+
+
+def column_step(width):
+    return max(t for t in (384, 256, 128) if width % t == 0)
+
+
+def expand_block(x_ref, weights, extra, stage):
+    step = column_step(weights[0].shape[1])
+
+    def some(j, carry):
+        span = pl.ds(pl.multiple_of(j * step, step), step)
+        gate = nn(x_ref[...], weights[0][:, span])
+        up = nn(x_ref[...], weights[1][:, span])
+        stage[0, :, span] = gate.astype(jnp.bfloat16)
+        stage[1, :, span] = up.astype(jnp.bfloat16)
+        stage[2, :, span] = (gate * jax.nn.sigmoid(gate) * up).astype(jnp.bfloat16)
+        return carry
+
+    lax.fori_loop(0, weights[0].shape[1] // step, some, 0)
+
+
+def shrink_block(x_ref, weights, extra, stage):
+    step = column_step(weights[0].shape[1])
+
+    def some(j, carry):
+        span = pl.ds(pl.multiple_of(j * step, step), step)
+        grad = nn(x_ref[...], weights[0][:, span])
+        gate = extra[0, :, span].astype(jnp.float32)
+        up = extra[1, :, span].astype(jnp.float32)
+        sigmoid = jax.nn.sigmoid(gate)
+        stage[0, :, span] = (grad * up * sigmoid * (1.0 + gate * (1.0 - sigmoid))).astype(jnp.bfloat16)
+        stage[1, :, span] = (grad * gate * sigmoid).astype(jnp.bfloat16)
+        return carry
+
+    lax.fori_loop(0, weights[0].shape[1] // step, some, 0)
+
+
+def gather_apply_kernel(size, pieces, work, n_weights, n_extra, n_made, *refs):
+    x_ref, refs = refs[0], refs[1:]
+    weights_from, refs = refs[:n_weights], refs[n_weights:]
+    extra_from, refs = refs[:n_extra], refs[n_extra:]
+    o_ref, refs = refs[0], refs[1:]
+    made_to, refs = refs[:n_made], refs[n_made:]
+    weights, refs = refs[:n_weights], refs[n_weights:]
+    extra, stage, refs = refs[0], refs[1], refs[2:]
+    local_sem, weight_sem, extra_sem, stage_sem = refs[:4]
+    up_send, up_recv, down_send, down_recv, mate_send, mate_recv = refs[4:]
+    place = lax.axis_index("ctx")
+    core = lax.axis_index("tensor")
+    rows = x_ref.shape[0]
+    part = rows // pieces
+    last = size - 1
+
+    loads = [pltpu.make_async_copy(weights_from[w], weights[w], weight_sem.at[w]) for w in range(n_weights)]
+    for load in loads:
+        load.start()
+
+    def first_of(rank, which):
+        return pl.multiple_of((rank * 2 + which) * rows, rows)
+
+    def block(rank, which, p):
+        return o_ref.at[pl.ds(pl.multiple_of((rank * 2 + which) * rows + p * part, part), part)]
+
+    def going_up(k, p):
+        there = block(place - k, core, p)
+        return remote(there, there, up_send.at[k, p], up_recv.at[k, p], {"ctx": place + 1})
+
+    def going_down(k, p):
+        there = block(place + k, core, p)
+        return remote(there, there, down_send.at[k, p], down_recv.at[k, p], {"ctx": place - 1})
+
+    def coming_up(k, p):
+        there = block(place - 1 - k, core, p)
+        return remote(there, there, up_send.at[k, p], up_recv.at[k, p], {"ctx": place - 1})
+
+    def coming_down(k, p):
+        there = block(place + 1 + k, core, p)
+        return remote(there, there, down_send.at[k, p], down_recv.at[k, p], {"ctx": place + 1})
+
+    def to_mate(rank, p):
+        there = block(rank, core, p)
+        return remote(there, there, mate_send.at[rank, p], mate_recv.at[rank, p], {"tensor": 1 - core})
+
+    def from_mate(rank, p):
+        there = block(rank, 1 - core, p)
+        return remote(there, there, mate_send.at[rank, p], mate_recv.at[rank, p], {"tensor": 1 - core})
+
+    own = pltpu.make_async_copy(x_ref, o_ref.at[pl.ds(first_of(place, core), rows)], local_sem)
+    own.start()
+    greet_chain(size, True)
+    own.wait()
+    for p in range(pieces):
+        pl.when(place < last)(lambda p=p: going_up(0, p).start())
+        pl.when(place > 0)(lambda p=p: going_down(0, p).start())
+    for p in range(pieces):
+        to_mate(place, p).start()
+
+    def forward(d):
+        for p in range(pieces):
+
+            @pl.when(place - d >= 0)
+            def _(p=p):
+                coming_up(d - 1, p).wait_recv()
+                pl.when(place < last)(lambda: going_up(d, p).start())
+                to_mate(place - d, p).start()
+
+            @pl.when(place + d <= last)
+            def _(p=p):
+                coming_down(d - 1, p).wait_recv()
+                pl.when(place > 0)(lambda: going_down(d, p).start())
+                to_mate(place + d, p).start()
+
+    for load in loads:
+        load.wait()
+    short = jnp.minimum(place, last - place)
+
+    def distance(s):
+        return jnp.where(s <= 2 * short, (s + 1) // 2, s - short)
+
+    def extra_load(rank, which, slot, e):
+        return pltpu.make_async_copy(
+            extra_from[e].at[pl.ds(first_of(rank, which), rows)], extra.at[slot, e], extra_sem.at[slot, e]
+        )
+
+    def store(rank, which, slot, m):
+        return pltpu.make_async_copy(
+            stage.at[slot, m], made_to[m].at[pl.ds(first_of(rank, which), rows)], stage_sem.at[slot, m]
+        )
+
+    def visit(s, carry):
+        d = distance(s)
+        below = jnp.where(s <= 2 * short, s % 2 == 1, place > last - place)
+        rank = jnp.where(below, place - d, place + d)
+        for slot, which in enumerate((core, 1 - core)):
+            for e in range(n_extra):
+                extra_load(rank, which, slot, e).start()
+        pl.when((s > 0) & (d != distance(s - 1)))(lambda: forward(d))
+        for slot, which in enumerate((core, 1 - core)):
+            if slot == 1:
+                for p in range(pieces):
+                    from_mate(rank, p).wait_recv()
+            for e in range(n_extra):
+                extra_load(rank, which, slot, e).wait()
+
+            @pl.when(s > 0)
+            def _():
+                for m in range(n_made):
+                    store(rank, which, slot, m).wait()
+
+            work(o_ref.at[pl.ds(first_of(rank, which), rows)], weights, extra.at[slot], stage.at[slot])
+            for m in range(n_made):
+                store(rank, which, slot, m).start()
+        return carry
+
+    lax.fori_loop(0, size, visit, 0)
+    for slot, which in enumerate((core, 1 - core)):
+        for m in range(n_made):
+            store(place, which, slot, m).wait()
+    for p in range(pieces):
+        for k in range(last):
+            pl.when((place < last) & (place - k >= 0))(lambda k=k, p=p: going_up(k, p).wait_send())
+            pl.when((place > 0) & (place + k <= last))(lambda k=k, p=p: going_down(k, p).wait_send())
+        for rank in range(size):
+            to_mate(rank, p).wait_send()
+
+
+def gather_apply(x, weights, extra, work, n_made, ident):
+    size = lax.axis_size("ctx")
+    rows, width = x.shape[0], weights[0].shape[1]
+    total = 2 * size * rows
+    pieces = pieces_of(*x.shape)
+    dma = pltpu.SemaphoreType.DMA
+    made = jax.ShapeDtypeStruct((total, width), jnp.bfloat16)
+    slots = max(1, len(extra))
+    return pl.pallas_call(
+        functools.partial(gather_apply_kernel, size, pieces, work, len(weights), len(extra), n_made),
+        in_specs=[IN_VMEM] + [ANY] * (len(weights) + len(extra)),
+        out_specs=[IN_VMEM] + [ANY] * n_made,
+        out_shape=[jax.ShapeDtypeStruct((total, x.shape[1]), x.dtype)] + [made] * n_made,
+        scratch_shapes=[pltpu.VMEM(w.shape, w.dtype) for w in weights]
+        + [
+            pltpu.VMEM((2, slots, rows, width) if extra else (2, 1, 16, 128), jnp.bfloat16),
+            pltpu.VMEM((2, n_made, rows, width), jnp.bfloat16),
+            dma,
+            dma((len(weights),)),
+            dma((2, slots)),
+            dma((2, n_made)),
+        ]
+        + [dma((size, pieces))] * 6,
+        compiler_params=pltpu.CompilerParams(collective_id=ident, has_side_effects=True, vmem_limit_bytes=60000000),
+        cost_estimate=pl.CostEstimate(flops=0, bytes_accessed=200000000, transcendentals=0),
+    )(x, *weights, *extra)
 
 
 def mask_into(bias_ref, first, seg_ref, place_ref):
@@ -577,10 +813,6 @@
     start = jnp.broadcast_to(seg_ref[...], (keys, rows))
     allowed = ((place >= start) & (place <= row_index)) | (key_index == row_index)
     bias_ref[...] = jnp.where(allowed, 0.0, VERY_LOW)
-
-
-def nn(first_op, second_op):
-    return jnp.dot(first_op, second_op, preferred_element_type=jnp.float32)
 
 
 def attend_kernel(scale, first_ref, seg_ref, place_ref, q_ref, k_ref, vt_ref, o_ref, lse_ref, bias_ref):
@@ -774,12 +1006,9 @@
     residual_mid = inputs + attention
     scale_mlp = lax.rsqrt(jnp.mean(residual_mid * residual_mid, axis=1, keepdims=True) + EPS)
     normed_mlp = residual_mid * scale_mlp
-    mlp_rows = gather((normed_mlp * gain_two).astype(jnp.bfloat16), ctx_size, True, 5)
-    gate_act = matmul(mlp_rows, full_gate)
-    up_act = matmul(mlp_rows, full_up)
-    sigmoid = jax.nn.sigmoid(gate_act)
-    silu_gate = gate_act * sigmoid
-    hidden = (silu_gate * up_act).astype(jnp.bfloat16)
+    mlp_rows, gate_act, up_act, hidden = gather_apply(
+        (normed_mlp * gain_two).astype(jnp.bfloat16), [full_gate, full_up], [], expand_block, 3, 5
+    )
     branch = scatter(matmul_nt(hidden, full_down).astype(jnp.bfloat16), ctx_size, True, 6)
     layer_result = residual_mid + branch
     valid_own = lax.dynamic_slice_in_dim(valid_mask, own_first, own_rows).astype(jnp.float32)
@@ -788,12 +1017,9 @@
     grad_result = cotangent.astype(jnp.float32) + 2.0 * valid_own[:, None] * difference / (
         valid_count * D
     )
-    grad_branch = gather(grad_result.astype(jnp.bfloat16), ctx_size, True, 5)
-    grad_hidden = matmul(grad_branch, full_down)
-    grad_gate_act = (grad_hidden * up_act * sigmoid * (1.0 + gate_act * (1.0 - sigmoid))).astype(
-        jnp.bfloat16
-    )
-    grad_up_act = (grad_hidden * silu_gate).astype(jnp.bfloat16)
+    grad_branch, grad_gate_act, grad_up_act = gather_apply(
+        grad_result.astype(jnp.bfloat16), [full_down], [gate_act, up_act], shrink_block, 2, 9
+    )
     summed = []
     for left, right in ((grad_branch, hidden), (mlp_rows, grad_gate_act), (mlp_rows, grad_up_act)):
         grad = matmul_tn(left, right).astype(jnp.bfloat16)
@@ -834,8 +1060,8 @@
         axis=1,
     )
     grad_pre, grad_out = lax.optimization_barrier((grad_pre, grad_out))
-    shard_out = lax.psum_scatter(grad_out, "ctx", scatter_dimension=0, tiled=True).astype(jnp.float32).T
-    shard_qkv = back(matmul_tn(normed_rows, grad_pre).astype(jnp.bfloat16), 8)
+    shard_out = lax.psum_scatter(grad_out, "ctx", scatter_dimension=0, tiled=True)
+    shard_out = shard_out.astype(jnp.float32).T
     grad_normed = scatter(matmul_nt(grad_pre, full_qkv), 1, True, 4)
     grad_gain_attn = jnp.sum(grad_normed * normed_attn, axis=0)
     grad_input = grad_mid + norm_back(grad_normed, normed_attn, scale_attn, gain_one)
@@ -855,7 +1081,11 @@
         spread(bias_sum[turned:], value_bias.shape[0]),
         loss_part,
     ]
-    sums = sum_everywhere(jnp.concatenate(parts).reshape(-1, 128)).reshape(-1)
+    flat = jnp.concatenate(parts)
+    small = jnp.pad(flat, (0, -flat.shape[0] % 1024)).reshape(-1, 128)
+    grad_qkv = matmul_tn(normed_rows, grad_pre).astype(jnp.bfloat16)
+    shard_qkv, sums = back(grad_qkv, small, 8)
+    sums = sums.reshape(-1)
     pieces, offset = [], 0
     for part in parts:
         pieces.append(sums[offset : offset + part.shape[0]])

time: 823 us -> 763 us (0.927)
  the two profiles are of different devices: /device:TPU:25 before, /device:TPU:0 now
where the time goes in v4:
time: 763 us; the launch traced here: 755 us
  Pallas kernels  513 us (67%)
  matrix products  107 us (14%)
  waiting for transfers between devices  37 us (5%)
  local copies, waits for them, and re-layouts  34.8 us (5%)
  other arithmetic  31.7 us (4%)
  between operations  19.6 us (3%)
  starting transfers between devices  11.5 us (2%)
    pallas_call x5, Pallas kernels, scatter(): pl.pallas_call(functools.partial(scatter_kernel, size, paired, pieces), i...  155 us
    pallas_call x2, Pallas kernels, gather_apply(): pl.pallas_call(functools.partial(gather_apply_kernel, size, pieces, work,...  135 us
    pallas_call x1, Pallas kernels, front(): pl.pallas_call(functools.partial(front_kernel, size, groups), in_specs=[I...  79.8 us
    pallas_call x1, Pallas kernels, back(): pl.pallas_call(functools.partial(back_kernel, size, groups), in_specs=[AN...  63.7 us
    dot_general x5, matrix products, matmul_nt(): lax.dot_general(first_op, second_op, (((1,), (1,)), ((), ())), preferred_...  51.6 us
    dot_general x5, matrix products, matmul_tn(): lax.dot_general(first_op, second_op, (((0,), (0,)), ((), ())), preferred_...  47.3 us
    pallas_call x3, Pallas kernels, gather(): pl.pallas_call(functools.partial(gather_kernel, size, paired, pieces), in...  33.9 us
    pallas_call x1, Pallas kernels, per_device(): backward(first, doc_start, key_place, query, grad_heads[:, span], log_tot...  26.4 us
  transfers between devices with their start and end apart: 14, of which 4 were waited for; matrix products, arithmetic and copies ran while one was open for 13% of the time, Pallas kernels for 41%

profile of v4, /device:TPU:0, one launch (start us, length us, event | category | flops | bytes accessed | tf_op | source)
XLA Modules:
  0.0 754.8 jit_solution(1312667325990775388)
XLA Ops:
  7.2 2.2 pad.17.g_ref
  12.2 79.8 %front.1 = (bf16[1536,1024]{1,0:T(8,128)(2,1)}, bf16[1536,768]{1,0:T(8,128)(2,1)}, bf16[384,1152]{1,0:T(8,128)(2,1)}, bf16[384,1152]{1,0:T(8,128)(2,1)}, bf16[384,1152]{1,0:T(8,128)(2,1)}) custom-call(bf16[96,1024]{1,0:T(8,128)(2,1)} %pad_maximum_fusion.6.a_ref, bf16[96,768]{1,0:T(8,128)(2,1)} %bitcast.84, bf16[96,4608]{1,0:T(8,128)(2,1)} %pad.17.g_ref, ...), custom_call_target="tpu_custom_call" | custom-call | bytes 200000000 | tf_op jit(solution)/shard_map/front/pallas_call | solution.py:476
  94.9 2.9 collective-permute-start
  97.8 1.5 collective-permute-start.1
  99.2 1.5 collective-permute-start.2
  101.1 1.1 fusion.4.x_ref
  102.2 4.2 gather.3
  106.5 4.2 convolution_add_fusion
  110.9 1.8 copy.37
  112.7 1.4 dynamic-slice_convert_fusion
  114.6 1.8 subtract_convert_fusion.1
  117.4 25.6 %gather.4 = bf16[2048,256]{1,0:T(8,128)(2,1)} custom-call(bf16[512,256]{1,0:T(8,128)(2,1)} %pad_maximum_fusion.5.x_ref), custom_call_target="tpu_custom_call" | custom-call | bytes 15728640 | tf_op jit(solution)/shard_map/gather/pallas_call | solution.py:211
  143.0 2.4 fusion.15
  146.3 1.2 copy.48.q_ref
  147.5 1.3 copy.41.place_ref
  148.9 19.2 %attend.1 = (bf16[512,768]{1,0:T(8,128)(2,1)}, f32[6,1,512]{2,1,0:T(1,128)}) custom-call(s32[1]{0:T(128)} %bitcast.first_ref, s32[1,512]{1,0:T(1,128)} %bitcast.86, s32[2048,1]{1,0:T(8,128)} %copy.41.place_ref, bf16[512,768]{1,0:T(8,128)(2,1)} %copy.48.q_ref, bf16[2048,128]{1,0:T(8,128)(2,1)} %get-tuple-element.117.k_ref, bf16[128,2048]{1,0:T(8,128)(2,1)} %copy.43.vt_ref), custom_call_target="tpu_custom_call" | custom-call | flops 3221225472 | bytes 1572864 | tf_op jit(solution)/shard_map/attend/pallas_call | solution.py:1003
  168.1 4.2 fusion.17.x_ref
  172.2 5.1 scatter.12
  177.3 1.7 multiply_reduce_fusion.2
  184.4 7.3 all-gather.6.cloned.1.call-done.refs_2_
  191.7 66.0 %shard_map.289 = (bf16[2048,1536]{1,0:T(8,128)(2,1)}, bf16[2048,1152]{1,0:T(8,128)(2,1)}, bf16[2048,1152]{1,0:T(8,128)(2,1)}, bf16[2048,1152]{1,0:T(8,128)(2,1)}) custom-call(bf16[256,1536]{1,0:T(8,128)(2,1)} %multiply_convert_fusion.refs_0_, bf16[1536,1152]{1,0:T(8,128)(2,1)} %all-gather.4.cloned.1.call-done.refs_1_, ...), custom_call_target="tpu_custom_call" | custom-call | bytes 200000000 | tf_op jit(solution)/shard_map/pallas_call | solution.py:788
  257.7 13.2 %convolution_convert_fusion.3.x_ref = bf16[2048,1536]{1,0:T(8,128)(2,1)} fusion(bf16[2048,1152]{1,0:T(8,128)(2,1)} %get-tuple-element.65, bf16[1536,1152]{1,0:T(8,128)(2,1)} %all-gather.8.cloned.1.call-done.refs_1_), kind=kOutput, calls=%fused_computation.4 | convolution fusion | flops 7250903040 | bytes 14548992 | tf_op jit(solution)/shard_map/dot_general | solution.py:54
  270.9 57.6 %scatter.13 = f32[256,1536]{1,0:T(8,128)} custom-call(bf16[2048,1536]{1,0:T(8,128)(2,1)} %convolution_convert_fusion.3.x_ref), custom_call_target="tpu_custom_call" | custom-call | bytes 94371840 | tf_op jit(solution)/shard_map/scatter/pallas_call | solution.py:343
  328.6 2.9 fusion.13.refs_0_
  331.5 69.3 %shard_map.290 = (bf16[2048,1536]{1,0:T(8,128)(2,1)}, bf16[2048,1152]{1,0:T(8,128)(2,1)}, bf16[2048,1152]{1,0:T(8,128)(2,1)}) custom-call(bf16[256,1536]{1,0:T(8,128)(2,1)} %fusion.13.refs_0_, bf16[1536,1152]{1,0:T(8,128)(2,1)} %all-gather.8.cloned.1.call-done.refs_1_, bf16[2048,1152]{1,0:T(8,128)(2,1)} %get-tuple-element.67.refs_2_, ...), custom_call_target="tpu_custom_call" | custom-call | bytes 200000000 | tf_op jit(solution)/shard_map/pallas_call | solution.py:788
  400.8 13.1 %convolution_convert_fusion = bf16[1536,1152]{1,0:T(8,128)(2,1)} fusion(bf16[2048,1536]{1,0:T(8,128)(2,1)} %get-tuple-element.74, bf16[2048,1152]{1,0:T(8,128)(2,1)} %get-tuple-element.78), kind=kOutput, calls=%fused_computation.1 | convolution fusion | flops 7249526784 | bytes 14548992 | tf_op jit(solution)/shard_map/dot_general | solution.py:48
  413.9 13.1 %convolution_convert_fusion.1 = bf16[1536,1152]{1,0:T(8,128)(2,1)} fusion(bf16[2048,1536]{1,0:T(8,128)(2,1)} %get-tuple-element.74, bf16[2048,1152]{1,0:T(8,128)(2,1)} %get-tuple-element.77), kind=kOutput, calls=%fused_computation.2 | convolution fusion | flops 7249526784 | bytes 14548992 | tf_op jit(solution)/shard_map/dot_general | solution.py:48
  427.0 13.3 %convolution_convert_fusion.2 = bf16[1536,1152]{1,0:T(8,128)(2,1)} fusion(bf16[2048,1536]{1,0:T(8,128)(2,1)} %get-tuple-element.71, bf16[2048,1152]{1,0:T(8,128)(2,1)} %get-tuple-element.65), kind=kOutput, calls=%fused_computation.3 | convolution fusion | flops 7249526784 | bytes 14548992 | tf_op jit(solution)/shard_map/dot_general | solution.py:48
  441.6 14.4 %fusion.18 = f32[2048,1536]{1,0:T(8,128)} fusion(bf16[2048,1152]{1,0:T(8,128)(2,1)} %get-tuple-element.77, bf16[1536,1152]{1,0:T(8,128)(2,1)} %all-gather.4.cloned.1.call-done.refs_1_), kind=kOutput, calls=%fused_computation.97 | convolution fusion | flops 7247757312 | bytes 20840448 | tf_op jit(solution)/shard_map/dot_general | solution.py:54
  456.0 14.3 %add_convert_fusion.x_ref = bf16[2048,1536]{1,0:T(8,128)(2,1)} fusion(f32[2048,1536]{1,0:T(8,128)} %fusion.18, bf16[2048,1152]{1,0:T(8,128)(2,1)} %get-tuple-element.78, bf16[1536,1152]{1,0:T(8,128)(2,1)S(1)} %copy-done.6), kind=kOutput, calls=%fused_computation | convolution fusion | flops 7254048768 | bytes 27131904 | tf_op jit(solution)/shard_map/dot_general | solution.py:54
  470.3 57.7 %scatter.14 = f32[256,1536]{1,0:T(8,128)} custom-call(bf16[2048,1536]{1,0:T(8,128)(2,1)} %add_convert_fusion.x_ref), custom_call_target="tpu_custom_call" | custom-call | bytes 94371840 | tf_op jit(solution)/shard_map/scatter/pallas_call | solution.py:343
  528.0 3.2 multiply_reduce_fusion
  531.2 2.6 fusion.14
  533.8 4.2 gather.5
  538.0 4.3 convolution_convert_fusion.5
  544.3 3.9 convolution_convert_fusion.6.do_ref
  548.2 26.4 %attend_back.1 = (f32[512,768]{1,0:T(8,128)}, bf16[2048,256]{1,0:T(8,128)(2,1)}) custom-call(s32[1]{0:T(128)} %bitcast.first_ref, s32[1,512]{1,0:T(1,128)} %bitcast.87, s32[2048,1]{1,0:T(8,128)} %copy.41.place_ref, bf16[512,768]{1,0:T(8,128)(2,1)} %copy.48.q_ref, bf16[512,768]{1,0:T(8,128)(2,1)} %convolution_convert_fusion.6.do_ref, ...), custom_call_target="tpu_custom_call" | custom-call | flops 8053063680 | bytes 3145728 | tf_op jit(solution)/shard_map/attend_back/pallas_call | solution.py:1041
  574.7 12.1 %reduce-scatter.6.cloned.1.call-done = bf16[384,1152]{1,0:T(8,128)(2,1)} async-done(((bf16[1536,1152]{1,0:T(8,128)(2,1)}), bf16[384,1152]{1,0:T(8,128)(2,1)}) %reduce-scatter.6.cloned.1.call-update) | async-done | bytes 884752 | tf_op jit(solution)/shard_map/reduce_scatter | solution.py:1027
  586.8 29.5 %scatter.15 = f32[512,256]{1,0:T(8,128)} custom-call(bf16[2048,256]{1,0:T(8,128)(2,1)} %get-tuple-element.85.x_ref), custom_call_target="tpu_custom_call" | custom-call | bytes 15728640 | tf_op jit(solution)/shard_map/scatter/pallas_call | solution.py:343
  618.5 1.7 copy.46
  620.3 1.8 subtract_convert_fusion
  622.2 5.0 reduce-scatter.12.cloned.1.call-done
  627.3 5.6 fusion.19.x_ref
  633.1 3.5 convolution_convert_fusion.4.x_ref
  636.9 1.4 dynamic-slice_bitcast_fusion
  638.9 1.5 collective-permute-start.3
  640.4 2.4 collective-permute-start.4
  642.8 1.4 collective-permute-start.5
  644.3 5.1 scatter.16
  649.3 1.9 fusion.6
  652.9 63.7 %back.1 = (f32[96,1024]{1,0:T(8,128)}, f32[48,128]{1,0:T(8,128)}) custom-call(bf16[1536,1024]{1,0:T(8,128)(2,1)} %convolution_convert_fusion.4.x_ref, f32[48,128]{1,0:T(8,128)} %pad_bitcast_fusion.s_ref), custom_call_target="tpu_custom_call" | custom-call | bytes 157286400 | tf_op jit(solution)/shard_map/back/pallas_call | solution.py:584
  716.6 1.7 slice.141
  718.3 1.2 slice.138
  720.1 3.0 fusion.9
  723.3 1.2 bitcast_dynamic-update-slice_fusion
  724.5 1.5 fusion.16
  727.2 1.2 constant_dynamic-update-slice_fusion.7
  728.4 1.2 constant_dynamic-update-slice_fusion.6
  729.5 1.2 constant_dynamic-update-slice_fusion.8
  731.0 1.3 convert_bitcast_fusion
  732.3 1.3 slice_convert_fusion
  733.6 1.3 slice_convert_fusion.1
  734.9 9.9 %reduce-scatter.14.cloned.1.call-done = bf16[96,768]{1,0:T(8,128)(2,1)} async-done(((bf16[384,768]{1,0:T(8,128)(2,1)}), bf16[96,768]{1,0:T(8,128)(2,1)}) %reduce-scatter.14.cloned.1.call-update) | async-done | bytes 147472 | tf_op jit(solution)/shard_map/reduce_scatter | solution.py:1063
  744.8 1.6 convert_bitcast_fusion.1
  (145 shorter events, 21.5 us)
Async XLA Ops:
  7.2 2.3 copy-start.16
  7.2 3.3 copy-start.17
  7.2 177.2 %all-gather.4.cloned.1.call-start = ((), (), s32[]{:S(2)}) async-start(), calls=%async_computation.5 | async-start | bytes 4423680 | tf_op jit(solution)/shard_map/all_gather | solution.py:959
  9.5 2.0 copy-start.18
  9.5 2.0 copy-start.21
  9.5 2.0 copy-start.22
  92.0 1.6 copy-start.19
  92.0 8.7 %copy-start.27 = (bf16[256]{0:T(256)(128)(2,1)S(1)}, bf16[256]{0:T(256)(128)(2,1)}, u32[]{:S(2)}) copy-start(bf16[256]{0:T(256)(128)(2,1)} %param.30) | copy-start | bytes 1540
  92.0 8.8 %copy-start.28 = (bf16[256]{0:T(256)(128)(2,1)S(1)}, bf16[256]{0:T(256)(128)(2,1)}, u32[]{:S(2)}) copy-start(bf16[256]{0:T(256)(128)(2,1)} %param.32) | copy-start | bytes 1540
  92.0 8.8 %copy-start.23 = (bf16[1536]{0:T(1024)(128)(2,1)S(1)}, bf16[1536]{0:T(1024)(128)(2,1)}, u32[]{:S(2)}) copy-start(bf16[1536]{0:T(1024)(128)(2,1)} %param.26) | copy-start | bytes 9220
  92.0 8.8 %copy-start.1 = (bf16[256,1536]{1,0:T(8,128)(2,1)S(1)}, bf16[256,1536]{1,0:T(8,128)(2,1)}, u32[]{:S(2)}) copy-start(bf16[256,1536]{1,0:T(8,128)(2,1)} %param.20) | copy-start | bytes 2359300
  92.1 99.7 %all-gather.6.cloned.1.call-start = ((), (), s32[]{:S(2)}) async-start(), calls=%async_computation.6 | async-start | bytes 4423680 | tf_op jit(solution)/shard_map/all_gather | solution.py:959
  92.8 164.9 %all-gather.8.cloned.1.call-start = ((), (), s32[]{:S(2)}) async-start(), calls=%async_computation.7 | async-start | bytes 4423680 | tf_op jit(solution)/shard_map/all_gather | solution.py:959
  93.6 481.1 %reduce-scatter.10.cloned.1.call-start = ((), (), s32[]{:S(2)}) async-start(), calls=%async_computation.10 | async-start | bytes 4423680 | tf_op jit(solution)/shard_map/reduce_scatter | solution.py:1027
  94.9 85.3 %collective-permute-start = (f32[8,128]{1,0:T(8,128)S(1)}, f32[8,128]{1,0:T(8,128)S(1)}, u32[]{:S(2)}, u32[]{:S(2)}) collective-permute-start(f32[8,128]{1,0:T(8,128)S(1)} %broadcast_in_dim.17), channel_id=1, source_target_pairs={{0,8},{8,16},{16,24},{24,0},{1,9},{9,17},{17,25},{25,1},{2,10},{10... | collective-permute-start | bytes 12296 | tf_op jit(solution)/shard_map/ppermute | solution.py:966
  97.8 84.3 %collective-permute-start.1 = (f32[8,128]{1,0:T(8,128)S(1)}, f32[8,128]{1,0:T(8,128)S(1)}, u32[]{:S(2)}, u32[]{:S(2)}) collective-permute-start(f32[8,128]{1,0:T(8,128)S(1)} %broadcast_in_dim.17), channel_id=1, source_target_pairs={{0,16},{8,24},{16,0},{24,8},{1,17},{9,25},{17,1},{25,9},{2,18},{10... | collective-permute-start | bytes 12296 | tf_op jit(solution)/shard_map/ppermute | solution.py:966
  99.2 84.0 %collective-permute-start.2 = (f32[8,128]{1,0:T(8,128)S(1)}, f32[8,128]{1,0:T(8,128)S(1)}, u32[]{:S(2)}, u32[]{:S(2)}) collective-permute-start(f32[8,128]{1,0:T(8,128)S(1)} %broadcast_in_dim.17), channel_id=1, source_target_pairs={{0,24},{8,0},{16,8},{24,16},{1,25},{9,1},{17,9},{25,17},{2,26},{10... | collective-permute-start | bytes 12296 | tf_op jit(solution)/shard_map/ppermute | solution.py:966
  101.1 5.3 copy-start.25
  148.9 19.2 %copy-start.26 = (bf16[1536,768]{1,0:T(8,128)(2,1)S(1)}, bf16[1536,768]{1,0:T(8,128)(2,1)}, u32[]{:S(2)}) copy-start(bf16[1536,768]{1,0:T(8,128)(2,1)} %get-tuple-element.62) | copy-start | bytes 7077892
  172.2 5.1 copy-start.24
  270.9 57.7 %copy-start.5 = (bf16[256,1536]{1,0:T(8,128)(2,1)S(1)}, bf16[256,1536]{1,0:T(8,128)(2,1)}, u32[]{:S(2)}) copy-start(bf16[256,1536]{1,0:T(8,128)(2,1)} %param.21) | copy-start | bytes 2359300
  270.9 57.7 %copy-start.7 = (bf16[256,1536]{1,0:T(8,128)(2,1)S(1)}, bf16[256,1536]{1,0:T(8,128)(2,1)}, u32[]{:S(2)}) copy-start(bf16[256,1536]{1,0:T(8,128)(2,1)} %param.22) | copy-start | bytes 2359300
  440.4 134.4 %reduce-scatter.8.cloned.1.call-start = ((), (), s32[]{:S(2)}) async-start(), calls=%async_computation.9 | async-start | bytes 4423680 | tf_op jit(solution)/shard_map/reduce_scatter | solution.py:1027
  441.0 145.9 %reduce-scatter.6.cloned.1.call-start = ((), (), s32[]{:S(2)}) async-start(), calls=%async_computation.8 | async-start | bytes 4423680 | tf_op jit(solution)/shard_map/reduce_scatter | solution.py:1027
  441.5 185.7 %reduce-scatter.12.cloned.1.call-start = ((), (), s32[]{:S(2)}) async-start(), calls=%async_computation.11 | async-start | bytes 2949120 | tf_op jit(solution)/shard_map/reduce_scatter | solution.py:1036
  441.6 14.4 %copy-start.6 = (bf16[1536,1152]{1,0:T(8,128)(2,1)S(1)}, bf16[1536,1152]{1,0:T(8,128)(2,1)}, u32[]{:S(2)}) copy-start(bf16[1536,1152]{1,0:T(8,128)(2,1)} %all-gather.6.cloned.1.call-done.refs_2_) | copy-start | bytes 10616836
  470.3 57.7 %copy-start = (f32[256,1536]{1,0:T(8,128)S(1)}, f32[256,1536]{1,0:T(8,128)}, u32[]{:S(2)}) copy-start(f32[256,1536]{1,0:T(8,128)} %scatter.13) | copy-start | bytes 4718596
  528.0 3.2 copy-start.3
  528.0 3.2 copy-start.8
  533.8 4.2 copy-start.29
  542.3 1.0 copy-start.9
  542.3 2.0 copy-start.12
  542.3 202.5 %reduce-scatter.14.cloned.1.call-start = ((), (), s32[]{:S(2)}) async-start(), calls=%async_computation.12 | async-start | bytes 737280 | tf_op jit(solution)/shard_map/reduce_scatter | solution.py:1063
  586.8 31.5 %copy-start.10 = (f32[512,768]{1,0:T(8,128)S(1)}, f32[512,768]{1,0:T(8,128)}, u32[]{:S(2)}) copy-start(f32[512,768]{1,0:T(8,128)} %get-tuple-element.80) | copy-start | bytes 4718596
  627.3 5.8 copy-start.11
  633.0 3.5 copy-start.13
  633.1 3.5 copy-start.14
  633.1 3.5 copy-start.15
  636.9 2.0 copy-start.4
  638.9 88.3 %collective-permute-start.3 = (bf16[3,96,1152]{2,1,0:T(8,128)(2,1)}, bf16[3,96,1152]{2,1,0:T(8,128)(2,1)}, u32[]{:S(2)}, u32[]{:S(2)}) collective-permute-start(bf16[3,96,1152]{2,1,0:T(8,128)(2,1)} %get-tuple-element.110), channel_id=1, source_target_pairs={{0,2},{2,4},{4,6},{6,0},{1,3},{3,5},{5,7},{7,1},{8,10},{10,12},{12... | collective-permute-start | bytes 1990664 | tf_op jit(solution)/shard_map/ppermute | solution.py:70
  640.4 87.9 %collective-permute-start.4 = (bf16[3,96,1152]{2,1,0:T(8,128)(2,1)}, bf16[3,96,1152]{2,1,0:T(8,128)(2,1)}, u32[]{:S(2)}, u32[]{:S(2)}) collective-permute-start(bf16[3,96,1152]{2,1,0:T(8,128)(2,1)} %get-tuple-element.109), channel_id=1, source_target_pairs={{0,4},{2,6},{4,0},{6,2},{1,5},{3,7},{5,1},{7,3},{8,12},{10,14},{12... | collective-permute-start | bytes 1990664 | tf_op jit(solution)/shard_map/ppermute | solution.py:70
  642.8 86.7 %collective-permute-start.5 = (bf16[3,96,1152]{2,1,0:T(8,128)(2,1)S(1)}, bf16[3,96,1152]{2,1,0:T(8,128)(2,1)}, u32[]{:S(2)}, u32[]{:S(2)}) collective-permute-start(bf16[3,96,1152]{2,1,0:T(8,128)(2,1)S(1)} %get-tuple-element.108), channel_id=1, source_target_pairs={{0,6},{2,0},{4,2},{6,4},{1,7},{3,1},{5,3},{7,5},{8,14},{10,8},{12,... | collective-permute-start | bytes 1990664 | tf_op jit(solution)/shard_map/ppermute | solution.py:70
  652.9 67.2 %copy-start.2 = (f32[256,1536]{1,0:T(8,128)S(1)}, f32[256,1536]{1,0:T(8,128)}, u32[]{:S(2)}) copy-start(f32[256,1536]{1,0:T(8,128)} %scatter.16) | copy-start | bytes 4718596
  723.1 2.9 copy-start.20
Sparse Core Ops, SparseCore 0:
  92.2 50.4 all-gather.3
  144.6 47.1 all-gather.5
  193.6 47.1 all-gather.7
  440.5 46.0 reduce-scatter.9
  489.5 47.1 reduce-scatter.7
  539.6 47.1 reduce-scatter.5
  589.9 37.3 reduce-scatter.11
  720.3 24.4 reduce-scatter.13

commit v5 on v4

--- a/solution.py
+++ b/solution.py
@@ -76,10 +76,7 @@
     size = lax.axis_size("ctx")
     rows, width = summed[0].shape[0] // size, summed[0].shape[1]
     blocks = jnp.stack([s.reshape(size, rows, width) for s in summed], axis=1)
-    shards = jnp.zeros((len(summed), rows, size * width), jnp.bfloat16)
-    for rank, block in exchange(blocks, "ctx"):
-        shards = lax.dynamic_update_slice_in_dim(shards, block, rank * width, 2)
-    return [s[:, :columns].astype(jnp.float32) for s in shards]
+    return assemble(exchange(blocks, "ctx"), columns)
 
 
 def nn(first_op, second_op):
@@ -614,7 +611,7 @@
 
 
 def column_step(width):
-    return max(t for t in (384, 256, 128) if width % t == 0)
+    return max(t for t in (768, 384, 256, 128) if width % t == 0)
 
 
 def expand_block(x_ref, weights, extra, stage):
@@ -803,6 +800,197 @@
         compiler_params=pltpu.CompilerParams(collective_id=ident, has_side_effects=True, vmem_limit_bytes=60000000),
         cost_estimate=pl.CostEstimate(flops=0, bytes_accessed=200000000, transcendentals=0),
     )(x, *weights, *extra)
+
+
+def sum_apply_kernel(size, pieces, count, *refs):
+    acts_from, refs = refs[:count], refs[count:]
+    weights_from, refs = refs[:count], refs[count:]
+    o_ref, acts, weights, mine, sent, mate, came, load_sem = refs[:8]
+    mate_send, mate_recv, up_send, up_recv, down_send, down_recv = refs[8:]
+    place, core = lax.axis_index("ctx"), lax.axis_index("tensor")
+    rows, depth = o_ref.shape
+    part = rows // pieces
+    last = size - 1
+
+    loads = []
+    for a in range(count):
+        loads.append(pltpu.make_async_copy(weights_from[a], weights.at[a], load_sem.at[a]))
+        loads.append(pltpu.make_async_copy(acts_from[a], acts.at[a], load_sem.at[count + a]))
+    for load in loads:
+        load.start()
+    greet_chain(size, True)
+    for load in loads:
+        load.wait()
+
+    def at(ref, d, p):
+        return ref.at[d, pl.ds(p * part, part)]
+
+    def to_mate(i, d, p):
+        slot = lax.rem(i, 2)
+        return remote(at(sent, slot, p), at(mate, d, p), mate_send.at[slot, p], mate_recv.at[d, p], {"tensor": 1 - core})
+
+    def going_up(d, p):
+        return remote(at(mine, d, p), at(came, d, p), up_send.at[d, p], up_recv.at[d, p], {"ctx": place + 1})
+
+    def going_down(d, p):
+        there = jnp.where(d == place - 1, size, d)
+        return remote(at(mine, d, p), at(came, there, p), down_send.at[d, p], down_recv.at[d, p], {"ctx": place - 1})
+
+    def coming_up(d, p):
+        there = at(came, d, p)
+        return remote(there, there, up_send.at[d, p], up_recv.at[d, p], {"ctx": place - 1})
+
+    def coming_down(d, p):
+        there = at(came, jnp.where(d == place, size, d), p)
+        return remote(there, there, down_send.at[d, p], down_recv.at[d, p], {"ctx": place + 1})
+
+    def compute(d, which, target):
+        step = column_step(depth)
+        span = pl.ds(pl.multiple_of((d * 2 + which) * rows, rows), rows)
+
+        def some(j, carry):
+            columns = pl.ds(pl.multiple_of(j * step, step), step)
+            total = matmul_nt(acts[0, span, :], weights[0, columns, :])
+            for a in range(1, count):
+                total += matmul_nt(acts[a, span, :], weights[a, columns, :])
+            target[:, columns] = total.astype(target.dtype)
+            return carry
+
+        lax.fori_loop(0, depth // step, some, 0)
+
+    def with_mate(d, p):
+        to_mate(0, d, p).wait_recv()
+        return [at(mine, d, p), at(mate, d, p)]
+
+    short = jnp.minimum(place, last - place)
+
+    def first_part(i, carry):
+        s = last - i
+        near = s <= 2 * short
+        d = jnp.where(near, (s + 1) // 2, s - short)
+        d = jnp.where(jnp.where(near, s % 2 == 1, place > last - place), place - d, place + d)
+        for p in range(pieces):
+            pl.when(i >= 2)(lambda p=p: to_mate(i, d, p).wait_send())
+        compute(d, 1 - core, sent.at[lax.rem(i, 2)])
+        for p in range(pieces):
+            to_mate(i, d, p).start()
+        compute(d, core, mine.at[d])
+
+        @pl.when((place == 0) & (d > 0))
+        def _():
+            for p in range(pieces):
+                add_blocks(at(mine, d, p), with_mate(d, p))
+                going_up(d, p).start()
+
+        @pl.when((place == last) & (d < last))
+        def _():
+            for p in range(pieces):
+                add_blocks(at(mine, d, p), with_mate(d, p))
+                going_down(d, p).start()
+
+        return carry
+
+    lax.fori_loop(0, size, first_part, 0)
+
+    def second_part(s, carry):
+        k, p = s // pieces, s % pieces
+
+        @pl.when((place > 0) & (place < last - k))
+        def _():
+            d = last - k
+            parts = with_mate(d, p)
+            coming_up(d, p).wait_recv()
+            add_blocks(at(mine, d, p), parts + [at(came, d, p)])
+            going_up(d, p).start()
+
+        @pl.when((place < last) & (place > k))
+        def _():
+            parts = with_mate(k, p)
+            coming_down(k, p).wait_recv()
+            add_blocks(at(mine, k, p), parts + [at(came, k, p)])
+            going_down(k, p).start()
+
+        return carry
+
+    lax.fori_loop(0, last * pieces, second_part, 0)
+
+    def final(p, carry):
+        target = o_ref.at[pl.ds(pl.multiple_of(p * part, part), part)]
+        parts = with_mate(place, p)
+        pl.when(place > 0)(lambda: coming_up(place, p).wait_recv())
+        pl.when(place < last)(lambda: coming_down(place, p).wait_recv())
+        up, down = at(came, place, p), at(came, size, p)
+        pl.when(place == 0)(lambda: add_blocks(target, parts + [down]))
+        pl.when(place == last)(lambda: add_blocks(target, parts + [up]))
+        pl.when((place > 0) & (place < last))(lambda: add_blocks(target, parts + [up, down]))
+        return carry
+
+    lax.fori_loop(0, pieces, final, 0)
+    for p in range(pieces):
+        for i in range(size - 2, size):
+            to_mate(i, 0, p).wait_send()
+        for d in range(size):
+            pl.when(place < d)(lambda d=d, p=p: going_up(d, p).wait_send())
+            pl.when(place > d)(lambda d=d, p=p: going_down(d, p).wait_send())
+
+
+def sum_apply(acts, weights, ident):
+    size, count = lax.axis_size("ctx"), len(acts)
+    total, width = acts[0].shape
+    depth = weights[0].shape[0]
+    block = total // (2 * size)
+    pieces = pieces_of(block, depth)
+    dma = pltpu.SemaphoreType.DMA
+
+    def slots(n):
+        return pltpu.VMEM((n, block, depth), jnp.bfloat16)
+
+    scratch = [
+        pltpu.VMEM((count, total, width), jnp.bfloat16),
+        pltpu.VMEM((count, depth, width), jnp.bfloat16),
+        slots(size),
+        slots(2),
+        slots(size),
+        slots(size + 1),
+        dma((2 * count,)),
+        dma((2, pieces)),
+    ] + [dma((size, pieces))] * 5
+    return pl.pallas_call(
+        functools.partial(sum_apply_kernel, size, pieces, count),
+        in_specs=[ANY] * (2 * count),
+        out_specs=IN_VMEM,
+        out_shape=jax.ShapeDtypeStruct((block, depth), jnp.float32),
+        scratch_shapes=scratch,
+        compiler_params=pltpu.CompilerParams(collective_id=ident, has_side_effects=True, vmem_limit_bytes=60000000),
+        cost_estimate=pl.CostEstimate(flops=0, bytes_accessed=200000000, transcendentals=0),
+    )(*acts, *weights)
+
+
+def assemble_kernel(size, ranks_ref, *refs):
+    parts, (down_ref, gate_ref, up_ref, whole) = refs[:size], refs[size:]
+    width = parts[0].shape[2]
+    for which, target in enumerate((down_ref, gate_ref, up_ref)):
+        for part, k in zip(parts, range(size)):
+            whole[:, pl.ds(pl.multiple_of(ranks_ref[k] * width, 128), width)] = part[which].astype(jnp.float32)
+        kept = whole[:, : gate_ref.shape[1]]
+        target[...] = kept.T if which == 0 else kept
+
+
+def assemble(received, columns):
+    ranks = jnp.stack([rank for rank, _ in received]).astype(jnp.int32)
+    blocks = [block for _, block in received]
+    _, rows, width = blocks[0].shape
+    f32 = jnp.float32
+    return pl.pallas_call(
+        functools.partial(assemble_kernel, len(blocks)),
+        in_specs=[pl.BlockSpec(memory_space=pltpu.SMEM)] + [IN_VMEM] * len(blocks),
+        out_specs=[IN_VMEM] * 3,
+        out_shape=[jax.ShapeDtypeStruct((columns, rows), f32)] + [jax.ShapeDtypeStruct((rows, columns), f32)] * 2,
+        scratch_shapes=[pltpu.VMEM((rows, len(blocks) * width), f32)],
+        compiler_params=pltpu.CompilerParams(vmem_limit_bytes=60000000),
+        cost_estimate=pl.CostEstimate(flops=0, bytes_accessed=20 * rows * columns, transcendentals=0),
+        name="assemble",
+    )(ranks, *blocks)
 
 
 def mask_into(bias_ref, first, seg_ref, place_ref):
@@ -1009,7 +1197,7 @@
     mlp_rows, gate_act, up_act, hidden = gather_apply(
         (normed_mlp * gain_two).astype(jnp.bfloat16), [full_gate, full_up], [], expand_block, 3, 5
     )
-    branch = scatter(matmul_nt(hidden, full_down).astype(jnp.bfloat16), ctx_size, True, 6)
+    branch = sum_apply([hidden], [full_down], 6)
     layer_result = residual_mid + branch
     valid_own = lax.dynamic_slice_in_dim(valid_mask, own_first, own_rows).astype(jnp.float32)
     difference = layer_result - teacher.astype(jnp.float32)
@@ -1025,8 +1213,7 @@
         grad = matmul_tn(left, right).astype(jnp.bfloat16)
         grad_gate_act, grad_up_act, grad = lax.optimization_barrier((grad_gate_act, grad_up_act, grad))
         summed.append(lax.psum_scatter(grad, "dp", scatter_dimension=0, tiled=True))
-    grad_mlp_rows = (matmul_nt(grad_gate_act, full_gate) + matmul_nt(grad_up_act, full_up)).astype(jnp.bfloat16)
-    grad_mlp_rows = scatter(grad_mlp_rows, ctx_size, True, 6)
+    grad_mlp_rows = sum_apply([grad_gate_act, grad_up_act], [full_gate, full_up], 10)
     grad_gain_mlp = jnp.sum(grad_mlp_rows * normed_mlp, axis=0)
     grad_mid = grad_result + norm_back(grad_mlp_rows, normed_mlp, scale_mlp, gain_two)
     grad_attn_rows = gather(grad_mid.astype(jnp.bfloat16), 1, True, 2)
@@ -1045,10 +1232,9 @@
         key_grads.append(grad_kv[:, :HEAD])
         value_grads.append(grad_kv[:, HEAD:])
     grad_kv = grad_kv if kv_local == 1 else jnp.concatenate(key_grads + value_grads, axis=1)
+    grad_kv = scatter(grad_kv, ctx_size, False, 7)
     grad_kv, *summed = lax.optimization_barrier((grad_kv, *summed))
     shard_down, shard_gate, shard_up = to_rows(summed, hidden_width)
-    shard_down = shard_down.T
-    grad_kv = scatter(grad_kv, ctx_size, False, 7)
     grad_turned = jnp.concatenate(query_grads + [grad_kv[:, :kv_width]], axis=1)
     grad_pre = jnp.concatenate(
         [

time: 763 us -> 778 us (1.020)
  the two profiles are of different devices: /device:TPU:0 before, /device:TPU:9 now
where the time goes in v5:
time: 778 us; the launch traced here: 770 us
  Pallas kernels  514 us (66%)
  waiting for transfers between devices  100 us (13%)
  matrix products  65.4 us (8%)
  local copies, waits for them, and re-layouts  34.7 us (4%)
  other arithmetic  29.2 us (4%)
  between operations  19.4 us (2%)
    pallas_call x2, Pallas kernels, sum_apply(): pl.pallas_call(functools.partial(sum_apply_kernel, size, pieces, count),...  149 us
    pallas_call x2, Pallas kernels, gather_apply(): pl.pallas_call(functools.partial(gather_apply_kernel, size, pieces, work,...  117 us
    pallas_call x1, Pallas kernels, front(): pl.pallas_call(functools.partial(front_kernel, size, groups), in_specs=[I...  78.2 us
    ppermute x3, waiting for transfers between devices, exchange(): lax.ppermute(going, axis, [(i, (i + step) % size) for i in range(size)])  60.9 us
    dot_general x5, matrix products, matmul_tn(): lax.dot_general(first_op, second_op, (((0,), (0,)), ((), ())), preferred_...  47.6 us
    pallas_call x1, Pallas kernels, back(): pl.pallas_call(functools.partial(back_kernel, size, groups), in_specs=[AN...  43.3 us
    pallas_call x3, Pallas kernels, gather(): pl.pallas_call(functools.partial(gather_kernel, size, paired, pieces), in...  38.1 us
    pallas_call x3, Pallas kernels, scatter(): pl.pallas_call(functools.partial(scatter_kernel, size, paired, pieces), i...  37.5 us
  transfers between devices with their start and end apart: 14, of which 5 were waited for; matrix products, arithmetic and copies ran while one was open for 8% of the time, Pallas kernels for 33%

profile of v5, /device:TPU:9, one launch (start us, length us, event | category | flops | bytes accessed | tf_op | source)
XLA Modules:
  0.0 769.9 jit_solution(514047665011068046)
XLA Ops:
  7.2 2.2 pad.17.g_ref
  9.5 1.0 pad.18.u_ref
  10.5 1.0 pad.19.d_ref
  12.2 78.2 %front.1 = (bf16[1536,1024]{1,0:T(8,128)(2,1)}, bf16[1536,768]{1,0:T(8,128)(2,1)}, bf16[384,1152]{1,0:T(8,128)(2,1)}, bf16[384,1152]{1,0:T(8,128)(2,1)}, bf16[384,1152]{1,0:T(8,128)(2,1)}) custom-call(bf16[96,1024]{1,0:T(8,128)(2,1)} %pad_maximum_fusion.6.a_ref, bf16[96,768]{1,0:T(8,128)(2,1)} %bitcast.80, bf16[96,4608]{1,0:T(8,128)(2,1)} %pad.17.g_ref, ...), custom_call_target="tpu_custom_call" | custom-call | bytes 200000000 | tf_op jit(solution)/shard_map/front/pallas_call | solution.py:473
  93.2 1.2 collective-permute-start
  94.4 1.2 collective-permute-start.1
  95.6 1.2 collective-permute-start.2
  97.2 1.1 fusion.4.x_ref
  98.3 6.8 gather.3
  105.3 4.2 convolution_add_fusion
  109.5 1.4 slice.143
  110.9 2.8 copy.41
  113.7 1.4 dynamic-slice_convert_fusion
  115.1 1.2 fusion.12
  116.3 1.8 subtract_convert_fusion.1
  119.1 22.0 %gather.4 = bf16[2048,256]{1,0:T(8,128)(2,1)} custom-call(bf16[512,256]{1,0:T(8,128)(2,1)} %pad_maximum_fusion.5.x_ref), custom_call_target="tpu_custom_call" | custom-call | bytes 15728640 | tf_op jit(solution)/shard_map/gather/pallas_call | solution.py:208
  141.0 2.4 fusion.15
  143.4 1.0 copy.47.vt_ref
  144.4 1.2 copy.56.q_ref
  145.6 1.3 copy.45.place_ref
  146.9 19.2 %attend.1 = (bf16[512,768]{1,0:T(8,128)(2,1)}, f32[6,1,512]{2,1,0:T(1,128)}) custom-call(s32[1]{0:T(128)} %bitcast.first_ref, s32[1,512]{1,0:T(1,128)} %bitcast.82, s32[2048,1]{1,0:T(8,128)} %copy.45.place_ref, bf16[512,768]{1,0:T(8,128)(2,1)} %copy.56.q_ref, bf16[2048,128]{1,0:T(8,128)(2,1)} %get-tuple-element.151.k_ref, bf16[128,2048]{1,0:T(8,128)(2,1)} %copy.47.vt_ref), custom_call_target="tpu_custom_call" | custom-call | flops 3221225472 | bytes 1572864 | tf_op jit(solution)/shard_map/attend/pallas_call | solution.py:1191
  166.1 4.2 fusion.17.x_ref
  170.3 6.9 scatter.10
  177.2 1.7 multiply_reduce_fusion.2
  178.9 1.1 multiply_convert_fusion.refs_0_
  184.3 5.8 all-gather.6.cloned.1.call-done.refs_2_.refs_3_
  190.1 56.0 %shard_map.289 = (bf16[2048,1536]{1,0:T(8,128)(2,1)}, bf16[2048,1152]{1,0:T(8,128)(2,1)}, bf16[2048,1152]{1,0:T(8,128)(2,1)}, bf16[2048,1152]{1,0:T(8,128)(2,1)}) custom-call(bf16[256,1536]{1,0:T(8,128)(2,1)} %multiply_convert_fusion.refs_0_, bf16[1536,1152]{1,0:T(8,128)(2,1)} %all-gather.4.cloned.1.call-done.refs_1_.refs_2_, ...), custom_call_target="tpu_custom_call" | custom-call | bytes 200000000 | tf_op jit(solution)/shard_map/pallas_call | solution.py:785
  246.2 70.9 %shard_map.290 = f32[256,1536]{1,0:T(8,128)} custom-call(bf16[2048,1152]{1,0:T(8,128)(2,1)} %get-tuple-element.68.refs_0_, bf16[1536,1152]{1,0:T(8,128)(2,1)} %all-gather.8.cloned.1.call-done.refs_1_), custom_call_target="tpu_custom_call" | custom-call | bytes 200000000 | tf_op jit(solution)/shard_map/pallas_call | solution.py:958
  317.1 3.0 fusion.13.refs_0_
  320.1 60.8 %shard_map.291 = (bf16[2048,1536]{1,0:T(8,128)(2,1)}, bf16[2048,1152]{1,0:T(8,128)(2,1)}, bf16[2048,1152]{1,0:T(8,128)(2,1)}) custom-call(bf16[256,1536]{1,0:T(8,128)(2,1)} %fusion.13.refs_0_, bf16[1536,1152]{1,0:T(8,128)(2,1)} %all-gather.8.cloned.1.call-done.refs_1_, bf16[2048,1152]{1,0:T(8,128)(2,1)} %get-tuple-element.70.refs_2_, ...), custom_call_target="tpu_custom_call" | custom-call | bytes 200000000 | tf_op jit(solution)/shard_map/pallas_call | solution.py:785
  380.9 13.2 %convolution_convert_fusion = bf16[1536,1152]{1,0:T(8,128)(2,1)} fusion(bf16[2048,1536]{1,0:T(8,128)(2,1)} %get-tuple-element.77, bf16[2048,1152]{1,0:T(8,128)(2,1)} %get-tuple-element.81.refs_1_), kind=kOutput, calls=%fused_computation | convolution fusion | flops 7249526784 | bytes 14548992 | tf_op jit(solution)/shard_map/dot_general | solution.py:48
  394.1 13.1 %convolution_convert_fusion.1 = bf16[1536,1152]{1,0:T(8,128)(2,1)} fusion(bf16[2048,1536]{1,0:T(8,128)(2,1)} %get-tuple-element.77, bf16[2048,1152]{1,0:T(8,128)(2,1)} %get-tuple-element.80.refs_0_), kind=kOutput, calls=%fused_computation.1 | convolution fusion | flops 7249526784 | bytes 14548992 | tf_op jit(solution)/shard_map/dot_general | solution.py:48
  407.2 13.5 %convolution_convert_fusion.2 = bf16[1536,1152]{1,0:T(8,128)(2,1)} fusion(bf16[2048,1536]{1,0:T(8,128)(2,1)} %get-tuple-element.74, bf16[2048,1152]{1,0:T(8,128)(2,1)} %get-tuple-element.68.refs_0_), kind=kOutput, calls=%fused_computation.2 | convolution fusion | flops 7249526784 | bytes 14548992 | tf_op jit(solution)/shard_map/dot_general | solution.py:48
  422.0 78.1 %shard_map.292 = f32[256,1536]{1,0:T(8,128)} custom-call(bf16[2048,1152]{1,0:T(8,128)(2,1)} %get-tuple-element.80.refs_0_, bf16[2048,1152]{1,0:T(8,128)(2,1)} %get-tuple-element.81.refs_1_, bf16[1536,1152]{1,0:T(8,128)(2,1)} %all-gather.4.cloned.1.call-done.refs_1_.refs_2_, bf16[1536,1152]{1,0:T(8,128)(2,1)} %all-gather.6.cloned.1.call-done.refs_2_.refs_3_), custom_call_target="tpu_custom_call" | custom-call | bytes 200000000 | tf_op jit(solution)/shard_map/pallas_call | solution.py:958
  500.1 3.2 multiply_reduce_fusion
  503.3 2.5 fusion.14
  505.9 9.3 %gather.5 = bf16[512,1536]{1,0:T(8,128)(2,1)} custom-call(bf16[256,1536]{1,0:T(8,128)(2,1)} %get-tuple-element.134.x_ref), custom_call_target="tpu_custom_call" | custom-call | bytes 23592960 | tf_op jit(solution)/shard_map/gather/pallas_call | solution.py:208
  515.2 4.2 convolution_convert_fusion.4
  519.5 1.0 copy-done.9
  520.5 1.0 copy.58
  522.2 4.0 convolution_convert_fusion.5.do_ref
  526.2 26.6 %attend_back.1 = (f32[512,768]{1,0:T(8,128)}, bf16[2048,256]{1,0:T(8,128)(2,1)}) custom-call(s32[1]{0:T(128)} %bitcast.first_ref, s32[1,512]{1,0:T(1,128)} %bitcast.83, s32[2048,1]{1,0:T(8,128)} %copy.45.place_ref, bf16[512,768]{1,0:T(8,128)(2,1)} %copy.56.q_ref, bf16[512,768]{1,0:T(8,128)(2,1)} %convolution_convert_fusion.5.do_ref, ...), custom_call_target="tpu_custom_call" | custom-call | flops 8053063680 | bytes 3145728 | tf_op jit(solution)/shard_map/attend_back/pallas_call | solution.py:1228
  552.8 25.1 %scatter.11 = f32[512,256]{1,0:T(8,128)} custom-call(bf16[2048,256]{1,0:T(8,128)(2,1)} %get-tuple-element.84.x_ref), custom_call_target="tpu_custom_call" | custom-call | bytes 15728640 | tf_op jit(solution)/shard_map/scatter/pallas_call | solution.py:340
  579.0 1.6 slice.171
  580.8 1.7 copy.50
  582.6 1.8 subtract_convert_fusion
  584.6 31.1 %reduce-scatter.12.cloned.1.call-done = bf16[384,768]{1,0:T(8,128)(2,1)} async-done(((bf16[1536,768]{1,0:T(8,128)(2,1)}), bf16[384,768]{1,0:T(8,128)(2,1)}) %reduce-scatter.12.cloned.1.call-update) | async-done | bytes 589840 | tf_op jit(solution)/shard_map/reduce_scatter | solution.py:1223
  615.6 5.5 fusion.18.x_ref
  621.4 3.5 convolution_convert_fusion.3.x_ref
  624.9 5.5 scatter.12
  630.5 1.9 fusion.6
  634.1 43.3 %back.1 = (f32[96,1024]{1,0:T(8,128)}, f32[48,128]{1,0:T(8,128)}) custom-call(bf16[1536,1024]{1,0:T(8,128)(2,1)} %convolution_convert_fusion.3.x_ref, f32[48,128]{1,0:T(8,128)} %pad_bitcast_fusion.s_ref), custom_call_target="tpu_custom_call" | custom-call | bytes 157286400 | tf_op jit(solution)/shard_map/back/pallas_call | solution.py:581
  677.3 1.4 slice_bitcast_fusion
  679.1 1.3 dynamic-slice_bitcast_fusion
  680.5 1.3 slice_bitcast_fusion.3
  682.1 3.0 collective-permute-start.4
  686.5 1.2 slice.129
  688.3 3.0 fusion.9
  691.3 15.0 %collective-permute-done.3.refs_1_ = bf16[3,96,1152]{2,1,0:T(8,128)(2,1)} collective-permute-done((bf16[3,96,1152]{2,1,0:T(8,128)(2,1)}, bf16[3,96,1152]{2,1,0:T(8,128)(2,1)}, u32[]{:S(2)}, u32[]{:S(2)}) %collective-permute-start.3) | collective-permute-done | bytes 663584 | tf_op jit(solution)/shard_map/ppermute | solution.py:70
  706.3 42.1 %collective-permute-done.4.refs_2_ = bf16[3,96,1152]{2,1,0:T(8,128)(2,1)} collective-permute-done((bf16[3,96,1152]{2,1,0:T(8,128)(2,1)}, bf16[3,96,1152]{2,1,0:T(8,128)(2,1)}, u32[]{:S(2)}, u32[]{:S(2)}) %collective-permute-start.4) | collective-permute-done | bytes 663584 | tf_op jit(solution)/shard_map/ppermute | solution.py:70
  748.5 3.7 collective-permute-done.5.refs_3_
  752.1 5.1 assemble.1
  757.2 2.9 copy.55
  760.1 1.6 convert_bitcast_fusion
  (146 shorter events, 14.0 us)
Async XLA Ops:
  7.2 2.3 copy-start.16
  7.2 3.3 copy-start.17
  7.2 177.1 %all-gather.4.cloned.1.call-start = ((), (), s32[]{:S(2)}) async-start(), calls=%async_computation.5 | async-start | bytes 4423680 | tf_op jit(solution)/shard_map/all_gather | solution.py:1147
  9.5 2.0 copy-start.21
  9.5 2.0 copy-start.23
  9.5 2.0 copy-start.24
  90.3 1.6 copy-start.22
  90.3 6.4 copy-start.32
  90.4 6.5 copy-start.33
  90.4 6.6 copy-start.28
  90.4 6.6 copy-start.1
  90.4 99.7 %all-gather.6.cloned.1.call-start = ((), (), s32[]{:S(2)}) async-start(), calls=%async_computation.6 | async-start | bytes 4423680 | tf_op jit(solution)/shard_map/all_gather | solution.py:1147
  91.2 155.0 %all-gather.8.cloned.1.call-start = ((), (), s32[]{:S(2)}) async-start(), calls=%async_computation.7 | async-start | bytes 4423680 | tf_op jit(solution)/shard_map/all_gather | solution.py:1147
  91.9 486.1 %reduce-scatter.10.cloned.1.call-start = ((), (), s32[]{:S(2)}) async-start(), calls=%async_computation.10 | async-start | bytes 4423680 | tf_op jit(solution)/shard_map/reduce_scatter | solution.py:1215
  93.2 86.9 %collective-permute-start = (f32[8,128]{1,0:T(8,128)S(1)}, f32[8,128]{1,0:T(8,128)S(1)}, u32[]{:S(2)}, u32[]{:S(2)}) collective-permute-start(f32[8,128]{1,0:T(8,128)S(1)} %broadcast_in_dim.15), channel_id=1, source_target_pairs={{0,8},{8,16},{16,24},{24,0},{1,9},{9,17},{17,25},{25,1},{2,10},{10... | collective-permute-start | bytes 12296 | tf_op jit(solution)/shard_map/ppermute | solution.py:1154
  94.4 87.5 %collective-permute-start.1 = (f32[8,128]{1,0:T(8,128)S(1)}, f32[8,128]{1,0:T(8,128)S(1)}, u32[]{:S(2)}, u32[]{:S(2)}) collective-permute-start(f32[8,128]{1,0:T(8,128)S(1)} %broadcast_in_dim.15), channel_id=1, source_target_pairs={{0,16},{8,24},{16,0},{24,8},{1,17},{9,25},{17,1},{25,9},{2,18},{10... | collective-permute-start | bytes 12296 | tf_op jit(solution)/shard_map/ppermute | solution.py:1154
  95.6 87.5 %collective-permute-start.2 = (f32[8,128]{1,0:T(8,128)S(1)}, f32[8,128]{1,0:T(8,128)S(1)}, u32[]{:S(2)}, u32[]{:S(2)}) collective-permute-start(f32[8,128]{1,0:T(8,128)S(1)} %broadcast_in_dim.15), channel_id=1, source_target_pairs={{0,24},{8,0},{16,8},{24,16},{1,25},{9,1},{17,9},{25,17},{2,26},{10... | collective-permute-start | bytes 12296 | tf_op jit(solution)/shard_map/ppermute | solution.py:1154
  97.2 8.0 %copy-start.26 = (f32[256]{0:T(256)}, f32[256]{0:T(256)S(1)}, u32[]{:S(2)}) copy-start(f32[256]{0:T(256)S(1)} %add_rsqrt_fusion.1) | copy-start | bytes 3076
  98.3 6.9 copy-start.30
  146.9 19.2 %copy-start.31 = (bf16[1536,768]{1,0:T(8,128)(2,1)S(1)}, bf16[1536,768]{1,0:T(8,128)(2,1)}, u32[]{:S(2)}) copy-start(bf16[1536,768]{1,0:T(8,128)(2,1)} %get-tuple-element.65) | copy-start | bytes 7077892
  170.3 6.9 copy-start.29
  246.1 71.0 %copy-start.5 = (bf16[256,1536]{1,0:T(8,128)(2,1)S(1)}, bf16[256,1536]{1,0:T(8,128)(2,1)}, u32[]{:S(2)}) copy-start(bf16[256,1536]{1,0:T(8,128)(2,1)} %param.21) | copy-start | bytes 2359300
  246.1 71.0 %copy-start.7 = (bf16[256,1536]{1,0:T(8,128)(2,1)S(1)}, bf16[256,1536]{1,0:T(8,128)(2,1)}, u32[]{:S(2)}) copy-start(bf16[256,1536]{1,0:T(8,128)(2,1)} %param.22) | copy-start | bytes 2359300
  420.7 157.3 %reduce-scatter.8.cloned.1.call-start = ((), (), s32[]{:S(2)}) async-start(), calls=%async_computation.9 | async-start | bytes 4423680 | tf_op jit(solution)/shard_map/reduce_scatter | solution.py:1215
  421.3 156.7 %reduce-scatter.6.cloned.1.call-start = ((), (), s32[]{:S(2)}) async-start(), calls=%async_computation.8 | async-start | bytes 4423680 | tf_op jit(solution)/shard_map/reduce_scatter | solution.py:1215
  421.9 78.2 %copy-start = (f32[256,1536]{1,0:T(8,128)S(1)}, f32[256,1536]{1,0:T(8,128)}, u32[]{:S(2)}) copy-start(f32[256,1536]{1,0:T(8,128)} %shard_map.290) | copy-start | bytes 4718596
  421.9 193.7 %reduce-scatter.12.cloned.1.call-start = ((), (), s32[]{:S(2)}) async-start(), calls=%async_computation.11 | async-start | bytes 2949120 | tf_op jit(solution)/shard_map/reduce_scatter | solution.py:1223
  421.9 78.1 %copy-start.6 = (bf16[256,1536]{1,0:T(8,128)(2,1)S(1)}, bf16[256,1536]{1,0:T(8,128)(2,1)}, u32[]{:S(2)}) copy-start(bf16[256,1536]{1,0:T(8,128)(2,1)} %param.21) | copy-start | bytes 2359300
  500.1 3.2 copy-start.3
  500.1 3.2 copy-start.8
  505.9 9.3 %copy-start.34 = (bf16[512,768]{1,0:T(8,128)(2,1)S(1)}, bf16[512,768]{1,0:T(8,128)(2,1)}, u32[]{:S(2)}) copy-start(bf16[512,768]{1,0:T(8,128)(2,1)} %get-tuple-element.64) | copy-start | bytes 2359300
  519.4 1.1 copy-start.9
  519.4 2.8 copy-start.12
  519.5 240.6 %reduce-scatter.14.cloned.1.call-start = ((), (), s32[]{:S(2)}) async-start(), calls=%async_computation.12 | async-start | bytes 737280 | tf_op jit(solution)/shard_map/reduce_scatter | solution.py:1249
  552.8 27.8 %copy-start.10 = (f32[512,768]{1,0:T(8,128)S(1)}, f32[512,768]{1,0:T(8,128)}, u32[]{:S(2)}) copy-start(f32[512,768]{1,0:T(8,128)} %get-tuple-element.83) | copy-start | bytes 4718596
  580.7 1.8 copy-start.19
  580.8 1.9 copy-start.18
  615.6 5.8 copy-start.11
  624.9 5.5 copy-start.2
  624.9 5.5 copy-start.27
  630.5 2.3 copy-start.25
  634.1 44.7 %copy-start.13 = (bf16[384,1152]{1,0:T(8,128)(2,1)S(1)}, bf16[384,1152]{1,0:T(8,128)(2,1)}, u32[]{:S(2)}) copy-start(bf16[384,1152]{1,0:T(8,128)(2,1)} %reduce-scatter.10.cloned.1.call-done) | copy-start | bytes 2654212
  634.1 44.7 %copy-start.14 = (bf16[384,1152]{1,0:T(8,128)(2,1)S(1)}, bf16[384,1152]{1,0:T(8,128)(2,1)}, u32[]{:S(2)}) copy-start(bf16[384,1152]{1,0:T(8,128)(2,1)} %reduce-scatter.8.cloned.1.call-done) | copy-start | bytes 2654212
  634.1 44.7 %copy-start.15 = (bf16[384,1152]{1,0:T(8,128)(2,1)S(1)}, bf16[384,1152]{1,0:T(8,128)(2,1)}, u32[]{:S(2)}) copy-start(bf16[384,1152]{1,0:T(8,128)(2,1)} %reduce-scatter.6.cloned.1.call-done) | copy-start | bytes 2654212
  679.1 6.0 copy-start.20
  679.1 9.2 %copy-start.4 = (f32[256,1536]{1,0:T(8,128)S(1)}, f32[256,1536]{1,0:T(8,128)}, u32[]{:S(2)}) copy-start(f32[256,1536]{1,0:T(8,128)} %scatter.12) | copy-start | bytes 4718596
  681.8 24.5 %collective-permute-start.3 = (bf16[3,96,1152]{2,1,0:T(8,128)(2,1)}, bf16[3,96,1152]{2,1,0:T(8,128)(2,1)}, u32[]{:S(2)}, u32[]{:S(2)}) collective-permute-start(bf16[3,96,1152]{2,1,0:T(8,128)(2,1)} %get-tuple-element.143), channel_id=1, source_target_pairs={{0,2},{2,4},{4,6},{6,0},{1,3},{3,5},{5,7},{7,1},{8,10},{10,12},{12... | collective-permute-start | bytes 1990664 | tf_op jit(solution)/shard_map/ppermute | solution.py:70
  682.1 66.4 %collective-permute-start.4 = (bf16[3,96,1152]{2,1,0:T(8,128)(2,1)}, bf16[3,96,1152]{2,1,0:T(8,128)(2,1)}, u32[]{:S(2)}, u32[]{:S(2)}) collective-permute-start(bf16[3,96,1152]{2,1,0:T(8,128)(2,1)} %get-tuple-element.142), channel_id=1, source_target_pairs={{0,4},{2,6},{4,0},{6,2},{1,5},{3,7},{5,1},{7,3},{8,12},{10,14},{12... | collective-permute-start | bytes 1990664 | tf_op jit(solution)/shard_map/ppermute | solution.py:70
  685.1 67.1 %collective-permute-start.5 = (bf16[3,96,1152]{2,1,0:T(8,128)(2,1)S(1)}, bf16[3,96,1152]{2,1,0:T(8,128)(2,1)}, u32[]{:S(2)}, u32[]{:S(2)}) collective-permute-start(bf16[3,96,1152]{2,1,0:T(8,128)(2,1)S(1)} %get-tuple-element.141), channel_id=1, source_target_pairs={{0,6},{2,0},{4,2},{6,4},{1,7},{3,1},{5,3},{7,5},{8,14},{10,8},{12,... | collective-permute-start | bytes 1990664 | tf_op jit(solution)/shard_map/ppermute | solution.py:70
Sparse Core Ops, SparseCore 0:
  90.5 50.4 all-gather.3
  142.9 47.2 all-gather.5
  192.0 47.1 all-gather.7
  420.8 53.9 reduce-scatter.9
  477.8 47.1 reduce-scatter.7
  528.0 47.1 reduce-scatter.5
  578.2 37.3 reduce-scatter.11
  678.9 58.3 reduce-scatter.13

commit v6 on v5

--- a/solution.py
+++ b/solution.py
@@ -483,8 +483,8 @@
 
 
 def back_kernel(
-    size, groups, x_ref, s_ref, o_ref, t_ref, mine, far, near, pair, crowd, row,
-    own_sem, far_send, far_recv, near_send, near_recv, pair_sems, crowd_send, crowd_recv, row_send, row_recv,
+    size, groups, x_ref, s_ref, p_ref, w_ref, n_ref, o_ref, t_ref, g_ref, mine, far, near, part, pair, crowd, row, give, got,
+    give_sems, own_sem, far_send, far_recv, near_send, near_recv, pair_sems, crowd_send, crowd_recv, row_send, row_recv,
 ):
     place, group = lax.axis_index("ctx"), lax.axis_index("dp")
     core = lax.axis_index("tensor")
@@ -507,7 +507,26 @@
     def along(k):
         return remote(mine.at[k], near.at[k], near_send.at[k], near_recv.at[k], {"ctx": rank_at(k)})
 
-    to_mate = remote(s_ref, pair, pair_sems.at[0], pair_sems.at[1], {"tensor": 1 - core})
+    to_mate = remote(part, pair, pair_sems.at[0], pair_sems.at[1], {"tensor": 1 - core})
+    half = remote(give, got, give_sems.at[0], give_sems.at[1], {"tensor": 1 - core})
+
+    def product(which, target):
+        own_rows, depth = target.shape
+        step = column_step(depth)
+        span = pl.ds(pl.multiple_of(which * own_rows, own_rows), own_rows)
+
+        def some(j, carry):
+            columns = pl.ds(pl.multiple_of(j * step, step), step)
+            target[:, columns] = matmul_nt(p_ref[span, :], w_ref[columns, :])
+            return carry
+
+        lax.fori_loop(0, depth // step, some, 0)
+
+    def gain_sums(i, total):
+        span = pl.ds(pl.multiple_of(i * 32, 32), 32)
+        grad = g_ref[span, :] + got[span, :]
+        g_ref[span, :] = grad
+        return total + jnp.sum(grad * n_ref[span, :], axis=0, keepdims=True)
 
     def to_crowd(step):
         return remote(
@@ -528,14 +547,22 @@
         greet(barrier, {"dp": lax.rem(group + step, groups)})
     greet(barrier, {"tensor": 1 - core})
     pl.semaphore_wait(barrier, size + groups - 1)
-    to_mate.start()
-    to_mate.wait_recv()
-    crowd[group] = s_ref[...] + pair[...]
-    for step in range(1, groups):
-        to_crowd(step).start()
     for k in range(size):
         for step in range(1, groups):
             across(k, step).start()
+    product(1 - core, give)
+    half.start()
+    product(core, g_ref)
+    part[...] = s_ref[...]
+    half.wait_recv()
+    gains = lax.fori_loop(0, g_ref.shape[0] // 32, gain_sums, jnp.zeros((1, g_ref.shape[1]), jnp.float32))
+    for j in range(g_ref.shape[1] // 128):
+        part[j : j + 1, :] = gains[:, j * 128 : (j + 1) * 128]
+    to_mate.start()
+    to_mate.wait_recv()
+    crowd[group] = part[...] + pair[...]
+    for step in range(1, groups):
+        to_crowd(step).start()
     for step in range(1, groups):
         to_crowd(step).wait_recv()
     total = crowd[0]
@@ -562,6 +589,7 @@
     for c in range(1, size):
         total += row[c]
     t_ref[...] = total
+    half.wait_send()
     to_mate.wait_send()
     for step in range(1, groups):
         to_crowd(step).wait_send()
@@ -574,25 +602,30 @@
             along(k).wait_send()
 
 
-def back(x, small, ident):
+def back(x, small, grad_pre, weight, normed, ident):
     size, groups = lax.axis_size("ctx"), lax.axis_size("dp")
     rows, columns = x.shape[0] // (size * groups), x.shape[1]
     dma = pltpu.SemaphoreType.DMA
     return pl.pallas_call(
         functools.partial(back_kernel, size, groups),
-        in_specs=[ANY, IN_VMEM],
-        out_specs=[IN_VMEM, IN_VMEM],
+        in_specs=[ANY] + [IN_VMEM] * 4,
+        out_specs=[IN_VMEM] * 3,
         out_shape=[
             jax.ShapeDtypeStruct((rows, columns), jnp.float32),
             jax.ShapeDtypeStruct(small.shape, jnp.float32),
+            jax.ShapeDtypeStruct(normed.shape, jnp.float32),
         ],
         scratch_shapes=[
             pltpu.VMEM((size, rows, columns), x.dtype),
             pltpu.VMEM((size, groups, rows, columns), x.dtype),
             pltpu.VMEM((size, rows, columns), x.dtype),
             pltpu.VMEM(small.shape, jnp.float32),
+            pltpu.VMEM(small.shape, jnp.float32),
             pltpu.VMEM((groups,) + small.shape, jnp.float32),
             pltpu.VMEM((size,) + small.shape, jnp.float32),
+            pltpu.VMEM(normed.shape, jnp.float32),
+            pltpu.VMEM(normed.shape, jnp.float32),
+            dma((2,)),
             dma((size,)),
             dma((size, groups)),
             dma((size, groups)),
@@ -607,7 +640,7 @@
         compiler_params=pltpu.CompilerParams(collective_id=ident, has_side_effects=True, vmem_limit_bytes=60000000),
         cost_estimate=pl.CostEstimate(flops=0, bytes_accessed=100 * x.size, transcendentals=0),
         name="back",
-    )(x, small)
+    )(x, small, grad_pre, weight, normed)
 
 
 def column_step(width):
@@ -972,8 +1005,7 @@
     for which, target in enumerate((down_ref, gate_ref, up_ref)):
         for part, k in zip(parts, range(size)):
             whole[:, pl.ds(pl.multiple_of(ranks_ref[k] * width, 128), width)] = part[which].astype(jnp.float32)
-        kept = whole[:, : gate_ref.shape[1]]
-        target[...] = kept.T if which == 0 else kept
+        target[...] = whole[:, : gate_ref.shape[1]]
 
 
 def assemble(received, columns):
@@ -985,7 +1017,7 @@
         functools.partial(assemble_kernel, len(blocks)),
         in_specs=[pl.BlockSpec(memory_space=pltpu.SMEM)] + [IN_VMEM] * len(blocks),
         out_specs=[IN_VMEM] * 3,
-        out_shape=[jax.ShapeDtypeStruct((columns, rows), f32)] + [jax.ShapeDtypeStruct((rows, columns), f32)] * 2,
+        out_shape=[jax.ShapeDtypeStruct((rows, columns), f32)] * 3,
         scratch_shapes=[pltpu.VMEM((rows, len(blocks) * width), f32)],
         compiler_params=pltpu.CompilerParams(vmem_limit_bytes=60000000),
         cost_estimate=pl.CostEstimate(flops=0, bytes_accessed=20 * rows * columns, transcendentals=0),
@@ -1235,6 +1267,7 @@
     grad_kv = scatter(grad_kv, ctx_size, False, 7)
     grad_kv, *summed = lax.optimization_barrier((grad_kv, *summed))
     shard_down, shard_gate, shard_up = to_rows(summed, hidden_width)
+    shard_down = shard_down.T
     grad_turned = jnp.concatenate(query_grads + [grad_kv[:, :kv_width]], axis=1)
     grad_pre = jnp.concatenate(
         [
@@ -1248,9 +1281,6 @@
     grad_pre, grad_out = lax.optimization_barrier((grad_pre, grad_out))
     shard_out = lax.psum_scatter(grad_out, "ctx", scatter_dimension=0, tiled=True)
     shard_out = shard_out.astype(jnp.float32).T
-    grad_normed = scatter(matmul_nt(grad_pre, full_qkv), 1, True, 4)
-    grad_gain_attn = jnp.sum(grad_normed * normed_attn, axis=0)
-    grad_input = grad_mid + norm_back(grad_normed, normed_attn, scale_attn, gain_one)
     bias_sum = jnp.sum(grad_pre.astype(jnp.float32), axis=0)
 
     def spread(part, size):
@@ -1260,7 +1290,7 @@
 
     loss_part = jnp.zeros((128,), jnp.float32).at[0].set(squared_sum)
     parts = [
-        grad_gain_attn,
+        jnp.zeros((D,), jnp.float32),
         grad_gain_mlp,
         spread(bias_sum[:q_width], query_bias.shape[0]),
         spread(bias_sum[q_width:turned], key_bias.shape[0]),
@@ -1270,7 +1300,8 @@
     flat = jnp.concatenate(parts)
     small = jnp.pad(flat, (0, -flat.shape[0] % 1024)).reshape(-1, 128)
     grad_qkv = matmul_tn(normed_rows, grad_pre).astype(jnp.bfloat16)
-    shard_qkv, sums = back(grad_qkv, small, 8)
+    shard_qkv, sums, grad_normed = back(grad_qkv, small, grad_pre, full_qkv, normed_attn, 8)
+    grad_input = grad_mid + norm_back(grad_normed, normed_attn, scale_attn, gain_one)
     sums = sums.reshape(-1)
     pieces, offset = [], 0
     for part in parts:

time: 778 us -> 781 us (level)
  Pallas kernels: 514 us -> 528 us
    pallas_call x1, Pallas kernels: 43.3 us -> 63.6 us  [back(): pl.pallas_call(functools.partial(back_kernel, size, groups), in_specs=[AN...]
    pallas_call x3 -> x2, Pallas kernels: 37.5 us -> 32.1 us  [scatter(): pl.pallas_call(functools.partial(scatter_kernel, size, paired, pieces), i...]
where the time goes in v6:
time: 781 us; the launch traced here: 773 us
  Pallas kernels  528 us (68%)
  waiting for transfers between devices  95.4 us (12%)
  matrix products  59.8 us (8%)
  local copies, waits for them, and re-layouts  32.2 us (4%)
  other arithmetic  30.7 us (4%)
  between operations  19.4 us (2%)
    pallas_call x2, Pallas kernels, sum_apply(): pl.pallas_call(functools.partial(sum_apply_kernel, size, pieces, count),...  149 us
    pallas_call x2, Pallas kernels, gather_apply(): pl.pallas_call(functools.partial(gather_apply_kernel, size, pieces, work,...  117 us
    pallas_call x1, Pallas kernels, front(): pl.pallas_call(functools.partial(front_kernel, size, groups), in_specs=[I...  78.2 us
    pallas_call x1, Pallas kernels, back(): pl.pallas_call(functools.partial(back_kernel, size, groups), in_specs=[AN...  63.6 us
    ppermute x3, waiting for transfers between devices, exchange(): lax.ppermute(going, axis, [(i, (i + step) % size) for i in range(size)])  58.3 us
    dot_general x5, matrix products, matmul_tn(): lax.dot_general(first_op, second_op, (((0,), (0,)), ((), ())), preferred_...  47.5 us
    pallas_call x3, Pallas kernels, gather(): pl.pallas_call(functools.partial(gather_kernel, size, paired, pieces), in...  38 us
    pallas_call x2, Pallas kernels, scatter(): pl.pallas_call(functools.partial(scatter_kernel, size, paired, pieces), i...  32.1 us
  transfers between devices with their start and end apart: 14, of which 5 were waited for; matrix products, arithmetic and copies ran while one was open for 8% of the time, Pallas kernels for 33%

profile of v6, /device:TPU:9, one launch (start us, length us, event | category | flops | bytes accessed | tf_op | source)
XLA Modules:
  0.0 772.9 jit_solution(10530339605318274800)
XLA Ops:
  7.2 2.2 pad.17.g_ref
  9.5 1.0 pad.18.u_ref
  10.5 1.0 pad.19.d_ref
  12.2 78.2 %front.1 = (bf16[1536,1024]{1,0:T(8,128)(2,1)}, bf16[1536,768]{1,0:T(8,128)(2,1)}, bf16[384,1152]{1,0:T(8,128)(2,1)}, bf16[384,1152]{1,0:T(8,128)(2,1)}, bf16[384,1152]{1,0:T(8,128)(2,1)}) custom-call(bf16[96,1024]{1,0:T(8,128)(2,1)} %pad_maximum_fusion.6.a_ref, bf16[96,768]{1,0:T(8,128)(2,1)} %bitcast.79, bf16[96,4608]{1,0:T(8,128)(2,1)} %pad.17.g_ref, ...), custom_call_target="tpu_custom_call" | custom-call | bytes 200000000 | tf_op jit(solution)/shard_map/front/pallas_call | solution.py:473
  93.2 1.2 collective-permute-start
  94.4 1.2 collective-permute-start.1
  95.6 1.2 collective-permute-start.2
  97.2 1.7 convert_multiply_fusion
  98.9 6.9 gather.3
  105.9 4.2 convolution_add_fusion
  110.1 1.4 slice.143
  111.5 2.8 copy.40
  114.3 1.4 dynamic-slice_convert_fusion
  115.7 1.2 fusion.2
  116.9 1.8 subtract_convert_fusion.1
  119.7 21.9 %gather.4 = bf16[2048,256]{1,0:T(8,128)(2,1)} custom-call(bf16[512,256]{1,0:T(8,128)(2,1)} %pad_maximum_fusion.5.x_ref), custom_call_target="tpu_custom_call" | custom-call | bytes 15728640 | tf_op jit(solution)/shard_map/gather/pallas_call | solution.py:208
  141.6 2.4 fusion.5
  143.9 1.0 copy.46.vt_ref
  144.9 1.2 copy.54.q_ref
  146.1 1.3 copy.44.place_ref
  147.4 19.2 %attend.1 = (bf16[512,768]{1,0:T(8,128)(2,1)}, f32[6,1,512]{2,1,0:T(1,128)}) custom-call(s32[1]{0:T(128)} %bitcast.first_ref, s32[1,512]{1,0:T(1,128)} %bitcast.81, s32[2048,1]{1,0:T(8,128)} %copy.44.place_ref, bf16[512,768]{1,0:T(8,128)(2,1)} %copy.54.q_ref, bf16[2048,128]{1,0:T(8,128)(2,1)} %get-tuple-element.121.k_ref, bf16[128,2048]{1,0:T(8,128)(2,1)} %copy.46.vt_ref), custom_call_target="tpu_custom_call" | custom-call | flops 3221225472 | bytes 1572864 | tf_op jit(solution)/shard_map/attend/pallas_call | solution.py:1223
  166.6 4.2 fusion.7.x_ref
  170.8 7.0 scatter.9
  177.8 1.7 multiply_reduce_fusion.3
  179.6 1.1 multiply_convert_fusion.refs_0_
  184.9 5.1 all-gather.6.cloned.1.call-done.refs_2_.refs_3_
  190.0 56.0 %shard_map.289 = (bf16[2048,1536]{1,0:T(8,128)(2,1)}, bf16[2048,1152]{1,0:T(8,128)(2,1)}, bf16[2048,1152]{1,0:T(8,128)(2,1)}, bf16[2048,1152]{1,0:T(8,128)(2,1)}) custom-call(bf16[256,1536]{1,0:T(8,128)(2,1)} %multiply_convert_fusion.refs_0_, bf16[1536,1152]{1,0:T(8,128)(2,1)} %all-gather.4.cloned.1.call-done.refs_1_.refs_2_, ...), custom_call_target="tpu_custom_call" | custom-call | bytes 200000000 | tf_op jit(solution)/shard_map/pallas_call | solution.py:818
  246.0 71.0 %shard_map.290 = f32[256,1536]{1,0:T(8,128)} custom-call(bf16[2048,1152]{1,0:T(8,128)(2,1)} %get-tuple-element.69.refs_0_, bf16[1536,1152]{1,0:T(8,128)(2,1)} %all-gather.8.cloned.1.call-done.refs_1_), custom_call_target="tpu_custom_call" | custom-call | bytes 200000000 | tf_op jit(solution)/shard_map/pallas_call | solution.py:991
  317.1 3.0 fusion.3.refs_0_
  320.0 60.8 %shard_map.291 = (bf16[2048,1536]{1,0:T(8,128)(2,1)}, bf16[2048,1152]{1,0:T(8,128)(2,1)}, bf16[2048,1152]{1,0:T(8,128)(2,1)}) custom-call(bf16[256,1536]{1,0:T(8,128)(2,1)} %fusion.3.refs_0_, bf16[1536,1152]{1,0:T(8,128)(2,1)} %all-gather.8.cloned.1.call-done.refs_1_, bf16[2048,1152]{1,0:T(8,128)(2,1)} %get-tuple-element.71.refs_2_, ...), custom_call_target="tpu_custom_call" | custom-call | bytes 200000000 | tf_op jit(solution)/shard_map/pallas_call | solution.py:818
  380.9 13.2 %convolution_convert_fusion = bf16[1536,1152]{1,0:T(8,128)(2,1)} fusion(bf16[2048,1536]{1,0:T(8,128)(2,1)} %get-tuple-element.78, bf16[2048,1152]{1,0:T(8,128)(2,1)} %get-tuple-element.82.refs_1_), kind=kOutput, calls=%fused_computation | convolution fusion | flops 7249526784 | bytes 14548992 | tf_op jit(solution)/shard_map/dot_general | solution.py:48
  394.0 13.1 %convolution_convert_fusion.1 = bf16[1536,1152]{1,0:T(8,128)(2,1)} fusion(bf16[2048,1536]{1,0:T(8,128)(2,1)} %get-tuple-element.78, bf16[2048,1152]{1,0:T(8,128)(2,1)} %get-tuple-element.81.refs_0_), kind=kOutput, calls=%fused_computation.1 | convolution fusion | flops 7249526784 | bytes 14548992 | tf_op jit(solution)/shard_map/dot_general | solution.py:48
  407.2 13.5 %convolution_convert_fusion.2 = bf16[1536,1152]{1,0:T(8,128)(2,1)} fusion(bf16[2048,1536]{1,0:T(8,128)(2,1)} %get-tuple-element.75, bf16[2048,1152]{1,0:T(8,128)(2,1)} %get-tuple-element.69.refs_0_), kind=kOutput, calls=%fused_computation.2 | convolution fusion | flops 7249526784 | bytes 14548992 | tf_op jit(solution)/shard_map/dot_general | solution.py:48
  421.9 78.2 %shard_map.292 = f32[256,1536]{1,0:T(8,128)} custom-call(bf16[2048,1152]{1,0:T(8,128)(2,1)} %get-tuple-element.81.refs_0_, bf16[2048,1152]{1,0:T(8,128)(2,1)} %get-tuple-element.82.refs_1_, bf16[1536,1152]{1,0:T(8,128)(2,1)} %all-gather.4.cloned.1.call-done.refs_1_.refs_2_, bf16[1536,1152]{1,0:T(8,128)(2,1)} %all-gather.6.cloned.1.call-done.refs_2_.refs_3_), custom_call_target="tpu_custom_call" | custom-call | bytes 200000000 | tf_op jit(solution)/shard_map/pallas_call | solution.py:991
  500.2 3.2 multiply_reduce_fusion.1
  503.4 2.5 fusion.4
  505.9 9.3 %gather.5 = bf16[512,1536]{1,0:T(8,128)(2,1)} custom-call(bf16[256,1536]{1,0:T(8,128)(2,1)} %get-tuple-element.104.x_ref), custom_call_target="tpu_custom_call" | custom-call | bytes 23592960 | tf_op jit(solution)/shard_map/gather/pallas_call | solution.py:208
  515.2 4.2 convolution_convert_fusion.4
  519.5 1.0 copy-done.10
  520.5 1.0 copy.56
  522.2 4.0 convolution_convert_fusion.5.do_ref
  526.1 26.6 %attend_back.1 = (f32[512,768]{1,0:T(8,128)}, bf16[2048,256]{1,0:T(8,128)(2,1)}) custom-call(s32[1]{0:T(128)} %bitcast.first_ref, s32[1,512]{1,0:T(1,128)} %bitcast.82, s32[2048,1]{1,0:T(8,128)} %copy.44.place_ref, bf16[512,768]{1,0:T(8,128)(2,1)} %copy.54.q_ref, bf16[512,768]{1,0:T(8,128)(2,1)} %convolution_convert_fusion.5.do_ref, ...), custom_call_target="tpu_custom_call" | custom-call | flops 8053063680 | bytes 3145728 | tf_op jit(solution)/shard_map/attend_back/pallas_call | solution.py:1260
  552.8 25.1 %scatter.10 = f32[512,256]{1,0:T(8,128)} custom-call(bf16[2048,256]{1,0:T(8,128)(2,1)} %get-tuple-element.85.x_ref), custom_call_target="tpu_custom_call" | custom-call | bytes 15728640 | tf_op jit(solution)/shard_map/scatter/pallas_call | solution.py:340
  578.0 1.0 slice.122
  578.9 1.6 slice.171
  580.7 1.7 copy.49
  582.5 1.8 subtract_convert_fusion
  584.9 1.2 pad_maximum_fusion.2.p_ref
  586.2 29.4 %reduce-scatter.12.cloned.1.call-done = bf16[384,768]{1,0:T(8,128)(2,1)} async-done(((bf16[1536,768]{1,0:T(8,128)(2,1)}), bf16[384,768]{1,0:T(8,128)(2,1)}) %reduce-scatter.12.cloned.1.call-update) | async-done | bytes 589840 | tf_op jit(solution)/shard_map/reduce_scatter | solution.py:1255
  615.8 3.5 convolution_convert_fusion.3.x_ref
  620.8 63.6 %back.1 = (f32[96,1024]{1,0:T(8,128)}, f32[48,128]{1,0:T(8,128)}, f32[256,1536]{1,0:T(8,128)}) custom-call(bf16[1536,1024]{1,0:T(8,128)(2,1)} %convolution_convert_fusion.3.x_ref, f32[48,128]{1,0:T(8,128)} %pad_bitcast_fusion.s_ref, bf16[512,1024]{1,0:T(8,128)(2,1)} %copy-done.4, bf16[1536,1024]{1,0:T(8,128)(2,1)} %get-tuple-element.64.w_ref, ...), custom_call_target="tpu_custom_call" | custom-call | bytes 157286400 | tf_op jit(solution)/shard_map/back/pallas_call | solution.py:609
  684.4 1.4 slice_bitcast_fusion
  685.8 1.3 slice_bitcast_fusion.3
  687.5 1.4 dynamic-slice_bitcast_fusion
  688.9 1.9 collective-permute-start.4
  690.8 1.5 collective-permute-start.5
  693.0 1.8 multiply_reduce_fusion
  695.5 1.2 slice.129
  697.4 3.0 multiply_add_fusion
  700.4 7.0 collective-permute-done.3.refs_1_
  707.4 47.1 %collective-permute-done.4.refs_2_ = bf16[3,96,1152]{2,1,0:T(8,128)(2,1)} collective-permute-done((bf16[3,96,1152]{2,1,0:T(8,128)(2,1)}, bf16[3,96,1152]{2,1,0:T(8,128)(2,1)}, u32[]{:S(2)}, u32[]{:S(2)}) %collective-permute-start.4) | collective-permute-done | bytes 663584 | tf_op jit(solution)/shard_map/ppermute | solution.py:70
  754.5 4.2 collective-permute-done.5.refs_3_
  758.7 4.4 assemble.1
  763.1 1.6 convert_bitcast_fusion
  (145 shorter events, 13.1 us)
Async XLA Ops:
  7.2 2.3 copy-start.17
  7.2 3.3 copy-start.18
  7.2 177.7 %all-gather.4.cloned.1.call-start = ((), (), s32[]{:S(2)}) async-start(), calls=%async_computation.5 | async-start | bytes 4423680 | tf_op jit(solution)/shard_map/all_gather | solution.py:1179
  9.5 2.0 copy-start.21
  9.5 2.0 copy-start.23
  9.5 2.0 copy-start.24
  90.3 1.6 copy-start.22
  90.3 6.4 copy-start.33
  90.4 6.5 copy-start.34
  90.4 6.6 copy-start.29
  90.4 6.6 copy-start.1
  90.4 99.6 %all-gather.6.cloned.1.call-start = ((), (), s32[]{:S(2)}) async-start(), calls=%async_computation.6 | async-start | bytes 4423680 | tf_op jit(solution)/shard_map/all_gather | solution.py:1179
  91.2 154.8 %all-gather.8.cloned.1.call-start = ((), (), s32[]{:S(2)}) async-start(), calls=%async_computation.7 | async-start | bytes 4423680 | tf_op jit(solution)/shard_map/all_gather | solution.py:1179
  91.9 486.0 %reduce-scatter.10.cloned.1.call-start = ((), (), s32[]{:S(2)}) async-start(), calls=%async_computation.10 | async-start | bytes 4423680 | tf_op jit(solution)/shard_map/reduce_scatter | solution.py:1247
  93.2 87.5 %collective-permute-start = (f32[8,128]{1,0:T(8,128)S(1)}, f32[8,128]{1,0:T(8,128)S(1)}, u32[]{:S(2)}, u32[]{:S(2)}) collective-permute-start(f32[8,128]{1,0:T(8,128)S(1)} %broadcast_in_dim.13), channel_id=1, source_target_pairs={{0,8},{8,16},{16,24},{24,0},{1,9},{9,17},{17,25},{25,1},{2,10},{10... | collective-permute-start | bytes 12296 | tf_op jit(solution)/shard_map/ppermute | solution.py:1186
  94.4 88.1 %collective-permute-start.1 = (f32[8,128]{1,0:T(8,128)S(1)}, f32[8,128]{1,0:T(8,128)S(1)}, u32[]{:S(2)}, u32[]{:S(2)}) collective-permute-start(f32[8,128]{1,0:T(8,128)S(1)} %broadcast_in_dim.13), channel_id=1, source_target_pairs={{0,16},{8,24},{16,0},{24,8},{1,17},{9,25},{17,1},{25,9},{2,18},{10... | collective-permute-start | bytes 12296 | tf_op jit(solution)/shard_map/ppermute | solution.py:1186
  95.6 88.1 %collective-permute-start.2 = (f32[8,128]{1,0:T(8,128)S(1)}, f32[8,128]{1,0:T(8,128)S(1)}, u32[]{:S(2)}, u32[]{:S(2)}) collective-permute-start(f32[8,128]{1,0:T(8,128)S(1)} %broadcast_in_dim.13), channel_id=1, source_target_pairs={{0,24},{8,0},{16,8},{24,16},{1,25},{9,1},{17,9},{25,17},{2,26},{10... | collective-permute-start | bytes 12296 | tf_op jit(solution)/shard_map/ppermute | solution.py:1186
  97.2 1.7 copy-start.27
  98.9 6.9 copy-start.31
  147.4 19.2 %copy-start.32 = (bf16[1536,768]{1,0:T(8,128)(2,1)S(1)}, bf16[1536,768]{1,0:T(8,128)(2,1)}, u32[]{:S(2)}) copy-start(bf16[1536,768]{1,0:T(8,128)(2,1)} %get-tuple-element.66) | copy-start | bytes 7077892
  170.8 7.0 copy-start.30
  246.0 71.0 %copy-start.5 = (bf16[256,1536]{1,0:T(8,128)(2,1)S(1)}, bf16[256,1536]{1,0:T(8,128)(2,1)}, u32[]{:S(2)}) copy-start(bf16[256,1536]{1,0:T(8,128)(2,1)} %param.21) | copy-start | bytes 2359300
  246.0 71.0 %copy-start.8 = (bf16[256,1536]{1,0:T(8,128)(2,1)S(1)}, bf16[256,1536]{1,0:T(8,128)(2,1)}, u32[]{:S(2)}) copy-start(bf16[256,1536]{1,0:T(8,128)(2,1)} %param.22) | copy-start | bytes 2359300
  420.7 157.3 %reduce-scatter.8.cloned.1.call-start = ((), (), s32[]{:S(2)}) async-start(), calls=%async_computation.9 | async-start | bytes 4423680 | tf_op jit(solution)/shard_map/reduce_scatter | solution.py:1247
  421.3 156.7 %reduce-scatter.6.cloned.1.call-start = ((), (), s32[]{:S(2)}) async-start(), calls=%async_computation.8 | async-start | bytes 4423680 | tf_op jit(solution)/shard_map/reduce_scatter | solution.py:1247
  421.8 78.3 %copy-start = (f32[256,1536]{1,0:T(8,128)S(1)}, f32[256,1536]{1,0:T(8,128)}, u32[]{:S(2)}) copy-start(f32[256,1536]{1,0:T(8,128)} %shard_map.290) | copy-start | bytes 4718596
  421.9 193.7 %reduce-scatter.12.cloned.1.call-start = ((), (), s32[]{:S(2)}) async-start(), calls=%async_computation.11 | async-start | bytes 2949120 | tf_op jit(solution)/shard_map/reduce_scatter | solution.py:1255
  421.9 78.3 %copy-start.6 = (bf16[256,1536]{1,0:T(8,128)(2,1)S(1)}, bf16[256,1536]{1,0:T(8,128)(2,1)}, u32[]{:S(2)}) copy-start(bf16[256,1536]{1,0:T(8,128)(2,1)} %param.21) | copy-start | bytes 2359300
  500.2 3.2 copy-start.3
  500.2 3.2 copy-start.9
  505.9 9.3 %copy-start.35 = (bf16[512,768]{1,0:T(8,128)(2,1)S(1)}, bf16[512,768]{1,0:T(8,128)(2,1)}, u32[]{:S(2)}) copy-start(bf16[512,768]{1,0:T(8,128)(2,1)} %get-tuple-element.65) | copy-start | bytes 2359300
  519.5 1.1 copy-start.10
  519.5 2.7 copy-start.13
  519.5 243.6 %reduce-scatter.14.cloned.1.call-start = ((), (), s32[]{:S(2)}) async-start(), calls=%async_computation.12 | async-start | bytes 737280 | tf_op jit(solution)/shard_map/reduce_scatter | solution.py:1282
  552.8 27.8 %copy-start.11 = (f32[512,768]{1,0:T(8,128)S(1)}, f32[512,768]{1,0:T(8,128)}, u32[]{:S(2)}) copy-start(f32[512,768]{1,0:T(8,128)} %get-tuple-element.84) | copy-start | bytes 4718596
  577.9 2.7 copy-start.25
  580.7 1.8 copy-start.19
  584.9 30.9 %copy-start.12 = (bf16[512,1536]{1,0:T(8,128)(2,1)S(1)}, bf16[512,1536]{1,0:T(8,128)(2,1)}, u32[]{:S(2)}) copy-start(bf16[512,1536]{1,0:T(8,128)(2,1)} %gather.3) | copy-start | bytes 4718596
  586.1 33.1 %copy-start.4 = (bf16[512,1024]{1,0:T(8,128)(2,1)}, bf16[512,1024]{1,0:T(8,128)(2,1)S(1)}, u32[]{:S(2)}) copy-start(bf16[512,1024]{1,0:T(8,128)(2,1)S(1)} %pad_maximum_fusion.2.p_ref) | copy-start | bytes 3145732
  615.8 3.8 copy-start.26
  620.8 66.3 %copy-start.14 = (bf16[384,1152]{1,0:T(8,128)(2,1)S(1)}, bf16[384,1152]{1,0:T(8,128)(2,1)}, u32[]{:S(2)}) copy-start(bf16[384,1152]{1,0:T(8,128)(2,1)} %reduce-scatter.10.cloned.1.call-done) | copy-start | bytes 2654212
  620.8 66.3 %copy-start.15 = (bf16[384,1152]{1,0:T(8,128)(2,1)S(1)}, bf16[384,1152]{1,0:T(8,128)(2,1)}, u32[]{:S(2)}) copy-start(bf16[384,1152]{1,0:T(8,128)(2,1)} %reduce-scatter.8.cloned.1.call-done) | copy-start | bytes 2654212
  620.8 66.3 %copy-start.16 = (bf16[384,1152]{1,0:T(8,128)(2,1)S(1)}, bf16[384,1152]{1,0:T(8,128)(2,1)}, u32[]{:S(2)}) copy-start(bf16[384,1152]{1,0:T(8,128)(2,1)} %reduce-scatter.6.cloned.1.call-done) | copy-start | bytes 2654212
  687.5 4.8 copy-start.20
  687.5 5.5 copy-start.2
  687.5 5.5 copy-start.28
  688.9 18.5 %collective-permute-start.3 = (bf16[3,96,1152]{2,1,0:T(8,128)(2,1)}, bf16[3,96,1152]{2,1,0:T(8,128)(2,1)}, u32[]{:S(2)}, u32[]{:S(2)}) collective-permute-start(bf16[3,96,1152]{2,1,0:T(8,128)(2,1)} %get-tuple-element.113), channel_id=1, source_target_pairs={{0,2},{2,4},{4,6},{6,0},{1,3},{3,5},{5,7},{7,1},{8,10},{10,12},{12... | collective-permute-start | bytes 1990664 | tf_op jit(solution)/shard_map/ppermute | solution.py:70
  688.9 65.7 %collective-permute-start.4 = (bf16[3,96,1152]{2,1,0:T(8,128)(2,1)}, bf16[3,96,1152]{2,1,0:T(8,128)(2,1)}, u32[]{:S(2)}, u32[]{:S(2)}) collective-permute-start(bf16[3,96,1152]{2,1,0:T(8,128)(2,1)} %get-tuple-element.112), channel_id=1, source_target_pairs={{0,4},{2,6},{4,0},{6,2},{1,5},{3,7},{5,1},{7,3},{8,12},{10,14},{12... | collective-permute-start | bytes 1990664 | tf_op jit(solution)/shard_map/ppermute | solution.py:70
  690.8 67.9 %collective-permute-start.5 = (bf16[3,96,1152]{2,1,0:T(8,128)(2,1)S(1)}, bf16[3,96,1152]{2,1,0:T(8,128)(2,1)}, u32[]{:S(2)}, u32[]{:S(2)}) collective-permute-start(bf16[3,96,1152]{2,1,0:T(8,128)(2,1)S(1)} %get-tuple-element.111), channel_id=1, source_target_pairs={{0,6},{2,0},{4,2},{6,4},{1,7},{3,1},{5,3},{7,5},{8,14},{10,8},{12,... | collective-permute-start | bytes 1990664 | tf_op jit(solution)/shard_map/ppermute | solution.py:70
  692.3 5.1 copy-start.7
Sparse Core Ops, SparseCore 0:
  90.5 50.4 all-gather.3
  142.8 47.1 all-gather.5
  191.8 47.1 all-gather.7
  420.8 53.9 reduce-scatter.9
  477.8 47.1 reduce-scatter.7
  527.9 47.1 reduce-scatter.5
  578.2 37.3 reduce-scatter.11
  692.4 54.1 reduce-scatter.13

commit v7 on v6

--- a/solution.py
+++ b/solution.py
@@ -349,14 +349,18 @@
     )(x)
 
 
-def front_kernel(
-    size, groups, a_ref, b_ref, g_ref, u_ref, d_ref, fa_ref, fb_ref, og_ref, ou_ref, od_ref,
-    local_sem, up_send, up_recv, down_send, down_recv, far_send, far_recv, swap_send, swap_recv,
-):
+def share_kernel(size, groups, kinds, count, *refs):
+    whole = len(kinds)
+    owns, refs = refs[:whole], refs[whole:]
+    parts, refs = refs[:count], refs[count:]
+    wholes, refs = refs[:whole], refs[whole:]
+    slices, refs = refs[:count], refs[count:]
+    local_sem, up_send, up_recv, down_send, down_recv, far_send, far_recv, swap_send, swap_recv = refs
     place, group = lax.axis_index("ctx"), lax.axis_index("dp")
-    rows, width = a_ref.shape[0], og_ref.shape[1]
-    wholes, owns = (fa_ref, fb_ref), (a_ref, b_ref)
-    parts, slices = (g_ref, u_ref, d_ref), (og_ref, ou_ref, od_ref)
+    rows, width = slices[0].shape[0] // size, slices[0].shape[1]
+    chained = [w for w in range(whole) if kinds[w][0]]
+    crossing = [w for w in range(whole) if kinds[w][1]]
+    last = size - 1
     barrier = pltpu.get_barrier_semaphore()
     for step in range(1, size):
         greet(barrier, {"ctx": lax.rem(place + step, size)})
@@ -364,122 +368,134 @@
         greet(barrier, {"dp": lax.rem(group + step, groups)})
     pl.semaphore_wait(barrier, size + groups - 2)
 
-    def chunk(which, in_group, rank):
-        return wholes[which].at[pl.ds(pl.multiple_of((in_group * size + rank) * rows, rows), rows)]
-
-    def source(which, rank, k):
-        return owns[which] if k == 0 else chunk(which, group, rank)
-
-    def going_up(which, k):
+    def chunk(w, in_group, rank):
+        along, over = kinds[w]
+        index = (in_group * size + rank if along else in_group) if over else rank
+        n = owns[w].shape[0]
+        return wholes[w].at[pl.ds(pl.multiple_of(index * n, n), n)]
+
+    def source(w, rank, k):
+        return owns[w] if k == 0 else chunk(w, group, rank)
+
+    def going_up(w, k):
         return remote(
-            source(which, place - k, k), chunk(which, group, place - k),
-            up_send.at[which, k], up_recv.at[which, k], {"ctx": place + 1},
-        )
-
-    def going_down(which, k):
+            source(w, place - k, k), chunk(w, group, place - k), up_send.at[w, k], up_recv.at[w, k], {"ctx": place + 1}
+        )
+
+    def going_down(w, k):
         return remote(
-            source(which, place + k, k), chunk(which, group, place + k),
-            down_send.at[which, k], down_recv.at[which, k], {"ctx": place - 1},
-        )
-
-    def across(which, rank, step, k):
+            source(w, place + k, k), chunk(w, group, place + k), down_send.at[w, k], down_recv.at[w, k], {"ctx": place - 1}
+        )
+
+    def across(w, rank, step, k):
+        slot = rank if kinds[w][0] else 0
         return remote(
-            source(which, rank, k), chunk(which, group, rank),
-            far_send.at[which, rank, step], far_recv.at[which, rank, step], {"dp": lax.rem(group + step, groups)},
-        )
-
-    def from_across(which, rank, step):
-        there = chunk(which, lax.rem(group - step + groups, groups), rank)
-        return remote(there, there, far_send.at[which, rank, step], far_recv.at[which, rank, step], {"dp": lax.rem(group + step, groups)})
-
-    def columns(which, rank):
-        return parts[which].at[:, pl.ds(pl.multiple_of(rank * width, 128), width)]
-
-    def swap(which, step):
+            source(w, rank, k), chunk(w, group, rank),
+            far_send.at[w, slot, step], far_recv.at[w, slot, step], {"dp": lax.rem(group + step, groups)},
+        )
+
+    def from_across(w, rank, step):
+        slot = rank if kinds[w][0] else 0
+        there = chunk(w, lax.rem(group - step + groups, groups), rank)
         return remote(
-            columns(which, lax.rem(place + step, size)),
-            slices[which].at[pl.ds(pl.multiple_of(place * rows, rows), rows)],
-            swap_send.at[which, step], swap_recv.at[which, step], {"ctx": lax.rem(place + step, size)},
-        )
-
-    def swapped(which, step):
-        there = slices[which].at[pl.ds(pl.multiple_of(lax.rem(place - step + size, size) * rows, rows), rows)]
-        return remote(there, there, swap_send.at[which, step], swap_recv.at[which, step], {"ctx": lax.rem(place + step, size)})
-
-    locals_ = [pltpu.make_async_copy(owns[w], chunk(w, group, place), local_sem.at[w]) for w in range(2)]
-    locals_ += [
-        pltpu.make_async_copy(
-            columns(w, place), slices[w].at[pl.ds(pl.multiple_of(place * rows, rows), rows)], local_sem.at[2 + w]
-        )
-        for w in range(3)
-    ]
-    for w in range(2):
-        pl.when(place < size - 1)(lambda w=w: going_up(w, 0).start())
-        pl.when(place > 0)(lambda w=w: going_down(w, 0).start())
-        for step in range(1, groups):
-            across(w, place, step, 0).start()
-    for copy in locals_:
+            there, there, far_send.at[w, slot, step], far_recv.at[w, slot, step], {"dp": lax.rem(group + step, groups)}
+        )
+
+    def columns(w, rank):
+        return parts[w].at[:, pl.ds(pl.multiple_of(rank * width, 128), width)]
+
+    def at_rank(w, rank):
+        return slices[w].at[pl.ds(pl.multiple_of(rank * rows, rows), rows)]
+
+    def swap(w, step):
+        to = lax.rem(place + step, size)
+        return remote(columns(w, to), at_rank(w, place), swap_send.at[w, step], swap_recv.at[w, step], {"ctx": to})
+
+    def swapped(w, step):
+        there = at_rank(w, lax.rem(place - step + size, size))
+        return remote(
+            there, there, swap_send.at[w, step], swap_recv.at[w, step], {"ctx": lax.rem(place + step, size)}
+        )
+
+    copies = [pltpu.make_async_copy(owns[w], chunk(w, group, place), local_sem.at[w]) for w in range(whole)]
+    copies += [pltpu.make_async_copy(columns(w, place), at_rank(w, place), local_sem.at[whole + w]) for w in range(count)]
+    for w in range(whole):
+        if w in chained:
+            pl.when(place < last)(lambda w=w: going_up(w, 0).start())
+            pl.when(place > 0)(lambda w=w: going_down(w, 0).start())
+        if w in crossing:
+            for step in range(1, groups):
+                across(w, place, step, 0).start()
+    for copy in copies:
         copy.start()
-    for k in range(size - 1):
-        for w in range(2):
+    for k in range(last):
+        for w in chained:
 
             @pl.when(place - 1 - k >= 0)
             def _(k=k, w=w):
                 there = chunk(w, group, place - 1 - k)
                 remote(there, there, up_send.at[w, k], up_recv.at[w, k], {"ctx": place - 1}).wait_recv()
-                if k + 1 < size - 1:
-                    pl.when(place < size - 1)(lambda: going_up(w, k + 1).start())
-                for step in range(1, groups):
-                    across(w, place - 1 - k, step, 1).start()
-
-            @pl.when(place + 1 + k <= size - 1)
+                if k + 1 < last:
+                    pl.when(place < last)(lambda: going_up(w, k + 1).start())
+                if w in crossing:
+                    for step in range(1, groups):
+                        across(w, place - 1 - k, step, 1).start()
+
+            @pl.when(place + 1 + k <= last)
             def _(k=k, w=w):
                 there = chunk(w, group, place + 1 + k)
                 remote(there, there, down_send.at[w, k], down_recv.at[w, k], {"ctx": place + 1}).wait_recv()
-                if k + 1 < size - 1:
+                if k + 1 < last:
                     pl.when(place > 0)(lambda: going_down(w, k + 1).start())
-                for step in range(1, groups):
-                    across(w, place + 1 + k, step, 1).start()
-
-    for w in range(3):
+                if w in crossing:
+                    for step in range(1, groups):
+                        across(w, place + 1 + k, step, 1).start()
+
+    for w in range(count):
         for step in range(1, size):
             swap(w, step).start()
-    for rank in range(size):
-        for w in range(2):
+    for w in crossing:
+        for rank in range(size) if w in chained else [place]:
             for step in range(1, groups):
                 from_across(w, rank, step).wait_recv()
-    for w in range(3):
+    for w in range(count):
         for step in range(1, size):
             swapped(w, step).wait_recv()
-    for copy in locals_:
+    for copy in copies:
         copy.wait()
-    for w in range(2):
-        for k in range(size - 1):
-            pl.when((place < size - 1) & (place - k >= 0))(lambda k=k, w=w: going_up(w, k).wait_send())
-            pl.when((place > 0) & (place + k <= size - 1))(lambda k=k, w=w: going_down(w, k).wait_send())
-        for rank in range(size):
-            for step in range(1, groups):
-                across(w, rank, step, 1).wait_send()
-    for w in range(3):
+    for w in range(whole):
+        if w in chained:
+            for k in range(last):
+                pl.when((place < last) & (place - k >= 0))(lambda k=k, w=w: going_up(w, k).wait_send())
+                pl.when((place > 0) & (place + k <= last))(lambda k=k, w=w: going_down(w, k).wait_send())
+        if w in crossing:
+            for rank in range(size) if w in chained else [place]:
+                for step in range(1, groups):
+                    across(w, rank, step, 1).wait_send()
+    for w in range(count):
         for step in range(1, size):
             swap(w, step).wait_send()
 
 
-def front(a, b, parts, width, ident):
+def share(wholes, kinds, parts, width, ident):
     size, groups = lax.axis_size("ctx"), lax.axis_size("dp")
-    rows = a.shape[0]
+    rows = parts[0].shape[0]
     dma = pltpu.SemaphoreType.DMA
-    slices = jax.ShapeDtypeStruct((size * rows, width), a.dtype)
+    n, m = len(wholes), len(parts)
+    shapes = [
+        jax.ShapeDtypeStruct(((size if along else 1) * (groups if over else 1) * x.shape[0], x.shape[1]), x.dtype)
+        for x, (along, over) in zip(wholes, kinds)
+    ]
+    shapes += [jax.ShapeDtypeStruct((size * rows, width), parts[0].dtype)] * m
     return pl.pallas_call(
-        functools.partial(front_kernel, size, groups),
-        in_specs=[IN_VMEM] * 5,
-        out_specs=[ANY] * 5,
-        out_shape=[jax.ShapeDtypeStruct((groups * size * rows, x.shape[1]), x.dtype) for x in (a, b)] + [slices] * 3,
-        scratch_shapes=[dma((5,))] + [dma((2, size))] * 4 + [dma((2, size, groups))] * 2 + [dma((3, size))] * 2,
+        functools.partial(share_kernel, size, groups, kinds, m),
+        in_specs=[IN_VMEM] * (n + m),
+        out_specs=[ANY] * (n + m),
+        out_shape=shapes,
+        scratch_shapes=[dma((n + m,))] + [dma((n, size))] * 4 + [dma((n, size, groups))] * 2 + [dma((m, size))] * 2,
         compiler_params=pltpu.CompilerParams(collective_id=ident, has_side_effects=True),
-        cost_estimate=pl.CostEstimate(flops=0, bytes_accessed=200000000, transcendentals=0),
-        name="front",
-    )(a, b, *parts)
+        cost_estimate=pl.CostEstimate(flops=0, bytes_accessed=150000000, transcendentals=0),
+    )(*wholes, *parts)
 
 
 def back_kernel(
@@ -1169,26 +1185,15 @@
     scale_attn = lax.rsqrt(jnp.mean(inputs * inputs, axis=1, keepdims=True) + EPS)
     normed_attn = inputs * scale_attn
     extra = ((0, 0), (0, ctx_size * slice_width - hidden_width))
-    full_qkv, full_out, *slices = front(
-        jnp.concatenate([query_weight, key_weight, value_weight], axis=1),
-        out_weight.T,
-        [jnp.pad(w, extra) for w in (gate_weight, up_weight, down_weight.T)],
+    full_qkv, *slices = share(
+        [jnp.concatenate([query_weight, key_weight, value_weight], axis=1)],
+        ((True, True),),
+        [jnp.pad(w, extra) for w in (gate_weight, up_weight)],
         slice_width,
         1,
     )
-    full_gate, full_up, full_down = [lax.all_gather(w, "dp", axis=0, tiled=True) for w in slices]
+    full_gate, full_up = [lax.all_gather(w, "dp", axis=0, tiled=True) for w in slices]
     normed_rows = gather((normed_attn * gain_one).astype(jnp.bfloat16), 1, True, 2)
-    valid_count = jnp.sum(valid_mask.astype(jnp.float32))
-    counts = [valid_count]
-    dp_size = lax.axis_size("dp")
-    for step in range(1, dp_size):
-        counts.append(
-            lax.ppermute(
-                jnp.full((8, 128), valid_count), "dp", [(i, (i + step) % dp_size) for i in range(dp_size)]
-            )[0, 0]
-        )
-    valid_count = sum(counts)
-
     bias = jnp.concatenate(
         [
             lax.dynamic_slice_in_dim(query_bias, tensor_rank * q_width, q_width),
@@ -1207,7 +1212,16 @@
     )
     queries = rotated[:, :q_width]
     own_kv = jnp.concatenate([rotated[:, q_width:], qkv_pre[:, turned:].astype(jnp.bfloat16)], axis=1)
-    all_kv = gather(own_kv, ctx_size, False, 3)
+    own_count = jnp.full((8, 128), jnp.sum(valid_mask.astype(jnp.float32)))
+    all_kv, full_out, counts, down_slice = share(
+        [own_kv, out_weight.T, own_count],
+        ((True, False), (True, True), (False, True)),
+        [jnp.pad(down_weight.T, extra)],
+        slice_width,
+        3,
+    )
+    full_down = lax.all_gather(down_slice, "dp", axis=0, tiled=True)
+    valid_count = jnp.sum(counts[::8, 0])
 
     key_index = jnp.arange(seq_len, dtype=jnp.int32)
     key_place = jnp.where(valid_mask > 0, key_index, -1)[:, None]

time: 781 us -> 782 us (level)
    pallas_call x1 -> x2, Pallas kernels: 78.2 us -> 105 us  [share(): pl.pallas_call(functools.partial(share_kernel, size, groups, kinds, m), i...]
    pallas_call x3 -> x2, Pallas kernels: 38 us -> 15.7 us  [gather(): pl.pallas_call(functools.partial(gather_kernel, size, paired, pieces), in...]
  transfers between devices with their start and end apart: 14 -> 11, of which waited for: 5 -> 4; matrix products, arithmetic and copies ran while one was open for 8% -> 9% of each run, Pallas kernels for 33% -> 37%
where the time goes in v7:
time: 782 us; the launch traced here: 773 us
  Pallas kernels  535 us (68%)
  waiting for transfers between devices  90.1 us (12%)
  matrix products  59.8 us (8%)
  local copies, waits for them, and re-layouts  35.9 us (5%)
  other arithmetic  31.3 us (4%)
  between operations  17.4 us (2%)
    pallas_call x2, Pallas kernels, sum_apply(): pl.pallas_call(functools.partial(sum_apply_kernel, size, pieces, count),...  149 us
    pallas_call x2, Pallas kernels, gather_apply(): pl.pallas_call(functools.partial(gather_apply_kernel, size, pieces, work,...  119 us
    pallas_call x2, Pallas kernels, share(): pl.pallas_call(functools.partial(share_kernel, size, groups, kinds, m), i...  105 us
    pallas_call x1, Pallas kernels, back(): pl.pallas_call(functools.partial(back_kernel, size, groups), in_specs=[AN...  63.5 us
    ppermute x3, waiting for transfers between devices, exchange(): lax.ppermute(going, axis, [(i, (i + step) % size) for i in range(size)])  58.3 us
    dot_general x5, matrix products, matmul_tn(): lax.dot_general(first_op, second_op, (((0,), (0,)), ((), ())), preferred_...  47.5 us
    pallas_call x2, Pallas kernels, scatter(): pl.pallas_call(functools.partial(scatter_kernel, size, paired, pieces), i...  33.4 us
    reduce_scatter x1, waiting for transfers between devices, per_device(): grad_out = lax.psum_scatter(grad_out, 'dp', scatter_dimension=0, tiled=True)  29.9 us
  transfers between devices with their start and end apart: 11, of which 4 were waited for; matrix products, arithmetic and copies ran while one was open for 9% of the time, Pallas kernels for 37%

profile of v7, /device:TPU:9, one launch (start us, length us, event | category | flops | bytes accessed | tf_op | source)
XLA Modules:
  0.0 773.2 jit_solution(12422872033876256203)
XLA Ops:
  7.3 2.2 pad.17.refs_1_
  9.5 1.0 pad.18.refs_2_
  11.2 53.1 %shard_map.289 = (bf16[1536,1024]{1,0:T(8,128)(2,1)}, bf16[384,1152]{1,0:T(8,128)(2,1)}, bf16[384,1152]{1,0:T(8,128)(2,1)}) custom-call(bf16[96,1024]{1,0:T(8,128)(2,1)} %pad_maximum_fusion.6.refs_0_, bf16[96,4608]{1,0:T(8,128)(2,1)} %pad.17.refs_1_, bf16[96,4608]{1,0:T(8,128)(2,1)} %pad.18.refs_2_), custom_call_target="tpu_custom_call" | custom-call | bytes 150000000 | tf_op jit(solution)/shard_map/pallas_call | solution.py:490
  65.5 1.6 convert_multiply_fusion
  67.2 6.2 gather.2
  73.5 4.2 convolution_add_fusion
  77.6 1.4 slice.135
  79.7 2.8 copy.40
  82.5 1.4 dynamic-slice_convert_fusion
  83.9 1.2 fusion.2
  85.1 1.7 subtract_convert_fusion.1
  87.1 0.9 copy-done.18
  88.0 1.0 pad.19.refs_3_
  90.3 1.2 broadcast_in_dim.13.refs_2_
  91.6 51.5 %shard_map.290 = (bf16[2048,256]{1,0:T(8,128)(2,1)}, bf16[1536,768]{1,0:T(8,128)(2,1)}, f32[32,128]{1,0:T(8,128)}, bf16[384,1152]{1,0:T(8,128)(2,1)}) custom-call(bf16[512,256]{1,0:T(8,128)(2,1)} %pad_maximum_fusion.5.refs_0_, bf16[96,768]{1,0:T(8,128)(2,1)} %bitcast.76, f32[8,128]{1,0:T(8,128)} %broadcast_in_dim.13.refs_2_, bf16[96,4608]{1,0:T(8,128)(2,1)} %pad.19.refs_3_), custom_call_target="tpu_custom_call" | custom-call | bytes 150000000 | tf_op jit(solution)/shard_map/pallas_call | solution.py:490
  143.2 2.3 copy.43
  145.5 2.1 slice_bitcast_fusion.5
  147.5 1.0 copy.45.k_ref
  148.5 0.9 fusion.5
  149.4 1.0 copy.46.vt_ref
  150.4 1.1 copy.54.q_ref
  151.6 1.3 copy.44.place_ref
  152.9 19.2 %attend.1 = (bf16[512,768]{1,0:T(8,128)(2,1)}, f32[6,1,512]{2,1,0:T(1,128)}) custom-call(s32[1]{0:T(128)} %bitcast.first_ref, s32[1,512]{1,0:T(1,128)} %bitcast.78, s32[2048,1]{1,0:T(8,128)} %copy.44.place_ref, bf16[512,768]{1,0:T(8,128)(2,1)} %copy.54.q_ref, bf16[2048,128]{1,0:T(8,128)(2,1)} %copy.45.k_ref, bf16[128,2048]{1,0:T(8,128)(2,1)} %copy.46.vt_ref), custom_call_target="tpu_custom_call" | custom-call | flops 3221225472 | bytes 1572864 | tf_op jit(solution)/shard_map/attend/pallas_call | solution.py:1237
  172.1 4.2 fusion.7.x_ref
  176.3 8.8 %scatter.9 = f32[256,1536]{1,0:T(8,128)} custom-call(f32[512,1536]{1,0:T(8,128)} %fusion.7.x_ref), custom_call_target="tpu_custom_call" | custom-call | bytes 23592960 | tf_op jit(solution)/shard_map/scatter/pallas_call | solution.py:340
  187.2 1.7 multiply_reduce_fusion.3
  188.9 1.1 multiply_convert_fusion.refs_0_
  190.0 57.8 %shard_map.291 = (bf16[2048,1536]{1,0:T(8,128)(2,1)}, bf16[2048,1152]{1,0:T(8,128)(2,1)}, bf16[2048,1152]{1,0:T(8,128)(2,1)}, bf16[2048,1152]{1,0:T(8,128)(2,1)}) custom-call(bf16[256,1536]{1,0:T(8,128)(2,1)} %multiply_convert_fusion.refs_0_, bf16[1536,1152]{1,0:T(8,128)(2,1)} %all-gather.4.cloned.1.call-done.refs_1_.refs_2_, ...), custom_call_target="tpu_custom_call" | custom-call | bytes 200000000 | tf_op jit(solution)/shard_map/pallas_call | solution.py:834
  247.9 70.5 %shard_map.292 = f32[256,1536]{1,0:T(8,128)} custom-call(bf16[2048,1152]{1,0:T(8,128)(2,1)} %get-tuple-element.72.refs_0_, bf16[1536,1152]{1,0:T(8,128)(2,1)} %all-gather.8.cloned.1.call-done.refs_1_), custom_call_target="tpu_custom_call" | custom-call | bytes 200000000 | tf_op jit(solution)/shard_map/pallas_call | solution.py:1007
  318.4 3.0 fusion.3.refs_0_
  321.4 60.8 %shard_map.293 = (bf16[2048,1536]{1,0:T(8,128)(2,1)}, bf16[2048,1152]{1,0:T(8,128)(2,1)}, bf16[2048,1152]{1,0:T(8,128)(2,1)}) custom-call(bf16[256,1536]{1,0:T(8,128)(2,1)} %fusion.3.refs_0_, bf16[1536,1152]{1,0:T(8,128)(2,1)} %all-gather.8.cloned.1.call-done.refs_1_, bf16[2048,1152]{1,0:T(8,128)(2,1)} %get-tuple-element.75.refs_2_, ...), custom_call_target="tpu_custom_call" | custom-call | bytes 200000000 | tf_op jit(solution)/shard_map/pallas_call | solution.py:834
  382.2 13.2 %convolution_convert_fusion = bf16[1536,1152]{1,0:T(8,128)(2,1)} fusion(bf16[2048,1536]{1,0:T(8,128)(2,1)} %get-tuple-element.82, bf16[2048,1152]{1,0:T(8,128)(2,1)} %get-tuple-element.86.refs_1_), kind=kOutput, calls=%fused_computation | convolution fusion | flops 7249526784 | bytes 14548992 | tf_op jit(solution)/shard_map/dot_general | solution.py:48
  395.4 13.1 %convolution_convert_fusion.1 = bf16[1536,1152]{1,0:T(8,128)(2,1)} fusion(bf16[2048,1536]{1,0:T(8,128)(2,1)} %get-tuple-element.82, bf16[2048,1152]{1,0:T(8,128)(2,1)} %get-tuple-element.85.refs_0_), kind=kOutput, calls=%fused_computation.1 | convolution fusion | flops 7249526784 | bytes 14548992 | tf_op jit(solution)/shard_map/dot_general | solution.py:48
  408.5 13.5 %convolution_convert_fusion.2 = bf16[1536,1152]{1,0:T(8,128)(2,1)} fusion(bf16[2048,1536]{1,0:T(8,128)(2,1)} %get-tuple-element.79, bf16[2048,1152]{1,0:T(8,128)(2,1)} %get-tuple-element.72.refs_0_), kind=kOutput, calls=%fused_computation.2 | convolution fusion | flops 7249526784 | bytes 14548992 | tf_op jit(solution)/shard_map/dot_general | solution.py:48
  423.3 78.3 %shard_map.294 = f32[256,1536]{1,0:T(8,128)} custom-call(bf16[2048,1152]{1,0:T(8,128)(2,1)} %get-tuple-element.85.refs_0_, bf16[2048,1152]{1,0:T(8,128)(2,1)} %get-tuple-element.86.refs_1_, bf16[1536,1152]{1,0:T(8,128)(2,1)} %all-gather.4.cloned.1.call-done.refs_1_.refs_2_, bf16[1536,1152]{1,0:T(8,128)(2,1)} %all-gather.6.cloned.1.call-done.refs_2_.refs_3_), custom_call_target="tpu_custom_call" | custom-call | bytes 200000000 | tf_op jit(solution)/shard_map/pallas_call | solution.py:1007
  501.6 3.2 multiply_reduce_fusion.1
  504.8 2.5 fusion.4
  507.4 9.5 %gather.3 = bf16[512,1536]{1,0:T(8,128)(2,1)} custom-call(bf16[256,1536]{1,0:T(8,128)(2,1)} %get-tuple-element.108.x_ref), custom_call_target="tpu_custom_call" | custom-call | bytes 23592960 | tf_op jit(solution)/shard_map/gather/pallas_call | solution.py:208
  516.9 4.2 convolution_convert_fusion.4
  522.6 4.0 convolution_convert_fusion.5.do_ref
  526.5 26.6 %attend_back.1 = (f32[512,768]{1,0:T(8,128)}, bf16[2048,256]{1,0:T(8,128)(2,1)}) custom-call(s32[1]{0:T(128)} %bitcast.first_ref, s32[1,512]{1,0:T(1,128)} %bitcast.79, s32[2048,1]{1,0:T(8,128)} %copy.44.place_ref, bf16[512,768]{1,0:T(8,128)(2,1)} %copy.54.q_ref, bf16[512,768]{1,0:T(8,128)(2,1)} %convolution_convert_fusion.5.do_ref, ...), custom_call_target="tpu_custom_call" | custom-call | flops 8053063680 | bytes 3145728 | tf_op jit(solution)/shard_map/attend_back/pallas_call | solution.py:1274
  553.2 24.7 %scatter.10 = f32[512,256]{1,0:T(8,128)} custom-call(bf16[2048,256]{1,0:T(8,128)(2,1)} %get-tuple-element.89.x_ref), custom_call_target="tpu_custom_call" | custom-call | bytes 15728640 | tf_op jit(solution)/shard_map/scatter/pallas_call | solution.py:340
  577.9 1.0 slice.114
  578.9 1.6 slice.165
  580.7 1.8 copy.49
  582.4 1.8 subtract_convert_fusion
  584.9 1.2 pad_maximum_fusion.2.p_ref
  586.1 29.9 %reduce-scatter.12.cloned.1.call-done = bf16[384,768]{1,0:T(8,128)(2,1)} async-done(((bf16[1536,768]{1,0:T(8,128)(2,1)}), bf16[384,768]{1,0:T(8,128)(2,1)}) %reduce-scatter.12.cloned.1.call-update) | async-done | bytes 589840 | tf_op jit(solution)/shard_map/reduce_scatter | solution.py:1269
  616.2 3.5 convolution_convert_fusion.3.x_ref
  621.3 63.5 %back.1 = (f32[96,1024]{1,0:T(8,128)}, f32[48,128]{1,0:T(8,128)}, f32[256,1536]{1,0:T(8,128)}) custom-call(bf16[1536,1024]{1,0:T(8,128)(2,1)} %convolution_convert_fusion.3.x_ref, f32[48,128]{1,0:T(8,128)} %pad_bitcast_fusion.s_ref, bf16[512,1024]{1,0:T(8,128)(2,1)} %copy-done.4, bf16[1536,1024]{1,0:T(8,128)(2,1)} %get-tuple-element.66.w_ref, ...), custom_call_target="tpu_custom_call" | custom-call | bytes 157286400 | tf_op jit(solution)/shard_map/back/pallas_call | solution.py:625
  684.8 1.4 slice_bitcast_fusion
  686.2 1.3 slice_bitcast_fusion.3
  687.9 1.3 dynamic-slice_bitcast_fusion
  689.2 2.0 collective-permute-start.1
  691.2 1.5 collective-permute-start.2
  693.4 1.8 multiply_reduce_fusion
  695.2 0.7 slice.124
  695.9 1.2 slice.121
  697.8 3.0 multiply_add_fusion
  700.8 6.9 collective-permute-done.refs_1_
  707.7 47.1 %collective-permute-done.1.refs_2_ = bf16[3,96,1152]{2,1,0:T(8,128)(2,1)} collective-permute-done((bf16[3,96,1152]{2,1,0:T(8,128)(2,1)}, bf16[3,96,1152]{2,1,0:T(8,128)(2,1)}, u32[]{:S(2)}, u32[]{:S(2)}) %collective-permute-start.1) | collective-permute-done | bytes 663584 | tf_op jit(solution)/shard_map/ppermute | solution.py:70
  754.8 4.2 collective-permute-done.2.refs_3_
  759.1 4.4 assemble.1
  763.4 1.6 convert_bitcast_fusion
  (142 shorter events, 12.1 us)
Async XLA Ops:
  7.2 2.3 copy-start.17
  7.2 3.3 copy-start.22
  7.2 3.2 copy-start.25
  7.2 3.2 copy-start.24
  7.2 182.7 %all-gather.4.cloned.1.call-start = ((), (), s32[]{:S(2)}) async-start(), calls=%async_computation.5 | async-start | bytes 4423680 | tf_op jit(solution)/shard_map/all_gather | solution.py:1195
  11.2 54.0 %copy-start.34 = (bf16[256]{0:T(256)(128)(2,1)S(1)}, bf16[256]{0:T(256)(128)(2,1)}, u32[]{:S(2)}) copy-start(bf16[256]{0:T(256)(128)(2,1)} %param.30) | copy-start | bytes 1540
  11.2 54.1 %copy-start.35 = (bf16[256]{0:T(256)(128)(2,1)S(1)}, bf16[256]{0:T(256)(128)(2,1)}, u32[]{:S(2)}) copy-start(bf16[256]{0:T(256)(128)(2,1)} %param.32) | copy-start | bytes 1540
  11.2 54.1 %copy-start.30 = (bf16[1536]{0:T(1024)(128)(2,1)S(1)}, bf16[1536]{0:T(1024)(128)(2,1)}, u32[]{:S(2)}) copy-start(bf16[1536]{0:T(1024)(128)(2,1)} %param.26) | copy-start | bytes 9220
  11.2 54.1 %copy-start.1 = (bf16[256,1536]{1,0:T(8,128)(2,1)S(1)}, bf16[256,1536]{1,0:T(8,128)(2,1)}, u32[]{:S(2)}) copy-start(bf16[256,1536]{1,0:T(8,128)(2,1)} %param.20) | copy-start | bytes 2359300
  64.3 125.7 %all-gather.6.cloned.1.call-start = ((), (), s32[]{:S(2)}) async-start(), calls=%async_computation.6 | async-start | bytes 4423680 | tf_op jit(solution)/shard_map/all_gather | solution.py:1195
  65.1 182.8 %all-gather.8.cloned.1.call-start = ((), (), s32[]{:S(2)}) async-start(), calls=%async_computation.7 | async-start | bytes 4423680 | tf_op jit(solution)/shard_map/all_gather | solution.py:1223
  65.5 1.7 copy-start.28
  67.2 6.2 copy-start.32
  86.8 1.2 copy-start.18
  86.9 2.1 copy-start.23
  86.9 2.6 copy-start.20
  143.1 434.8 %reduce-scatter.10.cloned.1.call-start = ((), (), s32[]{:S(2)}) async-start(), calls=%async_computation.10 | async-start | bytes 4423680 | tf_op jit(solution)/shard_map/reduce_scatter | solution.py:1261
  145.5 3.1 copy-start.10
  152.9 19.2 %copy-start.33 = (bf16[1536,768]{1,0:T(8,128)(2,1)S(1)}, bf16[1536,768]{1,0:T(8,128)(2,1)}, u32[]{:S(2)}) copy-start(bf16[1536,768]{1,0:T(8,128)(2,1)} %get-tuple-element.69) | copy-start | bytes 7077892
  176.3 8.8 %copy-start.31 = (bf16[1536]{0:T(1024)(128)(2,1)S(1)}, bf16[1536]{0:T(1024)(128)(2,1)}, u32[]{:S(2)}) copy-start(bf16[1536]{0:T(1024)(128)(2,1)} %param.34) | copy-start | bytes 9220
  247.8 70.6 %copy-start.5 = (bf16[256,1536]{1,0:T(8,128)(2,1)S(1)}, bf16[256,1536]{1,0:T(8,128)(2,1)}, u32[]{:S(2)}) copy-start(bf16[256,1536]{1,0:T(8,128)(2,1)} %param.21) | copy-start | bytes 2359300
  247.9 70.6 %copy-start.8 = (bf16[256,1536]{1,0:T(8,128)(2,1)S(1)}, bf16[256,1536]{1,0:T(8,128)(2,1)}, u32[]{:S(2)}) copy-start(bf16[256,1536]{1,0:T(8,128)(2,1)} %param.22) | copy-start | bytes 2359300
  422.0 155.9 %reduce-scatter.8.cloned.1.call-start = ((), (), s32[]{:S(2)}) async-start(), calls=%async_computation.9 | async-start | bytes 4423680 | tf_op jit(solution)/shard_map/reduce_scatter | solution.py:1261
  422.6 155.3 %reduce-scatter.6.cloned.1.call-start = ((), (), s32[]{:S(2)}) async-start(), calls=%async_computation.8 | async-start | bytes 4423680 | tf_op jit(solution)/shard_map/reduce_scatter | solution.py:1261
  423.2 78.3 %copy-start = (f32[256,1536]{1,0:T(8,128)S(1)}, f32[256,1536]{1,0:T(8,128)}, u32[]{:S(2)}) copy-start(f32[256,1536]{1,0:T(8,128)} %shard_map.292) | copy-start | bytes 4718596
  423.2 192.8 %reduce-scatter.12.cloned.1.call-start = ((), (), s32[]{:S(2)}) async-start(), calls=%async_computation.11 | async-start | bytes 2949120 | tf_op jit(solution)/shard_map/reduce_scatter | solution.py:1269
  423.3 78.3 %copy-start.6 = (bf16[256,1536]{1,0:T(8,128)(2,1)S(1)}, bf16[256,1536]{1,0:T(8,128)(2,1)}, u32[]{:S(2)}) copy-start(bf16[256,1536]{1,0:T(8,128)(2,1)} %param.21) | copy-start | bytes 2359300
  501.6 3.3 copy-start.3
  501.6 3.3 copy-start.9
  507.4 9.5 %copy-start.36 = (bf16[512,768]{1,0:T(8,128)(2,1)S(1)}, bf16[512,768]{1,0:T(8,128)(2,1)}, u32[]{:S(2)}) copy-start(bf16[512,768]{1,0:T(8,128)(2,1)} %get-tuple-element.68) | copy-start | bytes 2359300
  521.1 1.4 copy-start.13
  521.2 242.3 %reduce-scatter.14.cloned.1.call-start = ((), (), s32[]{:S(2)}) async-start(), calls=%async_computation.12 | async-start | bytes 737280 | tf_op jit(solution)/shard_map/reduce_scatter | solution.py:1296
  553.2 27.4 %copy-start.11 = (f32[512,768]{1,0:T(8,128)S(1)}, f32[512,768]{1,0:T(8,128)}, u32[]{:S(2)}) copy-start(f32[512,768]{1,0:T(8,128)} %get-tuple-element.88) | copy-start | bytes 4718596
  577.9 2.7 copy-start.26
  580.7 1.8 copy-start.19
  584.9 31.3 %copy-start.12 = (bf16[512,1536]{1,0:T(8,128)(2,1)S(1)}, bf16[512,1536]{1,0:T(8,128)(2,1)}, u32[]{:S(2)}) copy-start(bf16[512,1536]{1,0:T(8,128)(2,1)} %gather.2) | copy-start | bytes 4718596
  586.1 33.6 %copy-start.4 = (bf16[512,1024]{1,0:T(8,128)(2,1)}, bf16[512,1024]{1,0:T(8,128)(2,1)S(1)}, u32[]{:S(2)}) copy-start(bf16[512,1024]{1,0:T(8,128)(2,1)S(1)} %pad_maximum_fusion.2.p_ref) | copy-start | bytes 3145732
  616.2 3.8 copy-start.27
  621.3 66.2 %copy-start.14 = (bf16[384,1152]{1,0:T(8,128)(2,1)S(1)}, bf16[384,1152]{1,0:T(8,128)(2,1)}, u32[]{:S(2)}) copy-start(bf16[384,1152]{1,0:T(8,128)(2,1)} %reduce-scatter.10.cloned.1.call-done) | copy-start | bytes 2654212
  621.3 66.3 %copy-start.15 = (bf16[384,1152]{1,0:T(8,128)(2,1)S(1)}, bf16[384,1152]{1,0:T(8,128)(2,1)}, u32[]{:S(2)}) copy-start(bf16[384,1152]{1,0:T(8,128)(2,1)} %reduce-scatter.8.cloned.1.call-done) | copy-start | bytes 2654212
  621.3 66.3 %copy-start.16 = (bf16[384,1152]{1,0:T(8,128)(2,1)S(1)}, bf16[384,1152]{1,0:T(8,128)(2,1)}, u32[]{:S(2)}) copy-start(bf16[384,1152]{1,0:T(8,128)(2,1)} %reduce-scatter.6.cloned.1.call-done) | copy-start | bytes 2654212
  687.9 4.8 copy-start.21
  687.9 5.5 copy-start.2
  687.9 5.5 copy-start.29
  689.2 18.5 %collective-permute-start = (bf16[3,96,1152]{2,1,0:T(8,128)(2,1)}, bf16[3,96,1152]{2,1,0:T(8,128)(2,1)}, u32[]{:S(2)}, u32[]{:S(2)}) collective-permute-start(bf16[3,96,1152]{2,1,0:T(8,128)(2,1)} %get-tuple-element.117), channel_id=1, source_target_pairs={{0,2},{2,4},{4,6},{6,0},{1,3},{3,5},{5,7},{7,1},{8,10},{10,12},{12... | collective-permute-start | bytes 1990664 | tf_op jit(solution)/shard_map/ppermute | solution.py:70
  689.2 65.6 %collective-permute-start.1 = (bf16[3,96,1152]{2,1,0:T(8,128)(2,1)}, bf16[3,96,1152]{2,1,0:T(8,128)(2,1)}, u32[]{:S(2)}, u32[]{:S(2)}) collective-permute-start(bf16[3,96,1152]{2,1,0:T(8,128)(2,1)} %get-tuple-element.116), channel_id=1, source_target_pairs={{0,4},{2,6},{4,0},{6,2},{1,5},{3,7},{5,1},{7,3},{8,12},{10,14},{12... | collective-permute-start | bytes 1990664 | tf_op jit(solution)/shard_map/ppermute | solution.py:70
  691.2 67.9 %collective-permute-start.2 = (bf16[3,96,1152]{2,1,0:T(8,128)(2,1)S(1)}, bf16[3,96,1152]{2,1,0:T(8,128)(2,1)}, u32[]{:S(2)}, u32[]{:S(2)}) collective-permute-start(bf16[3,96,1152]{2,1,0:T(8,128)(2,1)S(1)} %get-tuple-element.115), channel_id=1, source_target_pairs={{0,6},{2,0},{4,2},{6,4},{1,7},{3,1},{5,3},{7,5},{8,14},{10,8},{12,... | collective-permute-start | bytes 1990664 | tf_op jit(solution)/shard_map/ppermute | solution.py:70
  692.7 5.0 copy-start.7
Sparse Core Ops, SparseCore 0:
  64.4 77.0 all-gather.3
  143.4 46.0 all-gather.5
  191.3 47.1 all-gather.7
  422.2 53.0 reduce-scatter.9
  478.2 47.1 reduce-scatter.7
  528.3 47.1 reduce-scatter.5
  578.6 37.3 reduce-scatter.11
  692.8 54.1 reduce-scatter.13

commit v8 on v7

--- a/solution.py
+++ b/solution.py
@@ -854,8 +854,8 @@
 def sum_apply_kernel(size, pieces, count, *refs):
     acts_from, refs = refs[:count], refs[count:]
     weights_from, refs = refs[:count], refs[count:]
-    o_ref, acts, weights, mine, sent, mate, came, load_sem = refs[:8]
-    mate_send, mate_recv, up_send, up_recv, down_send, down_recv = refs[8:]
+    o_ref, acts, weights, mine, sent, mate, came, load_sem, act_sem = refs[:9]
+    mate_send, mate_recv, up_send, up_recv, down_send, down_recv = refs[9:]
     place, core = lax.axis_index("ctx"), lax.axis_index("tensor")
     rows, depth = o_ref.shape
     part = rows // pieces
@@ -864,9 +864,24 @@
     loads = []
     for a in range(count):
         loads.append(pltpu.make_async_copy(weights_from[a], weights.at[a], load_sem.at[a]))
-        loads.append(pltpu.make_async_copy(acts_from[a], acts.at[a], load_sem.at[count + a]))
     for load in loads:
         load.start()
+
+    def load_acts(a, d):
+        span = pl.ds(pl.multiple_of(d * 2 * rows, rows), 2 * rows)
+        return pltpu.make_async_copy(acts_from[a].at[span], acts.at[a, span], act_sem.at[a, d])
+
+    short = jnp.minimum(place, last - place)
+
+    def visited(i):
+        s = last - i
+        near = s <= 2 * short
+        d = jnp.where(near, (s + 1) // 2, s - short)
+        return jnp.where(jnp.where(near, s % 2 == 1, place > last - place), place - d, place + d)
+
+    for i in range(size):
+        for a in range(count):
+            load_acts(a, visited(i)).start()
     greet_chain(size, True)
     for load in loads:
         load.wait()
@@ -911,13 +926,10 @@
         to_mate(0, d, p).wait_recv()
         return [at(mine, d, p), at(mate, d, p)]
 
-    short = jnp.minimum(place, last - place)
-
     def first_part(i, carry):
-        s = last - i
-        near = s <= 2 * short
-        d = jnp.where(near, (s + 1) // 2, s - short)
-        d = jnp.where(jnp.where(near, s % 2 == 1, place > last - place), place - d, place + d)
+        d = visited(i)
+        for a in range(count):
+            load_acts(a, d).wait()
         for p in range(pieces):
             pl.when(i >= 2)(lambda p=p: to_mate(i, d, p).wait_send())
         compute(d, 1 - core, sent.at[lax.rem(i, 2)])
@@ -1001,7 +1013,8 @@
         slots(2),
         slots(size),
         slots(size + 1),
-        dma((2 * count,)),
+        dma((count,)),
+        dma((count, size)),
         dma((2, pieces)),
     ] + [dma((size, pieces))] * 5
     return pl.pallas_call(
@@ -1051,7 +1064,11 @@
     bias_ref[...] = jnp.where(allowed, 0.0, VERY_LOW)
 
 
-def attend_kernel(scale, first_ref, seg_ref, place_ref, q_ref, k_ref, vt_ref, o_ref, lse_ref, bias_ref):
+def attend_kernel(scale, first_ref, seg_ref, place_ref, q_ref, k_ref, v_ref, o_ref, lse_ref, bias_ref, vt_ref):
+    @pl.when((pl.program_id(0) == 0) & (pl.program_id(1) == 0))
+    def _():
+        vt_ref[...] = v_ref[...].T
+
     @pl.when(pl.program_id(1) == 0)
     def _():
         mask_into(bias_ref, first_ref[0] + pl.program_id(0) * q_ref.shape[0], seg_ref, place_ref)
@@ -1066,8 +1083,8 @@
 
 
 def attend_back_kernel(
-    scale, first_ref, seg_ref, place_ref, q_ref, do_ref, lse_ref, k_ref, v_ref, kt_ref,
-    dq_ref, dkv_ref, bias_ref, dk_ref, dv_ref,
+    scale, first_ref, seg_ref, place_ref, q_ref, do_ref, lse_ref, k_ref, v_ref,
+    dq_ref, dkv_ref, bias_ref, dk_ref, dv_ref, kt_ref,
 ):
     block, head = pl.program_id(0), pl.program_id(1)
 
@@ -1077,6 +1094,7 @@
 
     @pl.when((head == 0) & (block == 0))
     def _():
+        kt_ref[...] = k_ref[...].T
         dk_ref[...] = jnp.zeros_like(dk_ref)
         dv_ref[...] = jnp.zeros_like(dv_ref)
 
@@ -1096,29 +1114,30 @@
         dkv_ref[:, HEAD:] = dv_ref[...].astype(jnp.bfloat16)
 
 
-def attention_calls(rows, keys, heads):
+def attention_calls(rows, keys, heads, which):
     block = math.gcd(256, rows)
     scale = 1.0 / math.sqrt(HEAD)
     smem = pl.BlockSpec(memory_space=pltpu.SMEM)
     seg = pl.BlockSpec((1, block), lambda i, h: (0, i))
     place = pl.BlockSpec((keys, 1), lambda i, h: (0, 0))
     head = pl.BlockSpec((block, HEAD), lambda i, h: (i, h))
+    of_all = pl.BlockSpec((block, HEAD), lambda i, h: (i, which * heads + h))
     lse = pl.BlockSpec((1, 1, block), lambda i, h: (h, 0, i))
-    tall = pl.BlockSpec((keys, HEAD), lambda i, h: (0, 0))
-    wide = pl.BlockSpec((HEAD, keys), lambda i, h: (0, 0))
+    tall = pl.BlockSpec((keys, HEAD), lambda i, h: (0, which))
+    turned = pltpu.VMEM((HEAD, keys), jnp.bfloat16)
     params = pltpu.CompilerParams(vmem_limit_bytes=60000000)
     grid = (rows // block, heads)
     size = heads * rows * keys
     forward = pl.pallas_call(
         functools.partial(attend_kernel, scale),
         grid=grid,
-        in_specs=[smem, seg, place, head, tall, wide],
+        in_specs=[smem, seg, place, of_all, tall, tall],
         out_specs=[head, lse],
         out_shape=[
             jax.ShapeDtypeStruct((rows, heads * HEAD), jnp.bfloat16),
             jax.ShapeDtypeStruct((heads, 1, rows), jnp.float32),
         ],
-        scratch_shapes=[pltpu.VMEM((keys, block), jnp.float32)],
+        scratch_shapes=[pltpu.VMEM((keys, block), jnp.float32), turned],
         compiler_params=params,
         cost_estimate=pl.CostEstimate(flops=4 * size * HEAD, bytes_accessed=4 * rows * heads * HEAD, transcendentals=size),
         name="attend",
@@ -1126,7 +1145,7 @@
     backward = pl.pallas_call(
         functools.partial(attend_back_kernel, scale),
         grid=grid,
-        in_specs=[smem, seg, place, head, head, lse, tall, tall, wide],
+        in_specs=[smem, seg, place, of_all, of_all, lse, tall, tall],
         out_specs=[head, pl.BlockSpec((keys, 2 * HEAD), lambda i, h: (0, 0))],
         out_shape=[
             jax.ShapeDtypeStruct((rows, heads * HEAD), jnp.float32),
@@ -1136,6 +1155,7 @@
             pltpu.VMEM((keys, block), jnp.float32),
             pltpu.VMEM((keys, HEAD), jnp.float32),
             pltpu.VMEM((keys, HEAD), jnp.float32),
+            turned,
         ],
         compiler_params=params,
         cost_estimate=pl.CostEstimate(flops=10 * size * HEAD, bytes_accessed=8 * rows * heads * HEAD, transcendentals=size),
@@ -1185,9 +1205,9 @@
     scale_attn = lax.rsqrt(jnp.mean(inputs * inputs, axis=1, keepdims=True) + EPS)
     normed_attn = inputs * scale_attn
     extra = ((0, 0), (0, ctx_size * slice_width - hidden_width))
-    full_qkv, *slices = share(
-        [jnp.concatenate([query_weight, key_weight, value_weight], axis=1)],
-        ((True, True),),
+    full_qkv, full_out, *slices = share(
+        [jnp.concatenate([query_weight, key_weight, value_weight], axis=1), out_weight.T],
+        ((True, True), (True, True)),
         [jnp.pad(w, extra) for w in (gate_weight, up_weight)],
         slice_width,
         1,
@@ -1210,12 +1230,10 @@
         .astype(jnp.bfloat16)
         .reshape(shard_rows, turned)
     )
-    queries = rotated[:, :q_width]
-    own_kv = jnp.concatenate([rotated[:, q_width:], qkv_pre[:, turned:].astype(jnp.bfloat16)], axis=1)
     own_count = jnp.full((8, 128), jnp.sum(valid_mask.astype(jnp.float32)))
-    all_kv, full_out, counts, down_slice = share(
-        [own_kv, out_weight.T, own_count],
-        ((True, False), (True, True), (False, True)),
+    all_keys, all_values, counts, down_slice = share(
+        [rotated[:, q_width:], qkv_pre[:, turned:].astype(jnp.bfloat16), own_count],
+        ((True, False), (True, False), (False, True)),
         [jnp.pad(down_weight.T, extra)],
         slice_width,
         3,
@@ -1228,14 +1246,11 @@
     seq_first = lax.axis_index("dp") * seq_len
     doc_start = (lax.dynamic_slice_in_dim(segment_ids, first_row, shard_rows) - seq_first)[None, :]
     first = jnp.reshape(first_row, (1,)).astype(jnp.int32)
-    forward, backward = attention_calls(shard_rows, seq_len, group)
     kept = []
     for c in range(kv_local):
-        key = all_kv[:, c * HEAD : (c + 1) * HEAD]
-        value = all_kv[:, kv_width + c * HEAD : kv_width + (c + 1) * HEAD]
-        query = queries[:, c * group * HEAD : (c + 1) * group * HEAD]
-        kept.append((query, key, value) + tuple(forward(first, doc_start, key_place, query, key, value.T)))
-    heads_out = jnp.concatenate([k[3] for k in kept], axis=1)
+        forward, backward = attention_calls(shard_rows, seq_len, group, c)
+        kept.append((backward,) + tuple(forward(first, doc_start, key_place, rotated, all_keys, all_values)))
+    heads_out = jnp.concatenate([k[1] for k in kept], axis=1)
     attention = scatter(matmul_nt(heads_out, full_out), 1, True, 4)
     residual_mid = inputs + attention
     scale_mlp = lax.rsqrt(jnp.mean(residual_mid * residual_mid, axis=1, keepdims=True) + EPS)
@@ -1269,10 +1284,9 @@
     grad_out = lax.psum_scatter(grad_out, "dp", scatter_dimension=0, tiled=True)
     query_grads, key_grads, value_grads = [], [], []
     for c in range(kv_local):
-        query, key, value, _, log_total = kept[c]
-        span = slice(c * group * HEAD, (c + 1) * group * HEAD)
+        backward, _, log_total = kept[c]
         grad_query, grad_kv = backward(
-            first, doc_start, key_place, query, grad_heads[:, span], log_total, key, value, key.T
+            first, doc_start, key_place, rotated, grad_heads, log_total, all_keys, all_values
         )
         query_grads.append(grad_query)
         key_grads.append(grad_kv[:, :HEAD])

time: 782 us -> 775 us (level)
  transfers between devices with their start and end apart: 11 -> 11, of which waited for: 4 -> 4; matrix products, arithmetic and copies ran while one was open for 9% -> 8% of each run, Pallas kernels for 37% -> 36%
where the time goes in v8:
time: 775 us; the launch traced here: 767 us
  Pallas kernels  533 us (69%)
  waiting for transfers between devices  92.2 us (12%)
  matrix products  60.3 us (8%)
  other arithmetic  30.5 us (4%)
  local copies, waits for them, and re-layouts  29 us (4%)
  between operations  17.4 us (2%)
    pallas_call x2, Pallas kernels, sum_apply(): pl.pallas_call(functools.partial(sum_apply_kernel, size, pieces, count),...  149 us
    pallas_call x2, Pallas kernels, gather_apply(): pl.pallas_call(functools.partial(gather_apply_kernel, size, pieces, work,...  120 us
    pallas_call x2, Pallas kernels, share(): pl.pallas_call(functools.partial(share_kernel, size, groups, kinds, m), i...  100 us
    pallas_call x1, Pallas kernels, back(): pl.pallas_call(functools.partial(back_kernel, size, groups), in_specs=[AN...  63.6 us
    ppermute x3, waiting for transfers between devices, exchange(): lax.ppermute(going, axis, [(i, (i + step) % size) for i in range(size)])  58.3 us
    dot_general x5, matrix products, matmul_tn(): lax.dot_general(first_op, second_op, (((0,), (0,)), ((), ())), preferred_...  47.5 us
    pallas_call x2, Pallas kernels, scatter(): pl.pallas_call(functools.partial(scatter_kernel, size, paired, pieces), i...  36.1 us
    reduce_scatter x1, waiting for transfers between devices, per_device(): grad_out = lax.psum_scatter(grad_out, 'dp', scatter_dimension=0, tiled=True)  32 us
  transfers between devices with their start and end apart: 11, of which 4 were waited for; matrix products, arithmetic and copies ran while one was open for 8% of the time, Pallas kernels for 36%

profile of v8, /device:TPU:9, one launch (start us, length us, event | category | flops | bytes accessed | tf_op | source)
XLA Modules:
  0.0 766.7 jit_solution(6581569642419683542)
XLA Ops:
  7.3 2.2 pad.17.refs_2_
  9.5 1.0 pad.18.refs_3_
  10.5 0.7 pad_maximum_fusion.5.refs_0_
  11.2 65.9 %shard_map.289 = (bf16[1536,1024]{1,0:T(8,128)(2,1)}, bf16[1536,768]{1,0:T(8,128)(2,1)}, bf16[384,1152]{1,0:T(8,128)(2,1)}, bf16[384,1152]{1,0:T(8,128)(2,1)}) custom-call(bf16[96,1024]{1,0:T(8,128)(2,1)} %pad_maximum_fusion.5.refs_0_, bf16[96,768]{1,0:T(8,128)(2,1)} %bitcast.71, bf16[96,4608]{1,0:T(8,128)(2,1)} %pad.17.refs_2_, bf16[96,4608]{1,0:T(8,128)(2,1)} %pad.18.refs_3_), custom_call_target="tpu_custom_call" | custom-call | bytes 150000000 | tf_op jit(solution)/shard_map/pallas_call | solution.py:490
  77.2 0.7 all-gather.6.cloned.1.call-update
  78.3 1.7 convert_multiply_fusion
  80.1 5.2 gather.2
  85.4 4.6 convolution_add_fusion
  90.0 1.4 slice.123
  91.3 0.7 slice.150.refs_1_
  92.0 2.8 copy.36
  94.8 1.4 dynamic-slice_convert_fusion
  96.2 1.2 fusion.2
  97.4 1.7 subtract_convert_fusion.1
  99.9 0.7 slice.126.refs_0_
  100.6 2.1 pad.19.refs_3_
  103.3 1.2 broadcast_in_dim.13.refs_2_
  104.5 34.6 %shard_map.290 = (bf16[2048,128]{1,0:T(8,128)(2,1)}, bf16[2048,128]{1,0:T(8,128)(2,1)}, f32[32,128]{1,0:T(8,128)}, bf16[384,1152]{1,0:T(8,128)(2,1)}) custom-call(bf16[512,128]{1,0:T(8,128)(2,1)} %slice.126.refs_0_, bf16[512,128]{1,0:T(8,128)(2,1)} %slice.150.refs_1_, f32[8,128]{1,0:T(8,128)} %broadcast_in_dim.13.refs_2_, bf16[96,4608]{1,0:T(8,128)(2,1)} %pad.19.refs_3_), custom_call_target="tpu_custom_call" | custom-call | bytes 150000000 | tf_op jit(solution)/shard_map/pallas_call | solution.py:490
  139.2 1.3 copy.38.place_ref
  140.6 19.4 %attend.1 = (bf16[512,768]{1,0:T(8,128)(2,1)}, f32[6,1,512]{2,1,0:T(1,128)}) custom-call(s32[1]{0:T(128)} %bitcast.first_ref, s32[1,512]{1,0:T(1,128)} %bitcast.73, s32[2048,1]{1,0:T(8,128)} %copy.38.place_ref, bf16[512,896]{1,0:T(8,128)(2,1)} %copy-done.13, bf16[2048,128]{1,0:T(8,128)(2,1)} %get-tuple-element.68.k_ref, ...), custom_call_target="tpu_custom_call" | custom-call | flops 3221225472 | bytes 1572864 | tf_op jit(solution)/shard_map/attend/pallas_call | solution.py:1252
  160.0 4.2 fusion.6.x_ref
  164.2 10.9 %scatter.9 = f32[256,1536]{1,0:T(8,128)} custom-call(f32[512,1536]{1,0:T(8,128)} %fusion.6.x_ref), custom_call_target="tpu_custom_call" | custom-call | bytes 23592960 | tf_op jit(solution)/shard_map/scatter/pallas_call | solution.py:340
  175.1 0.7 slice.101
  177.2 1.7 multiply_reduce_fusion.3
  178.9 1.1 multiply_convert_fusion.refs_0_
  180.0 58.9 %shard_map.291 = (bf16[2048,1536]{1,0:T(8,128)(2,1)}, bf16[2048,1152]{1,0:T(8,128)(2,1)}, bf16[2048,1152]{1,0:T(8,128)(2,1)}, bf16[2048,1152]{1,0:T(8,128)(2,1)}) custom-call(bf16[256,1536]{1,0:T(8,128)(2,1)} %multiply_convert_fusion.refs_0_, bf16[1536,1152]{1,0:T(8,128)(2,1)} %all-gather.4.cloned.1.call-done.refs_1_.refs_2_, ...), custom_call_target="tpu_custom_call" | custom-call | bytes 200000000 | tf_op jit(solution)/shard_map/pallas_call | solution.py:834
  238.9 70.4 %shard_map.292 = f32[256,1536]{1,0:T(8,128)} custom-call(bf16[2048,1152]{1,0:T(8,128)(2,1)} %get-tuple-element.74.refs_0_, bf16[1536,1152]{1,0:T(8,128)(2,1)} %all-gather.8.cloned.1.call-done.refs_1_), custom_call_target="tpu_custom_call" | custom-call | bytes 200000000 | tf_op jit(solution)/shard_map/pallas_call | solution.py:1020
  309.3 3.0 fusion.3.refs_0_
  312.3 60.8 %shard_map.293 = (bf16[2048,1536]{1,0:T(8,128)(2,1)}, bf16[2048,1152]{1,0:T(8,128)(2,1)}, bf16[2048,1152]{1,0:T(8,128)(2,1)}) custom-call(bf16[256,1536]{1,0:T(8,128)(2,1)} %fusion.3.refs_0_, bf16[1536,1152]{1,0:T(8,128)(2,1)} %all-gather.8.cloned.1.call-done.refs_1_, bf16[2048,1152]{1,0:T(8,128)(2,1)} %get-tuple-element.77.refs_2_, ...), custom_call_target="tpu_custom_call" | custom-call | bytes 200000000 | tf_op jit(solution)/shard_map/pallas_call | solution.py:834
  373.1 13.2 %convolution_convert_fusion = bf16[1536,1152]{1,0:T(8,128)(2,1)} fusion(bf16[2048,1536]{1,0:T(8,128)(2,1)} %get-tuple-element.84, bf16[2048,1152]{1,0:T(8,128)(2,1)} %get-tuple-element.88.refs_1_), kind=kOutput, calls=%fused_computation | convolution fusion | flops 7249526784 | bytes 14548992 | tf_op jit(solution)/shard_map/dot_general | solution.py:48
  386.3 13.1 %convolution_convert_fusion.1 = bf16[1536,1152]{1,0:T(8,128)(2,1)} fusion(bf16[2048,1536]{1,0:T(8,128)(2,1)} %get-tuple-element.84, bf16[2048,1152]{1,0:T(8,128)(2,1)} %get-tuple-element.87.refs_0_), kind=kOutput, calls=%fused_computation.1 | convolution fusion | flops 7249526784 | bytes 14548992 | tf_op jit(solution)/shard_map/dot_general | solution.py:48
  399.4 13.5 %convolution_convert_fusion.2 = bf16[1536,1152]{1,0:T(8,128)(2,1)} fusion(bf16[2048,1536]{1,0:T(8,128)(2,1)} %get-tuple-element.81, bf16[2048,1152]{1,0:T(8,128)(2,1)} %get-tuple-element.74.refs_0_), kind=kOutput, calls=%fused_computation.2 | convolution fusion | flops 7249526784 | bytes 14548992 | tf_op jit(solution)/shard_map/dot_general | solution.py:48
  414.2 78.4 %shard_map.294 = f32[256,1536]{1,0:T(8,128)} custom-call(bf16[2048,1152]{1,0:T(8,128)(2,1)} %get-tuple-element.87.refs_0_, bf16[2048,1152]{1,0:T(8,128)(2,1)} %get-tuple-element.88.refs_1_, bf16[1536,1152]{1,0:T(8,128)(2,1)} %all-gather.4.cloned.1.call-done.refs_1_.refs_2_, bf16[1536,1152]{1,0:T(8,128)(2,1)} %all-gather.6.cloned.1.call-done.refs_2_.refs_3_), custom_call_target="tpu_custom_call" | custom-call | bytes 200000000 | tf_op jit(solution)/shard_map/pallas_call | solution.py:1020
  492.6 3.2 multiply_reduce_fusion.1
  495.9 2.5 fusion.4
  498.4 9.2 %gather.3 = bf16[512,1536]{1,0:T(8,128)(2,1)} custom-call(bf16[256,1536]{1,0:T(8,128)(2,1)} %get-tuple-element.110.x_ref), custom_call_target="tpu_custom_call" | custom-call | bytes 23592960 | tf_op jit(solution)/shard_map/gather/pallas_call | solution.py:208
  507.7 4.2 convolution_convert_fusion.4
  512.6 0.7 copy-done.12
  513.3 4.0 convolution_convert_fusion.5.do_ref
  517.3 26.6 %attend_back.1 = (f32[512,768]{1,0:T(8,128)}, bf16[2048,256]{1,0:T(8,128)(2,1)}) custom-call(s32[1]{0:T(128)} %bitcast.first_ref, s32[1,512]{1,0:T(1,128)} %bitcast.74, s32[2048,1]{1,0:T(8,128)} %copy.38.place_ref, bf16[512,896]{1,0:T(8,128)(2,1)} %copy-done.13, bf16[512,768]{1,0:T(8,128)(2,1)} %convolution_convert_fusion.5.do_ref, ...), custom_call_target="tpu_custom_call" | custom-call | flops 8053063680 | bytes 3145728 | tf_op jit(solution)/shard_map/attend_back/pallas_call | solution.py:1288
  543.9 25.2 %scatter.10 = f32[512,256]{1,0:T(8,128)} custom-call(bf16[2048,256]{1,0:T(8,128)(2,1)} %get-tuple-element.91.x_ref), custom_call_target="tpu_custom_call" | custom-call | bytes 15728640 | tf_op jit(solution)/shard_map/scatter/pallas_call | solution.py:340
  569.3 1.0 slice.102
  570.2 1.6 slice.149
  572.0 1.8 copy.42
  573.8 1.8 subtract_convert_fusion
  576.2 1.2 pad_maximum_fusion.2.p_ref
  577.4 32.0 %reduce-scatter.12.cloned.1.call-done = bf16[384,768]{1,0:T(8,128)(2,1)} async-done(((bf16[1536,768]{1,0:T(8,128)(2,1)}), bf16[384,768]{1,0:T(8,128)(2,1)}) %reduce-scatter.12.cloned.1.call-update) | async-done | bytes 589840 | tf_op jit(solution)/shard_map/reduce_scatter | solution.py:1284
  609.6 3.5 convolution_convert_fusion.3.x_ref
  613.4 0.7 constant_dynamic-update-slice_fusion
  614.6 63.6 %back.1 = (f32[96,1024]{1,0:T(8,128)}, f32[48,128]{1,0:T(8,128)}, f32[256,1536]{1,0:T(8,128)}) custom-call(bf16[1536,1024]{1,0:T(8,128)(2,1)} %convolution_convert_fusion.3.x_ref, f32[48,128]{1,0:T(8,128)} %pad_bitcast_fusion.s_ref, bf16[512,1024]{1,0:T(8,128)(2,1)} %copy-done.4, bf16[1536,1024]{1,0:T(8,128)(2,1)} %get-tuple-element.67.w_ref, ...), custom_call_target="tpu_custom_call" | custom-call | bytes 157286400 | tf_op jit(solution)/shard_map/back/pallas_call | solution.py:625
  678.2 1.4 slice_bitcast_fusion
  679.6 1.3 slice_bitcast_fusion.3
  681.3 1.4 dynamic-slice_bitcast_fusion
  682.7 2.0 collective-permute-start.1
  684.6 1.5 collective-permute-start.2
  686.8 1.8 multiply_reduce_fusion
  688.6 0.7 slice.112
  689.3 1.2 slice.109
  691.2 3.0 multiply_add_fusion
  694.2 7.0 collective-permute-done.refs_1_
  701.2 47.1 %collective-permute-done.1.refs_2_ = bf16[3,96,1152]{2,1,0:T(8,128)(2,1)} collective-permute-done((bf16[3,96,1152]{2,1,0:T(8,128)(2,1)}, bf16[3,96,1152]{2,1,0:T(8,128)(2,1)}, u32[]{:S(2)}, u32[]{:S(2)}) %collective-permute-start.1) | collective-permute-done | bytes 663584 | tf_op jit(solution)/shard_map/ppermute | solution.py:70
  748.3 4.2 collective-permute-done.2.refs_3_
  752.5 4.4 assemble.1
  756.9 1.6 convert_bitcast_fusion
  (130 shorter events, 7.6 us)
Async XLA Ops:
  7.2 2.3 copy-start.17
  7.2 3.3 copy-start.20
  7.2 3.2 copy-start.23
  7.2 3.2 copy-start.22
  7.2 172.7 %all-gather.4.cloned.1.call-start = ((), (), s32[]{:S(2)}) async-start(), calls=%async_computation.5 | async-start | bytes 4423680 | tf_op jit(solution)/shard_map/all_gather | solution.py:1215
  11.2 66.8 %copy-start.32 = (bf16[256]{0:T(256)(128)(2,1)S(1)}, bf16[256]{0:T(256)(128)(2,1)}, u32[]{:S(2)}) copy-start(bf16[256]{0:T(256)(128)(2,1)} %param.30) | copy-start | bytes 1540
  11.2 66.9 %copy-start.33 = (bf16[256]{0:T(256)(128)(2,1)S(1)}, bf16[256]{0:T(256)(128)(2,1)}, u32[]{:S(2)}) copy-start(bf16[256]{0:T(256)(128)(2,1)} %param.32) | copy-start | bytes 1540
  11.2 66.9 %copy-start.28 = (bf16[1536]{0:T(1024)(128)(2,1)S(1)}, bf16[1536]{0:T(1024)(128)(2,1)}, u32[]{:S(2)}) copy-start(bf16[1536]{0:T(1024)(128)(2,1)} %param.26) | copy-start | bytes 9220
  11.2 66.9 %copy-start.1 = (bf16[256,1536]{1,0:T(8,128)(2,1)S(1)}, bf16[256,1536]{1,0:T(8,128)(2,1)}, u32[]{:S(2)}) copy-start(bf16[256,1536]{1,0:T(8,128)(2,1)} %param.20) | copy-start | bytes 2359300
  77.1 102.9 %all-gather.6.cloned.1.call-start = ((), (), s32[]{:S(2)}) async-start(), calls=%async_computation.6 | async-start | bytes 4423680 | tf_op jit(solution)/shard_map/all_gather | solution.py:1215
  77.9 161.0 %all-gather.8.cloned.1.call-start = ((), (), s32[]{:S(2)}) async-start(), calls=%async_computation.7 | async-start | bytes 4423680 | tf_op jit(solution)/shard_map/all_gather | solution.py:1241
  78.3 1.7 copy-start.26
  80.1 5.2 copy-start.30
  99.2 3.5 copy-start.21
  99.8 39.3 %copy-start.13 = (bf16[512,896]{1,0:T(8,128)(2,1)}, bf16[512,896]{1,0:T(8,128)(2,1)S(1)}, u32[]{:S(2)}) copy-start(bf16[512,896]{1,0:T(8,128)(2,1)S(1)} %copy.39.q_ref) | copy-start | bytes 2752516
  139.2 430.0 %reduce-scatter.10.cloned.1.call-start = ((), (), s32[]{:S(2)}) async-start(), calls=%async_computation.10 | async-start | bytes 4423680 | tf_op jit(solution)/shard_map/reduce_scatter | solution.py:1276
  140.6 19.4 %copy-start.31 = (bf16[1536,768]{1,0:T(8,128)(2,1)S(1)}, bf16[1536,768]{1,0:T(8,128)(2,1)}, u32[]{:S(2)}) copy-start(bf16[1536,768]{1,0:T(8,128)(2,1)} %get-tuple-element.71) | copy-start | bytes 7077892
  164.2 10.9 %copy-start.29 = (bf16[1536]{0:T(1024)(128)(2,1)S(1)}, bf16[1536]{0:T(1024)(128)(2,1)}, u32[]{:S(2)}) copy-start(bf16[1536]{0:T(1024)(128)(2,1)} %param.34) | copy-start | bytes 9220
  238.9 70.4 %copy-start.5 = (bf16[256,1536]{1,0:T(8,128)(2,1)S(1)}, bf16[256,1536]{1,0:T(8,128)(2,1)}, u32[]{:S(2)}) copy-start(bf16[256,1536]{1,0:T(8,128)(2,1)} %param.21) | copy-start | bytes 2359300
  238.9 70.4 %copy-start.8 = (bf16[256,1536]{1,0:T(8,128)(2,1)S(1)}, bf16[256,1536]{1,0:T(8,128)(2,1)}, u32[]{:S(2)}) copy-start(bf16[256,1536]{1,0:T(8,128)(2,1)} %param.22) | copy-start | bytes 2359300
  412.9 156.3 %reduce-scatter.8.cloned.1.call-start = ((), (), s32[]{:S(2)}) async-start(), calls=%async_computation.9 | async-start | bytes 4423680 | tf_op jit(solution)/shard_map/reduce_scatter | solution.py:1276
  413.5 155.7 %reduce-scatter.6.cloned.1.call-start = ((), (), s32[]{:S(2)}) async-start(), calls=%async_computation.8 | async-start | bytes 4423680 | tf_op jit(solution)/shard_map/reduce_scatter | solution.py:1276
  414.1 78.4 %copy-start = (f32[256,1536]{1,0:T(8,128)S(1)}, f32[256,1536]{1,0:T(8,128)}, u32[]{:S(2)}) copy-start(f32[256,1536]{1,0:T(8,128)} %shard_map.292) | copy-start | bytes 4718596
  414.1 195.3 %reduce-scatter.12.cloned.1.call-start = ((), (), s32[]{:S(2)}) async-start(), calls=%async_computation.11 | async-start | bytes 2949120 | tf_op jit(solution)/shard_map/reduce_scatter | solution.py:1284
  414.2 78.4 %copy-start.6 = (bf16[256,1536]{1,0:T(8,128)(2,1)S(1)}, bf16[256,1536]{1,0:T(8,128)(2,1)}, u32[]{:S(2)}) copy-start(bf16[256,1536]{1,0:T(8,128)(2,1)} %param.21) | copy-start | bytes 2359300
  492.6 3.3 copy-start.3
  492.6 3.3 copy-start.9
  498.4 9.3 %copy-start.34 = (bf16[512,768]{1,0:T(8,128)(2,1)S(1)}, bf16[512,768]{1,0:T(8,128)(2,1)}, u32[]{:S(2)}) copy-start(bf16[512,768]{1,0:T(8,128)(2,1)} %get-tuple-element.70) | copy-start | bytes 2359300
  511.9 1.4 copy-start.12
  511.9 244.9 %reduce-scatter.14.cloned.1.call-start = ((), (), s32[]{:S(2)}) async-start(), calls=%async_computation.12 | async-start | bytes 737280 | tf_op jit(solution)/shard_map/reduce_scatter | solution.py:1310
  543.9 28.0 %copy-start.10 = (f32[512,768]{1,0:T(8,128)S(1)}, f32[512,768]{1,0:T(8,128)}, u32[]{:S(2)}) copy-start(f32[512,768]{1,0:T(8,128)} %get-tuple-element.90) | copy-start | bytes 4718596
  569.2 2.7 copy-start.24
  572.0 1.8 copy-start.18
  576.2 33.4 %copy-start.11 = (bf16[512,1536]{1,0:T(8,128)(2,1)S(1)}, bf16[512,1536]{1,0:T(8,128)(2,1)}, u32[]{:S(2)}) copy-start(bf16[512,1536]{1,0:T(8,128)(2,1)} %gather.2) | copy-start | bytes 4718596
  577.4 35.7 %copy-start.4 = (bf16[512,1024]{1,0:T(8,128)(2,1)}, bf16[512,1024]{1,0:T(8,128)(2,1)S(1)}, u32[]{:S(2)}) copy-start(bf16[512,1024]{1,0:T(8,128)(2,1)S(1)} %pad_maximum_fusion.2.p_ref) | copy-start | bytes 3145732
  609.6 3.8 copy-start.25
  614.6 66.3 %copy-start.14 = (bf16[384,1152]{1,0:T(8,128)(2,1)S(1)}, bf16[384,1152]{1,0:T(8,128)(2,1)}, u32[]{:S(2)}) copy-start(bf16[384,1152]{1,0:T(8,128)(2,1)} %reduce-scatter.10.cloned.1.call-done) | copy-start | bytes 2654212
  614.6 66.3 %copy-start.15 = (bf16[384,1152]{1,0:T(8,128)(2,1)S(1)}, bf16[384,1152]{1,0:T(8,128)(2,1)}, u32[]{:S(2)}) copy-start(bf16[384,1152]{1,0:T(8,128)(2,1)} %reduce-scatter.8.cloned.1.call-done) | copy-start | bytes 2654212
  614.6 66.3 %copy-start.16 = (bf16[384,1152]{1,0:T(8,128)(2,1)S(1)}, bf16[384,1152]{1,0:T(8,128)(2,1)}, u32[]{:S(2)}) copy-start(bf16[384,1152]{1,0:T(8,128)(2,1)} %reduce-scatter.6.cloned.1.call-done) | copy-start | bytes 2654212
  681.3 4.8 copy-start.19
  681.3 5.5 copy-start.2
  681.3 5.5 copy-start.27
  682.7 18.5 %collective-permute-start = (bf16[3,96,1152]{2,1,0:T(8,128)(2,1)}, bf16[3,96,1152]{2,1,0:T(8,128)(2,1)}, u32[]{:S(2)}, u32[]{:S(2)}) collective-permute-start(bf16[3,96,1152]{2,1,0:T(8,128)(2,1)} %get-tuple-element.119), channel_id=1, source_target_pairs={{0,2},{2,4},{4,6},{6,0},{1,3},{3,5},{5,7},{7,1},{8,10},{10,12},{12... | collective-permute-start | bytes 1990664 | tf_op jit(solution)/shard_map/ppermute | solution.py:70
  682.7 65.6 %collective-permute-start.1 = (bf16[3,96,1152]{2,1,0:T(8,128)(2,1)}, bf16[3,96,1152]{2,1,0:T(8,128)(2,1)}, u32[]{:S(2)}, u32[]{:S(2)}) collective-permute-start(bf16[3,96,1152]{2,1,0:T(8,128)(2,1)} %get-tuple-element.118), channel_id=1, source_target_pairs={{0,4},{2,6},{4,0},{6,2},{1,5},{3,7},{5,1},{7,3},{8,12},{10,14},{12... | collective-permute-start | bytes 1990664 | tf_op jit(solution)/shard_map/ppermute | solution.py:70
  684.6 67.9 %collective-permute-start.2 = (bf16[3,96,1152]{2,1,0:T(8,128)(2,1)S(1)}, bf16[3,96,1152]{2,1,0:T(8,128)(2,1)}, u32[]{:S(2)}, u32[]{:S(2)}) collective-permute-start(bf16[3,96,1152]{2,1,0:T(8,128)(2,1)S(1)} %get-tuple-element.117), channel_id=1, source_target_pairs={{0,6},{2,0},{4,2},{6,4},{1,7},{3,1},{5,3},{7,5},{8,14},{10,8},{12,... | collective-permute-start | bytes 1990664 | tf_op jit(solution)/shard_map/ppermute | solution.py:70
  686.1 5.1 copy-start.7
Sparse Core Ops, SparseCore 0:
  77.2 48.3 all-gather.3
  127.5 47.1 all-gather.5
  176.5 47.0 all-gather.7
  413.1 55.5 reduce-scatter.9
  471.6 47.1 reduce-scatter.7
  521.7 47.1 reduce-scatter.5
  572.0 37.3 reduce-scatter.11
  686.2 54.1 reduce-scatter.13

commit v9 on v8

--- a/solution.py
+++ b/solution.py
@@ -23,21 +23,6 @@
     frequency = THETA ** (-(jnp.arange(half_dim, dtype=jnp.float32) * 2.0 / HEAD))
     angles = places.astype(jnp.float32)[:, None] * frequency[None, :]
     return (jnp.cos(angles), jnp.sin(angles))
-
-
-def rotate(stacked, cosine, sine_table):
-    half_dim = HEAD // 2
-    first_half = stacked[..., :half_dim]
-    second_half = stacked[..., half_dim:]
-    cosine = cosine[:, None, :]
-    sine_table = sine_table[:, None, :]
-    return jnp.concatenate(
-        [
-            first_half * cosine - second_half * sine_table,
-            second_half * cosine + first_half * sine_table,
-        ],
-        axis=-1,
-    )
 
 
 def matmul(first_op, second_op):
@@ -72,11 +57,10 @@
     return received
 
 
-def to_rows(summed, columns):
+def swapped_rows(summed):
     size = lax.axis_size("ctx")
     rows, width = summed[0].shape[0] // size, summed[0].shape[1]
-    blocks = jnp.stack([s.reshape(size, rows, width) for s in summed], axis=1)
-    return assemble(exchange(blocks, "ctx"), columns)
+    return exchange(jnp.stack([s.reshape(size, rows, width) for s in summed], axis=1), "ctx")
 
 
 def nn(first_op, second_op):
@@ -499,7 +483,7 @@
 
 
 def back_kernel(
-    size, groups, x_ref, s_ref, p_ref, w_ref, n_ref, o_ref, t_ref, g_ref, mine, far, near, part, pair, crowd, row, give, got,
+    size, groups, x_ref, s_ref, p_ref, w_ref, n_ref, mid_ref, scale_ref, gain_ref, o_ref, t_ref, g_ref, mine, far, near, part, pair, crowd, row, give, got,
     give_sems, own_sem, far_send, far_recv, near_send, near_recv, pair_sems, crowd_send, crowd_recv, row_send, row_recv,
 ):
     place, group = lax.axis_index("ctx"), lax.axis_index("dp")
@@ -540,9 +524,11 @@
 
     def gain_sums(i, total):
         span = pl.ds(pl.multiple_of(i * 32, 32), 32)
-        grad = g_ref[span, :] + got[span, :]
-        g_ref[span, :] = grad
-        return total + jnp.sum(grad * n_ref[span, :], axis=0, keepdims=True)
+        grad, normed = g_ref[span, :] + got[span, :], n_ref[span, :]
+        scaled = grad * gain_ref[...]
+        mean = jnp.mean(scaled * normed, axis=1, keepdims=True)
+        g_ref[span, :] = mid_ref[span, :] + scale_ref[span, :] * (scaled - normed * mean)
+        return total + jnp.sum(grad * normed, axis=0, keepdims=True)
 
     def to_crowd(step):
         return remote(
@@ -618,13 +604,13 @@
             along(k).wait_send()
 
 
-def back(x, small, grad_pre, weight, normed, ident):
+def back(x, small, grad_pre, weight, normed, mid, scale, gain, ident):
     size, groups = lax.axis_size("ctx"), lax.axis_size("dp")
     rows, columns = x.shape[0] // (size * groups), x.shape[1]
     dma = pltpu.SemaphoreType.DMA
     return pl.pallas_call(
         functools.partial(back_kernel, size, groups),
-        in_specs=[ANY] + [IN_VMEM] * 4,
+        in_specs=[ANY] + [IN_VMEM] * 7,
         out_specs=[IN_VMEM] * 3,
         out_shape=[
             jax.ShapeDtypeStruct((rows, columns), jnp.float32),
@@ -656,7 +642,7 @@
         compiler_params=pltpu.CompilerParams(collective_id=ident, has_side_effects=True, vmem_limit_bytes=60000000),
         cost_estimate=pl.CostEstimate(flops=0, bytes_accessed=100 * x.size, transcendentals=0),
         name="back",
-    )(x, small, grad_pre, weight, normed)
+    )(x, small, grad_pre, weight, normed, mid, scale, gain)
 
 
 def column_step(width):
@@ -1028,30 +1014,71 @@
     )(*acts, *weights)
 
 
-def assemble_kernel(size, ranks_ref, *refs):
-    parts, (down_ref, gate_ref, up_ref, whole) = refs[:size], refs[size:]
+def assemble_kernel(groups, size, ranks_ref, *refs):
+    parts, targets, whole = refs[: size * len(groups)], refs[size * len(groups) : -1], refs[-1]
     width = parts[0].shape[2]
-    for which, target in enumerate((down_ref, gate_ref, up_ref)):
-        for part, k in zip(parts, range(size)):
-            whole[:, pl.ds(pl.multiple_of(ranks_ref[k] * width, 128), width)] = part[which].astype(jnp.float32)
-        target[...] = whole[:, : gate_ref.shape[1]]
+    taken = [(g, which) for g, held in enumerate(groups) for which in range(held)]
+    for (g, which), target in zip(taken, targets):
+        for k in range(size):
+            span = pl.ds(pl.multiple_of(ranks_ref[k] * width, 128), width)
+            whole[:, span] = parts[g * size + k][which].astype(jnp.float32)
+        target[...] = whole[:, : target.shape[1]]
 
 
 def assemble(received, columns):
-    ranks = jnp.stack([rank for rank, _ in received]).astype(jnp.int32)
-    blocks = [block for _, block in received]
+    ranks = jnp.stack([rank for rank, _ in received[0]]).astype(jnp.int32)
+    blocks = [block for group in received for _, block in group]
+    groups, size = tuple(group[0][1].shape[0] for group in received), len(received[0])
     _, rows, width = blocks[0].shape
     f32 = jnp.float32
     return pl.pallas_call(
-        functools.partial(assemble_kernel, len(blocks)),
+        functools.partial(assemble_kernel, groups, size),
         in_specs=[pl.BlockSpec(memory_space=pltpu.SMEM)] + [IN_VMEM] * len(blocks),
-        out_specs=[IN_VMEM] * 3,
-        out_shape=[jax.ShapeDtypeStruct((rows, columns), f32)] * 3,
-        scratch_shapes=[pltpu.VMEM((rows, len(blocks) * width), f32)],
+        out_specs=[IN_VMEM] * sum(groups),
+        out_shape=[jax.ShapeDtypeStruct((rows, columns), f32)] * sum(groups),
+        scratch_shapes=[pltpu.VMEM((rows, size * width), f32)],
         compiler_params=pltpu.CompilerParams(vmem_limit_bytes=60000000),
         cost_estimate=pl.CostEstimate(flops=0, bytes_accessed=20 * rows * columns, transcendentals=0),
         name="assemble",
     )(ranks, *blocks)
+
+
+def turn(part, cosine, sine):
+    return part * cosine + pltpu.roll(part, HEAD // 2, 1) * sine
+
+
+def rope_kernel(x_ref, cosine_ref, sine_ref, q_ref, k_ref, v_ref):
+    start = 0
+    for target in (q_ref, k_ref, v_ref):
+        for h in range(target.shape[1] // HEAD):
+            part = x_ref[:, start : start + HEAD]
+            if target is not v_ref:
+                part = turn(part, cosine_ref[...], sine_ref[...])
+            target[:, h * HEAD : (h + 1) * HEAD] = part.astype(jnp.bfloat16)
+            start += HEAD
+
+
+def rope_back_kernel(q_ref, kv_ref, cosine_ref, sine_ref, o_ref):
+    start, kv_heads = 0, kv_ref.shape[1] // (2 * HEAD)
+    for source, heads, turning in ((q_ref, q_ref.shape[1] // HEAD, True), (kv_ref, kv_heads, True), (kv_ref, kv_heads, False)):
+        for h in range(heads):
+            first = (h if turning else h + kv_heads) * HEAD
+            part = source[:, first : first + HEAD]
+            if turning:
+                part = turn(part, cosine_ref[...], -sine_ref[...])
+            o_ref[:, start : start + HEAD] = part.astype(jnp.bfloat16)
+            start += HEAD
+
+
+def rope_call(kernel, arrays, widths):
+    rows = arrays[0].shape[0]
+    return pl.pallas_call(
+        kernel,
+        in_specs=[IN_VMEM] * len(arrays),
+        out_specs=[IN_VMEM] * len(widths),
+        out_shape=[jax.ShapeDtypeStruct((rows, w), jnp.bfloat16) for w in widths],
+        cost_estimate=pl.CostEstimate(flops=0, bytes_accessed=6 * rows * sum(widths), transcendentals=0),
+    )(*arrays)
 
 
 def mask_into(bias_ref, first, seg_ref, place_ref):
@@ -1225,14 +1252,12 @@
     cosine, sine_table = rope_tables(places)
     qkv_pre = matmul(normed_rows, full_qkv) + bias
     turned = q_width + kv_width
-    rotated = (
-        rotate(qkv_pre[:, :turned].reshape(shard_rows, turned // HEAD, HEAD), cosine, sine_table)
-        .astype(jnp.bfloat16)
-        .reshape(shard_rows, turned)
-    )
+    cosines = jnp.concatenate([cosine, cosine], axis=1)
+    sines = jnp.concatenate([-sine_table, sine_table], axis=1)
+    queries, own_keys, own_values = rope_call(rope_kernel, (qkv_pre, cosines, sines), (q_width, kv_width, kv_width))
     own_count = jnp.full((8, 128), jnp.sum(valid_mask.astype(jnp.float32)))
     all_keys, all_values, counts, down_slice = share(
-        [rotated[:, q_width:], qkv_pre[:, turned:].astype(jnp.bfloat16), own_count],
+        [own_keys, own_values, own_count],
         ((True, False), (True, False), (False, True)),
         [jnp.pad(down_weight.T, extra)],
         slice_width,
@@ -1249,7 +1274,7 @@
     kept = []
     for c in range(kv_local):
         forward, backward = attention_calls(shard_rows, seq_len, group, c)
-        kept.append((backward,) + tuple(forward(first, doc_start, key_place, rotated, all_keys, all_values)))
+        kept.append((backward,) + tuple(forward(first, doc_start, key_place, queries, all_keys, all_values)))
     heads_out = jnp.concatenate([k[1] for k in kept], axis=1)
     attention = scatter(matmul_nt(heads_out, full_out), 1, True, 4)
     residual_mid = inputs + attention
@@ -1282,30 +1307,24 @@
     grad_out = matmul_tn(grad_attn_rows, heads_out).astype(jnp.bfloat16)
 
     grad_out = lax.psum_scatter(grad_out, "dp", scatter_dimension=0, tiled=True)
+    early = swapped_rows(summed[:2])
     query_grads, key_grads, value_grads = [], [], []
     for c in range(kv_local):
         backward, _, log_total = kept[c]
         grad_query, grad_kv = backward(
-            first, doc_start, key_place, rotated, grad_heads, log_total, all_keys, all_values
+            first, doc_start, key_place, queries, grad_heads, log_total, all_keys, all_values
         )
         query_grads.append(grad_query)
         key_grads.append(grad_kv[:, :HEAD])
         value_grads.append(grad_kv[:, HEAD:])
     grad_kv = grad_kv if kv_local == 1 else jnp.concatenate(key_grads + value_grads, axis=1)
     grad_kv = scatter(grad_kv, ctx_size, False, 7)
-    grad_kv, *summed = lax.optimization_barrier((grad_kv, *summed))
-    shard_down, shard_gate, shard_up = to_rows(summed, hidden_width)
+    grad_kv, up_summed = lax.optimization_barrier((grad_kv, summed[2]))
+    late = swapped_rows([up_summed])
+    shard_down, shard_gate, shard_up = assemble([early, late], hidden_width)
     shard_down = shard_down.T
-    grad_turned = jnp.concatenate(query_grads + [grad_kv[:, :kv_width]], axis=1)
-    grad_pre = jnp.concatenate(
-        [
-            rotate(grad_turned.reshape(shard_rows, turned // HEAD, HEAD), cosine, -sine_table)
-            .reshape(shard_rows, turned)
-            .astype(jnp.bfloat16),
-            grad_kv[:, kv_width:].astype(jnp.bfloat16),
-        ],
-        axis=1,
-    )
+    grad_turned = query_grads[0] if kv_local == 1 else jnp.concatenate(query_grads, axis=1)
+    (grad_pre,) = rope_call(rope_back_kernel, (grad_turned, grad_kv, cosines, sines), (turned + kv_width,))
     grad_pre, grad_out = lax.optimization_barrier((grad_pre, grad_out))
     shard_out = lax.psum_scatter(grad_out, "ctx", scatter_dimension=0, tiled=True)
     shard_out = shard_out.astype(jnp.float32).T
@@ -1328,8 +1347,9 @@
     flat = jnp.concatenate(parts)
     small = jnp.pad(flat, (0, -flat.shape[0] % 1024)).reshape(-1, 128)
     grad_qkv = matmul_tn(normed_rows, grad_pre).astype(jnp.bfloat16)
-    shard_qkv, sums, grad_normed = back(grad_qkv, small, grad_pre, full_qkv, normed_attn, 8)
-    grad_input = grad_mid + norm_back(grad_normed, normed_attn, scale_attn, gain_one)
+    shard_qkv, sums, grad_input = back(
+        grad_qkv, small, grad_pre, full_qkv, normed_attn, grad_mid, scale_attn, gain_one[None, :], 8
+    )
     sums = sums.reshape(-1)
     pieces, offset = [], 0
     for part in parts:

time: 775 us -> 702 us (0.906)
  the two profiles are of different devices: /device:TPU:9 before, /device:TPU:0 now
where the time goes in v9:
time: 702 us; the launch traced here: 694 us
  Pallas kernels  546 us (78%)
  matrix products  60.5 us (9%)
  other arithmetic  25.8 us (4%)
  local copies, waits for them, and re-layouts  21.9 us (3%)
  between operations  17.3 us (2%)
  starting transfers between devices  12.1 us (2%)
  waiting for transfers between devices  10.6 us (2%)
    pallas_call x2, Pallas kernels, gather_apply(): pl.pallas_call(functools.partial(gather_apply_kernel, size, pieces, work,...  135 us
    pallas_call x2, Pallas kernels, sum_apply(): pl.pallas_call(functools.partial(sum_apply_kernel, size, pieces, count),...  129 us
    pallas_call x2, Pallas kernels, share(): pl.pallas_call(functools.partial(share_kernel, size, groups, kinds, m), i...  112 us
    pallas_call x1, Pallas kernels, back(): pl.pallas_call(functools.partial(back_kernel, size, groups), in_specs=[AN...  62.4 us
    dot_general x5, matrix products, matmul_tn(): lax.dot_general(first_op, second_op, (((0,), (0,)), ((), ())), preferred_...  47.4 us
    pallas_call x2, Pallas kernels, scatter(): pl.pallas_call(functools.partial(scatter_kernel, size, paired, pieces), i...  42.6 us
    pallas_call x1, Pallas kernels, per_device(): backward(first, doc_start, key_place, queries, grad_heads, log_total, all...  26.4 us
    pallas_call x1, Pallas kernels, per_device(): forward(first, doc_start, key_place, queries, all_keys, all_values)  19.4 us
  transfers between devices with their start and end apart: 14, of which 2 were waited for; matrix products, arithmetic and copies ran while one was open for 10% of the time, Pallas kernels for 50%

profile of v9, /device:TPU:0, one launch (start us, length us, event | category | flops | bytes accessed | tf_op | source)
XLA Modules:
  0.0 694.2 jit_solution(3905213249585409587)
XLA Ops:
  7.3 2.2 pad.17.refs_2_
  9.5 1.0 pad.18.refs_3_
  10.5 0.7 pad_maximum_fusion.2.refs_0_
  11.2 69.2 %shard_map.289 = (bf16[1536,1024]{1,0:T(8,128)(2,1)}, bf16[1536,768]{1,0:T(8,128)(2,1)}, bf16[384,1152]{1,0:T(8,128)(2,1)}, bf16[384,1152]{1,0:T(8,128)(2,1)}) custom-call(bf16[96,1024]{1,0:T(8,128)(2,1)} %pad_maximum_fusion.2.refs_0_, bf16[96,768]{1,0:T(8,128)(2,1)} %bitcast.75, bf16[96,4608]{1,0:T(8,128)(2,1)} %pad.17.refs_2_, bf16[96,4608]{1,0:T(8,128)(2,1)} %pad.18.refs_3_), custom_call_target="tpu_custom_call" | custom-call | bytes 150000000 | tf_op jit(solution)/shard_map/pallas_call | solution.py:474
  80.5 0.7 all-gather.6.cloned.1.call-update
  81.6 1.7 convert_multiply_fusion
  83.3 4.1 gather.2
  87.5 1.0 pad.19.refs_3_
  88.5 1.4 dynamic-slice_convert_fusion
  89.9 1.0 fusion.10
  90.9 0.8 pad_maximum_fusion.cosine_ref
  91.8 0.8 pad_maximum_fusion.1.sine_ref
  92.6 5.0 convolution_add_fusion.x_ref
  97.6 3.1 shard_map.290
  101.3 1.2 broadcast_in_dim.15.refs_2_
  102.6 43.2 %shard_map.291 = (bf16[2048,128]{1,0:T(8,128)(2,1)}, bf16[2048,128]{1,0:T(8,128)(2,1)}, f32[32,128]{1,0:T(8,128)}, bf16[384,1152]{1,0:T(8,128)(2,1)}) custom-call(bf16[512,128]{1,0:T(8,128)(2,1)} %get-tuple-element.70.refs_0_, bf16[512,128]{1,0:T(8,128)(2,1)} %get-tuple-element.71.refs_1_, f32[8,128]{1,0:T(8,128)} %broadcast_in_dim.15.refs_2_, ...), custom_call_target="tpu_custom_call" | custom-call | bytes 150000000 | tf_op jit(solution)/shard_map/pallas_call | solution.py:474
  145.8 1.3 copy.39.place_ref
  147.2 19.4 %attend.1 = (bf16[512,768]{1,0:T(8,128)(2,1)}, f32[6,1,512]{2,1,0:T(1,128)}) custom-call(s32[1]{0:T(128)} %bitcast.first_ref, s32[1,512]{1,0:T(1,128)} %bitcast.78, s32[2048,1]{1,0:T(8,128)} %copy.39.place_ref, bf16[512,768]{1,0:T(8,128)(2,1)} %get-tuple-element.69.q_ref, bf16[2048,128]{1,0:T(8,128)(2,1)} %get-tuple-element.72.k_ref, ...), custom_call_target="tpu_custom_call" | custom-call | flops 3221225472 | bytes 1572864 | tf_op jit(solution)/shard_map/attend/pallas_call | solution.py:1277
  166.6 4.2 fusion.14.x_ref
  170.8 5.1 scatter.9
  175.9 0.7 slice.67
  176.6 0.6 reduce_sum.75
  178.0 1.7 multiply_reduce_fusion.2
  179.7 1.1 multiply_convert_fusion.refs_0_
  180.8 65.7 %shard_map.292 = (bf16[2048,1536]{1,0:T(8,128)(2,1)}, bf16[2048,1152]{1,0:T(8,128)(2,1)}, bf16[2048,1152]{1,0:T(8,128)(2,1)}, bf16[2048,1152]{1,0:T(8,128)(2,1)}) custom-call(bf16[256,1536]{1,0:T(8,128)(2,1)} %multiply_convert_fusion.refs_0_, bf16[1536,1152]{1,0:T(8,128)(2,1)} %all-gather.4.cloned.1.call-done.refs_1_.refs_2_, ...), custom_call_target="tpu_custom_call" | custom-call | bytes 200000000 | tf_op jit(solution)/shard_map/pallas_call | solution.py:820
  246.5 60.3 %shard_map.293 = f32[256,1536]{1,0:T(8,128)} custom-call(bf16[2048,1152]{1,0:T(8,128)(2,1)} %get-tuple-element.78.refs_0_, bf16[1536,1152]{1,0:T(8,128)(2,1)} %all-gather.8.cloned.1.call-done.refs_1_), custom_call_target="tpu_custom_call" | custom-call | bytes 200000000 | tf_op jit(solution)/shard_map/pallas_call | solution.py:1006
  306.9 3.0 fusion.11.refs_0_
  309.9 68.8 %shard_map.294 = (bf16[2048,1536]{1,0:T(8,128)(2,1)}, bf16[2048,1152]{1,0:T(8,128)(2,1)}, bf16[2048,1152]{1,0:T(8,128)(2,1)}) custom-call(bf16[256,1536]{1,0:T(8,128)(2,1)} %fusion.11.refs_0_, bf16[1536,1152]{1,0:T(8,128)(2,1)} %all-gather.8.cloned.1.call-done.refs_1_, bf16[2048,1152]{1,0:T(8,128)(2,1)} %get-tuple-element.81.refs_2_, ...), custom_call_target="tpu_custom_call" | custom-call | bytes 200000000 | tf_op jit(solution)/shard_map/pallas_call | solution.py:820
  378.7 13.2 %convolution_convert_fusion.2 = bf16[1536,1152]{1,0:T(8,128)(2,1)} fusion(bf16[2048,1536]{1,0:T(8,128)(2,1)} %get-tuple-element.85, bf16[2048,1152]{1,0:T(8,128)(2,1)} %get-tuple-element.78.refs_0_), kind=kOutput, calls=%fused_computation.2 | convolution fusion | flops 7249526784 | bytes 14548992 | tf_op jit(solution)/shard_map/dot_general | solution.py:33
  391.9 13.2 %convolution_convert_fusion.1 = bf16[1536,1152]{1,0:T(8,128)(2,1)} fusion(bf16[2048,1536]{1,0:T(8,128)(2,1)} %get-tuple-element.88, bf16[2048,1152]{1,0:T(8,128)(2,1)} %get-tuple-element.91.refs_0_), kind=kOutput, calls=%fused_computation.1 | convolution fusion | flops 7249526784 | bytes 14548992 | tf_op jit(solution)/shard_map/dot_general | solution.py:33
  405.9 13.2 %convolution_convert_fusion = bf16[1536,1152]{1,0:T(8,128)(2,1)} fusion(bf16[2048,1536]{1,0:T(8,128)(2,1)} %get-tuple-element.88, bf16[2048,1152]{1,0:T(8,128)(2,1)} %get-tuple-element.92.refs_1_), kind=kOutput, calls=%fused_computation | convolution fusion | flops 7249526784 | bytes 14548992 | tf_op jit(solution)/shard_map/dot_general | solution.py:33
  419.2 68.7 %shard_map.295 = f32[256,1536]{1,0:T(8,128)} custom-call(bf16[2048,1152]{1,0:T(8,128)(2,1)} %get-tuple-element.91.refs_0_, bf16[2048,1152]{1,0:T(8,128)(2,1)} %get-tuple-element.92.refs_1_, bf16[1536,1152]{1,0:T(8,128)(2,1)} %all-gather.4.cloned.1.call-done.refs_1_.refs_2_, bf16[1536,1152]{1,0:T(8,128)(2,1)} %all-gather.6.cloned.1.call-done.refs_2_.refs_3_), custom_call_target="tpu_custom_call" | custom-call | bytes 200000000 | tf_op jit(solution)/shard_map/pallas_call | solution.py:1006
  488.0 3.2 multiply_reduce_fusion
  491.2 2.5 fusion.12
  493.7 4.1 gather.3
  497.9 4.3 convolution_convert_fusion.4
  503.1 0.8 copy.41.scale_ref
  503.9 0.6 pad_add_fusion.ranks_ref
  504.5 3.9 convolution_convert_fusion.5.do_ref
  508.5 26.4 %attend_back.1 = (f32[512,768]{1,0:T(8,128)}, bf16[2048,256]{1,0:T(8,128)(2,1)}) custom-call(s32[1]{0:T(128)} %bitcast.first_ref, s32[1,512]{1,0:T(1,128)} %bitcast.79, s32[2048,1]{1,0:T(8,128)} %copy.39.place_ref, bf16[512,768]{1,0:T(8,128)(2,1)} %get-tuple-element.69.q_ref, bf16[512,768]{1,0:T(8,128)(2,1)} %convolution_convert_fusion.5.do_ref, ...), custom_call_target="tpu_custom_call" | custom-call | flops 8053063680 | bytes 3145728 | tf_op jit(solution)/shard_map/attend_back/pallas_call | solution.py:1314
  534.8 37.6 %scatter.10.kv_ref = f32[512,256]{1,0:T(8,128)} custom-call(bf16[2048,256]{1,0:T(8,128)(2,1)} %get-tuple-element.95.x_ref), custom_call_target="tpu_custom_call" | custom-call | bytes 15728640 | tf_op jit(solution)/shard_map/scatter/pallas_call | solution.py:324
  572.5 2.7 fusion.3
  575.2 1.8 collective-permute-start.1
  577.0 2.9 collective-permute-start.2
  579.9 2.2 dynamic-slice_bitcast_fusion
  582.1 1.2 collective-permute-start.4
  583.2 3.5 shard_map.296.p_ref
  586.8 6.8 reduce-scatter.8.cloned.1.call-done
  593.6 1.4 convert_reduce_fusion
  595.3 0.7 constant_dynamic-update-slice_fusion
  596.0 0.6 pad_bitcast_fusion.s_ref
  596.6 3.5 convolution_convert_fusion.3.x_ref
  600.1 62.4 %back.1 = (f32[96,1024]{1,0:T(8,128)}, f32[48,128]{1,0:T(8,128)}, f32[256,1536]{1,0:T(8,128)}) custom-call(bf16[1536,1024]{1,0:T(8,128)(2,1)} %convolution_convert_fusion.3.x_ref, f32[48,128]{1,0:T(8,128)} %pad_bitcast_fusion.s_ref, bf16[512,1024]{1,0:T(8,128)(2,1)} %shard_map.296.p_ref, bf16[1536,1024]{1,0:T(8,128)(2,1)} %get-tuple-element.68.w_ref, ...), custom_call_target="tpu_custom_call" | custom-call | bytes 157286400 | tf_op jit(solution)/shard_map/back/pallas_call | solution.py:611
  662.5 1.7 slice.74
  664.2 1.2 slice.71
  666.0 1.5 fusion.13
  667.5 1.4 slice_bitcast_fusion
  668.9 5.5 collective-permute-start.5
  674.4 1.3 slice_bitcast_fusion.3
  675.7 2.4 collective-permute-done.5.refs_7_
  678.2 0.7 copy-done.14
  678.8 4.3 assemble.1
  683.2 1.6 convert_bitcast_fusion
  684.8 1.1 copy.59
  (109 shorter events, 3.7 us)
Async XLA Ops:
  7.2 2.3 copy-start.12
  7.2 3.3 copy-start.16
  7.2 3.2 copy-start.19
  7.2 3.2 copy-start.18
  7.2 173.5 %all-gather.4.cloned.1.call-start = ((), (), s32[]{:S(2)}) async-start(), calls=%async_computation.5 | async-start | bytes 4423680 | tf_op jit(solution)/shard_map/all_gather | solution.py:1242
  11.2 70.1 %copy-start.24 = (bf16[256]{0:T(256)(128)(2,1)S(1)}, bf16[256]{0:T(256)(128)(2,1)}, u32[]{:S(2)}) copy-start(bf16[256]{0:T(256)(128)(2,1)} %param.30) | copy-start | bytes 1540
  11.2 70.2 %copy-start.25 = (bf16[256]{0:T(256)(128)(2,1)S(1)}, bf16[256]{0:T(256)(128)(2,1)}, u32[]{:S(2)}) copy-start(bf16[256]{0:T(256)(128)(2,1)} %param.32) | copy-start | bytes 1540
  11.2 70.2 %copy-start.20 = (bf16[1536]{0:T(1024)(128)(2,1)S(1)}, bf16[1536]{0:T(1024)(128)(2,1)}, u32[]{:S(2)}) copy-start(bf16[1536]{0:T(1024)(128)(2,1)} %param.26) | copy-start | bytes 9220
  11.2 70.2 %copy-start.5 = (bf16[256,1536]{1,0:T(8,128)(2,1)S(1)}, bf16[256,1536]{1,0:T(8,128)(2,1)}, u32[]{:S(2)}) copy-start(bf16[256,1536]{1,0:T(8,128)(2,1)} %param.20) | copy-start | bytes 2359300
  80.4 100.4 %all-gather.6.cloned.1.call-start = ((), (), s32[]{:S(2)}) async-start(), calls=%async_computation.6 | async-start | bytes 4423680 | tf_op jit(solution)/shard_map/all_gather | solution.py:1242
  81.2 165.4 %all-gather.8.cloned.1.call-start = ((), (), s32[]{:S(2)}) async-start(), calls=%async_computation.7 | async-start | bytes 4423680 | tf_op jit(solution)/shard_map/all_gather | solution.py:1266
  83.3 4.2 copy-start.13
  83.3 5.1 copy-start.22
  87.5 5.1 copy-start.8
  97.6 3.1 copy-start.17
  145.8 426.7 %reduce-scatter.14.cloned.1.call-start = ((), (), s32[]{:S(2)}) async-start(), calls=%async_computation.12 | async-start | bytes 4423680 | tf_op jit(solution)/shard_map/reduce_scatter | solution.py:1301
  147.2 19.4 %copy-start.23 = (bf16[1536,768]{1,0:T(8,128)(2,1)S(1)}, bf16[1536,768]{1,0:T(8,128)(2,1)}, u32[]{:S(2)}) copy-start(bf16[1536,768]{1,0:T(8,128)(2,1)} %get-tuple-element.75) | copy-start | bytes 7077892
  170.8 5.1 copy-start.21
  246.5 60.4 %copy-start.3 = (bf16[256,1536]{1,0:T(8,128)(2,1)S(1)}, bf16[256,1536]{1,0:T(8,128)(2,1)}, u32[]{:S(2)}) copy-start(bf16[256,1536]{1,0:T(8,128)(2,1)} %param.21) | copy-start | bytes 2359300
  246.5 60.4 %copy-start.6 = (bf16[256,1536]{1,0:T(8,128)(2,1)S(1)}, bf16[256,1536]{1,0:T(8,128)(2,1)}, u32[]{:S(2)}) copy-start(bf16[256,1536]{1,0:T(8,128)(2,1)} %param.22) | copy-start | bytes 2359300
  405.1 167.4 %reduce-scatter.12.cloned.1.call-start = ((), (), s32[]{:S(2)}) async-start(), calls=%async_computation.11 | async-start | bytes 4423680 | tf_op jit(solution)/shard_map/reduce_scatter | solution.py:1301
  405.7 174.2 %reduce-scatter.6.cloned.1.call-start = ((), (), s32[]{:S(2)}) async-start(), calls=%async_computation.8 | async-start | bytes 4423680 | tf_op jit(solution)/shard_map/reduce_scatter | solution.py:1301
  419.1 68.8 %copy-start = (f32[256,1536]{1,0:T(8,128)S(1)}, f32[256,1536]{1,0:T(8,128)}, u32[]{:S(2)}) copy-start(f32[256,1536]{1,0:T(8,128)} %shard_map.293) | copy-start | bytes 4718596
  419.1 174.4 %reduce-scatter.8.cloned.1.call-start = ((), (), s32[]{:S(2)}) async-start(), calls=%async_computation.9 | async-start | bytes 2949120 | tf_op jit(solution)/shard_map/reduce_scatter | solution.py:1309
  419.2 68.8 %copy-start.4 = (bf16[256,1536]{1,0:T(8,128)(2,1)S(1)}, bf16[256,1536]{1,0:T(8,128)(2,1)}, u32[]{:S(2)}) copy-start(bf16[256,1536]{1,0:T(8,128)(2,1)} %param.21) | copy-start | bytes 2359300
  488.0 3.2 copy-start.1
  488.0 3.2 copy-start.7
  493.7 4.1 copy-start.26
  502.2 2.3 copy-start.10
  502.2 181.0 %reduce-scatter.10.cloned.1.call-start = ((), (), s32[]{:S(2)}) async-start(), calls=%async_computation.10 | async-start | bytes 737280 | tf_op jit(solution)/shard_map/reduce_scatter | solution.py:1329
  575.2 103.0 %collective-permute-start = (bf16[2,96,1152]{2,1,0:T(8,128)(2,1)}, bf16[2,96,1152]{2,1,0:T(8,128)(2,1)}, u32[]{:S(2)}, u32[]{:S(2)}) collective-permute-start(bf16[2,96,1152]{2,1,0:T(8,128)(2,1)} %get-tuple-element.121), channel_id=1, source_target_pairs={{0,2},{2,4},{4,6},{6,0},{1,3},{3,5},{5,7},{7,1},{8,10},{10,12},{12... | collective-permute-start | bytes 1327112 | tf_op jit(solution)/shard_map/ppermute | solution.py:55
  575.2 103.0 %collective-permute-start.1 = (bf16[2,96,1152]{2,1,0:T(8,128)(2,1)S(1)}, bf16[2,96,1152]{2,1,0:T(8,128)(2,1)}, u32[]{:S(2)}, u32[]{:S(2)}) collective-permute-start(bf16[2,96,1152]{2,1,0:T(8,128)(2,1)S(1)} %get-tuple-element.122), channel_id=1, source_target_pairs={{0,4},{2,6},{4,0},{6,2},{1,5},{3,7},{5,1},{7,3},{8,12},{10,14},{12... | collective-permute-start | bytes 1327112 | tf_op jit(solution)/shard_map/ppermute | solution.py:55
  577.0 101.2 %collective-permute-start.2 = (bf16[2,96,1152]{2,1,0:T(8,128)(2,1)S(1)}, bf16[2,96,1152]{2,1,0:T(8,128)(2,1)}, u32[]{:S(2)}, u32[]{:S(2)}) collective-permute-start(bf16[2,96,1152]{2,1,0:T(8,128)(2,1)S(1)} %get-tuple-element.119), channel_id=1, source_target_pairs={{0,6},{2,0},{4,2},{6,4},{1,7},{3,1},{5,3},{7,5},{8,14},{10,8},{12,... | collective-permute-start | bytes 1327112 | tf_op jit(solution)/shard_map/ppermute | solution.py:55
  582.1 86.8 %collective-permute-start.3 = (bf16[1,96,1152]{2,1,0:T(8,128)(2,1)}, bf16[1,96,1152]{2,1,0:T(8,128)(2,1)}, u32[]{:S(2)}, u32[]{:S(2)}) collective-permute-start(bf16[1,96,1152]{2,1,0:T(8,128)(2,1)} %get-tuple-element.125), channel_id=1, source_target_pairs={{0,2},{2,4},{4,6},{6,0},{1,3},{3,5},{5,7},{7,1},{8,10},{10,12},{12... | collective-permute-start | bytes 663560 | tf_op jit(solution)/shard_map/ppermute | solution.py:55
  582.1 93.6 %collective-permute-start.4 = (bf16[1,96,1152]{2,1,0:T(8,128)(2,1)}, bf16[1,96,1152]{2,1,0:T(8,128)(2,1)}, u32[]{:S(2)}, u32[]{:S(2)}) collective-permute-start(bf16[1,96,1152]{2,1,0:T(8,128)(2,1)} %get-tuple-element.124), channel_id=1, source_target_pairs={{0,4},{2,6},{4,0},{6,2},{1,5},{3,7},{5,1},{7,3},{8,12},{10,14},{12... | collective-permute-start | bytes 663560 | tf_op jit(solution)/shard_map/ppermute | solution.py:55
  583.2 13.4 %copy-start.9 = (bf16[512,1536]{1,0:T(8,128)(2,1)S(1)}, bf16[512,1536]{1,0:T(8,128)(2,1)}, u32[]{:S(2)}) copy-start(bf16[512,1536]{1,0:T(8,128)(2,1)} %gather.2) | copy-start | bytes 4718596
  586.8 9.8 %copy-start.2 = (bf16[512,1024]{1,0:T(8,128)(2,1)S(1)}, bf16[512,1024]{1,0:T(8,128)(2,1)}, u32[]{:S(2)}) copy-start(bf16[512,1024]{1,0:T(8,128)(2,1)} %shard_map.296.p_ref) | copy-start | bytes 3145732
  600.1 68.8 %copy-start.15 = (bf16[1,96,1152]{2,1,0:T(8,128)(2,1)S(1)}, bf16[1,96,1152]{2,1,0:T(8,128)(2,1)}, u32[]{:S(2)}) copy-start(bf16[1,96,1152]{2,1,0:T(8,128)(2,1)} %get-tuple-element.123) | copy-start | bytes 663556
  668.9 16.0 %copy-start.11 = (f32[256,1536]{1,0:T(8,128)S(1)}, f32[256,1536]{1,0:T(8,128)}, u32[]{:S(2)}) copy-start(f32[256,1536]{1,0:T(8,128)} %get-tuple-element.158) | copy-start | bytes 4718596
  668.9 9.3 %collective-permute-start.5 = (bf16[1,96,1152]{2,1,0:T(8,128)(2,1)S(1)}, bf16[1,96,1152]{2,1,0:T(8,128)(2,1)S(1)}, u32[]{:S(2)}, u32[]{:S(2)}) collective-permute-start(bf16[1,96,1152]{2,1,0:T(8,128)(2,1)S(1)} %copy-done.15), channel_id=1, source_target_pairs={{0,6},{2,0},{4,2},{6,4},{1,7},{3,1},{5,3},{7,5},{8,14},{10,8},{12,... | collective-permute-start | bytes 663560 | tf_op jit(solution)/shard_map/ppermute | solution.py:55
  678.1 0.7 copy-start.14
Sparse Core Ops, SparseCore 0:
  80.5 46.7 all-gather.3
  129.1 46.9 all-gather.5
  178.0 47.1 all-gather.7
  405.2 47.5 reduce-scatter.13
  455.7 47.1 reduce-scatter.11
  505.9 47.1 reduce-scatter.5
  556.2 37.3 reduce-scatter.7
  595.8 27.2 reduce-scatter.9
